TPU v7x, 256 devices: a whole 4x4x8 slice. The times are simulated.
256 devices in a mesh: gx: 16 (over z, y_hi), gy: 4 (over y_lo, core), gz: 4 (over x).
Axes of the slice: x: 4, y: 4 (y_hi: 2, y_lo: 2; y = y_hi * 2 + y_lo), z: 8, core: 2. Of those that a mesh axis runs over, the one named last changes fastest.
Arguments:
- node_feat: bfloat16 [128, 32, 32, 128], P('gx', 'gy', 'gz'), may hold values from -6 to 6
- edge_feat: bfloat16 [4, 128, 32, 32, 128], P(None, 'gx', 'gy', 'gz'), may hold values from -6 to 6
- copies: int32 [128, 32, 32], P('gx', 'gy', 'gz'), may hold values from 1 to 8
- offsets: int32 [4, 3], replicated, may hold values from -1 to 1
- w_edge_in: bfloat16 [384, 128], replicated, may hold values from -0.3125 to 0.3125
- w_edge_out: bfloat16 [128, 128], replicated, may hold values from -0.5 to 0.5
- w_node_in: bfloat16 [256, 128], replicated, may hold values from -0.375 to 0.375
- w_node_out: bfloat16 [128, 128], replicated, may hold values from -0.5 to 0.5
- node_cot: bfloat16 [128, 32, 32, 128], P('gx', 'gy', 'gz'), may hold values from -6 to 6
Outputs:
- node_grad: bfloat16 [128, 32, 32, 128], P('gx', 'gy', 'gz')
- edge_grad: bfloat16 [4, 128, 32, 32, 128], P(None, 'gx', 'gy', 'gz')
- grad_edge_in: float32 [384, 128], replicated
- grad_edge_out: float32 [128, 128], replicated
- grad_node_in: float32 [256, 128], replicated
- grad_node_out: float32 [128, 128], replicated
Inputs may be any that keep to these rules, and one draw needn't show every extreme that they name: `offsets`: each row is one lattice offset, its three entries along the first, second and third dimension.
All inputs are finite; a program needn't handle non-finite values.
Results may differ from a plain program's by a relative error of at most 0.0068.
Values sent between devices are 32-bit elements; how exact they have to be, the bound alone decides.
No kernel may reach another device: no remote copies, remote signals or barrier semaphores. Data moves between devices by JAX's collectives and lax.ppermute only.
A program may use at most 64 MiB of HBM per device.

v0:
```python
import math

import jax
import jax.numpy as jnp
from jax import lax
from jax.sharding import PartitionSpec as P


def extended(block, sides, width):
    for axis, dim in sides:
        count = lax.axis_size(axis)
        forward = [(i, i + 1) for i in range(count - 1)]
        backward = [(target, source) for source, target in forward]
        low = lax.ppermute(
            lax.slice_in_dim(block, block.shape[dim] - width, None, axis=dim), axis, forward
        )
        high = lax.ppermute(lax.slice_in_dim(block, 0, width, axis=dim), axis, backward)
        block = jnp.concatenate([low, block, high], axis=dim)
    return block


def in_one(arrays, axis):
    line, at, done = (jnp.concatenate([a.reshape(-1) for a in arrays]), 0, [])
    total = lax.psum(line, axis)
    for a in arrays:
        done.append(total[at : at + a.size].reshape(a.shape))
        at += a.size
    return tuple(done)


def neighbour_valid(offset, brick):
    coords = jnp.arange(brick, dtype=jnp.int32)
    inside = [
        (coords + offset[which] >= 0) & (coords + offset[which] < brick) for which in range(3)
    ]
    joined = inside[0][:, None, None] & inside[1][None, :, None] & inside[2][None, None, :]
    return joined.astype(jnp.float32).reshape(brick * brick * brick, 1)


def moved_view(field, corner):
    padded = jnp.pad(field, ((1, 1), (1, 1), (1, 1), (0, 0)))
    start = 1 + corner
    return lax.dynamic_slice(padded, (start[0], start[1], start[2], jnp.int32(0)), field.shape)


def silu_slope(preact):
    sigma = jax.nn.sigmoid(preact)
    return sigma * (1.0 + preact * (1.0 - sigma))


def outer_product(left, right):
    return lax.dot_general(
        left, right, (((0,), (0,)), ((), ())), preferred_element_type=jnp.float32
    )


def edge_preact(sender, receiver, feature, w_edge_in, width):
    total = jnp.dot(sender, w_edge_in[:width], preferred_element_type=jnp.float32)
    total = total + jnp.dot(
        receiver, w_edge_in[width : 2 * width], preferred_element_type=jnp.float32
    )
    return total + jnp.dot(feature, w_edge_in[2 * width :], preferred_element_type=jnp.float32)


def edge_messages(nodes, edges, offsets, w_edge_in, w_edge_out):
    brick = nodes.shape[0]
    width = nodes.shape[3]
    count = brick * brick * brick
    receiver = nodes.reshape(count, width)
    total = jnp.zeros((count, width), jnp.float32)
    preacts = []
    hiddens = []
    for kind_index in range(edges.shape[0]):
        offset = offsets[kind_index]
        sender = moved_view(nodes, offset).reshape(count, width)
        preact = edge_preact(
            sender, receiver, edges[kind_index].reshape(count, width), w_edge_in, width
        )
        hidden = jax.nn.silu(preact).astype(jnp.bfloat16)
        message = jnp.dot(hidden, w_edge_out, preferred_element_type=jnp.float32)
        total = total + neighbour_valid(offset, brick) * message
        preacts.append(preact)
        hiddens.append(hidden)
    return (total.reshape(nodes.shape), preacts, hiddens)


def node_backward(nodes, summed, copies, node_cot, w_node_in, w_node_out):
    width = nodes.shape[3]
    count = nodes.shape[0] * nodes.shape[1] * nodes.shape[2]
    receiver = nodes.reshape(count, width)
    scale = copies.reshape(count, 1).astype(jnp.float32)
    gathered = (summed.reshape(count, width) / scale).astype(jnp.bfloat16)
    preact = jnp.dot(receiver, w_node_in[:width], preferred_element_type=jnp.float32)
    preact = preact + jnp.dot(gathered, w_node_in[width:], preferred_element_type=jnp.float32)
    hidden = jax.nn.silu(preact).astype(jnp.bfloat16)
    upstream = node_cot.reshape(count, width)
    grad_out = outer_product(hidden, upstream)
    slope = (
        jnp.dot(upstream, w_node_out.T, preferred_element_type=jnp.float32) * silu_slope(preact)
    ).astype(jnp.bfloat16)
    grad_in = jnp.concatenate(
        [outer_product(receiver, slope), outer_product(gathered, slope)], axis=0
    )
    to_nodes = jnp.dot(slope, w_node_in[:width].T, preferred_element_type=jnp.float32)
    to_agg = jnp.dot(slope, w_node_in[width:].T, preferred_element_type=jnp.float32) / scale
    return (to_nodes.reshape(nodes.shape), to_agg.reshape(nodes.shape), grad_in, grad_out)


def edge_backward(nodes, edges, offsets, incoming, w_edge_in, w_edge_out, preacts, hiddens):
    brick = nodes.shape[0]
    width = nodes.shape[3]
    count = brick * brick * brick
    receiver = nodes.reshape(count, width)
    arriving = incoming.reshape(count, width)
    grad_in = jnp.zeros((3 * width, width), jnp.float32)
    grad_out = jnp.zeros((width, width), jnp.float32)
    to_nodes = jnp.zeros((count, width), jnp.float32)
    sent_back = jnp.zeros(nodes.shape, jnp.float32)
    edge_grads = []
    for kind_index in range(edges.shape[0]):
        offset = offsets[kind_index]
        sender = moved_view(nodes, offset).reshape(count, width)
        feature = edges[kind_index].reshape(count, width)
        message_cot = (neighbour_valid(offset, brick) * arriving).astype(jnp.bfloat16)
        grad_out = grad_out + outer_product(hiddens[kind_index], message_cot)
        slope = jnp.dot(message_cot, w_edge_out.T, preferred_element_type=jnp.float32) * silu_slope(
            preacts[kind_index]
        )
        slope = slope.astype(jnp.bfloat16)
        grad_in = grad_in + jnp.concatenate(
            [
                outer_product(sender, slope),
                outer_product(receiver, slope),
                outer_product(feature, slope),
            ],
            axis=0,
        )
        to_nodes = to_nodes + jnp.dot(
            slope, w_edge_in[width : 2 * width].T, preferred_element_type=jnp.float32
        )
        from_sender = jnp.dot(
            slope, w_edge_in[:width].T, preferred_element_type=jnp.float32
        ).reshape(nodes.shape)
        sent_back = sent_back + moved_view(from_sender, -offset)
        edge_grads.append(
            jnp.dot(slope, w_edge_in[2 * width :].T, preferred_element_type=jnp.float32)
            .astype(jnp.bfloat16)
            .reshape(nodes.shape)
        )
    return (to_nodes.reshape(nodes.shape) + sent_back, jnp.stack(edge_grads), grad_in, grad_out)


def clip_all(grads):
    squares = sum((jnp.sum(single * single) for single in grads))
    entries = sum((single.size for single in grads))
    factor = math.sqrt(entries) / jnp.sqrt(squares)
    return tuple((single * factor for single in grads))


def rim_planes(field, which):
    depth = field.shape[which]
    lower = lax.slice_in_dim(field, 0, 1, axis=which)
    upper = lax.slice_in_dim(field, depth - 1, depth, axis=which)
    return (lower, upper)


def joined_rims(field, which, lower, upper, before, after):
    depth = field.shape[which]
    middle = lax.slice_in_dim(field, 1, depth - 1, axis=which)
    return jnp.concatenate([lower + before, middle, upper + after], axis=which)


def fold_rims(padded, which):
    depth = padded.shape[which]
    first = lax.slice_in_dim(padded, 0, 1, axis=which)
    last = lax.slice_in_dim(padded, depth - 1, depth, axis=which)
    inner = lax.slice_in_dim(padded, 1, depth - 1, axis=which)
    lower, upper = rim_planes(inner, which)
    return joined_rims(inner, which, lower, upper, first, last)


def assemble(field):
    padded = extended(field, (("gx", 0), ("gy", 1), ("gz", 2)), 1)
    for which in range(3):
        padded = fold_rims(padded, which)
    return padded


def on_device(
    node_feat, edge_feat, copies, offsets, w_edge_in, w_edge_out, w_node_in, w_node_out, node_cot
):
    local_sum, preacts, hiddens = edge_messages(
        node_feat, edge_feat, offsets, w_edge_in, w_edge_out
    )
    summed = assemble(local_sum)
    node_part, agg_part, node_in_grad, node_out_grad = node_backward(
        node_feat, summed, copies, node_cot, w_node_in, w_node_out
    )
    incoming = assemble(agg_part)
    edge_part, edge_grad, edge_in_grad, edge_out_grad = edge_backward(
        node_feat, edge_feat, offsets, incoming, w_edge_in, w_edge_out, preacts, hiddens
    )
    edge_in_grad, edge_out_grad, node_in_grad, node_out_grad = in_one(
        (edge_in_grad, edge_out_grad, node_in_grad, node_out_grad), ("gx", "gy", "gz")
    )
    local = node_cot.astype(jnp.float32) + node_part + edge_part
    node_grad = assemble(local).astype(jnp.bfloat16)
    clipped = clip_all((edge_in_grad, edge_out_grad, node_in_grad, node_out_grad))
    return (node_grad, edge_grad, clipped[0], clipped[1], clipped[2], clipped[3])


def solution(mesh):
    placed = (
        P("gx", "gy", "gz", None),
        P(None, "gx", "gy", "gz", None),
        P("gx", "gy", "gz"),
        P(),
        P(),
        P(),
        P(),
        P(),
        P("gx", "gy", "gz", None),
    )
    return jax.shard_map(
        on_device,
        mesh=mesh,
        in_specs=placed,
        out_specs=(P("gx", "gy", "gz", None), P(None, "gx", "gy", "gz", None), P(), P(), P(), P()),
        check_vma=False,
    )
```

profile of v0, /device:TPU:1, one launch (start us, length us, event | category | flops | bytes accessed | tf_op | source)
XLA Modules:
  0.0 423.0 jit_solution(17790856029961947640)
XLA Ops:
  7.2 0.8 negate_add_fusion
  8.1 0.6 fusion.65
  16.4 0.7 fusion.67
  24.4 0.7 fusion.60
  25.1 1.3 compare_and_fusion.8
  26.3 1.3 compare_and_fusion.10
  27.8 1.2 compare_and_fusion.6
  29.3 1.4 compare_and_fusion.2
  30.7 1.3 compare_and_fusion.4
  32.2 1.2 compare_and_fusion
  41.5 0.4 pad_dynamic-slice_fusion.4
  42.6 0.7 copy-done.4
  44.9 5.6 %collective-permute-start = (f32[1,8,8,128]{3,2,1,0:T(8,128)S(1)}, f32[1,8,8,128]{3,2,1,0:T(8,128)S(1)}, u32[]{:S(2)}, u32[]{:S(2)}) collective-permute-start(f32[1,8,8,128]{3,2,1,0:T(8,128)S(1)} %get-tuple-element.44), channel_id=1, source_target_pairs={{0,16},{16,32},{32,48},{48,64},{64,80},{80,96},{96,112},{112,128},... | collective-permute-start | bytes 98312 | tf_op jit(solution)/shard_map/ppermute | solution.py:14
  50.5 1.3 collective-permute-start.1
  52.0 4.7 %collective-permute-done.1 = f32[1,8,8,128]{3,2,1,0:T(8,128)S(1)} collective-permute-done((f32[1,8,8,128]{3,2,1,0:T(8,128)S(1)}, f32[1,8,8,128]{3,2,1,0:T(8,128)S(1)}, u32[]{:S(2)}, u32[]{:S(2)}) %collective-permute-start.1) | collective-permute-done | bytes 32800 | tf_op jit(solution)/shard_map/ppermute | solution.py:17
  56.7 4.3 %collective-permute-start.2 = (f32[10,1,8,128]{3,2,1,0:T(8,128)S(1)}, f32[10,1,8,128]{3,2,1,0:T(8,128)S(1)}, u32[]{:S(2)}, u32[]{:S(2)}) collective-permute-start(f32[10,1,8,128]{3,2,1,0:T(8,128)S(1)} %get-tuple-element.34), channel_id=1, source_target_pairs={{0,4},{4,8},{8,12},{1,5},{5,9},{9,13},{2,6},{6,10},{10,14},{3,7},{... | collective-permute-start | bytes 122888 | tf_op jit(solution)/shard_map/ppermute | solution.py:14
  61.0 1.9 collective-permute-start.3
  62.9 0.7 fusion.61
  63.6 2.7 collective-permute-done.3
  66.4 3.1 collective-permute-start.4
  69.5 1.3 collective-permute-start.5
  70.8 0.6 fusion.63
  95.1 0.7 copy-done.6
  96.2 0.2 convolution_bitcast_fusion.1
  96.7 5.7 %collective-permute-start.6 = (f32[1,8,8,128]{3,2,1,0:T(8,128)S(1)}, f32[1,8,8,128]{3,2,1,0:T(8,128)S(1)}, u32[]{:S(2)}, u32[]{:S(2)}) collective-permute-start(f32[1,8,8,128]{3,2,1,0:T(8,128)S(1)} %get-tuple-element.42), channel_id=1, source_target_pairs={{0,16},{16,32},{32,48},{48,64},{64,80},{80,96},{96,112},{112,128},... | collective-permute-start | bytes 98312 | tf_op jit(solution)/shard_map/ppermute | solution.py:14
  102.4 1.3 collective-permute-start.7
  103.8 4.8 %collective-permute-done.7 = f32[1,8,8,128]{3,2,1,0:T(8,128)S(1)} collective-permute-done((f32[1,8,8,128]{3,2,1,0:T(8,128)S(1)}, f32[1,8,8,128]{3,2,1,0:T(8,128)S(1)}, u32[]{:S(2)}, u32[]{:S(2)}) %collective-permute-start.7) | collective-permute-done | bytes 32800 | tf_op jit(solution)/shard_map/ppermute | solution.py:17
  108.6 3.0 collective-permute-start.8
  111.6 1.9 collective-permute-start.9
  113.7 3.2 collective-permute-done.9
  117.0 4.3 %collective-permute-start.10 = (f32[10,10,1,128]{3,2,1,0:T(1,128)S(1)}, f32[10,10,1,128]{3,2,1,0:T(1,128)S(1)}, u32[]{:S(2)}, u32[]{:S(2)}) collective-permute-start(f32[10,10,1,128]{3,2,1,0:T(1,128)S(1)} %get-tuple-element.26), channel_id=1, source_target_pairs={{0,1},{1,2},{2,3},{4,5},{5,6},{6,7},{8,9},{9,10},{10,11},{12,13},{... | collective-permute-start | bytes 153608 | tf_op jit(solution)/shard_map/ppermute | solution.py:14
  121.3 1.3 collective-permute-start.11
  122.6 0.3 convolution_bitcast_fusion
  122.8 3.3 collective-permute-done.11
  126.8 0.3 fusion.17
  127.3 0.2 convolution_bitcast_fusion.8
  128.2 0.2 convolution_bitcast_fusion.6
  128.9 0.2 convolution_bitcast_fusion.4
  129.6 0.2 convolution_bitcast_fusion.2
  130.0 0.2 convolution_bitcast_fusion.3
  130.3 0.2 convolution_bitcast_fusion.5
  132.3 0.3 convolution_add_fusion.14
  132.6 0.3 convolution_add_fusion.13
  132.9 0.3 fusion.8
  133.7 0.4 fusion.13
  134.1 4.5 %collective-permute-start.12 = (f32[1,8,8,128]{3,2,1,0:T(8,128)S(1)}, f32[1,8,8,128]{3,2,1,0:T(8,128)S(1)}, u32[]{:S(2)}, u32[]{:S(2)}) collective-permute-start(f32[1,8,8,128]{3,2,1,0:T(8,128)S(1)} %get-tuple-element.36), channel_id=1, source_target_pairs={{0,16},{16,32},{32,48},{48,64},{64,80},{80,96},{96,112},{112,128},... | collective-permute-start | bytes 98312 | tf_op jit(solution)/shard_map/ppermute | solution.py:14
  138.6 1.3 collective-permute-start.13
  140.0 0.8 pad_maximum_fusion.10
  141.0 4.4 %collective-permute-done.13 = f32[1,8,8,128]{3,2,1,0:T(8,128)S(1)} collective-permute-done((f32[1,8,8,128]{3,2,1,0:T(8,128)S(1)}, f32[1,8,8,128]{3,2,1,0:T(8,128)S(1)}, u32[]{:S(2)}, u32[]{:S(2)}) %collective-permute-start.13) | collective-permute-done | bytes 32800 | tf_op jit(solution)/shard_map/ppermute | solution.py:17
  145.4 3.5 collective-permute-start.14
  148.9 1.9 collective-permute-start.15
  151.1 3.2 collective-permute-done.15
  154.3 3.1 collective-permute-start.16
  157.5 1.3 collective-permute-start.17
  158.8 0.9 pad_maximum_fusion.9
  159.6 2.7 collective-permute-done.17
  162.9 0.8 pad_maximum_fusion.13
  163.7 243.1 %all-reduce.7.cloned.1.call-done = f32[114688]{0:T(1024)} async-done(((f32[114688]{0:T(1024)}), f32[114688]{0:T(1024)}) %all-reduce.7.cloned.1.call-update) | async-done | bytes 458768 | tf_op jit(solution)/shard_map/psum | solution.py:24
  406.8 1.7 multiply_reduce_fusion
  408.4 1.5 multiply_reduce_fusion.2
  411.2 1.5 multiply_reduce_fusion.1
  414.1 0.7 multiply_bitcast_fusion.1
  414.8 0.7 multiply_bitcast_fusion.2
  415.4 0.7 multiply_bitcast_fusion
  (132 shorter events, 11.4 us)
Async XLA Ops:
  7.2 36.9 %copy-start = (bf16[128,128]{1,0:T(8,128)(2,1)S(1)}, bf16[128,128]{1,0:T(8,128)(2,1)}, u32[]{:S(2)}) copy-start(bf16[128,128]{1,0:T(8,128)(2,1)} %param.14) | copy-start | bytes 98308
  7.2 399.6 %all-reduce.7.cloned.1.call-start = ((), (), s32[]{:S(2)}) async-start(), calls=%async_computation | async-start | bytes 917504 | tf_op jit(solution)/shard_map/psum | solution.py:24
  23.2 1.1 copy-start.7
  29.2 12.1 %copy-start.1 = (bf16[8,8,8,128]{3,2,1,0:T(8,128)(2,1)S(1)}, bf16[8,8,8,128]{3,2,1,0:T(8,128)(2,1)}, u32[]{:S(2)}) copy-start(bf16[8,8,8,128]{3,2,1,0:T(8,128)(2,1)} %param.9) | copy-start | bytes 393220
  30.7 10.6 %copy-start.2 = (bf16[384,128]{1,0:T(8,128)(2,1)S(1)}, bf16[384,128]{1,0:T(8,128)(2,1)}, u32[]{:S(2)}) copy-start(bf16[384,128]{1,0:T(8,128)(2,1)} %param.13) | copy-start | bytes 294916
  42.2 1.0 copy-start.4
  44.9 7.0 %copy-start.5 = (bf16[256,128]{1,0:T(8,128)(2,1)S(1)}, bf16[256,128]{1,0:T(8,128)(2,1)}, u32[]{:S(2)}) copy-start(bf16[256,128]{1,0:T(8,128)(2,1)} %param.15) | copy-start | bytes 196612
  44.9 7.1 %collective-permute-start = (f32[1,8,8,128]{3,2,1,0:T(8,128)S(1)}, f32[1,8,8,128]{3,2,1,0:T(8,128)S(1)}, u32[]{:S(2)}, u32[]{:S(2)}) collective-permute-start(f32[1,8,8,128]{3,2,1,0:T(8,128)S(1)} %get-tuple-element.44), channel_id=1, source_target_pairs={{0,16},{16,32},{32,48},{48,64},{64,80},{80,96},{96,112},{112,128},... | collective-permute-start | bytes 98312 | tf_op jit(solution)/shard_map/ppermute | solution.py:14
  50.5 6.2 %collective-permute-start.1 = (f32[1,8,8,128]{3,2,1,0:T(8,128)S(1)}, f32[1,8,8,128]{3,2,1,0:T(8,128)S(1)}, u32[]{:S(2)}, u32[]{:S(2)}) collective-permute-start(f32[1,8,8,128]{3,2,1,0:T(8,128)S(1)} %get-tuple-element.45), channel_id=1, source_target_pairs={{16,0},{32,16},{48,32},{64,48},{80,64},{96,80},{112,96},{128,112},... | collective-permute-start | bytes 98312 | tf_op jit(solution)/shard_map/ppermute | solution.py:17
  56.7 6.9 %collective-permute-start.2 = (f32[10,1,8,128]{3,2,1,0:T(8,128)S(1)}, f32[10,1,8,128]{3,2,1,0:T(8,128)S(1)}, u32[]{:S(2)}, u32[]{:S(2)}) collective-permute-start(f32[10,1,8,128]{3,2,1,0:T(8,128)S(1)} %get-tuple-element.34), channel_id=1, source_target_pairs={{0,4},{4,8},{8,12},{1,5},{5,9},{9,13},{2,6},{6,10},{10,14},{3,7},{... | collective-permute-start | bytes 122888 | tf_op jit(solution)/shard_map/ppermute | solution.py:14
  61.0 5.3 %collective-permute-start.3 = (f32[10,1,8,128]{3,2,1,0:T(8,128)S(1)}, f32[10,1,8,128]{3,2,1,0:T(8,128)S(1)}, u32[]{:S(2)}, u32[]{:S(2)}) collective-permute-start(f32[10,1,8,128]{3,2,1,0:T(8,128)S(1)} %get-tuple-element.35), channel_id=1, source_target_pairs={{4,0},{8,4},{12,8},{5,1},{9,5},{13,9},{6,2},{10,6},{14,10},{7,3},{... | collective-permute-start | bytes 122888 | tf_op jit(solution)/shard_map/ppermute | solution.py:17
  66.4 27.7 %collective-permute-start.4 = (f32[10,10,1,128]{3,2,1,0:T(1,128)S(1)}, f32[10,10,1,128]{3,2,1,0:T(1,128)S(1)}, u32[]{:S(2)}, u32[]{:S(2)}) collective-permute-start(f32[10,10,1,128]{3,2,1,0:T(1,128)S(1)} %get-tuple-element.28), channel_id=1, source_target_pairs={{0,1},{1,2},{2,3},{4,5},{5,6},{6,7},{8,9},{9,10},{10,11},{12,13},{... | collective-permute-start | bytes 153608 | tf_op jit(solution)/shard_map/ppermute | solution.py:14
  69.5 24.6 %collective-permute-start.5 = (f32[10,10,1,128]{3,2,1,0:T(1,128)S(1)}, f32[10,10,1,128]{3,2,1,0:T(1,128)S(1)}, u32[]{:S(2)}, u32[]{:S(2)}) collective-permute-start(f32[10,10,1,128]{3,2,1,0:T(1,128)S(1)} %get-tuple-element.29), channel_id=1, source_target_pairs={{1,0},{2,1},{3,2},{5,4},{6,5},{7,6},{9,8},{10,9},{11,10},{13,12},{... | collective-permute-start | bytes 153608 | tf_op jit(solution)/shard_map/ppermute | solution.py:17
  75.1 11.4 %copy-start.8 = (s32[8,8,8]{2,1,0:T(8,128)S(1)}, s32[8,8,8]{2,1,0:T(8,128)}, u32[]{:S(2)}) copy-start(s32[8,8,8]{2,1,0:T(8,128)} %param.11) | copy-start | bytes 6148
  94.9 0.9 copy-start.6
  94.9 0.9 copy-start.9
  96.7 7.1 %collective-permute-start.6 = (f32[1,8,8,128]{3,2,1,0:T(8,128)S(1)}, f32[1,8,8,128]{3,2,1,0:T(8,128)S(1)}, u32[]{:S(2)}, u32[]{:S(2)}) collective-permute-start(f32[1,8,8,128]{3,2,1,0:T(8,128)S(1)} %get-tuple-element.42), channel_id=1, source_target_pairs={{0,16},{16,32},{32,48},{48,64},{64,80},{80,96},{96,112},{112,128},... | collective-permute-start | bytes 98312 | tf_op jit(solution)/shard_map/ppermute | solution.py:14
  102.4 6.2 %collective-permute-start.7 = (f32[1,8,8,128]{3,2,1,0:T(8,128)S(1)}, f32[1,8,8,128]{3,2,1,0:T(8,128)S(1)}, u32[]{:S(2)}, u32[]{:S(2)}) collective-permute-start(f32[1,8,8,128]{3,2,1,0:T(8,128)S(1)} %get-tuple-element.43), channel_id=1, source_target_pairs={{16,0},{32,16},{48,32},{64,48},{80,64},{96,80},{112,96},{128,112},... | collective-permute-start | bytes 98312 | tf_op jit(solution)/shard_map/ppermute | solution.py:17
  108.6 5.1 %collective-permute-start.8 = (f32[10,1,8,128]{3,2,1,0:T(8,128)S(1)}, f32[10,1,8,128]{3,2,1,0:T(8,128)S(1)}, u32[]{:S(2)}, u32[]{:S(2)}) collective-permute-start(f32[10,1,8,128]{3,2,1,0:T(8,128)S(1)} %get-tuple-element.32), channel_id=1, source_target_pairs={{0,4},{4,8},{8,12},{1,5},{5,9},{9,13},{2,6},{6,10},{10,14},{3,7},{... | collective-permute-start | bytes 122888 | tf_op jit(solution)/shard_map/ppermute | solution.py:14
  111.6 5.3 %collective-permute-start.9 = (f32[10,1,8,128]{3,2,1,0:T(8,128)S(1)}, f32[10,1,8,128]{3,2,1,0:T(8,128)S(1)}, u32[]{:S(2)}, u32[]{:S(2)}) collective-permute-start(f32[10,1,8,128]{3,2,1,0:T(8,128)S(1)} %get-tuple-element.33), channel_id=1, source_target_pairs={{4,0},{8,4},{12,8},{5,1},{9,5},{13,9},{6,2},{10,6},{14,10},{7,3},{... | collective-permute-start | bytes 122888 | tf_op jit(solution)/shard_map/ppermute | solution.py:17
  117.0 5.8 %collective-permute-start.10 = (f32[10,10,1,128]{3,2,1,0:T(1,128)S(1)}, f32[10,10,1,128]{3,2,1,0:T(1,128)S(1)}, u32[]{:S(2)}, u32[]{:S(2)}) collective-permute-start(f32[10,10,1,128]{3,2,1,0:T(1,128)S(1)} %get-tuple-element.26), channel_id=1, source_target_pairs={{0,1},{1,2},{2,3},{4,5},{5,6},{6,7},{8,9},{9,10},{10,11},{12,13},{... | collective-permute-start | bytes 153608 | tf_op jit(solution)/shard_map/ppermute | solution.py:14
  121.3 4.9 %collective-permute-start.11 = (f32[10,10,1,128]{3,2,1,0:T(1,128)S(1)}, f32[10,10,1,128]{3,2,1,0:T(1,128)S(1)}, u32[]{:S(2)}, u32[]{:S(2)}) collective-permute-start(f32[10,10,1,128]{3,2,1,0:T(1,128)S(1)} %get-tuple-element.27), channel_id=1, source_target_pairs={{1,0},{2,1},{3,2},{5,4},{6,5},{7,6},{9,8},{10,9},{11,10},{13,12},{... | collective-permute-start | bytes 153608 | tf_op jit(solution)/shard_map/ppermute | solution.py:17
  134.1 6.9 %collective-permute-start.12 = (f32[1,8,8,128]{3,2,1,0:T(8,128)S(1)}, f32[1,8,8,128]{3,2,1,0:T(8,128)S(1)}, u32[]{:S(2)}, u32[]{:S(2)}) collective-permute-start(f32[1,8,8,128]{3,2,1,0:T(8,128)S(1)} %get-tuple-element.36), channel_id=1, source_target_pairs={{0,16},{16,32},{32,48},{48,64},{64,80},{80,96},{96,112},{112,128},... | collective-permute-start | bytes 98312 | tf_op jit(solution)/shard_map/ppermute | solution.py:14
  138.6 6.8 %collective-permute-start.13 = (f32[1,8,8,128]{3,2,1,0:T(8,128)S(1)}, f32[1,8,8,128]{3,2,1,0:T(8,128)S(1)}, u32[]{:S(2)}, u32[]{:S(2)}) collective-permute-start(f32[1,8,8,128]{3,2,1,0:T(8,128)S(1)} %get-tuple-element.37), channel_id=1, source_target_pairs={{16,0},{32,16},{48,32},{64,48},{80,64},{96,80},{112,96},{128,112},... | collective-permute-start | bytes 98312 | tf_op jit(solution)/shard_map/ppermute | solution.py:17
  145.4 5.7 %collective-permute-start.14 = (f32[10,1,8,128]{3,2,1,0:T(8,128)S(1)}, f32[10,1,8,128]{3,2,1,0:T(8,128)S(1)}, u32[]{:S(2)}, u32[]{:S(2)}) collective-permute-start(f32[10,1,8,128]{3,2,1,0:T(8,128)S(1)} %get-tuple-element.30), channel_id=1, source_target_pairs={{0,4},{4,8},{8,12},{1,5},{5,9},{9,13},{2,6},{6,10},{10,14},{3,7},{... | collective-permute-start | bytes 122888 | tf_op jit(solution)/shard_map/ppermute | solution.py:14
  148.9 5.3 %collective-permute-start.15 = (f32[10,1,8,128]{3,2,1,0:T(8,128)S(1)}, f32[10,1,8,128]{3,2,1,0:T(8,128)S(1)}, u32[]{:S(2)}, u32[]{:S(2)}) collective-permute-start(f32[10,1,8,128]{3,2,1,0:T(8,128)S(1)} %get-tuple-element.31), channel_id=1, source_target_pairs={{4,0},{8,4},{12,8},{5,1},{9,5},{13,9},{6,2},{10,6},{14,10},{7,3},{... | collective-permute-start | bytes 122888 | tf_op jit(solution)/shard_map/ppermute | solution.py:17
  154.3 5.3 %collective-permute-start.16 = (f32[10,10,1,128]{3,2,1,0:T(1,128)S(1)}, f32[10,10,1,128]{3,2,1,0:T(1,128)S(1)}, u32[]{:S(2)}, u32[]{:S(2)}) collective-permute-start(f32[10,10,1,128]{3,2,1,0:T(1,128)S(1)} %get-tuple-element.24), channel_id=1, source_target_pairs={{0,1},{1,2},{2,3},{4,5},{5,6},{6,7},{8,9},{9,10},{10,11},{12,13},{... | collective-permute-start | bytes 153608 | tf_op jit(solution)/shard_map/ppermute | solution.py:14
  157.5 4.9 %collective-permute-start.17 = (f32[10,10,1,128]{3,2,1,0:T(1,128)S(1)}, f32[10,10,1,128]{3,2,1,0:T(1,128)S(1)}, u32[]{:S(2)}, u32[]{:S(2)}) collective-permute-start(f32[10,10,1,128]{3,2,1,0:T(1,128)S(1)} %get-tuple-element.25), channel_id=1, source_target_pairs={{1,0},{2,1},{3,2},{5,4},{6,5},{7,6},{9,8},{10,9},{11,10},{13,12},{... | collective-permute-start | bytes 153608 | tf_op jit(solution)/shard_map/ppermute | solution.py:17
  406.8 7.3 %copy-start.3 = (f32[114688]{0:T(1024)S(1)}, f32[114688]{0:T(1024)}, u32[]{:S(2)}) copy-start(f32[114688]{0:T(1024)} %all-reduce.7.cloned.1.call-done) | copy-start | bytes 1376260
Sparse Core Ops, SparseCore 0:
  151.2 255.5 all-reduce.6
where the time goes:
time: 425 us; the launch traced here: 423 us
  waiting for transfers between devices  272 us (64%)
  between operations  62.9 us (15%)
  starting transfers between devices  50.8 us (12%)
  other arithmetic  20.8 us (5%)
  matrix products  10.7 us (3%)
  local copies, waits for them, and re-layouts  5.83 us (1%)
    psum x1, waiting for transfers between devices, in_one(): total = lax.psum(line, axis)  243 us
    ppermute x9, starting transfers between devices, extended(): lax.ppermute(lax.slice_in_dim(block, block.shape[dim] - width, None, axis...  37.2 us
    ppermute x9, waiting for transfers between devices, extended(): lax.ppermute(lax.slice_in_dim(block, 0, width, axis=dim), axis, backward)  29 us
    ppermute x9, starting transfers between devices, extended(): lax.ppermute(lax.slice_in_dim(block, 0, width, axis=dim), axis, backward)  13.5 us
  transfers between devices with their start and end apart: 19, of which 9 were waited for; matrix products, arithmetic and copies ran while one was open for 1% of the time, Pallas kernels for 0%

commit v1 on v0

v1 whole, which is shorter than its diff:
```python
import functools
import math

import jax
import jax.numpy as jnp
from jax import lax
from jax.experimental import pallas as pl
from jax.experimental.pallas import tpu as pltpu
from jax.sharding import Mesh
from jax.sharding import PartitionSpec as P

B = 8
W = 128
K = 4
N = B * B * B
CUBE = (B, B, B, W)
FACE = (B, B, W)
F32 = jnp.float32
BF16 = jnp.bfloat16

VMEM = pl.BlockSpec(memory_space=pltpu.VMEM)
SMEM = pl.BlockSpec(memory_space=pltpu.SMEM)


def call(body, outs, specs, name, scratch=(), interpret=False):
    return pl.pallas_call(
        body,
        out_shape=[jax.ShapeDtypeStruct(s, t) for s, t in outs],
        in_specs=specs,
        out_specs=[VMEM] * len(outs),
        scratch_shapes=list(scratch),
        name=name,
        interpret=interpret,
    )


def dot(a, b):
    return jnp.dot(a, b, preferred_element_type=F32)


def dot_t(a, b):
    return lax.dot_general(a, b, (((1,), (1,)), ((), ())), preferred_element_type=F32)


def fill_ring(pad, value):
    pad[1:9, 1:9] = value
    pad[0, 1:9] = value[7]
    pad[9, 1:9] = value[0]
    pad[:, 0] = pad[:, 8]
    pad[:, 9] = pad[:, 1]


def ring_shift(pad, o0, o1, o2):
    moved = pad[pl.ds(1 + o0, B), pl.ds(1 + o1, B)].reshape(B * B, B, W)
    moved = pltpu.roll(moved, lax.rem(B - o2, B), 1)
    return moved.reshape(N, W)


def inside(offs, k):
    ok = None
    for which in range(3):
        at = lax.broadcasted_iota(jnp.int32, CUBE, which) + offs[k, which]
        one = (at >= 0) & (at < B)
        ok = one if ok is None else ok & one
    return ok


def forward_kernel(offs, nodes, edges, w_in, w_out, local, xlo, xhi, preact, hidden, pad):
    node = nodes[...]
    fill_ring(pad, dot(node, w_in[:W]).reshape(CUBE))
    receiver = dot(node, w_in[W : 2 * W])
    total = jnp.zeros((N, W), F32)
    for k in range(K):
        pre = ring_shift(pad, offs[k, 0], offs[k, 1], offs[k, 2]) + receiver + dot(edges[k], w_in[2 * W :])
        preact[k] = pre
        act = pre * jax.nn.sigmoid(pre)
        hid = act.astype(BF16)
        hidden[k] = hid
        kept = jnp.where(inside(offs, k), act.reshape(CUBE), 0.0).reshape(N, W).astype(BF16)
        total = total + dot(kept, w_out[...])
    total = total.reshape(CUBE)
    local[...] = total
    xlo[...] = total[0]
    xhi[...] = total[B - 1]


def prepare_kernel(preact, hidden, nodes, edges, dact, hidden_t, edges_t, nodes_t):
    for k in range(K):
        pre = preact[k]
        sigma = jax.nn.sigmoid(pre)
        dact[k] = sigma * (1.0 + pre * (1.0 - sigma))
        hidden_t[k] = hidden[k].T
        edges_t[k] = edges[k].T
    nodes_t[...] = nodes[...].T


def after_x_kernel(rim, field, rlo, rhi, out, lo, hi):
    out[1 : B - 1] = field[1 : B - 1]
    out[0] = field[0] + jnp.where(rim[0] > 0, rlo[...], 0.0)
    out[B - 1] = field[B - 1] + jnp.where(rim[1] > 0, rhi[...], 0.0)
    lo[...] = out[:, 0]
    hi[...] = out[:, B - 1]


def after_y_kernel(rim, field, rlo, rhi, out, lo, hi):
    out[:, 1 : B - 1] = field[:, 1 : B - 1]
    out[:, 0] = field[:, 0] + jnp.where(rim[2] > 0, rlo[...], 0.0)
    out[:, B - 1] = field[:, B - 1] + jnp.where(rim[3] > 0, rhi[...], 0.0)
    lo[...] = out[:, :, 0, :]
    hi[...] = out[:, :, B - 1, :]


def with_z(rim, field, rlo, rhi, work):
    work[...] = field[...]
    work[:, :, 0, :] = field[:, :, 0, :] + jnp.where(rim[4] > 0, rlo[...], 0.0)
    work[:, :, B - 1, :] = field[:, :, B - 1, :] + jnp.where(rim[5] > 0, rhi[...], 0.0)
    return work[...].reshape(N, W)


def node_kernel(
    rim, field, rlo, rhi, inverse, nodes, cot, w_in, w_out, local, xlo, xhi, gathered, slope, hidden, work
):
    inv = inverse[...]
    agg = (with_z(rim, field, rlo, rhi, work) * inv).astype(BF16)
    gathered[...] = agg
    pre = dot(nodes[...], w_in[:W]) + dot(agg, w_in[W:])
    sigma = jax.nn.sigmoid(pre)
    hidden[...] = (pre * sigma).astype(BF16)
    slo = (dot_t(cot[...], w_out[...]) * (sigma * (1.0 + pre * (1.0 - sigma)))).astype(BF16)
    slope[...] = slo
    part = (dot_t(slo, w_in[W:]) * inv).reshape(CUBE)
    local[...] = part
    xlo[...] = part[0]
    xhi[...] = part[B - 1]


def node_grads_kernel(nodes_t, gathered, slope, hidden, cot, w_in, grads, base):
    slo = slope[...]
    grads[:W] = dot(nodes_t[...], slo)
    grads[W : 2 * W] = dot(gathered[...].T, slo)
    grads[2 * W :] = dot(hidden[...].T, cot[...])
    base[...] = cot[...].astype(F32) + dot_t(slo, w_in[:W])


def edge_kernel(
    rim, offs, field, rlo, rhi, dact, hidden_t, edges_t, nodes_t, base, node_grads, w_in, w_out,
    local, xlo, xhi, slopes, grads, work, pad,
):
    agg = with_z(rim, field, rlo, rhi, work).reshape(CUBE)
    node_t = nodes_t[...]
    part = base[...]
    g_send = jnp.zeros((W, W), F32)
    g_recv = jnp.zeros((W, W), F32)
    g_edge = jnp.zeros((W, W), F32)
    g_out = jnp.zeros((W, W), F32)
    for k in range(K):
        cot = jnp.where(inside(offs, k), agg, 0.0).reshape(N, W).astype(BF16)
        g_out = g_out + dot(hidden_t[k], cot)
        slo = (dot_t(cot, w_out[...]) * dact[k]).astype(BF16)
        slopes[k] = slo
        fill_ring(pad, slo.astype(F32).reshape(CUBE))
        sent = ring_shift(pad, -offs[k, 0], -offs[k, 1], -offs[k, 2]).astype(BF16)
        g_send = g_send + dot(node_t, sent)
        g_recv = g_recv + dot(node_t, slo)
        g_edge = g_edge + dot(edges_t[k], slo)
        part = part + dot_t(slo, w_in[W : 2 * W]) + dot_t(sent, w_in[:W])
    grads[:W] = g_send
    grads[W : 2 * W] = g_recv
    grads[2 * W : 3 * W] = g_edge
    grads[3 * W : 4 * W] = g_out
    grads[4 * W :] = node_grads[...]
    part = part.reshape(CUBE)
    local[...] = part
    xlo[...] = part[0]
    xhi[...] = part[B - 1]


def edge_grad_kernel(slopes, w_in, out):
    for k in range(K):
        out[k] = dot_t(slopes[k], w_in[2 * W :]).astype(BF16)


def last_kernel(rim, field, rlo, rhi, out, work):
    out[...] = with_z(rim, field, rlo, rhi, work).astype(BF16)


def pair_sum(ref, rows, pairs):
    total = ref[: 2 * rows]
    for i in range(1, pairs):
        total = total + ref[2 * rows * i : 2 * rows * (i + 1)]
    return total + jnp.concatenate([total[rows:], total[:rows]], axis=0)


def fold_kernel(rows, pairs, copies, arrived, out):
    total = pair_sum(arrived, rows, pairs)
    for i in range(copies):
        out[2 * rows * i : 2 * rows * (i + 1)] = total


def clip_kernel(grads, edge_in, edge_out, node_in, node_out):
    total = grads[...]
    squares = jnp.sum(jnp.sum(total * total, axis=0, keepdims=True), axis=1, keepdims=True)
    factor = math.sqrt(7 * W * W) / jnp.sqrt(squares)
    edge_in[...] = total[: 3 * W] * factor
    edge_out[...] = total[3 * W : 4 * W] * factor
    node_in[...] = total[4 * W : 6 * W] * factor
    node_out[...] = total[6 * W :] * factor


GX, GY, GZ = ("z", "yh"), ("yl", "c"), ("x",)
NEAR, FAR = ("yh", "yl", "c", "x"), ("z",)


def exchange(lo, hi, axis):
    count = lax.axis_size(axis)
    up = [(i, (i + 1) % count) for i in range(count)]
    down = [(t, s) for s, t in up]
    return lax.ppermute(hi, axis, up), lax.ppermute(lo, axis, down)


def assemble(rim, field, xlo, xhi, tag, interpret):
    rlo, rhi = exchange(xlo, xhi, GX)
    step = [(CUBE, F32), (FACE, F32), (FACE, F32)]
    field, lo, hi = call(after_x_kernel, step, [SMEM] + [VMEM] * 3, "after_x" + tag, interpret=interpret)(
        rim, field, rlo, rhi
    )
    rlo, rhi = exchange(lo, hi, GY)
    field, lo, hi = call(after_y_kernel, step, [SMEM] + [VMEM] * 3, "after_y" + tag, interpret=interpret)(
        rim, field, rlo, rhi
    )
    rlo, rhi = exchange(lo, hi, GZ)
    return field, rlo, rhi


def swap(rows, axes, count):
    return lax.all_to_all(rows.reshape(count, -1), axes, 0, 0, tiled=True).reshape(-1, W)


def reduce_all(grads, interpret):
    near, far = lax.axis_size(NEAR), lax.axis_size(FAR)
    rows = grads.shape[0] // near
    got = swap(grads, NEAR, near)
    (got,) = call(
        functools.partial(fold_kernel, rows, near // 2, far // 2), [((rows * far, W), F32)], [VMEM], "fold_near",
        interpret=interpret,
    )(got)
    got = swap(got, FAR, far)
    (got,) = call(
        functools.partial(fold_kernel, rows, far // 2, near // 2), [((rows * near, W), F32)], [VMEM], "fold_far",
        interpret=interpret,
    )(got)
    return swap(got, NEAR, near)


def on_device(
    node_feat, edge_feat, copies, offsets, w_edge_in, w_edge_out, w_node_in, w_node_out, node_cot, interpret=False
):
    ends = []
    for axis in (GX, GY, GZ):
        at = lax.axis_index(axis)
        ends += [at > 0, at < lax.axis_size(axis) - 1]
    rim = jnp.stack(ends).astype(jnp.int32)
    nodes = node_feat.reshape(N, W)
    edges = edge_feat.reshape(K, N, W)
    cot = node_cot.reshape(N, W)
    inverse = jnp.broadcast_to(1.0 / copies.reshape(N, 1).astype(F32), (N, W))
    cube = [(CUBE, F32), (FACE, F32), (FACE, F32)]
    pad = pltpu.VMEM((B + 2, B + 2, B, W), F32)
    work = pltpu.VMEM(CUBE, F32)
    run = functools.partial(call, interpret=interpret)

    local, xlo, xhi, preact, hidden = run(
        forward_kernel, cube + [((K, N, W), F32), ((K, N, W), BF16)], [SMEM] + [VMEM] * 4, "forward", [pad]
    )(offsets, nodes, edges, w_edge_in, w_edge_out)
    field, rlo, rhi = assemble(rim, local, xlo, xhi, "_1", interpret)
    dact, hidden_t, edges_t, nodes_t = run(
        prepare_kernel,
        [((K, N, W), F32), ((K, W, N), BF16), ((K, W, N), BF16), ((W, N), BF16)],
        [VMEM] * 4,
        "prepare",
    )(preact, hidden, nodes, edges)
    local, xlo, xhi, gathered, slope, node_hidden = run(
        node_kernel, cube + [((N, W), BF16)] * 3, [SMEM] + [VMEM] * 8, "node", [work]
    )(rim, field, rlo, rhi, inverse, nodes, cot, w_node_in, w_node_out)
    field, rlo, rhi = assemble(rim, local, xlo, xhi, "_2", interpret)
    node_grads, base = run(
        node_grads_kernel, [((3 * W, W), F32), ((N, W), F32)], [VMEM] * 6, "node_grads"
    )(nodes_t, gathered, slope, node_hidden, cot, w_node_in)
    local, xlo, xhi, slopes, grads = run(
        edge_kernel,
        cube + [((K, N, W), BF16), ((7 * W, W), F32)],
        [SMEM] * 2 + [VMEM] * 11,
        "edge",
        [work, pad],
    )(rim, offsets, field, rlo, rhi, dact, hidden_t, edges_t, nodes_t, base, node_grads, w_edge_in, w_edge_out)
    total = reduce_all(grads, interpret)
    field, rlo, rhi = assemble(rim, local, xlo, xhi, "_3", interpret)
    (edge_grad,) = run(edge_grad_kernel, [((K, N, W), BF16)], [VMEM] * 2, "edge_grad")(slopes, w_edge_in)
    (node_grad,) = run(last_kernel, [((N, W), BF16)], [SMEM] + [VMEM] * 3, "last", [work])(rim, field, rlo, rhi)
    clipped = run(
        clip_kernel, [((3 * W, W), F32), ((W, W), F32), ((2 * W, W), F32), ((W, W), F32)], [VMEM], "clip"
    )(total)
    return (node_grad.reshape(node_feat.shape), edge_grad.reshape(edge_feat.shape), *clipped)


def solution(mesh):
    split = Mesh(mesh.devices.reshape(8, 2, 2, 2, 4), ("z", "yh", "yl", "c", "x"))
    place = (GX, GY, GZ)
    placed = (
        P(*place, None),
        P(None, *place, None),
        P(*place),
        P(),
        P(),
        P(),
        P(),
        P(),
        P(*place, None),
    )
    return jax.shard_map(
        on_device,
        mesh=split,
        in_specs=placed,
        out_specs=(P(*place, None), P(None, *place, None), P(), P(), P(), P()),
        check_vma=False,
    )
```

time: 425 us -> 135 us (0.32)
  waiting for transfers between devices: 272 us -> 20.6 us
  between operations: 62.9 us -> 0.72 us
  Pallas kernels: 0 us -> 34.7 us
  blocking collectives: 0 us -> 32.1 us
  other arithmetic: 20.8 us -> 0.5 us
  starting transfers between devices: 50.8 us -> 38.7 us
  matrix products: 10.7 us -> 0 us
    psum x1 -> x0, waiting for transfers between devices: 243 us -> none  [in_one(): total = lax.psum(line, axis)]
    pallas_call x0 -> x16, Pallas kernels: none -> 34.7 us  [the longest x3 5.23 us: assemble(): call(after_y_kernel, step, [SMEM] + [VMEM] * 3, 'after_y' + tag, interpre...]
    all_to_all x0 -> x2, blocking collectives: none -> 32.1 us  [swap(): lax.all_to_all(rows.reshape(count, -1), axes, 0, 0, tiled=True)]
    ppermute x18, starting transfers between devices: 50.7 us -> 32.8 us  [exchange(): return (lax.ppermute(hi, axis, up), lax.ppermute(lo, axis, down))]
    dot_general x53 -> x0, matrix products: 10.7 us -> none  [the longest x19 4.48 us: outer_product(): lax.dot_general(left, right, (((0,), (0,)), ((), ())), preferred_element_...]
    ppermute x18, waiting for transfers between devices: 29 us -> 20.6 us  [exchange(): return (lax.ppermute(hi, axis, up), lax.ppermute(lo, axis, down))]
    and x10 -> x0, other arithmetic: 7.93 us -> none  [the longest x6 7.63 us: neighbour_valid(): (coords + offset[which] >= 0) & (coords + offset[which] < brick)]
    all_to_all x0 -> x1, starting transfers between devices: none -> 5.96 us  [swap(): lax.all_to_all(rows.reshape(count, -1), axes, 0, 0, tiled=True)]
  transfers between devices with their start and end apart: 19 -> 19, of which waited for: 9 -> 11; matrix products, arithmetic and copies ran while one was open for 1% -> 1% of each run, Pallas kernels for 0% -> 10%
where the time goes in v1:
time: 135 us; the launch traced here: 134 us
  starting transfers between devices  38.7 us (29%)
  Pallas kernels  34.7 us (26%)
  blocking collectives  32.1 us (24%)
  waiting for transfers between devices  20.6 us (15%)
  local copies, waits for them, and re-layouts  6.76 us (5%)
    ppermute x18, starting transfers between devices, exchange(): return (lax.ppermute(hi, axis, up), lax.ppermute(lo, axis, down))  32.8 us
    all_to_all x2, blocking collectives, swap(): lax.all_to_all(rows.reshape(count, -1), axes, 0, 0, tiled=True)  32.1 us
    ppermute x18, waiting for transfers between devices, exchange(): return (lax.ppermute(hi, axis, up), lax.ppermute(lo, axis, down))  20.6 us
    all_to_all x1, starting transfers between devices, swap(): lax.all_to_all(rows.reshape(count, -1), axes, 0, 0, tiled=True)  5.96 us
    unnamed x44, local copies, waits for them, and re-layouts  5.73 us
    pallas_call x3, Pallas kernels, assemble(): call(after_y_kernel, step, [SMEM] + [VMEM] * 3, 'after_y' + tag, interpre...  5.23 us
    pallas_call x3, Pallas kernels, assemble(): call(after_x_kernel, step, [SMEM] + [VMEM] * 3, 'after_x' + tag, interpre...  5.14 us
    pallas_call x1, Pallas kernels, on_device(): run(edge_kernel, cube + [((K, N, W), BF16), ((7 * W, W), F32)], [SMEM] *...  4.35 us
  transfers between devices with their start and end apart: 19, of which 11 were waited for; matrix products, arithmetic and copies ran while one was open for 1% of the time, Pallas kernels for 10%

profile of v1, /device:TPU:1, one launch (start us, length us, event | category | flops | bytes accessed | tf_op | source)
XLA Modules:
  0.0 134.1 jit_solution(7340069059291916538)
XLA Ops:
  0.6 2.9 %forward.1 = (f32[8,8,8,128]{3,2,1,0:T(8,128)}, f32[8,8,128]{2,1,0:T(8,128)}, f32[8,8,128]{2,1,0:T(8,128)}, f32[4,512,128]{2,1,0:T(8,128)}, bf16[4,512,128]{2,1,0:T(8,128)(2,1)}) custom-call(s32[4,3]{1,0:T(4,128)} %offs.3, bf16[512,128]{1,0:T(8,128)(2,1)} %bitcast.22, bf16[4,512,128]{2,1,0:T(8,128)(2,1)} %bitcast.17, bf16[384,128]{1,0:T(8,128)(2,1)} %w_in.9, ...), custom_call_target="tpu_custom_call" | custom-call | tf_op jit(solution)/shard_map/forward/pallas_call | solution.py:272
  3.5 3.7 %collective-permute-start = (f32[8,8,128]{2,1,0:T(8,128)}, f32[8,8,128]{2,1,0:T(8,128)S(1)}, u32[]{:S(2)}, u32[]{:S(2)}) collective-permute-start(f32[8,8,128]{2,1,0:T(8,128)} %get-tuple-element.51), channel_id=1, source_target_pairs={{0,16},{16,32},{32,48},{48,64},{64,80},{80,96},{96,112},{112,128},... | collective-permute-start | bytes 98312 | tf_op jit(solution)/shard_map/ppermute | solution.py:218
  7.3 5.4 %collective-permute-start.1 = (f32[8,8,128]{2,1,0:T(8,128)}, f32[8,8,128]{2,1,0:T(8,128)S(1)}, u32[]{:S(2)}, u32[]{:S(2)}) collective-permute-start(f32[8,8,128]{2,1,0:T(8,128)} %get-tuple-element.52), channel_id=1, source_target_pairs={{16,0},{32,16},{48,32},{64,48},{80,64},{96,80},{112,96},{128,112},... | collective-permute-start | bytes 98312 | tf_op jit(solution)/shard_map/ppermute | solution.py:218
  12.6 0.1 stack.27
  12.7 0.5 convert_element_type.12.rim
  13.2 0.8 collective-permute-done.rlo
  14.1 0.6 copy-done.3
  14.7 0.0 copy-done.4
  14.7 1.7 %after_x_1.1 = (f32[8,8,8,128]{3,2,1,0:T(8,128)}, f32[8,8,128]{2,1,0:T(8,128)}, f32[8,8,128]{2,1,0:T(8,128)}) custom-call(s32[6]{0:T(128)} %convert_element_type.12.rim, f32[8,8,8,128]{3,2,1,0:T(8,128)} %get-tuple-element.50.field, f32[8,8,128]{2,1,0:T(8,128)} %copy-done.3, f32[8,8,128]{2,1,0:T(8,128)} %copy-done.4), custom_call_target="tpu_custom_call" | custom-call | tf_op jit(solution)/shard_map/after_x_1/pallas_call | solution.py:224
  16.4 1.8 %collective-permute-start.2 = (f32[8,8,128]{2,1,0:T(8,128)}, f32[8,8,128]{2,1,0:T(8,128)S(1)}, u32[]{:S(2)}, u32[]{:S(2)}) collective-permute-start(f32[8,8,128]{2,1,0:T(8,128)} %get-tuple-element.54), channel_id=1, source_target_pairs={{0,4},{4,8},{8,12},{12,0},{1,5},{5,9},{9,13},{13,1},{2,6},{6,10},{... | collective-permute-start | bytes 98312 | tf_op jit(solution)/shard_map/ppermute | solution.py:218
  18.2 1.3 collective-permute-done.2.rlo
  19.6 2.2 %collective-permute-done.3.rhi = f32[8,8,128]{2,1,0:T(8,128)S(1)} collective-permute-done((f32[8,8,128]{2,1,0:T(8,128)}, f32[8,8,128]{2,1,0:T(8,128)S(1)}, u32[]{:S(2)}, u32[]{:S(2)}) %collective-permute-start.3) | collective-permute-done | bytes 32800 | tf_op jit(solution)/shard_map/ppermute | solution.py:218
  21.8 0.6 copy-done.14
  22.4 1.8 %after_y_1.1 = (f32[8,8,8,128]{3,2,1,0:T(8,128)}, f32[8,8,128]{2,1,0:T(8,128)}, f32[8,8,128]{2,1,0:T(8,128)}) custom-call(s32[6]{0:T(128)} %convert_element_type.12.rim, f32[8,8,8,128]{3,2,1,0:T(8,128)} %get-tuple-element.53.field, f32[8,8,128]{2,1,0:T(8,128)} %copy-done.8, f32[8,8,128]{2,1,0:T(8,128)} %copy-done.14), custom_call_target="tpu_custom_call" | custom-call | tf_op jit(solution)/shard_map/after_y_1/pallas_call | solution.py:228
  24.2 1.2 collective-permute-start.4
  25.4 1.5 %collective-permute-start.5 = (f32[8,8,128]{2,1,0:T(8,128)}, f32[8,8,128]{2,1,0:T(8,128)S(1)}, u32[]{:S(2)}, u32[]{:S(2)}) collective-permute-start(f32[8,8,128]{2,1,0:T(8,128)} %get-tuple-element.58), channel_id=1, source_target_pairs={{1,0},{2,1},{3,2},{0,3},{5,4},{6,5},{7,6},{4,7},{9,8},{10,9},{11,1... | collective-permute-start | bytes 98312 | tf_op jit(solution)/shard_map/ppermute | solution.py:218
  26.9 0.1 div.16
  26.9 1.8 %collective-permute-done.4.rlo = f32[8,8,128]{2,1,0:T(8,128)S(1)} collective-permute-done((f32[8,8,128]{2,1,0:T(8,128)}, f32[8,8,128]{2,1,0:T(8,128)S(1)}, u32[]{:S(2)}, u32[]{:S(2)}) %collective-permute-start.4) | collective-permute-done | bytes 32800 | tf_op jit(solution)/shard_map/ppermute | solution.py:218
  28.7 0.8 broadcast_in_dim.2.inverse
  29.5 2.4 %node.1 = (f32[8,8,8,128]{3,2,1,0:T(8,128)}, f32[8,8,128]{2,1,0:T(8,128)}, f32[8,8,128]{2,1,0:T(8,128)}, bf16[512,128]{1,0:T(8,128)(2,1)}, bf16[512,128]{1,0:T(8,128)(2,1)}, /*index=5*/bf16[512,128]{1,0:T(8,128)(2,1)}) custom-call(s32[6]{0:T(128)} %convert_element_type.12.rim, f32[8,8,8,128]{3,2,1,0:T(8,128)} %get-tuple-element.56.field, ...), custom_call_target="tpu_custom_call" | custom-call | tf_op jit(solution)/shard_map/node/pallas_call | solution.py:282
  31.9 1.8 %collective-permute-start.6 = (f32[8,8,128]{2,1,0:T(8,128)}, f32[8,8,128]{2,1,0:T(8,128)S(1)}, u32[]{:S(2)}, u32[]{:S(2)}) collective-permute-start(f32[8,8,128]{2,1,0:T(8,128)} %get-tuple-element.60), channel_id=1, source_target_pairs={{0,16},{16,32},{32,48},{48,64},{64,80},{80,96},{96,112},{112,128},... | collective-permute-start | bytes 98312 | tf_op jit(solution)/shard_map/ppermute | solution.py:218
  33.7 4.6 %collective-permute-start.7 = (f32[8,8,128]{2,1,0:T(8,128)}, f32[8,8,128]{2,1,0:T(8,128)S(1)}, u32[]{:S(2)}, u32[]{:S(2)}) collective-permute-start(f32[8,8,128]{2,1,0:T(8,128)} %get-tuple-element.61), channel_id=1, source_target_pairs={{16,0},{32,16},{48,32},{64,48},{80,64},{96,80},{112,96},{128,112},... | collective-permute-start | bytes 98312 | tf_op jit(solution)/shard_map/ppermute | solution.py:218
  38.3 1.4 %collective-permute-done.6.rlo = f32[8,8,128]{2,1,0:T(8,128)S(1)} collective-permute-done((f32[8,8,128]{2,1,0:T(8,128)}, f32[8,8,128]{2,1,0:T(8,128)S(1)}, u32[]{:S(2)}, u32[]{:S(2)}) %collective-permute-start.6) | collective-permute-done | bytes 32800 | tf_op jit(solution)/shard_map/ppermute | solution.py:218
  39.8 0.6 copy-done.11
  40.4 0.0 copy-done.17
  40.4 1.7 %after_x_2.1 = (f32[8,8,8,128]{3,2,1,0:T(8,128)}, f32[8,8,128]{2,1,0:T(8,128)}, f32[8,8,128]{2,1,0:T(8,128)}) custom-call(s32[6]{0:T(128)} %convert_element_type.12.rim, f32[8,8,8,128]{3,2,1,0:T(8,128)} %get-tuple-element.59.field, f32[8,8,128]{2,1,0:T(8,128)} %copy-done.11, f32[8,8,128]{2,1,0:T(8,128)} %copy-done.17), custom_call_target="tpu_custom_call" | custom-call | tf_op jit(solution)/shard_map/after_x_2/pallas_call | solution.py:224
  42.1 1.4 %collective-permute-start.8 = (f32[8,8,128]{2,1,0:T(8,128)}, f32[8,8,128]{2,1,0:T(8,128)S(1)}, u32[]{:S(2)}, u32[]{:S(2)}) collective-permute-start(f32[8,8,128]{2,1,0:T(8,128)} %get-tuple-element.63), channel_id=1, source_target_pairs={{0,4},{4,8},{8,12},{12,0},{1,5},{5,9},{9,13},{13,1},{2,6},{6,10},{... | collective-permute-start | bytes 98312 | tf_op jit(solution)/shard_map/ppermute | solution.py:218
  43.5 1.3 collective-permute-done.8.rlo
  44.9 2.2 %collective-permute-done.9.rhi = f32[8,8,128]{2,1,0:T(8,128)S(1)} collective-permute-done((f32[8,8,128]{2,1,0:T(8,128)}, f32[8,8,128]{2,1,0:T(8,128)S(1)}, u32[]{:S(2)}, u32[]{:S(2)}) %collective-permute-start.9) | collective-permute-done | bytes 32800 | tf_op jit(solution)/shard_map/ppermute | solution.py:218
  47.1 0.6 copy-done.15
  47.7 1.7 %after_y_2.1 = (f32[8,8,8,128]{3,2,1,0:T(8,128)}, f32[8,8,128]{2,1,0:T(8,128)}, f32[8,8,128]{2,1,0:T(8,128)}) custom-call(s32[6]{0:T(128)} %convert_element_type.12.rim, f32[8,8,8,128]{3,2,1,0:T(8,128)} %get-tuple-element.62.field, f32[8,8,128]{2,1,0:T(8,128)} %copy-done.9, f32[8,8,128]{2,1,0:T(8,128)} %copy-done.15), custom_call_target="tpu_custom_call" | custom-call | tf_op jit(solution)/shard_map/after_y_2/pallas_call | solution.py:228
  49.4 1.2 collective-permute-start.10
  50.6 1.5 %collective-permute-start.11 = (f32[8,8,128]{2,1,0:T(8,128)}, f32[8,8,128]{2,1,0:T(8,128)S(1)}, u32[]{:S(2)}, u32[]{:S(2)}) collective-permute-start(f32[8,8,128]{2,1,0:T(8,128)} %get-tuple-element.67), channel_id=1, source_target_pairs={{1,0},{2,1},{3,2},{0,3},{5,4},{6,5},{7,6},{4,7},{9,8},{10,9},{11,1... | collective-permute-start | bytes 98312 | tf_op jit(solution)/shard_map/ppermute | solution.py:218
  52.1 3.2 %prepare.1 = (f32[4,512,128]{2,1,0:T(8,128)}, bf16[4,128,512]{2,1,0:T(8,128)(2,1)}, bf16[4,128,512]{2,1,0:T(8,128)(2,1)}, bf16[128,512]{1,0:T(8,128)(2,1)}) custom-call(f32[4,512,128]{2,1,0:T(8,128)} %get-tuple-element.68.preact, bf16[4,512,128]{2,1,0:T(8,128)(2,1)} %get-tuple-element.69.hidden, bf16[512,128]{1,0:T(8,128)(2,1)} %bitcast.24, ...), custom_call_target="tpu_custom_call" | custom-call | tf_op jit(solution)/shard_map/prepare/pallas_call | solution.py:276
  55.3 2.2 %node_grads.1 = (f32[384,128]{1,0:T(8,128)}, f32[512,128]{1,0:T(8,128)}) custom-call(bf16[128,512]{1,0:T(8,128)(2,1)} %get-tuple-element.73.nodes_t, bf16[512,128]{1,0:T(8,128)(2,1)} %get-tuple-element.74.gathered, bf16[512,128]{1,0:T(8,128)(2,1)} %get-tuple-element.75.slope, bf16[512,128]{1,0:T(8,128)(2,1)} %get-tuple-element.76.hidden, ...), custom_call_target="tpu_custom_call" | custom-call | tf_op jit(solution)/shard_map/node_grads/pallas_call | solution.py:286
  57.5 0.0 copy-start.2
  57.5 0.6 copy-done.1
  58.1 0.0 copy-done.2
  58.1 4.4 %edge.1 = (f32[8,8,8,128]{3,2,1,0:T(8,128)}, f32[8,8,128]{2,1,0:T(8,128)}, f32[8,8,128]{2,1,0:T(8,128)}, bf16[4,512,128]{2,1,0:T(8,128)(2,1)}, f32[896,128]{1,0:T(8,128)}) custom-call(s32[6]{0:T(128)} %convert_element_type.12.rim, s32[4,3]{1,0:T(4,128)} %offs.3, f32[8,8,8,128]{3,2,1,0:T(8,128)} %get-tuple-element.65.field, f32[8,8,128]{2,1,0:T(8,128)} %copy-done.1, ...), custom_call_target="tpu_custom_call" | custom-call | tf_op jit(solution)/shard_map/edge/pallas_call | solution.py:289
  62.5 16.1 %all_to_all.27 = f32[32,1,3584]{2,1,0:T(1,128)} all-to-all(f32[32,1,3584]{2,1,0:T(1,128)} %bitcast.28), channel_id=1, replica_groups=mesh['z'=8,'yh'=2,'yl'=2,'c'=2,'x'=4] {'yh','yl','c','x'}, dimensions={0} | all-to-all | bytes 917504 | tf_op jit(solution)/shard_map/all_to_all | solution.py:236
  78.6 1.7 %fold_near.1 = f32[224,128]{1,0:T(8,128)} custom-call(f32[896,128]{1,0:T(8,128)} %bitcast.21), custom_call_target="tpu_custom_call" | custom-call | tf_op jit(solution)/shard_map/fold_near/pallas_call | solution.py:243
  80.3 16.0 %all_to_all.28 = f32[8,1,3584]{2,1,0:T(1,128)} all-to-all(f32[8,1,3584]{2,1,0:T(1,128)} %bitcast.29), channel_id=1, replica_groups=mesh['z'=8,'yh'=2,'yl'=2,'c'=2,'x'=4] {'z'}, dimensions={0} | all-to-all | bytes 229376 | tf_op jit(solution)/shard_map/all_to_all | solution.py:236
  96.3 1.7 %fold_far.1 = f32[896,128]{1,0:T(8,128)} custom-call(f32[224,128]{1,0:T(8,128)} %bitcast.30), custom_call_target="tpu_custom_call" | custom-call | tf_op jit(solution)/shard_map/fold_far/pallas_call | solution.py:248
  98.0 6.0 %all-to-all-start.2 = ((f32[32,1,3584]{2,1,0:T(1,128)}), f32[32,1,3584]{2,1,0:T(1,128)S(1)}, u32[]{:S(2)}, u32[]{:S(2)}) async-start(f32[32,1,3584]{2,1,0:T(1,128)} %bitcast.20), calls=%async_computation.2 | async-start | bytes 917504 | tf_op jit(solution)/shard_map/all_to_all | solution.py:236
  104.0 2.9 %collective-permute-start.12 = (f32[8,8,128]{2,1,0:T(8,128)S(1)}, f32[8,8,128]{2,1,0:T(8,128)S(1)}, u32[]{:S(2)}, u32[]{:S(2)}) collective-permute-start(f32[8,8,128]{2,1,0:T(8,128)S(1)} %copy-done.21), channel_id=1, source_target_pairs={{0,16},{16,32},{32,48},{48,64},{64,80},{80,96},{96,112},{112,128},... | collective-permute-start | bytes 98312 | tf_op jit(solution)/shard_map/ppermute | solution.py:218
  106.9 2.2 %collective-permute-start.13 = (f32[8,8,128]{2,1,0:T(8,128)S(1)}, f32[8,8,128]{2,1,0:T(8,128)S(1)}, u32[]{:S(2)}, u32[]{:S(2)}) collective-permute-start(f32[8,8,128]{2,1,0:T(8,128)S(1)} %copy-done.20), channel_id=1, source_target_pairs={{16,0},{32,16},{48,32},{64,48},{80,64},{96,80},{112,96},{128,112},... | collective-permute-start | bytes 98312 | tf_op jit(solution)/shard_map/ppermute | solution.py:218
  109.1 1.9 %collective-permute-done.12.rlo = f32[8,8,128]{2,1,0:T(8,128)S(1)} collective-permute-done((f32[8,8,128]{2,1,0:T(8,128)S(1)}, f32[8,8,128]{2,1,0:T(8,128)S(1)}, u32[]{:S(2)}, u32[]{:S(2)}) %collective-permute-start.12) | collective-permute-done | bytes 32800 | tf_op jit(solution)/shard_map/ppermute | solution.py:218
  111.0 4.1 %collective-permute-done.13.rhi = f32[8,8,128]{2,1,0:T(8,128)S(1)} collective-permute-done((f32[8,8,128]{2,1,0:T(8,128)S(1)}, f32[8,8,128]{2,1,0:T(8,128)S(1)}, u32[]{:S(2)}, u32[]{:S(2)}) %collective-permute-start.13) | collective-permute-done | bytes 32800 | tf_op jit(solution)/shard_map/ppermute | solution.py:218
  115.1 0.6 copy-done.18
  115.7 1.7 %after_x_3.1 = (f32[8,8,8,128]{3,2,1,0:T(8,128)}, f32[8,8,128]{2,1,0:T(8,128)}, f32[8,8,128]{2,1,0:T(8,128)}) custom-call(s32[6]{0:T(128)} %convert_element_type.12.rim, f32[8,8,8,128]{3,2,1,0:T(8,128)} %get-tuple-element.79.field, f32[8,8,128]{2,1,0:T(8,128)} %copy-done.12, f32[8,8,128]{2,1,0:T(8,128)} %copy-done.18), custom_call_target="tpu_custom_call" | custom-call | tf_op jit(solution)/shard_map/after_x_3/pallas_call | solution.py:224
  117.4 0.8 collective-permute-start.14
  118.3 1.3 collective-permute-done.14.rlo
  119.6 2.2 %collective-permute-done.15.rhi = f32[8,8,128]{2,1,0:T(8,128)S(1)} collective-permute-done((f32[8,8,128]{2,1,0:T(8,128)}, f32[8,8,128]{2,1,0:T(8,128)S(1)}, u32[]{:S(2)}, u32[]{:S(2)}) %collective-permute-start.15) | collective-permute-done | bytes 32800 | tf_op jit(solution)/shard_map/ppermute | solution.py:218
  121.8 0.6 copy-done.16
  122.4 1.7 %after_y_3.1 = (f32[8,8,8,128]{3,2,1,0:T(8,128)}, f32[8,8,128]{2,1,0:T(8,128)}, f32[8,8,128]{2,1,0:T(8,128)}) custom-call(s32[6]{0:T(128)} %convert_element_type.12.rim, f32[8,8,8,128]{3,2,1,0:T(8,128)} %get-tuple-element.82.field, f32[8,8,128]{2,1,0:T(8,128)} %copy-done.10, f32[8,8,128]{2,1,0:T(8,128)} %copy-done.16), custom_call_target="tpu_custom_call" | custom-call | tf_op jit(solution)/shard_map/after_y_3/pallas_call | solution.py:228
  124.2 0.4 collective-permute-start.16
  124.5 2.3 %collective-permute-start.17 = (f32[8,8,128]{2,1,0:T(8,128)}, f32[8,8,128]{2,1,0:T(8,128)S(1)}, u32[]{:S(2)}, u32[]{:S(2)}) collective-permute-start(f32[8,8,128]{2,1,0:T(8,128)} %get-tuple-element.87), channel_id=1, source_target_pairs={{1,0},{2,1},{3,2},{0,3},{5,4},{6,5},{7,6},{4,7},{9,8},{10,9},{11,1... | collective-permute-start | bytes 98312 | tf_op jit(solution)/shard_map/ppermute | solution.py:218
  126.8 2.1 %edge_grad.1 = bf16[4,512,128]{2,1,0:T(8,128)(2,1)} custom-call(bf16[4,512,128]{2,1,0:T(8,128)(2,1)} %get-tuple-element.88.slopes, bf16[384,128]{1,0:T(8,128)(2,1)} %w_in.9), custom_call_target="tpu_custom_call" | custom-call | tf_op jit(solution)/shard_map/edge_grad/pallas_call | solution.py:298
  129.0 0.0 copy-start.13
  129.0 0.6 copy-done.7
  129.6 0.0 copy-done.13
  129.6 1.7 %last.1 = bf16[512,128]{1,0:T(8,128)(2,1)} custom-call(s32[6]{0:T(128)} %convert_element_type.12.rim, f32[8,8,8,128]{3,2,1,0:T(8,128)} %get-tuple-element.85.field, f32[8,8,128]{2,1,0:T(8,128)} %copy-done.7, f32[8,8,128]{2,1,0:T(8,128)} %copy-done.13), custom_call_target="tpu_custom_call" | custom-call | tf_op jit(solution)/shard_map/last/pallas_call | solution.py:299
  131.4 0.8 copy-done
  132.1 2.0 %clip.1 = (f32[384,128]{1,0:T(8,128)}, f32[128,128]{1,0:T(8,128)}, f32[256,128]{1,0:T(8,128)}, f32[128,128]{1,0:T(8,128)}) custom-call(f32[896,128]{1,0:T(8,128)} %bitcast.19), custom_call_target="tpu_custom_call" | custom-call | tf_op jit(solution)/shard_map/clip/pallas_call | solution.py:300
  (41 shorter events, 0.1 us)
Async XLA Ops:
  3.5 10.5 %collective-permute-start = (f32[8,8,128]{2,1,0:T(8,128)}, f32[8,8,128]{2,1,0:T(8,128)S(1)}, u32[]{:S(2)}, u32[]{:S(2)}) collective-permute-start(f32[8,8,128]{2,1,0:T(8,128)} %get-tuple-element.51), channel_id=1, source_target_pairs={{0,16},{16,32},{32,48},{48,64},{64,80},{80,96},{96,112},{112,128},... | collective-permute-start | bytes 98312 | tf_op jit(solution)/shard_map/ppermute | solution.py:218
  7.3 6.8 %collective-permute-start.1 = (f32[8,8,128]{2,1,0:T(8,128)}, f32[8,8,128]{2,1,0:T(8,128)S(1)}, u32[]{:S(2)}, u32[]{:S(2)}) collective-permute-start(f32[8,8,128]{2,1,0:T(8,128)} %get-tuple-element.52), channel_id=1, source_target_pairs={{16,0},{32,16},{48,32},{64,48},{80,64},{96,80},{112,96},{128,112},... | collective-permute-start | bytes 98312 | tf_op jit(solution)/shard_map/ppermute | solution.py:218
  14.1 0.6 copy-start.3
  14.1 0.6 copy-start.4
  16.4 3.2 %collective-permute-start.2 = (f32[8,8,128]{2,1,0:T(8,128)}, f32[8,8,128]{2,1,0:T(8,128)S(1)}, u32[]{:S(2)}, u32[]{:S(2)}) collective-permute-start(f32[8,8,128]{2,1,0:T(8,128)} %get-tuple-element.54), channel_id=1, source_target_pairs={{0,4},{4,8},{8,12},{12,0},{1,5},{5,9},{9,13},{13,1},{2,6},{6,10},{... | collective-permute-start | bytes 98312 | tf_op jit(solution)/shard_map/ppermute | solution.py:218
  18.2 3.6 %collective-permute-start.3 = (f32[8,8,128]{2,1,0:T(8,128)}, f32[8,8,128]{2,1,0:T(8,128)S(1)}, u32[]{:S(2)}, u32[]{:S(2)}) collective-permute-start(f32[8,8,128]{2,1,0:T(8,128)} %get-tuple-element.55), channel_id=1, source_target_pairs={{4,0},{8,4},{12,8},{0,12},{5,1},{9,5},{13,9},{1,13},{6,2},{10,6},{... | collective-permute-start | bytes 98312 | tf_op jit(solution)/shard_map/ppermute | solution.py:218
  19.6 2.2 %copy-start.8 = (f32[8,8,128]{2,1,0:T(8,128)}, f32[8,8,128]{2,1,0:T(8,128)S(1)}, u32[]{:S(2)}) copy-start(f32[8,8,128]{2,1,0:T(8,128)S(1)} %collective-permute-done.2.rlo) | copy-start | bytes 98308
  21.8 0.6 copy-start.14
  22.4 4.4 %copy-start.19 = (s32[8,8,8]{2,1,0:T(8,128)S(1)}, s32[8,8,8]{2,1,0:T(8,128)}, u32[]{:S(2)}) copy-start(s32[8,8,8]{2,1,0:T(8,128)} %param.11) | copy-start | bytes 6148
  24.2 4.5 %collective-permute-start.4 = (f32[8,8,128]{2,1,0:T(8,128)}, f32[8,8,128]{2,1,0:T(8,128)S(1)}, u32[]{:S(2)}, u32[]{:S(2)}) collective-permute-start(f32[8,8,128]{2,1,0:T(8,128)} %get-tuple-element.57), channel_id=1, source_target_pairs={{0,1},{1,2},{2,3},{3,0},{4,5},{5,6},{6,7},{7,4},{8,9},{9,10},{10,1... | collective-permute-start | bytes 98312 | tf_op jit(solution)/shard_map/ppermute | solution.py:218
  25.4 3.3 %collective-permute-start.5 = (f32[8,8,128]{2,1,0:T(8,128)}, f32[8,8,128]{2,1,0:T(8,128)S(1)}, u32[]{:S(2)}, u32[]{:S(2)}) collective-permute-start(f32[8,8,128]{2,1,0:T(8,128)} %get-tuple-element.58), channel_id=1, source_target_pairs={{1,0},{2,1},{3,2},{0,3},{5,4},{6,5},{7,6},{4,7},{9,8},{10,9},{11,1... | collective-permute-start | bytes 98312 | tf_op jit(solution)/shard_map/ppermute | solution.py:218
  28.7 0.8 copy-start.5
  28.7 0.8 copy-start.6
  31.9 7.8 %collective-permute-start.6 = (f32[8,8,128]{2,1,0:T(8,128)}, f32[8,8,128]{2,1,0:T(8,128)S(1)}, u32[]{:S(2)}, u32[]{:S(2)}) collective-permute-start(f32[8,8,128]{2,1,0:T(8,128)} %get-tuple-element.60), channel_id=1, source_target_pairs={{0,16},{16,32},{32,48},{48,64},{64,80},{80,96},{96,112},{112,128},... | collective-permute-start | bytes 98312 | tf_op jit(solution)/shard_map/ppermute | solution.py:218
  33.7 6.1 %collective-permute-start.7 = (f32[8,8,128]{2,1,0:T(8,128)}, f32[8,8,128]{2,1,0:T(8,128)S(1)}, u32[]{:S(2)}, u32[]{:S(2)}) collective-permute-start(f32[8,8,128]{2,1,0:T(8,128)} %get-tuple-element.61), channel_id=1, source_target_pairs={{16,0},{32,16},{48,32},{64,48},{80,64},{96,80},{112,96},{128,112},... | collective-permute-start | bytes 98312 | tf_op jit(solution)/shard_map/ppermute | solution.py:218
  39.8 0.6 copy-start.11
  39.8 0.6 copy-start.17
  42.1 2.8 %collective-permute-start.8 = (f32[8,8,128]{2,1,0:T(8,128)}, f32[8,8,128]{2,1,0:T(8,128)S(1)}, u32[]{:S(2)}, u32[]{:S(2)}) collective-permute-start(f32[8,8,128]{2,1,0:T(8,128)} %get-tuple-element.63), channel_id=1, source_target_pairs={{0,4},{4,8},{8,12},{12,0},{1,5},{5,9},{9,13},{13,1},{2,6},{6,10},{... | collective-permute-start | bytes 98312 | tf_op jit(solution)/shard_map/ppermute | solution.py:218
  43.5 3.6 %collective-permute-start.9 = (f32[8,8,128]{2,1,0:T(8,128)}, f32[8,8,128]{2,1,0:T(8,128)S(1)}, u32[]{:S(2)}, u32[]{:S(2)}) collective-permute-start(f32[8,8,128]{2,1,0:T(8,128)} %get-tuple-element.64), channel_id=1, source_target_pairs={{4,0},{8,4},{12,8},{0,12},{5,1},{9,5},{13,9},{1,13},{6,2},{10,6},{... | collective-permute-start | bytes 98312 | tf_op jit(solution)/shard_map/ppermute | solution.py:218
  44.8 2.2 %copy-start.9 = (f32[8,8,128]{2,1,0:T(8,128)}, f32[8,8,128]{2,1,0:T(8,128)S(1)}, u32[]{:S(2)}) copy-start(f32[8,8,128]{2,1,0:T(8,128)S(1)} %collective-permute-done.8.rlo) | copy-start | bytes 98308
  47.1 0.6 copy-start.15
  49.4 8.1 %collective-permute-start.10 = (f32[8,8,128]{2,1,0:T(8,128)}, f32[8,8,128]{2,1,0:T(8,128)S(1)}, u32[]{:S(2)}, u32[]{:S(2)}) collective-permute-start(f32[8,8,128]{2,1,0:T(8,128)} %get-tuple-element.66), channel_id=1, source_target_pairs={{0,1},{1,2},{2,3},{3,0},{4,5},{5,6},{6,7},{7,4},{8,9},{9,10},{10,1... | collective-permute-start | bytes 98312 | tf_op jit(solution)/shard_map/ppermute | solution.py:218
  50.6 6.9 %collective-permute-start.11 = (f32[8,8,128]{2,1,0:T(8,128)}, f32[8,8,128]{2,1,0:T(8,128)S(1)}, u32[]{:S(2)}, u32[]{:S(2)}) collective-permute-start(f32[8,8,128]{2,1,0:T(8,128)} %get-tuple-element.67), channel_id=1, source_target_pairs={{1,0},{2,1},{3,2},{0,3},{5,4},{6,5},{7,6},{4,7},{9,8},{10,9},{11,1... | collective-permute-start | bytes 98312 | tf_op jit(solution)/shard_map/ppermute | solution.py:218
  57.5 0.6 copy-start.1
  57.5 0.6 copy-start.2
  98.0 6.0 %copy-start.21 = (f32[8,8,128]{2,1,0:T(8,128)S(1)}, f32[8,8,128]{2,1,0:T(8,128)}, u32[]{:S(2)}) copy-start(f32[8,8,128]{2,1,0:T(8,128)} %get-tuple-element.80) | copy-start | bytes 98308
  98.0 8.9 %copy-start.20 = (f32[8,8,128]{2,1,0:T(8,128)S(1)}, f32[8,8,128]{2,1,0:T(8,128)}, u32[]{:S(2)}) copy-start(f32[8,8,128]{2,1,0:T(8,128)} %get-tuple-element.81) | copy-start | bytes 98308
  98.0 33.4 %all-to-all-start.2 = ((f32[32,1,3584]{2,1,0:T(1,128)}), f32[32,1,3584]{2,1,0:T(1,128)S(1)}, u32[]{:S(2)}, u32[]{:S(2)}) async-start(f32[32,1,3584]{2,1,0:T(1,128)} %bitcast.20), calls=%async_computation.2 | async-start | bytes 917504 | tf_op jit(solution)/shard_map/all_to_all | solution.py:236
  104.0 7.0 %collective-permute-start.12 = (f32[8,8,128]{2,1,0:T(8,128)S(1)}, f32[8,8,128]{2,1,0:T(8,128)S(1)}, u32[]{:S(2)}, u32[]{:S(2)}) collective-permute-start(f32[8,8,128]{2,1,0:T(8,128)S(1)} %copy-done.21), channel_id=1, source_target_pairs={{0,16},{16,32},{32,48},{48,64},{64,80},{80,96},{96,112},{112,128},... | collective-permute-start | bytes 98312 | tf_op jit(solution)/shard_map/ppermute | solution.py:218
  106.9 8.2 %collective-permute-start.13 = (f32[8,8,128]{2,1,0:T(8,128)S(1)}, f32[8,8,128]{2,1,0:T(8,128)S(1)}, u32[]{:S(2)}, u32[]{:S(2)}) collective-permute-start(f32[8,8,128]{2,1,0:T(8,128)S(1)} %copy-done.20), channel_id=1, source_target_pairs={{16,0},{32,16},{48,32},{64,48},{80,64},{96,80},{112,96},{128,112},... | collective-permute-start | bytes 98312 | tf_op jit(solution)/shard_map/ppermute | solution.py:218
  111.0 4.1 %copy-start.12 = (f32[8,8,128]{2,1,0:T(8,128)}, f32[8,8,128]{2,1,0:T(8,128)S(1)}, u32[]{:S(2)}) copy-start(f32[8,8,128]{2,1,0:T(8,128)S(1)} %collective-permute-done.12.rlo) | copy-start | bytes 98308
  115.1 0.6 copy-start.18
  117.4 2.2 %collective-permute-start.14 = (f32[8,8,128]{2,1,0:T(8,128)}, f32[8,8,128]{2,1,0:T(8,128)S(1)}, u32[]{:S(2)}, u32[]{:S(2)}) collective-permute-start(f32[8,8,128]{2,1,0:T(8,128)} %get-tuple-element.83), channel_id=1, source_target_pairs={{0,4},{4,8},{8,12},{12,0},{1,5},{5,9},{9,13},{13,1},{2,6},{6,10},{... | collective-permute-start | bytes 98312 | tf_op jit(solution)/shard_map/ppermute | solution.py:218
  118.3 3.6 %collective-permute-start.15 = (f32[8,8,128]{2,1,0:T(8,128)}, f32[8,8,128]{2,1,0:T(8,128)S(1)}, u32[]{:S(2)}, u32[]{:S(2)}) collective-permute-start(f32[8,8,128]{2,1,0:T(8,128)} %get-tuple-element.84), channel_id=1, source_target_pairs={{4,0},{8,4},{12,8},{0,12},{5,1},{9,5},{13,9},{1,13},{6,2},{10,6},{... | collective-permute-start | bytes 98312 | tf_op jit(solution)/shard_map/ppermute | solution.py:218
  119.6 2.2 %copy-start.10 = (f32[8,8,128]{2,1,0:T(8,128)}, f32[8,8,128]{2,1,0:T(8,128)S(1)}, u32[]{:S(2)}) copy-start(f32[8,8,128]{2,1,0:T(8,128)S(1)} %collective-permute-done.14.rlo) | copy-start | bytes 98308
  121.8 0.6 copy-start.16
  124.2 4.8 %collective-permute-start.16 = (f32[8,8,128]{2,1,0:T(8,128)}, f32[8,8,128]{2,1,0:T(8,128)S(1)}, u32[]{:S(2)}, u32[]{:S(2)}) collective-permute-start(f32[8,8,128]{2,1,0:T(8,128)} %get-tuple-element.86), channel_id=1, source_target_pairs={{0,1},{1,2},{2,3},{3,0},{4,5},{5,6},{6,7},{7,4},{8,9},{9,10},{10,1... | collective-permute-start | bytes 98312 | tf_op jit(solution)/shard_map/ppermute | solution.py:218
  124.5 4.5 %collective-permute-start.17 = (f32[8,8,128]{2,1,0:T(8,128)}, f32[8,8,128]{2,1,0:T(8,128)S(1)}, u32[]{:S(2)}, u32[]{:S(2)}) collective-permute-start(f32[8,8,128]{2,1,0:T(8,128)} %get-tuple-element.87), channel_id=1, source_target_pairs={{1,0},{2,1},{3,2},{0,3},{5,4},{6,5},{7,6},{4,7},{9,8},{10,9},{11,1... | collective-permute-start | bytes 98312 | tf_op jit(solution)/shard_map/ppermute | solution.py:218
  129.0 0.6 copy-start.7
  129.0 0.6 copy-start.13
  131.4 0.8 copy-start

commit v2 on v1

--- a/solution.py
+++ b/solution.py
@@ -18,6 +18,8 @@
 F32 = jnp.float32
 BF16 = jnp.bfloat16
 
+GRANT = 12 * 1024 * 1024
+
 VMEM = pl.BlockSpec(memory_space=pltpu.VMEM)
 SMEM = pl.BlockSpec(memory_space=pltpu.SMEM)
 
@@ -29,6 +31,7 @@
         in_specs=specs,
         out_specs=[VMEM] * len(outs),
         scratch_shapes=list(scratch),
+        compiler_params=pltpu.CompilerParams(vmem_limit_bytes=GRANT),
         name=name,
         interpret=interpret,
     )
@@ -191,10 +194,20 @@
     return total + jnp.concatenate([total[rows:], total[:rows]], axis=0)
 
 
-def fold_kernel(rows, pairs, copies, arrived, out):
+def fold(rows, pairs, copies, arrived, out):
     total = pair_sum(arrived, rows, pairs)
     for i in range(copies):
         out[2 * rows * i : 2 * rows * (i + 1)] = total
+
+
+def after_x_fold_kernel(rows, pairs, copies, rim, field, rlo, rhi, arrived, out, lo, hi, spread):
+    fold(rows, pairs, copies, arrived, spread)
+    after_x_kernel(rim, field, rlo, rhi, out, lo, hi)
+
+
+def after_y_fold_kernel(rows, pairs, copies, rim, field, rlo, rhi, arrived, out, lo, hi, spread):
+    fold(rows, pairs, copies, arrived, spread)
+    after_y_kernel(rim, field, rlo, rhi, out, lo, hi)
 
 
 def clip_kernel(grads, edge_in, edge_out, node_in, node_out):
@@ -236,20 +249,30 @@
     return lax.all_to_all(rows.reshape(count, -1), axes, 0, 0, tiled=True).reshape(-1, W)
 
 
-def reduce_all(grads, interpret):
+def assemble_and_reduce(rim, field, xlo, xhi, grads, interpret):
     near, far = lax.axis_size(NEAR), lax.axis_size(FAR)
     rows = grads.shape[0] // near
+    step = [(CUBE, F32), (FACE, F32), (FACE, F32)]
+    rlo, rhi = exchange(xlo, xhi, GX)
     got = swap(grads, NEAR, near)
-    (got,) = call(
-        functools.partial(fold_kernel, rows, near // 2, far // 2), [((rows * far, W), F32)], [VMEM], "fold_near",
+    field, lo, hi, spread = call(
+        functools.partial(after_x_fold_kernel, rows, near // 2, far // 2),
+        step + [((rows * far, W), F32)],
+        [SMEM] + [VMEM] * 4,
+        "after_x_fold",
         interpret=interpret,
-    )(got)
-    got = swap(got, FAR, far)
-    (got,) = call(
-        functools.partial(fold_kernel, rows, far // 2, near // 2), [((rows * near, W), F32)], [VMEM], "fold_far",
+    )(rim, field, rlo, rhi, got)
+    rlo, rhi = exchange(lo, hi, GY)
+    got = swap(spread, FAR, far)
+    field, lo, hi, spread = call(
+        functools.partial(after_y_fold_kernel, rows, far // 2, near // 2),
+        step + [((rows * near, W), F32)],
+        [SMEM] + [VMEM] * 4,
+        "after_y_fold",
         interpret=interpret,
-    )(got)
-    return swap(got, NEAR, near)
+    )(rim, field, rlo, rhi, got)
+    rlo, rhi = exchange(lo, hi, GZ)
+    return field, rlo, rhi, swap(spread, NEAR, near)
 
 
 def on_device(
@@ -293,8 +316,7 @@
         "edge",
         [work, pad],
     )(rim, offsets, field, rlo, rhi, dact, hidden_t, edges_t, nodes_t, base, node_grads, w_edge_in, w_edge_out)
-    total = reduce_all(grads, interpret)
-    field, rlo, rhi = assemble(rim, local, xlo, xhi, "_3", interpret)
+    field, rlo, rhi, total = assemble_and_reduce(rim, local, xlo, xhi, grads, interpret)
     (edge_grad,) = run(edge_grad_kernel, [((K, N, W), BF16)], [VMEM] * 2, "edge_grad")(slopes, w_edge_in)
     (node_grad,) = run(last_kernel, [((N, W), BF16)], [SMEM] + [VMEM] * 3, "last", [work])(rim, field, rlo, rhi)
     clipped = run(

time: 135 us -> 105 us (0.78)
  blocking collectives: 32.1 us -> 0 us
  Pallas kernels: 34.7 us -> 14.6 us
  starting transfers between devices: 38.7 us -> 56.9 us
  waiting for transfers between devices: 20.6 us -> 26.9 us
    all_to_all x2 -> x0, blocking collectives: 32.1 us -> none  [swap(): lax.all_to_all(rows.reshape(count, -1), axes, 0, 0, tiled=True)]
    all_to_all x1 -> x3, starting transfers between devices: 5.96 us -> 21.3 us  [swap(): lax.all_to_all(rows.reshape(count, -1), axes, 0, 0, tiled=True)]
    all_to_all x1 -> x3, waiting for transfers between devices: 0.01 us -> 4.15 us  [swap(): lax.all_to_all(rows.reshape(count, -1), axes, 0, 0, tiled=True)]
    pallas_call x3 -> x2, Pallas kernels: 5.23 us -> 1.2 us  [assemble(): call(after_y_kernel, step, [SMEM] + [VMEM] * 3, 'after_y' + tag, interpre...]
    pallas_call x3 -> x2, Pallas kernels: 5.14 us -> 1.13 us  [assemble(): call(after_x_kernel, step, [SMEM] + [VMEM] * 3, 'after_x' + tag, interpre...]
    ppermute x18, starting transfers between devices: 32.8 us -> 35.6 us  [exchange(): return (lax.ppermute(hi, axis, up), lax.ppermute(lo, axis, down))]
    pallas_call x1, Pallas kernels: 3.2 us -> 0.56 us  [on_device(): run(prepare_kernel, [((K, N, W), F32), ((K, W, N), BF16), ((K, W, N), BF1...]
    ppermute x18, waiting for transfers between devices: 20.6 us -> 22.7 us  [exchange(): return (lax.ppermute(hi, axis, up), lax.ppermute(lo, axis, down))]
  transfers between devices with their start and end apart: 19 -> 21, of which waited for: 11 -> 16; matrix products, arithmetic and copies ran while one was open for 1% -> 0% of each run, Pallas kernels for 10% -> 3%
where the time goes in v2:
time: 105 us
  starting transfers between devices  56.9 us (54%)
  waiting for transfers between devices  26.9 us (26%)
  Pallas kernels  14.6 us (14%)
  local copies, waits for them, and re-layouts  5.51 us (5%)
    ppermute x18, starting transfers between devices, exchange(): return (lax.ppermute(hi, axis, up), lax.ppermute(lo, axis, down))  35.6 us
    ppermute x18, waiting for transfers between devices, exchange(): return (lax.ppermute(hi, axis, up), lax.ppermute(lo, axis, down))  22.7 us
    all_to_all x3, starting transfers between devices, swap(): lax.all_to_all(rows.reshape(count, -1), axes, 0, 0, tiled=True)  21.3 us
    unnamed x26, local copies, waits for them, and re-layouts  5.2 us
    all_to_all x3, waiting for transfers between devices, swap(): lax.all_to_all(rows.reshape(count, -1), axes, 0, 0, tiled=True)  4.15 us
    pallas_call x1, Pallas kernels, on_device(): run(edge_kernel, cube + [((K, N, W), BF16), ((7 * W, W), F32)], [SMEM] *...  2.99 us
  transfers between devices with their start and end apart: 21, of which 16 were waited for; matrix products, arithmetic and copies ran while one was open for 0% of the time, Pallas kernels for 3%

profile of v2, /device:TPU:1, one launch (start us, length us, event | category | flops | bytes accessed | tf_op | source)
XLA Modules:
  0.0 104.7 jit_solution(7407547972892050762)
XLA Ops:
  0.6 0.7 copy-done.11
  1.3 1.0 copy-done
  2.4 0.9 copy-done.2
  3.3 0.9 copy-done.4
  4.2 0.8 copy-done.8
  4.9 1.3 %forward.1 = (f32[8,8,8,128]{3,2,1,0:T(8,128)S(1)}, f32[8,8,128]{2,1,0:T(8,128)S(1)}, f32[8,8,128]{2,1,0:T(8,128)S(1)}, f32[4,512,128]{2,1,0:T(8,128)S(1)}, bf16[4,512,128]{2,1,0:T(8,128)(2,1)S(1)}) custom-call(s32[4,3]{1,0:T(4,128)S(1)} %copy-done.11, bf16[512,128]{1,0:T(8,128)(2,1)S(1)} %bitcast.21, bf16[4,512,128]{2,1,0:T(8,128)(2,1)S(1)} %bitcast.17, ...), custom_call_target="tpu_custom_call" | custom-call | tf_op jit(solution)/shard_map/forward/pallas_call | solution.py:295
  6.2 3.8 %collective-permute-start = (f32[8,8,128]{2,1,0:T(8,128)S(1)}, f32[8,8,128]{2,1,0:T(8,128)S(1)}, u32[]{:S(2)}, u32[]{:S(2)}) collective-permute-start(f32[8,8,128]{2,1,0:T(8,128)S(1)} %get-tuple-element.53), channel_id=1, source_target_pairs={{0,16},{16,32},{32,48},{48,64},{64,80},{80,96},{96,112},{112,128},... | collective-permute-start | bytes 98312 | tf_op jit(solution)/shard_map/ppermute | solution.py:231
  10.0 5.4 %collective-permute-start.1 = (f32[8,8,128]{2,1,0:T(8,128)S(1)}, f32[8,8,128]{2,1,0:T(8,128)S(1)}, u32[]{:S(2)}, u32[]{:S(2)}) collective-permute-start(f32[8,8,128]{2,1,0:T(8,128)S(1)} %get-tuple-element.54), channel_id=1, source_target_pairs={{16,0},{32,16},{48,32},{64,48},{80,64},{96,80},{112,96},{128,112},... | collective-permute-start | bytes 98312 | tf_op jit(solution)/shard_map/ppermute | solution.py:231
  15.4 0.1 stack.27
  15.5 1.1 %collective-permute-done.rlo = f32[8,8,128]{2,1,0:T(8,128)S(1)} collective-permute-done((f32[8,8,128]{2,1,0:T(8,128)S(1)}, f32[8,8,128]{2,1,0:T(8,128)S(1)}, u32[]{:S(2)}, u32[]{:S(2)}) %collective-permute-start) | collective-permute-done | bytes 32800 | tf_op jit(solution)/shard_map/ppermute | solution.py:231
  16.6 0.6 after_x_1.1
  17.2 1.9 %collective-permute-start.2 = (f32[8,8,128]{2,1,0:T(8,128)S(1)}, f32[8,8,128]{2,1,0:T(8,128)S(1)}, u32[]{:S(2)}, u32[]{:S(2)}) collective-permute-start(f32[8,8,128]{2,1,0:T(8,128)S(1)} %get-tuple-element.56), channel_id=1, source_target_pairs={{0,4},{4,8},{8,12},{12,0},{1,5},{5,9},{9,13},{13,1},{2,6},{6,10},{... | collective-permute-start | bytes 98312 | tf_op jit(solution)/shard_map/ppermute | solution.py:231
  19.1 0.0 collective-permute-start.3
  19.1 1.0 collective-permute-done.2.rlo
  20.2 2.3 %collective-permute-done.3.rhi = f32[8,8,128]{2,1,0:T(8,128)S(1)} collective-permute-done((f32[8,8,128]{2,1,0:T(8,128)S(1)}, f32[8,8,128]{2,1,0:T(8,128)S(1)}, u32[]{:S(2)}, u32[]{:S(2)}) %collective-permute-start.3) | collective-permute-done | bytes 32800 | tf_op jit(solution)/shard_map/ppermute | solution.py:231
  22.5 0.6 after_y_1.1
  23.1 1.3 %collective-permute-start.4 = (f32[8,8,128]{2,1,0:T(8,128)S(1)}, f32[8,8,128]{2,1,0:T(8,128)S(1)}, u32[]{:S(2)}, u32[]{:S(2)}) collective-permute-start(f32[8,8,128]{2,1,0:T(8,128)S(1)} %get-tuple-element.59), channel_id=1, source_target_pairs={{0,1},{1,2},{2,3},{3,0},{4,5},{5,6},{6,7},{7,4},{8,9},{9,10},{10,1... | collective-permute-start | bytes 98312 | tf_op jit(solution)/shard_map/ppermute | solution.py:231
  24.4 1.5 %collective-permute-start.5 = (f32[8,8,128]{2,1,0:T(8,128)S(1)}, f32[8,8,128]{2,1,0:T(8,128)S(1)}, u32[]{:S(2)}, u32[]{:S(2)}) collective-permute-start(f32[8,8,128]{2,1,0:T(8,128)S(1)} %get-tuple-element.60), channel_id=1, source_target_pairs={{1,0},{2,1},{3,2},{0,3},{5,4},{6,5},{7,6},{4,7},{9,8},{10,9},{11,1... | collective-permute-start | bytes 98312 | tf_op jit(solution)/shard_map/ppermute | solution.py:231
  25.9 0.0 copy-start.10
  25.9 0.1 div.16
  26.0 1.6 %collective-permute-done.4.rlo = f32[8,8,128]{2,1,0:T(8,128)S(1)} collective-permute-done((f32[8,8,128]{2,1,0:T(8,128)S(1)}, f32[8,8,128]{2,1,0:T(8,128)S(1)}, u32[]{:S(2)}, u32[]{:S(2)}) %collective-permute-start.4) | collective-permute-done | bytes 32800 | tf_op jit(solution)/shard_map/ppermute | solution.py:231
  27.6 0.1 broadcast_in_dim.2.inverse
  27.7 0.8 copy-done.3
  28.5 0.1 copy-done.6
  28.6 1.1 %node.1 = (f32[8,8,8,128]{3,2,1,0:T(8,128)S(1)}, f32[8,8,128]{2,1,0:T(8,128)S(1)}, f32[8,8,128]{2,1,0:T(8,128)S(1)}, bf16[512,128]{1,0:T(8,128)(2,1)S(1)}, bf16[...) custom-call(s32[6]{0:T(128)S(1)} %convert_element_type.12.rim, f32[8,8,8,128]{3,2,1,0:T(8,128)S(1)} %get-tuple-element.58.field, ...), custom_call_target="tpu_custom_call" | custom-call | tf_op jit(solution)/shard_map/node/pallas_call | solution.py:305
  29.6 0.0 copy-start.1
  29.6 1.7 %collective-permute-start.6 = (f32[8,8,128]{2,1,0:T(8,128)S(1)}, f32[8,8,128]{2,1,0:T(8,128)S(1)}, u32[]{:S(2)}, u32[]{:S(2)}) collective-permute-start(f32[8,8,128]{2,1,0:T(8,128)S(1)} %get-tuple-element.62), channel_id=1, source_target_pairs={{0,16},{16,32},{32,48},{48,64},{64,80},{80,96},{96,112},{112,128},... | collective-permute-start | bytes 98312 | tf_op jit(solution)/shard_map/ppermute | solution.py:231
  31.3 4.4 %collective-permute-start.7 = (f32[8,8,128]{2,1,0:T(8,128)S(1)}, f32[8,8,128]{2,1,0:T(8,128)S(1)}, u32[]{:S(2)}, u32[]{:S(2)}) collective-permute-start(f32[8,8,128]{2,1,0:T(8,128)S(1)} %get-tuple-element.63), channel_id=1, source_target_pairs={{16,0},{32,16},{48,32},{64,48},{80,64},{96,80},{112,96},{128,112},... | collective-permute-start | bytes 98312 | tf_op jit(solution)/shard_map/ppermute | solution.py:231
  35.7 1.2 %collective-permute-done.6.rlo = f32[8,8,128]{2,1,0:T(8,128)S(1)} collective-permute-done((f32[8,8,128]{2,1,0:T(8,128)S(1)}, f32[8,8,128]{2,1,0:T(8,128)S(1)}, u32[]{:S(2)}, u32[]{:S(2)}) %collective-permute-start.6) | collective-permute-done | bytes 32800 | tf_op jit(solution)/shard_map/ppermute | solution.py:231
  37.0 0.6 after_x_2.1
  37.5 1.5 %collective-permute-start.8 = (f32[8,8,128]{2,1,0:T(8,128)S(1)}, f32[8,8,128]{2,1,0:T(8,128)S(1)}, u32[]{:S(2)}, u32[]{:S(2)}) collective-permute-start(f32[8,8,128]{2,1,0:T(8,128)S(1)} %get-tuple-element.65), channel_id=1, source_target_pairs={{0,4},{4,8},{8,12},{12,0},{1,5},{5,9},{9,13},{13,1},{2,6},{6,10},{... | collective-permute-start | bytes 98312 | tf_op jit(solution)/shard_map/ppermute | solution.py:231
  39.0 1.0 collective-permute-done.8.rlo
  40.1 2.3 %collective-permute-done.9.rhi = f32[8,8,128]{2,1,0:T(8,128)S(1)} collective-permute-done((f32[8,8,128]{2,1,0:T(8,128)S(1)}, f32[8,8,128]{2,1,0:T(8,128)S(1)}, u32[]{:S(2)}, u32[]{:S(2)}) %collective-permute-start.9) | collective-permute-done | bytes 32800 | tf_op jit(solution)/shard_map/ppermute | solution.py:231
  42.4 0.6 after_y_2.1
  43.0 1.3 %collective-permute-start.10 = (f32[8,8,128]{2,1,0:T(8,128)S(1)}, f32[8,8,128]{2,1,0:T(8,128)S(1)}, u32[]{:S(2)}, u32[]{:S(2)}) collective-permute-start(f32[8,8,128]{2,1,0:T(8,128)S(1)} %get-tuple-element.68), channel_id=1, source_target_pairs={{0,1},{1,2},{2,3},{3,0},{4,5},{5,6},{6,7},{7,4},{8,9},{9,10},{10,1... | collective-permute-start | bytes 98312 | tf_op jit(solution)/shard_map/ppermute | solution.py:231
  44.3 1.7 %collective-permute-start.11 = (f32[8,8,128]{2,1,0:T(8,128)S(1)}, f32[8,8,128]{2,1,0:T(8,128)S(1)}, u32[]{:S(2)}, u32[]{:S(2)}) collective-permute-start(f32[8,8,128]{2,1,0:T(8,128)S(1)} %get-tuple-element.69), channel_id=1, source_target_pairs={{1,0},{2,1},{3,2},{0,3},{5,4},{6,5},{7,6},{4,7},{9,8},{10,9},{11,1... | collective-permute-start | bytes 98312 | tf_op jit(solution)/shard_map/ppermute | solution.py:231
  46.0 0.6 prepare.1
  46.6 0.0 copy-start.5
  46.6 0.0 copy-start.9
  46.6 0.3 node_grads.1
  46.9 0.5 collective-permute-done.10.rlo
  47.4 0.1 copy-done.5
  47.5 3.0 %edge.1 = (f32[8,8,8,128]{3,2,1,0:T(8,128)S(1)}, f32[8,8,128]{2,1,0:T(8,128)S(1)}, f32[8,8,128]{2,1,0:T(8,128)S(1)}, bf16[4,512,128]{2,1,0:T(8,128)(2,1)S(1)}, f32[896,128]{1,0:T(8,128)}) custom-call(s32[6]{0:T(128)S(1)} %convert_element_type.12.rim, s32[4,3]{1,0:T(4,128)S(1)} %copy-done.11, f32[8,8,8,128]{3,2,1,0:T(8,128)S(1)} %get-tuple-element.67.field, ...), custom_call_target="tpu_custom_call" | custom-call | tf_op jit(solution)/shard_map/edge/pallas_call | solution.py:312
  50.5 6.3 %all-to-all-start = ((f32[32,1,3584]{2,1,0:T(1,128)}), f32[32,1,3584]{2,1,0:T(1,128)S(1)}, u32[]{:S(2)}, u32[]{:S(2)}) async-start(f32[32,1,3584]{2,1,0:T(1,128)} %bitcast.9), calls=%async_computation | async-start | bytes 917504 | tf_op jit(solution)/shard_map/all_to_all | solution.py:249
  56.8 2.9 %collective-permute-start.12 = (f32[8,8,128]{2,1,0:T(8,128)S(1)}, f32[8,8,128]{2,1,0:T(8,128)S(1)}, u32[]{:S(2)}, u32[]{:S(2)}) collective-permute-start(f32[8,8,128]{2,1,0:T(8,128)S(1)} %get-tuple-element.82), channel_id=1, source_target_pairs={{0,16},{16,32},{32,48},{48,64},{64,80},{80,96},{96,112},{112,128},... | collective-permute-start | bytes 98312 | tf_op jit(solution)/shard_map/ppermute | solution.py:231
  59.8 4.4 %collective-permute-start.13 = (f32[8,8,128]{2,1,0:T(8,128)S(1)}, f32[8,8,128]{2,1,0:T(8,128)S(1)}, u32[]{:S(2)}, u32[]{:S(2)}) collective-permute-start(f32[8,8,128]{2,1,0:T(8,128)S(1)} %get-tuple-element.83), channel_id=1, source_target_pairs={{16,0},{32,16},{48,32},{64,48},{80,64},{96,80},{112,96},{128,112},... | collective-permute-start | bytes 98312 | tf_op jit(solution)/shard_map/ppermute | solution.py:231
  64.2 1.8 %collective-permute-done.12.rlo = f32[8,8,128]{2,1,0:T(8,128)S(1)} collective-permute-done((f32[8,8,128]{2,1,0:T(8,128)S(1)}, f32[8,8,128]{2,1,0:T(8,128)S(1)}, u32[]{:S(2)}, u32[]{:S(2)}) %collective-permute-start.12) | collective-permute-done | bytes 32800 | tf_op jit(solution)/shard_map/ppermute | solution.py:231
  66.0 1.4 %collective-permute-done.13.rhi = f32[8,8,128]{2,1,0:T(8,128)S(1)} collective-permute-done((f32[8,8,128]{2,1,0:T(8,128)S(1)}, f32[8,8,128]{2,1,0:T(8,128)S(1)}, u32[]{:S(2)}, u32[]{:S(2)}) %collective-permute-start.13) | collective-permute-done | bytes 32800 | tf_op jit(solution)/shard_map/ppermute | solution.py:231
  67.4 0.2 all-to-all-done
  67.6 1.2 %after_x_fold.1 = (f32[8,8,8,128]{3,2,1,0:T(8,128)S(1)}, f32[8,8,128]{2,1,0:T(8,128)S(1)}, f32[8,8,128]{2,1,0:T(8,128)S(1)}, f32[224,128]{1,0:T(8,128)}) custom-call(s32[6]{0:T(128)S(1)} %convert_element_type.12.rim, f32[8,8,8,128]{3,2,1,0:T(8,128)S(1)} %get-tuple-element.81.field, f32[8,8,128]{2,1,0:T(8,128)S(1)} %collective-permute-done.12.rlo, ...), custom_call_target="tpu_custom_call" | custom-call | tf_op jit(solution)/shard_map/after_x_fold/pallas_call | solution.py:258
  68.8 8.3 %all-to-all-start.1 = ((f32[8,1,3584]{2,1,0:T(1,128)}), f32[8,1,3584]{2,1,0:T(1,128)S(1)}, u32[]{:S(2)}, u32[]{:S(2)}) async-start(f32[8,1,3584]{2,1,0:T(1,128)} %bitcast.11), calls=%async_computation.1 | async-start | bytes 229376 | tf_op jit(solution)/shard_map/all_to_all | solution.py:249
  77.1 1.0 collective-permute-start.14
  78.1 1.0 collective-permute-done.14.rlo
  79.1 2.4 %collective-permute-done.15.rhi = f32[8,8,128]{2,1,0:T(8,128)S(1)} collective-permute-done((f32[8,8,128]{2,1,0:T(8,128)S(1)}, f32[8,8,128]{2,1,0:T(8,128)S(1)}, u32[]{:S(2)}, u32[]{:S(2)}) %collective-permute-start.15) | collective-permute-done | bytes 32800 | tf_op jit(solution)/shard_map/ppermute | solution.py:231
  81.5 3.2 %all-to-all-done.1 = f32[8,1,3584]{2,1,0:T(1,128)S(1)} async-done(((f32[8,1,3584]{2,1,0:T(1,128)}), f32[8,1,3584]{2,1,0:T(1,128)S(1)}, u32[]{:S(2)}, u32[]{:S(2)}) %all-to-all-start.1) | async-done | bytes 114720 | tf_op jit(solution)/shard_map/all_to_all | solution.py:249
  84.7 1.4 %after_y_fold.1 = (f32[8,8,8,128]{3,2,1,0:T(8,128)S(1)}, f32[8,8,128]{2,1,0:T(8,128)S(1)}, f32[8,8,128]{2,1,0:T(8,128)S(1)}, f32[896,128]{1,0:T(8,128)}) custom-call(s32[6]{0:T(128)S(1)} %convert_element_type.12.rim, f32[8,8,8,128]{3,2,1,0:T(8,128)S(1)} %get-tuple-element.85.field, f32[8,8,128]{2,1,0:T(8,128)S(1)} %collective-permute-done.14.rlo, ...), custom_call_target="tpu_custom_call" | custom-call | tf_op jit(solution)/shard_map/after_y_fold/pallas_call | solution.py:267
  86.1 6.7 %all-to-all-start.2 = ((f32[32,1,3584]{2,1,0:T(1,128)}), f32[32,1,3584]{2,1,0:T(1,128)S(1)}, u32[]{:S(2)}, u32[]{:S(2)}) async-start(f32[32,1,3584]{2,1,0:T(1,128)} %bitcast.15), calls=%async_computation.2 | async-start | bytes 917504 | tf_op jit(solution)/shard_map/all_to_all | solution.py:249
  92.8 1.4 %collective-permute-start.16 = (f32[8,8,128]{2,1,0:T(8,128)S(1)}, f32[8,8,128]{2,1,0:T(8,128)S(1)}, u32[]{:S(2)}, u32[]{:S(2)}) collective-permute-start(f32[8,8,128]{2,1,0:T(8,128)S(1)} %get-tuple-element.90), channel_id=1, source_target_pairs={{0,1},{1,2},{2,3},{3,0},{4,5},{5,6},{6,7},{7,4},{8,9},{9,10},{10,1... | collective-permute-start | bytes 98312 | tf_op jit(solution)/shard_map/ppermute | solution.py:231
  94.3 1.3 %collective-permute-start.17 = (f32[8,8,128]{2,1,0:T(8,128)S(1)}, f32[8,8,128]{2,1,0:T(8,128)S(1)}, u32[]{:S(2)}, u32[]{:S(2)}) collective-permute-start(f32[8,8,128]{2,1,0:T(8,128)S(1)} %get-tuple-element.91), channel_id=1, source_target_pairs={{1,0},{2,1},{3,2},{0,3},{5,4},{6,5},{7,6},{4,7},{9,8},{10,9},{11,1... | collective-permute-start | bytes 98312 | tf_op jit(solution)/shard_map/ppermute | solution.py:231
  95.6 1.1 %edge_grad.1 = bf16[4,512,128]{2,1,0:T(8,128)(2,1)} custom-call(bf16[4,512,128]{2,1,0:T(8,128)(2,1)S(1)} %get-tuple-element.92.slopes, bf16[384,128]{1,0:T(8,128)(2,1)S(1)} %copy-done.5), custom_call_target="tpu_custom_call" | custom-call | tf_op jit(solution)/shard_map/edge_grad/pallas_call | solution.py:320
  96.7 5.0 %collective-permute-done.16.rlo = f32[8,8,128]{2,1,0:T(8,128)S(1)} collective-permute-done((f32[8,8,128]{2,1,0:T(8,128)S(1)}, f32[8,8,128]{2,1,0:T(8,128)S(1)}, u32[]{:S(2)}, u32[]{:S(2)}) %collective-permute-start.16) | collective-permute-done | bytes 32800 | tf_op jit(solution)/shard_map/ppermute | solution.py:231
  101.7 1.3 %last.1 = bf16[512,128]{1,0:T(8,128)(2,1)} custom-call(s32[6]{0:T(128)S(1)} %convert_element_type.12.rim, f32[8,8,8,128]{3,2,1,0:T(8,128)S(1)} %get-tuple-element.89.field, f32[8,8,128]{2,1,0:T(8,128)S(1)} %collective-permute-done.16.rlo, f32[8,8,128]{2,1,0:T(8,128)S(1)} %collective-permute-done.17.rhi), custom_call_target="tpu_custom_call" | custom-call | tf_op jit(solution)/shard_map/last/pallas_call | solution.py:321
  103.0 0.8 all-to-all-done.2
  103.7 1.0 clip.1
  (23 shorter events, 0.1 us)
Async XLA Ops:
  0.6 0.7 copy-start.11
  1.3 1.0 copy-start
  2.4 0.9 copy-start.2
  3.3 0.9 copy-start.4
  4.2 0.8 copy-start.8
  6.2 10.4 %collective-permute-start = (f32[8,8,128]{2,1,0:T(8,128)S(1)}, f32[8,8,128]{2,1,0:T(8,128)S(1)}, u32[]{:S(2)}, u32[]{:S(2)}) collective-permute-start(f32[8,8,128]{2,1,0:T(8,128)S(1)} %get-tuple-element.53), channel_id=1, source_target_pairs={{0,16},{16,32},{32,48},{48,64},{64,80},{80,96},{96,112},{112,128},... | collective-permute-start | bytes 98312 | tf_op jit(solution)/shard_map/ppermute | solution.py:231
  10.0 6.6 %collective-permute-start.1 = (f32[8,8,128]{2,1,0:T(8,128)S(1)}, f32[8,8,128]{2,1,0:T(8,128)S(1)}, u32[]{:S(2)}, u32[]{:S(2)}) collective-permute-start(f32[8,8,128]{2,1,0:T(8,128)S(1)} %get-tuple-element.54), channel_id=1, source_target_pairs={{16,0},{32,16},{48,32},{64,48},{80,64},{96,80},{112,96},{128,112},... | collective-permute-start | bytes 98312 | tf_op jit(solution)/shard_map/ppermute | solution.py:231
  17.2 2.9 %collective-permute-start.2 = (f32[8,8,128]{2,1,0:T(8,128)S(1)}, f32[8,8,128]{2,1,0:T(8,128)S(1)}, u32[]{:S(2)}, u32[]{:S(2)}) collective-permute-start(f32[8,8,128]{2,1,0:T(8,128)S(1)} %get-tuple-element.56), channel_id=1, source_target_pairs={{0,4},{4,8},{8,12},{12,0},{1,5},{5,9},{9,13},{13,1},{2,6},{6,10},{... | collective-permute-start | bytes 98312 | tf_op jit(solution)/shard_map/ppermute | solution.py:231
  19.1 3.3 %collective-permute-start.3 = (f32[8,8,128]{2,1,0:T(8,128)S(1)}, f32[8,8,128]{2,1,0:T(8,128)S(1)}, u32[]{:S(2)}, u32[]{:S(2)}) collective-permute-start(f32[8,8,128]{2,1,0:T(8,128)S(1)} %get-tuple-element.57), channel_id=1, source_target_pairs={{4,0},{8,4},{12,8},{0,12},{5,1},{9,5},{13,9},{1,13},{6,2},{10,6},{... | collective-permute-start | bytes 98312 | tf_op jit(solution)/shard_map/ppermute | solution.py:231
  22.5 3.4 %copy-start.12 = (s32[8,8,8]{2,1,0:T(8,128)S(1)}, s32[8,8,8]{2,1,0:T(8,128)}, u32[]{:S(2)}) copy-start(s32[8,8,8]{2,1,0:T(8,128)} %param.11) | copy-start | bytes 6148
  23.1 4.5 %collective-permute-start.4 = (f32[8,8,128]{2,1,0:T(8,128)S(1)}, f32[8,8,128]{2,1,0:T(8,128)S(1)}, u32[]{:S(2)}, u32[]{:S(2)}) collective-permute-start(f32[8,8,128]{2,1,0:T(8,128)S(1)} %get-tuple-element.59), channel_id=1, source_target_pairs={{0,1},{1,2},{2,3},{3,0},{4,5},{5,6},{6,7},{7,4},{8,9},{9,10},{10,1... | collective-permute-start | bytes 98312 | tf_op jit(solution)/shard_map/ppermute | solution.py:231
  24.4 3.2 %collective-permute-start.5 = (f32[8,8,128]{2,1,0:T(8,128)S(1)}, f32[8,8,128]{2,1,0:T(8,128)S(1)}, u32[]{:S(2)}, u32[]{:S(2)}) collective-permute-start(f32[8,8,128]{2,1,0:T(8,128)S(1)} %get-tuple-element.60), channel_id=1, source_target_pairs={{1,0},{2,1},{3,2},{0,3},{5,4},{6,5},{7,6},{4,7},{9,8},{10,9},{11,1... | collective-permute-start | bytes 98312 | tf_op jit(solution)/shard_map/ppermute | solution.py:231
  25.8 1.9 %copy-start.7 = (bf16[256,128]{1,0:T(8,128)(2,1)S(1)}, bf16[256,128]{1,0:T(8,128)(2,1)}, u32[]{:S(2)}) copy-start(bf16[256,128]{1,0:T(8,128)(2,1)} %w_in.7) | copy-start | bytes 196612
  25.9 1.9 %copy-start.10 = (bf16[128,128]{1,0:T(8,128)(2,1)S(1)}, bf16[128,128]{1,0:T(8,128)(2,1)}, u32[]{:S(2)}) copy-start(bf16[128,128]{1,0:T(8,128)(2,1)} %w_out.4) | copy-start | bytes 98308
  27.6 0.9 copy-start.3
  27.6 1.0 copy-start.6
  29.6 16.4 %copy-start.1 = (bf16[4,8,8,8,128]{4,3,2,1,0:T(8,128)(2,1)S(1)}, bf16[4,8,8,8,128]{4,3,2,1,0:T(8,128)(2,1)}, u32[]{:S(2)}) copy-start(bf16[4,8,8,8,128]{4,3,2,1,0:T(8,128)(2,1)} %param.10) | copy-start | bytes 1572868
  29.6 7.3 %collective-permute-start.6 = (f32[8,8,128]{2,1,0:T(8,128)S(1)}, f32[8,8,128]{2,1,0:T(8,128)S(1)}, u32[]{:S(2)}, u32[]{:S(2)}) collective-permute-start(f32[8,8,128]{2,1,0:T(8,128)S(1)} %get-tuple-element.62), channel_id=1, source_target_pairs={{0,16},{16,32},{32,48},{48,64},{64,80},{80,96},{96,112},{112,128},... | collective-permute-start | bytes 98312 | tf_op jit(solution)/shard_map/ppermute | solution.py:231
  31.3 5.7 %collective-permute-start.7 = (f32[8,8,128]{2,1,0:T(8,128)S(1)}, f32[8,8,128]{2,1,0:T(8,128)S(1)}, u32[]{:S(2)}, u32[]{:S(2)}) collective-permute-start(f32[8,8,128]{2,1,0:T(8,128)S(1)} %get-tuple-element.63), channel_id=1, source_target_pairs={{16,0},{32,16},{48,32},{64,48},{80,64},{96,80},{112,96},{128,112},... | collective-permute-start | bytes 98312 | tf_op jit(solution)/shard_map/ppermute | solution.py:231
  37.5 2.5 %collective-permute-start.8 = (f32[8,8,128]{2,1,0:T(8,128)S(1)}, f32[8,8,128]{2,1,0:T(8,128)S(1)}, u32[]{:S(2)}, u32[]{:S(2)}) collective-permute-start(f32[8,8,128]{2,1,0:T(8,128)S(1)} %get-tuple-element.65), channel_id=1, source_target_pairs={{0,4},{4,8},{8,12},{12,0},{1,5},{5,9},{9,13},{13,1},{2,6},{6,10},{... | collective-permute-start | bytes 98312 | tf_op jit(solution)/shard_map/ppermute | solution.py:231
  39.0 3.3 %collective-permute-start.9 = (f32[8,8,128]{2,1,0:T(8,128)S(1)}, f32[8,8,128]{2,1,0:T(8,128)S(1)}, u32[]{:S(2)}, u32[]{:S(2)}) collective-permute-start(f32[8,8,128]{2,1,0:T(8,128)S(1)} %get-tuple-element.66), channel_id=1, source_target_pairs={{4,0},{8,4},{12,8},{0,12},{5,1},{9,5},{13,9},{1,13},{6,2},{10,6},{... | collective-permute-start | bytes 98312 | tf_op jit(solution)/shard_map/ppermute | solution.py:231
  43.0 4.4 %collective-permute-start.10 = (f32[8,8,128]{2,1,0:T(8,128)S(1)}, f32[8,8,128]{2,1,0:T(8,128)S(1)}, u32[]{:S(2)}, u32[]{:S(2)}) collective-permute-start(f32[8,8,128]{2,1,0:T(8,128)S(1)} %get-tuple-element.68), channel_id=1, source_target_pairs={{0,1},{1,2},{2,3},{3,0},{4,5},{5,6},{6,7},{7,4},{8,9},{9,10},{10,1... | collective-permute-start | bytes 98312 | tf_op jit(solution)/shard_map/ppermute | solution.py:231
  44.3 3.1 %collective-permute-start.11 = (f32[8,8,128]{2,1,0:T(8,128)S(1)}, f32[8,8,128]{2,1,0:T(8,128)S(1)}, u32[]{:S(2)}, u32[]{:S(2)}) collective-permute-start(f32[8,8,128]{2,1,0:T(8,128)S(1)} %get-tuple-element.69), channel_id=1, source_target_pairs={{1,0},{2,1},{3,2},{0,3},{5,4},{6,5},{7,6},{4,7},{9,8},{10,9},{11,1... | collective-permute-start | bytes 98312 | tf_op jit(solution)/shard_map/ppermute | solution.py:231
  46.6 0.9 copy-start.5
  46.6 0.9 copy-start.9
  50.5 17.1 %all-to-all-start = ((f32[32,1,3584]{2,1,0:T(1,128)}), f32[32,1,3584]{2,1,0:T(1,128)S(1)}, u32[]{:S(2)}, u32[]{:S(2)}) async-start(f32[32,1,3584]{2,1,0:T(1,128)} %bitcast.9), calls=%async_computation | async-start | bytes 917504 | tf_op jit(solution)/shard_map/all_to_all | solution.py:249
  56.8 9.2 %collective-permute-start.12 = (f32[8,8,128]{2,1,0:T(8,128)S(1)}, f32[8,8,128]{2,1,0:T(8,128)S(1)}, u32[]{:S(2)}, u32[]{:S(2)}) collective-permute-start(f32[8,8,128]{2,1,0:T(8,128)S(1)} %get-tuple-element.82), channel_id=1, source_target_pairs={{0,16},{16,32},{32,48},{48,64},{64,80},{80,96},{96,112},{112,128},... | collective-permute-start | bytes 98312 | tf_op jit(solution)/shard_map/ppermute | solution.py:231
  59.8 7.6 %collective-permute-start.13 = (f32[8,8,128]{2,1,0:T(8,128)S(1)}, f32[8,8,128]{2,1,0:T(8,128)S(1)}, u32[]{:S(2)}, u32[]{:S(2)}) collective-permute-start(f32[8,8,128]{2,1,0:T(8,128)S(1)} %get-tuple-element.83), channel_id=1, source_target_pairs={{16,0},{32,16},{48,32},{64,48},{80,64},{96,80},{112,96},{128,112},... | collective-permute-start | bytes 98312 | tf_op jit(solution)/shard_map/ppermute | solution.py:231
  68.8 15.9 %all-to-all-start.1 = ((f32[8,1,3584]{2,1,0:T(1,128)}), f32[8,1,3584]{2,1,0:T(1,128)S(1)}, u32[]{:S(2)}, u32[]{:S(2)}) async-start(f32[8,1,3584]{2,1,0:T(1,128)} %bitcast.11), calls=%async_computation.1 | async-start | bytes 229376 | tf_op jit(solution)/shard_map/all_to_all | solution.py:249
  77.1 2.0 %collective-permute-start.14 = (f32[8,8,128]{2,1,0:T(8,128)S(1)}, f32[8,8,128]{2,1,0:T(8,128)S(1)}, u32[]{:S(2)}, u32[]{:S(2)}) collective-permute-start(f32[8,8,128]{2,1,0:T(8,128)S(1)} %get-tuple-element.86), channel_id=1, source_target_pairs={{0,4},{4,8},{8,12},{12,0},{1,5},{5,9},{9,13},{13,1},{2,6},{6,10},{... | collective-permute-start | bytes 98312 | tf_op jit(solution)/shard_map/ppermute | solution.py:231
  78.1 3.4 %collective-permute-start.15 = (f32[8,8,128]{2,1,0:T(8,128)S(1)}, f32[8,8,128]{2,1,0:T(8,128)S(1)}, u32[]{:S(2)}, u32[]{:S(2)}) collective-permute-start(f32[8,8,128]{2,1,0:T(8,128)S(1)} %get-tuple-element.87), channel_id=1, source_target_pairs={{4,0},{8,4},{12,8},{0,12},{5,1},{9,5},{13,9},{1,13},{6,2},{10,6},{... | collective-permute-start | bytes 98312 | tf_op jit(solution)/shard_map/ppermute | solution.py:231
  86.1 17.6 %all-to-all-start.2 = ((f32[32,1,3584]{2,1,0:T(1,128)}), f32[32,1,3584]{2,1,0:T(1,128)S(1)}, u32[]{:S(2)}, u32[]{:S(2)}) async-start(f32[32,1,3584]{2,1,0:T(1,128)} %bitcast.15), calls=%async_computation.2 | async-start | bytes 917504 | tf_op jit(solution)/shard_map/all_to_all | solution.py:249
  92.8 8.8 %collective-permute-start.16 = (f32[8,8,128]{2,1,0:T(8,128)S(1)}, f32[8,8,128]{2,1,0:T(8,128)S(1)}, u32[]{:S(2)}, u32[]{:S(2)}) collective-permute-start(f32[8,8,128]{2,1,0:T(8,128)S(1)} %get-tuple-element.90), channel_id=1, source_target_pairs={{0,1},{1,2},{2,3},{3,0},{4,5},{5,6},{6,7},{7,4},{8,9},{9,10},{10,1... | collective-permute-start | bytes 98312 | tf_op jit(solution)/shard_map/ppermute | solution.py:231
  94.3 7.4 %collective-permute-start.17 = (f32[8,8,128]{2,1,0:T(8,128)S(1)}, f32[8,8,128]{2,1,0:T(8,128)S(1)}, u32[]{:S(2)}, u32[]{:S(2)}) collective-permute-start(f32[8,8,128]{2,1,0:T(8,128)S(1)} %get-tuple-element.91), channel_id=1, source_target_pairs={{1,0},{2,1},{3,2},{0,3},{5,4},{6,5},{7,6},{4,7},{9,8},{10,9},{11,1... | collective-permute-start | bytes 98312 | tf_op jit(solution)/shard_map/ppermute | solution.py:231

commit v3 on v1

v3 whole, which is shorter than its diff:
```python
import functools
import math

import jax
import jax.numpy as jnp
from jax import lax
from jax.experimental import pallas as pl
from jax.experimental.pallas import tpu as pltpu
from jax.sharding import Mesh
from jax.sharding import PartitionSpec as P

B = 8
W = 128
K = 4
N = B * B * B
CUBE = (B, B, B, W)
FACE = (B, B, W)
F32 = jnp.float32
BF16 = jnp.bfloat16
GRANT = 12 * 1024 * 1024

VMEM = pl.BlockSpec(memory_space=pltpu.VMEM)
SMEM = pl.BlockSpec(memory_space=pltpu.SMEM)
HBM = pl.BlockSpec(memory_space=pltpu.HBM)
PAD = pltpu.VMEM((B + 2, B + 2, B, W), F32)
WORK = pltpu.VMEM(CUBE, F32)

GX, GY, GZ = ("z", "yh"), ("yl", "c"), ("x",)
NEAR, FAR = ("yh", "yl", "c", "x"), ("z",)


def call(body, outs, specs, name, scratch=()):
    return pl.pallas_call(
        body,
        out_shape=[jax.ShapeDtypeStruct(s, t) for s, t in outs],
        in_specs=specs,
        out_specs=[VMEM] * len(outs),
        scratch_shapes=list(scratch),
        compiler_params=pltpu.CompilerParams(vmem_limit_bytes=GRANT),
        name=name,
    )


def in_hbm(array):
    return pltpu.with_memory_space_constraint(array, pltpu.HBM)


def dot(a, b):
    return jnp.dot(a, b, preferred_element_type=F32)


def dot_t(a, b):
    return lax.dot_general(a, b, (((1,), (1,)), ((), ())), preferred_element_type=F32)


def fill_ring(pad, value):
    pad[1:9, 1:9] = value
    pad[0, 1:9] = value[7]
    pad[9, 1:9] = value[0]
    pad[:, 0] = pad[:, 8]
    pad[:, 9] = pad[:, 1]


def ring_shift(pad, o0, o1, o2):
    moved = pad[pl.ds(1 + o0, B), pl.ds(1 + o1, B)].reshape(B * B, B, W)
    moved = pltpu.roll(moved, lax.rem(B - o2, B), 1)
    return moved.reshape(N, W)


def inside(offs, k):
    ok = None
    for which in range(3):
        at = lax.broadcasted_iota(jnp.int32, CUBE, which) + offs[k, which]
        one = (at >= 0) & (at < B)
        ok = one if ok is None else ok & one
    return ok


def forward_kernel(
    nodes_h, edges_h, w_in_h, w_out_h, offs_h,
    local, xlo, xhi, preact, hidden, nodes, edges, w_in, w_out,
    pad, offs, sems,
):
    pairs = [(nodes_h, nodes), (w_in_h, w_in), (offs_h, offs), (w_out_h, w_out)]
    pairs += [(edges_h.at[k], edges.at[k]) for k in range(K)]
    copies = [pltpu.make_async_copy(a, b, sems.at[i]) for i, (a, b) in enumerate(pairs)]
    for copy in copies:
        copy.start()
    for copy in copies[:3]:
        copy.wait()
    node = nodes[...]
    fill_ring(pad, dot(node, w_in[:W]).reshape(CUBE))
    receiver = dot(node, w_in[W : 2 * W])
    copies[3].wait()
    total = jnp.zeros((N, W), F32)
    for k in range(K):
        copies[4 + k].wait()
        pre = ring_shift(pad, offs[k, 0], offs[k, 1], offs[k, 2]) + receiver + dot(edges[k], w_in[2 * W :])
        preact[k] = pre
        act = (pre * jax.nn.sigmoid(pre)).reshape(CUBE)
        kept = jnp.where(inside(offs, k), act, 0.0).reshape(N, W).astype(BF16)
        hidden[k] = kept
        total = total + dot(kept, w_out[...])
    total = total.reshape(CUBE)
    local[...] = total
    xlo[...] = total[0]
    xhi[...] = total[B - 1]


def prepare_node_kernel(nodes, cot, w_in, w_out, pre, upstream, w_back):
    pre[...] = dot(nodes[...], w_in[:W])
    upstream[...] = dot_t(cot[...], w_out[...])
    w_back[...] = w_in[W:].T


def prepare_edge_kernel(offs, preact, hidden, nodes, edges, w_in, w_out, dact, hidden_t, left, w_out_t, w_back, pad):
    node = nodes[...]
    node_t = node.T
    fill_ring(pad, node.astype(F32).reshape(CUBE))
    for k in range(K):
        pre = preact[k]
        sigma = jax.nn.sigmoid(pre)
        rate = (sigma * (1.0 + pre * (1.0 - sigma))).reshape(CUBE)
        dact[k] = jnp.where(inside(offs, k), rate, 0.0).reshape(N, W)
        hidden_t[k * W : (k + 1) * W] = hidden[k].T
        here = pl.ds(k * N, N)
        left[:W, here] = ring_shift(pad, offs[k, 0], offs[k, 1], offs[k, 2]).astype(BF16).T
        left[W : 2 * W, here] = node_t
        left[2 * W :, here] = edges[k].T
    w_out_t[...] = w_out[...].T
    w_back[:W] = w_in[W : 2 * W].T
    w_back[W:] = w_in[:W].T


def shown(rim, which, plane):
    return jnp.where(rim[which] > 0, plane, 0.0)


def add_x(rim, x, out):
    out[0] = out[0] + shown(rim, 0, x[0][...])
    out[B - 1] = out[B - 1] + shown(rim, 1, x[1][...])


def add_y(rim, y, out):
    out[:, 0] = out[:, 0] + shown(rim, 2, y[0][...])
    out[:, B - 1] = out[:, B - 1] + shown(rim, 3, y[1][...])


def add_z(rim, z, out):
    out[:, :, 0, :] = out[:, :, 0, :] + shown(rim, 4, z[0][...])
    out[:, :, B - 1, :] = out[:, :, B - 1, :] + shown(rim, 5, z[1][...])


def y_faces_after_x(rim, field, x0, x1, lo, hi):
    for at, out in ((0, lo), (B - 1, hi)):
        out[...] = field[:, at]
        out[0] = out[0] + shown(rim, 0, x0[at])
        out[B - 1] = out[B - 1] + shown(rim, 1, x1[at])


def z_faces_after_y(rim, field, x0, x1, y0, y1, lo, hi):
    for at, out in ((0, lo), (B - 1, hi)):
        out[...] = field[:, :, at, :]
        out[0] = out[0] + shown(rim, 0, x0[:, at, :])
        out[B - 1] = out[B - 1] + shown(rim, 1, x1[:, at, :])
        out[:, 0, :] = out[:, 0, :] + shown(rim, 2, y0[:, at, :])
        out[:, B - 1, :] = out[:, B - 1, :] + shown(rim, 3, y1[:, at, :])


def y_faces_after_z(rim, field, z0, z1, lo, hi):
    for at, out in ((0, lo), (B - 1, hi)):
        out[...] = field[:, at]
        out[:, 0, :] = out[:, 0, :] + shown(rim, 4, z0[:, at, :])
        out[:, B - 1, :] = out[:, B - 1, :] + shown(rim, 5, z1[:, at, :])


def x_faces_after_y(rim, field, z0, z1, y0, y1, lo, hi):
    for at, out in ((0, lo), (B - 1, hi)):
        out[...] = field[at]
        out[:, 0, :] = out[:, 0, :] + shown(rim, 4, z0[at])
        out[:, B - 1, :] = out[:, B - 1, :] + shown(rim, 5, z1[at])
        out[0] = out[0] + shown(rim, 2, y0[at])
        out[B - 1] = out[B - 1] + shown(rim, 3, y1[at])


def whole(rim, field, x0, x1, y0, y1, z0, z1, work):
    work[...] = field[...]
    add_x(rim, (x0, x1), work)
    add_y(rim, (y0, y1), work)
    add_z(rim, (z0, z1), work)
    return work[...].reshape(N, W)


def node_kernel(
    rim, field, x0, x1, y0, y1, z0, z1, inverse, begun, upstream, w_in, w_back,
    local, xlo, xhi, gathered, slope, hidden, work,
):
    inv = inverse[...]
    agg = (whole(rim, field, x0, x1, y0, y1, z0, z1, work) * inv).astype(BF16)
    gathered[...] = agg
    pre = begun[...] + dot(agg, w_in[W:])
    sigma = jax.nn.sigmoid(pre)
    hidden[...] = (pre * sigma).astype(BF16)
    slo = (upstream[...] * (sigma * (1.0 + pre * (1.0 - sigma)))).astype(BF16)
    slope[...] = slo
    part = (dot(slo, w_back[...]) * inv).reshape(CUBE)
    local[...] = part
    xlo[...] = part[0]
    xhi[...] = part[B - 1]


def node_grads_kernel(nodes, gathered, slope, hidden, cot, w_in, grads, base):
    slo = slope[...]
    grads[:W] = dot(nodes[...].T, slo)
    grads[W : 2 * W] = dot(gathered[...].T, slo)
    grads[2 * W :] = dot(hidden[...].T, cot[...])
    base[...] = cot[...].astype(F32) + dot_t(slo, w_in[:W])


def edge_kernel(
    rim, field, x0, x1, y0, y1, z0, z1, dact, hidden_t, left, w_out_t, node_grads, slopes, grads, work
):
    agg = whole(rim, field, x0, x1, y0, y1, z0, z1, work).astype(BF16)
    back = dot(agg, w_out_t[...])
    for k in range(K):
        slopes[k * N : (k + 1) * N] = (back * dact[k]).astype(BF16)
    outer = dot(hidden_t[...], agg)
    grads[3 * W : 4 * W] = (outer[:W] + outer[W : 2 * W]) + (outer[2 * W : 3 * W] + outer[3 * W :])
    grads[4 * W :] = node_grads[...]
    grads[: 3 * W] = dot(left[...], slopes[...])


def node_part_kernel(offs, slopes, base, w_back, local, zlo, zhi, pad):
    part = base[...]
    for k in range(K):
        slo = slopes[k * N : (k + 1) * N]
        fill_ring(pad, slo.astype(F32).reshape(CUBE))
        sent = ring_shift(pad, -offs[k, 0], -offs[k, 1], -offs[k, 2]).astype(BF16)
        part = part + dot(jnp.concatenate([slo, sent], axis=1), w_back[...])
    local[...] = part.reshape(CUBE)
    zlo[...] = local[:, :, 0, :]
    zhi[...] = local[:, :, B - 1, :]


def edge_grad_kernel(slopes, w_in, out):
    out[...] = dot_t(slopes[...], w_in[2 * W :]).astype(BF16)


def last_kernel(rim, field, z0, z1, y0, y1, x0, x1, clipped, out, work):
    work[...] = field[...]
    add_z(rim, (z0, z1), work)
    add_y(rim, (y0, y1), work)
    add_x(rim, (x0, x1), work)
    out[...] = work[...].reshape(N, W).astype(BF16)


def fold(rows, pairs, copies, arrived, out):
    total = arrived[: 2 * rows]
    for i in range(1, pairs):
        total = total + arrived[2 * rows * i : 2 * rows * (i + 1)]
    total = total + jnp.concatenate([total[rows:], total[:rows]], axis=0)
    for i in range(copies):
        out[2 * rows * i : 2 * rows * (i + 1)] = total


def fold_with_faces_kernel(faces, rows, pairs, copies, arrived, *refs):
    fold(rows, pairs, copies, arrived, refs[-1])
    faces(*refs[:-1])


def clip_kernel(grads, edge_in, edge_out, node_in, node_out):
    total = grads[...]
    squares = jnp.sum(jnp.sum(total * total, axis=0, keepdims=True), axis=1, keepdims=True)
    factor = math.sqrt(7 * W * W) / jnp.sqrt(squares)
    edge_in[...] = total[: 3 * W] * factor
    edge_out[...] = total[3 * W : 4 * W] * factor
    node_in[...] = total[4 * W : 6 * W] * factor
    node_out[...] = total[6 * W :] * factor


def exchange(lo, hi, axis):
    count = lax.axis_size(axis)
    up = [(i, (i + 1) % count) for i in range(count)]
    down = [(t, s) for s, t in up]
    return lax.ppermute(hi, axis, up), lax.ppermute(lo, axis, down)


FACES = [(FACE, F32), (FACE, F32)]


def arrivals(rim, field, xlo, xhi, tag):
    x = exchange(xlo, xhi, GX)
    lo, hi = call(y_faces_after_x, FACES, [VMEM] * 4, "after_x" + tag)(rim, field, *x)
    y = exchange(lo, hi, GY)
    lo, hi = call(z_faces_after_y, FACES, [VMEM] * 6, "after_y" + tag)(rim, field, *x, *y)
    return (*x, *y, *exchange(lo, hi, GZ))


def swap(rows, axes):
    return lax.all_to_all(rows.reshape(lax.axis_size(axes), -1), axes, 0, 0, tiled=True).reshape(-1, W)


def arrivals_and_sum(rim, field, zlo, zhi, grads):
    near, far = lax.axis_size(NEAR), lax.axis_size(FAR)
    rows = grads.shape[0] // near
    got = swap(grads, NEAR)
    z = exchange(zlo, zhi, GZ)
    lo, hi, spread = call(
        functools.partial(fold_with_faces_kernel, y_faces_after_z, rows, near // 2, far // 2),
        FACES + [((rows * far, W), F32)],
        [VMEM] * 5,
        "after_z_fold",
    )(got, rim, field, *z)
    got = swap(spread, FAR)
    y = exchange(lo, hi, GY)
    lo, hi, spread = call(
        functools.partial(fold_with_faces_kernel, x_faces_after_y, rows, far // 2, near // 2),
        FACES + [((rows * near, W), F32)],
        [VMEM] * 7,
        "after_y_fold",
    )(got, rim, field, *z, *y)
    total = swap(spread, NEAR)
    return (*z, *y, *exchange(lo, hi, GX)), total


def on_device(node_feat, edge_feat, copies, offsets, w_edge_in, w_edge_out, w_node_in, w_node_out, node_cot):
    ends = []
    for axis in (GX, GY, GZ):
        at = lax.axis_index(axis)
        ends += [at > 0, at < lax.axis_size(axis) - 1]
    rim = jnp.broadcast_to(jnp.stack(ends).astype(F32)[:, None, None], (6, B, W))
    cot = node_cot.reshape(N, W)
    inverse = jnp.broadcast_to(1.0 / copies.reshape(N, 1).astype(F32), (N, W))
    square = ((W, W), BF16)
    many = ((K, N, W), BF16)

    local, xlo, xhi, preact, hidden, nodes, edges, w_in, w_out = call(
        forward_kernel,
        [(CUBE, F32)] + FACES + [((K, N, W), F32), many, ((N, W), BF16), many, ((3 * W, W), BF16), square],
        [HBM] * 5,
        "forward",
        [PAD, pltpu.SMEM((K, 3), jnp.int32), pltpu.SemaphoreType.DMA((4 + K,))],
    )(*map(in_hbm, (node_feat.reshape(N, W), edge_feat.reshape(K, N, W), w_edge_in, w_edge_out, offsets)))
    begun, upstream, w_node_back = call(
        prepare_node_kernel, [((N, W), F32), ((N, W), F32), square], [VMEM] * 4, "prepare_node"
    )(nodes, cot, w_node_in, w_node_out)
    arrived = arrivals(rim, local, xlo, xhi, "_1")
    dact, hidden_t, left, w_out_t, w_back = call(
        prepare_edge_kernel,
        [((K, N, W), F32), ((K * W, N), BF16), ((3 * W, K * N), BF16), square, ((2 * W, W), BF16)],
        [SMEM] + [VMEM] * 6,
        "prepare_edge",
        [PAD],
    )(offsets, preact, hidden, nodes, edges, w_in, w_out)
    local, xlo, xhi, gathered, slope, node_hidden = call(
        node_kernel, [(CUBE, F32)] + FACES + [((N, W), BF16)] * 3, [VMEM] * 13, "node", [WORK]
    )(rim, local, *arrived, inverse, begun, upstream, w_node_in, w_node_back)
    arrived = arrivals(rim, local, xlo, xhi, "_2")
    node_grads, base = call(node_grads_kernel, [((3 * W, W), F32), ((N, W), F32)], [VMEM] * 6, "node_grads")(
        nodes, gathered, slope, node_hidden, cot, w_node_in
    )
    slopes, grads = call(
        edge_kernel, [((K * N, W), BF16), ((7 * W, W), F32)], [VMEM] * 13, "edge", [WORK]
    )(rim, local, *arrived, dact, hidden_t, left, w_out_t, node_grads)
    local, zlo, zhi = call(
        node_part_kernel, [(CUBE, F32)] + FACES, [SMEM] + [VMEM] * 3, "node_part", [PAD]
    )(offsets, slopes, base, w_back)
    arrived, total = arrivals_and_sum(rim, local, zlo, zhi, grads)
    (edge_grad,) = call(edge_grad_kernel, [((K * N, W), BF16)], [VMEM] * 2, "edge_grad")(slopes, w_in)
    clipped = call(
        clip_kernel, [((3 * W, W), F32), ((W, W), F32), ((2 * W, W), F32), ((W, W), F32)], [VMEM], "clip"
    )(total)
    (node_grad,) = call(last_kernel, [((N, W), BF16)], [VMEM] * 8 + [HBM], "last", [WORK])(
        rim, local, *arrived, in_hbm(clipped[1])
    )
    return (node_grad.reshape(node_feat.shape), edge_grad.reshape(edge_feat.shape), *clipped)


def solution(mesh):
    split = Mesh(mesh.devices.reshape(8, 2, 2, 2, 4), ("z", "yh", "yl", "c", "x"))
    place = (GX, GY, GZ)
    placed = (
        P(*place, None),
        P(None, *place, None),
        P(*place),
        P(),
        P(),
        P(),
        P(),
        P(),
        P(*place, None),
    )
    return jax.shard_map(
        on_device,
        mesh=split,
        in_specs=placed,
        out_specs=(P(*place, None), P(None, *place, None), P(), P(), P(), P()),
        check_vma=False,
    )
```

time: 135 us -> 96.2 us (0.71)
  blocking collectives: 32.1 us -> 0 us
  Pallas kernels: 34.7 us -> 12.2 us
  starting transfers between devices: 38.7 us -> 53.9 us
  waiting for transfers between devices: 20.6 us -> 28.4 us
  local copies, waits for them, and re-layouts: 6.76 us -> 0.41 us
    all_to_all x2 -> x0, blocking collectives: 32.1 us -> none  [swap(): lax.all_to_all(rows.reshape(count, -1), axes, 0, 0, tiled=True)]
    pallas_call x16, Pallas kernels: 34.7 us -> 12.2 us  [the longest x1 2.42 us: on_device(): call(forward_kernel, [(CUBE, F32)] + FACES + [((K, N, W), F32), many, ((N...]
    all_to_all x1 -> x3, starting transfers between devices: 5.96 us -> 20.2 us  [swap(): lax.all_to_all(rows.reshape(lax.axis_size(axes), -1), axes, 0, 0, tiled=T...]
    all_to_all x1 -> x3, waiting for transfers between devices: 0.01 us -> 9.72 us  [swap(): lax.all_to_all(rows.reshape(lax.axis_size(axes), -1), axes, 0, 0, tiled=T...]
    unnamed x44 -> x10, local copies, waits for them, and re-layouts: 5.73 us -> 0.02 us
    ppermute x18, waiting for transfers between devices: 20.6 us -> 18.7 us  [exchange(): return (lax.ppermute(hi, axis, up), lax.ppermute(lo, axis, down))]
  transfers between devices with their start and end apart: 19 -> 21, of which waited for: 11 -> 13; matrix products, arithmetic and copies ran while one was open for 1% -> 0% of each run, Pallas kernels for 10% -> 5%
where the time goes in v3:
time: 96.2 us; the launch traced here: 95.7 us
  starting transfers between devices  53.9 us (56%)
  waiting for transfers between devices  28.4 us (30%)
  Pallas kernels  12.2 us (13%)
    ppermute x18, starting transfers between devices, exchange(): return (lax.ppermute(hi, axis, up), lax.ppermute(lo, axis, down))  33.7 us
    all_to_all x3, starting transfers between devices, swap(): lax.all_to_all(rows.reshape(lax.axis_size(axes), -1), axes, 0, 0, tiled=T...  20.2 us
    ppermute x18, waiting for transfers between devices, exchange(): return (lax.ppermute(hi, axis, up), lax.ppermute(lo, axis, down))  18.7 us
    all_to_all x3, waiting for transfers between devices, swap(): lax.all_to_all(rows.reshape(lax.axis_size(axes), -1), axes, 0, 0, tiled=T...  9.72 us
    pallas_call x1, Pallas kernels, on_device(): call(forward_kernel, [(CUBE, F32)] + FACES + [((K, N, W), F32), many, ((N...  2.42 us
  transfers between devices with their start and end apart: 21, of which 13 were waited for; matrix products, arithmetic and copies ran while one was open for 0% of the time, Pallas kernels for 5%

profile of v3, /device:TPU:1, one launch (start us, length us, event | category | flops | bytes accessed | tf_op | source)
XLA Modules:
  0.0 95.7 jit_solution(3933150601803440269)
XLA Ops:
  0.6 0.0 copy-start.4
  0.6 0.0 copy-start.1
  0.7 0.0 copy-start
  0.7 0.0 copy-start.2
  0.7 2.4 %forward.1 = (f32[8,8,8,128]{3,2,1,0:T(8,128)S(1)}, f32[8,8,128]{2,1,0:T(8,128)S(1)}, f32[8,8,128]{2,1,0:T(8,128)S(1)}, f32[4,512,128]{2,1,0:T(8,128)S(1)}, bf16...) custom-call(bf16[512,128]{1,0:T(8,128)(2,1)} %bitcast.24, ...), custom_call_target="tpu_custom_call" | custom-call | tf_op jit(solution)/shard_map/forward/pallas_call | solution.py:337
  3.1 3.8 %collective-permute-start = (f32[8,8,128]{2,1,0:T(8,128)S(1)}, f32[8,8,128]{2,1,0:T(8,128)S(1)}, u32[]{:S(2)}, u32[]{:S(2)}) collective-permute-start(f32[8,8,128]{2,1,0:T(8,128)S(1)} %get-tuple-element.55), channel_id=1, source_target_pairs={{0,16},{16,32},{32,48},{48,64},{64,80},{80,96},{96,112},{112,128},... | collective-permute-start | bytes 98312 | tf_op jit(solution)/shard_map/ppermute | solution.py:285
  6.9 5.4 %collective-permute-start.1 = (f32[8,8,128]{2,1,0:T(8,128)S(1)}, f32[8,8,128]{2,1,0:T(8,128)S(1)}, u32[]{:S(2)}, u32[]{:S(2)}) collective-permute-start(f32[8,8,128]{2,1,0:T(8,128)S(1)} %get-tuple-element.56), channel_id=1, source_target_pairs={{16,0},{32,16},{48,32},{64,48},{80,64},{96,80},{112,96},{128,112},... | collective-permute-start | bytes 98312 | tf_op jit(solution)/shard_map/ppermute | solution.py:285
  12.3 0.1 stack.27
  12.4 1.1 %collective-permute-done.x0 = f32[8,8,128]{2,1,0:T(8,128)S(1)} collective-permute-done((f32[8,8,128]{2,1,0:T(8,128)S(1)}, f32[8,8,128]{2,1,0:T(8,128)S(1)}, u32[]{:S(2)}, u32[]{:S(2)}) %collective-permute-start) | collective-permute-done | bytes 32800 | tf_op jit(solution)/shard_map/ppermute | solution.py:285
  13.5 0.0 collective-permute-done.1.x1
  13.5 0.1 broadcast_in_dim.4.rim.refs_0_
  13.6 1.9 %collective-permute-start.2 = (f32[8,8,128]{2,1,0:T(8,128)S(1)}, f32[8,8,128]{2,1,0:T(8,128)S(1)}, u32[]{:S(2)}, u32[]{:S(2)}) collective-permute-start(f32[8,8,128]{2,1,0:T(8,128)S(1)} %get-tuple-element.57), channel_id=1, source_target_pairs={{0,4},{4,8},{8,12},{12,0},{1,5},{5,9},{9,13},{13,1},{2,6},{6,10},{... | collective-permute-start | bytes 98312 | tf_op jit(solution)/shard_map/ppermute | solution.py:285
  15.5 0.0 collective-permute-start.3
  15.5 1.0 %collective-permute-done.2.y0 = f32[8,8,128]{2,1,0:T(8,128)S(1)} collective-permute-done((f32[8,8,128]{2,1,0:T(8,128)S(1)}, f32[8,8,128]{2,1,0:T(8,128)S(1)}, u32[]{:S(2)}, u32[]{:S(2)}) %collective-permute-start.2) | collective-permute-done | bytes 32800 | tf_op jit(solution)/shard_map/ppermute | solution.py:285
  16.5 2.3 %collective-permute-done.3.y1 = f32[8,8,128]{2,1,0:T(8,128)S(1)} collective-permute-done((f32[8,8,128]{2,1,0:T(8,128)S(1)}, f32[8,8,128]{2,1,0:T(8,128)S(1)}, u32[]{:S(2)}, u32[]{:S(2)}) %collective-permute-start.3) | collective-permute-done | bytes 32800 | tf_op jit(solution)/shard_map/ppermute | solution.py:285
  18.8 0.1 after_y_1.1
  18.9 1.3 %collective-permute-start.4 = (f32[8,8,128]{2,1,0:T(8,128)S(1)}, f32[8,8,128]{2,1,0:T(8,128)S(1)}, u32[]{:S(2)}, u32[]{:S(2)}) collective-permute-start(f32[8,8,128]{2,1,0:T(8,128)S(1)} %get-tuple-element.59), channel_id=1, source_target_pairs={{0,1},{1,2},{2,3},{3,0},{4,5},{5,6},{6,7},{7,4},{8,9},{9,10},{10,1... | collective-permute-start | bytes 98312 | tf_op jit(solution)/shard_map/ppermute | solution.py:285
  20.2 1.5 %collective-permute-start.5 = (f32[8,8,128]{2,1,0:T(8,128)S(1)}, f32[8,8,128]{2,1,0:T(8,128)S(1)}, u32[]{:S(2)}, u32[]{:S(2)}) collective-permute-start(f32[8,8,128]{2,1,0:T(8,128)S(1)} %get-tuple-element.60), channel_id=1, source_target_pairs={{1,0},{2,1},{3,2},{0,3},{5,4},{6,5},{7,6},{4,7},{9,8},{10,9},{11,1... | collective-permute-start | bytes 98312 | tf_op jit(solution)/shard_map/ppermute | solution.py:285
  21.7 0.1 div.16
  21.8 0.2 prepare_node.1
  22.0 1.4 %collective-permute-done.4.z0 = f32[8,8,128]{2,1,0:T(8,128)S(1)} collective-permute-done((f32[8,8,128]{2,1,0:T(8,128)S(1)}, f32[8,8,128]{2,1,0:T(8,128)S(1)}, u32[]{:S(2)}, u32[]{:S(2)}) %collective-permute-start.4) | collective-permute-done | bytes 32800 | tf_op jit(solution)/shard_map/ppermute | solution.py:285
  23.4 0.0 collective-permute-done.5.z1
  23.4 0.1 broadcast_in_dim.5.inverse
  23.6 0.4 node.1
  24.0 1.7 %collective-permute-start.6 = (f32[8,8,128]{2,1,0:T(8,128)S(1)}, f32[8,8,128]{2,1,0:T(8,128)S(1)}, u32[]{:S(2)}, u32[]{:S(2)}) collective-permute-start(f32[8,8,128]{2,1,0:T(8,128)S(1)} %get-tuple-element.66), channel_id=1, source_target_pairs={{0,16},{16,32},{32,48},{48,64},{64,80},{80,96},{96,112},{112,128},... | collective-permute-start | bytes 98312 | tf_op jit(solution)/shard_map/ppermute | solution.py:285
  25.6 4.4 %collective-permute-start.7 = (f32[8,8,128]{2,1,0:T(8,128)S(1)}, f32[8,8,128]{2,1,0:T(8,128)S(1)}, u32[]{:S(2)}, u32[]{:S(2)}) collective-permute-start(f32[8,8,128]{2,1,0:T(8,128)S(1)} %get-tuple-element.67), channel_id=1, source_target_pairs={{16,0},{32,16},{48,32},{64,48},{80,64},{96,80},{112,96},{128,112},... | collective-permute-start | bytes 98312 | tf_op jit(solution)/shard_map/ppermute | solution.py:285
  30.1 1.2 %collective-permute-done.6.x0 = f32[8,8,128]{2,1,0:T(8,128)S(1)} collective-permute-done((f32[8,8,128]{2,1,0:T(8,128)S(1)}, f32[8,8,128]{2,1,0:T(8,128)S(1)}, u32[]{:S(2)}, u32[]{:S(2)}) %collective-permute-start.6) | collective-permute-done | bytes 32800 | tf_op jit(solution)/shard_map/ppermute | solution.py:285
  31.3 0.0 collective-permute-done.7.x1
  31.3 1.5 %collective-permute-start.8 = (f32[8,8,128]{2,1,0:T(8,128)S(1)}, f32[8,8,128]{2,1,0:T(8,128)S(1)}, u32[]{:S(2)}, u32[]{:S(2)}) collective-permute-start(f32[8,8,128]{2,1,0:T(8,128)S(1)} %get-tuple-element.68), channel_id=1, source_target_pairs={{0,4},{4,8},{8,12},{12,0},{1,5},{5,9},{9,13},{13,1},{2,6},{6,10},{... | collective-permute-start | bytes 98312 | tf_op jit(solution)/shard_map/ppermute | solution.py:285
  32.8 0.0 collective-permute-start.9
  32.8 1.0 %collective-permute-done.8.y0 = f32[8,8,128]{2,1,0:T(8,128)S(1)} collective-permute-done((f32[8,8,128]{2,1,0:T(8,128)S(1)}, f32[8,8,128]{2,1,0:T(8,128)S(1)}, u32[]{:S(2)}, u32[]{:S(2)}) %collective-permute-start.8) | collective-permute-done | bytes 32800 | tf_op jit(solution)/shard_map/ppermute | solution.py:285
  33.8 2.3 %collective-permute-done.9.y1 = f32[8,8,128]{2,1,0:T(8,128)S(1)} collective-permute-done((f32[8,8,128]{2,1,0:T(8,128)S(1)}, f32[8,8,128]{2,1,0:T(8,128)S(1)}, u32[]{:S(2)}, u32[]{:S(2)}) %collective-permute-start.9) | collective-permute-done | bytes 32800 | tf_op jit(solution)/shard_map/ppermute | solution.py:285
  36.2 0.1 after_y_2.1
  36.2 1.3 %collective-permute-start.10 = (f32[8,8,128]{2,1,0:T(8,128)S(1)}, f32[8,8,128]{2,1,0:T(8,128)S(1)}, u32[]{:S(2)}, u32[]{:S(2)}) collective-permute-start(f32[8,8,128]{2,1,0:T(8,128)S(1)} %get-tuple-element.70), channel_id=1, source_target_pairs={{0,1},{1,2},{2,3},{3,0},{4,5},{5,6},{6,7},{7,4},{8,9},{9,10},{10,1... | collective-permute-start | bytes 98312 | tf_op jit(solution)/shard_map/ppermute | solution.py:285
  37.5 1.7 %collective-permute-start.11 = (f32[8,8,128]{2,1,0:T(8,128)S(1)}, f32[8,8,128]{2,1,0:T(8,128)S(1)}, u32[]{:S(2)}, u32[]{:S(2)}) collective-permute-start(f32[8,8,128]{2,1,0:T(8,128)S(1)} %get-tuple-element.71), channel_id=1, source_target_pairs={{1,0},{2,1},{3,2},{0,3},{5,4},{6,5},{7,6},{4,7},{9,8},{10,9},{11,1... | collective-permute-start | bytes 98312 | tf_op jit(solution)/shard_map/ppermute | solution.py:285
  39.3 1.5 %prepare_edge.1 = (f32[4,512,128]{2,1,0:T(8,128)S(1)}, bf16[512,512]{1,0:T(8,128)(2,1)S(1)}, bf16[384,2048]{1,0:T(8,128)(2,1)S(1)}, bf16[128,128]{1,0:T(8,128)(2,1)S(1)}, bf16[256,128]{1,0:T(8,128)(2,1)S(1)}) custom-call(s32[4,3]{1,0:T(4,128)S(1)} %copy-done.3, f32[4,512,128]{2,1,0:T(8,128)S(1)} %get-tuple-element.72.preact, ...), custom_call_target="tpu_custom_call" | custom-call | tf_op jit(solution)/shard_map/prepare_edge/pallas_call | solution.py:348
  40.7 0.3 node_grads.1
  41.1 0.0 collective-permute-done.10.z0
  41.1 0.0 collective-permute-done.11.z1
  41.1 1.7 %edge.1 = (bf16[2048,128]{1,0:T(8,128)(2,1)S(1)}, f32[896,128]{1,0:T(8,128)}) custom-call(f32[6,8,128]{2,1,0:T(8,128)S(1)} %broadcast_in_dim.4.rim.refs_0_, f32[8,8,8,128]{3,2,1,0:T(8,128)S(1)} %get-tuple-element.65.field, f32[8,8,128]{2,1,0:T(8,128)S(1)} %collective-permute-done.6.x0, f32[8,8,128]{2,1,0:T(8,128)S(1)} %collective-permute-done.7.x1, ...), custom_call_target="tpu_custom_call" | custom-call | tf_op jit(solution)/shard_map/edge/pallas_call | solution.py:362
  42.8 5.9 %all-to-all-start = ((f32[32,1,3584]{2,1,0:T(1,128)}), f32[32,1,3584]{2,1,0:T(1,128)S(1)}, u32[]{:S(2)}, u32[]{:S(2)}) async-start(f32[32,1,3584]{2,1,0:T(1,128)} %bitcast.9), calls=%async_computation | async-start | bytes 917504 | tf_op jit(solution)/shard_map/all_to_all | solution.py:300
  48.7 1.1 %node_part.1 = (f32[8,8,8,128]{3,2,1,0:T(8,128)S(1)}, f32[8,8,128]{2,1,0:T(8,128)S(1)}, f32[8,8,128]{2,1,0:T(8,128)S(1)}) custom-call(s32[4,3]{1,0:T(4,128)S(1)} %copy-done.3, bf16[2048,128]{1,0:T(8,128)(2,1)S(1)} %get-tuple-element.85.slopes, f32[512,128]{1,0:T(8,128)S(1)} %get-tuple-element.86.base, bf16[256,128]{1,0:T(8,128)(2,1)S(1)} %get-tuple-element.87.w_back), custom_call_target="tpu_custom_call" | custom-call | tf_op jit(solution)/shard_map/node_part/pallas_call | solution.py:365
  49.9 1.4 %collective-permute-start.12 = (f32[8,8,128]{2,1,0:T(8,128)S(1)}, f32[8,8,128]{2,1,0:T(8,128)S(1)}, u32[]{:S(2)}, u32[]{:S(2)}) collective-permute-start(f32[8,8,128]{2,1,0:T(8,128)S(1)} %get-tuple-element.89), channel_id=1, source_target_pairs={{0,1},{1,2},{2,3},{3,0},{4,5},{5,6},{6,7},{7,4},{8,9},{9,10},{10,1... | collective-permute-start | bytes 98312 | tf_op jit(solution)/shard_map/ppermute | solution.py:285
  51.3 1.3 %collective-permute-start.13 = (f32[8,8,128]{2,1,0:T(8,128)S(1)}, f32[8,8,128]{2,1,0:T(8,128)S(1)}, u32[]{:S(2)}, u32[]{:S(2)}) collective-permute-start(f32[8,8,128]{2,1,0:T(8,128)S(1)} %get-tuple-element.90), channel_id=1, source_target_pairs={{1,0},{2,1},{3,2},{0,3},{5,4},{6,5},{7,6},{4,7},{9,8},{10,9},{11,1... | collective-permute-start | bytes 98312 | tf_op jit(solution)/shard_map/ppermute | solution.py:285
  52.6 4.9 %collective-permute-done.12.refs_2_.z0 = f32[8,8,128]{2,1,0:T(8,128)S(1)} collective-permute-done((f32[8,8,128]{2,1,0:T(8,128)S(1)}, f32[8,8,128]{2,1,0:T(8,128)S(1)}, u32[]{:S(2)}, u32[]{:S(2)}) %collective-permute-start.12) | collective-permute-done | bytes 32800 | tf_op jit(solution)/shard_map/ppermute | solution.py:285
  57.6 0.0 collective-permute-done.13.refs_3_.z1
  57.6 2.1 %all-to-all-done = f32[32,1,3584]{2,1,0:T(1,128)S(1)} async-done(((f32[32,1,3584]{2,1,0:T(1,128)}), f32[32,1,3584]{2,1,0:T(1,128)S(1)}, u32[]{:S(2)}, u32[]{:S(2)}) %all-to-all-start) | async-done | bytes 458784 | tf_op jit(solution)/shard_map/all_to_all | solution.py:300
  59.6 0.7 after_z_fold.1
  60.3 8.3 %all-to-all-start.1 = ((f32[8,1,3584]{2,1,0:T(1,128)}), f32[8,1,3584]{2,1,0:T(1,128)S(1)}, u32[]{:S(2)}, u32[]{:S(2)}) async-start(f32[8,1,3584]{2,1,0:T(1,128)} %bitcast.11), calls=%async_computation.1 | async-start | bytes 229376 | tf_op jit(solution)/shard_map/all_to_all | solution.py:300
  68.6 1.3 %collective-permute-start.14 = (f32[8,8,128]{2,1,0:T(8,128)S(1)}, f32[8,8,128]{2,1,0:T(8,128)S(1)}, u32[]{:S(2)}, u32[]{:S(2)}) collective-permute-start(f32[8,8,128]{2,1,0:T(8,128)S(1)} %get-tuple-element.92), channel_id=1, source_target_pairs={{0,4},{4,8},{8,12},{12,0},{1,5},{5,9},{9,13},{13,1},{2,6},{6,10},{... | collective-permute-start | bytes 98312 | tf_op jit(solution)/shard_map/ppermute | solution.py:285
  69.9 0.0 collective-permute-start.15
  69.9 1.0 %collective-permute-done.14.refs_4_.y0 = f32[8,8,128]{2,1,0:T(8,128)S(1)} collective-permute-done((f32[8,8,128]{2,1,0:T(8,128)S(1)}, f32[8,8,128]{2,1,0:T(8,128)S(1)}, u32[]{:S(2)}, u32[]{:S(2)}) %collective-permute-start.14) | collective-permute-done | bytes 32800 | tf_op jit(solution)/shard_map/ppermute | solution.py:285
  71.0 2.3 %collective-permute-done.15.refs_5_.y1 = f32[8,8,128]{2,1,0:T(8,128)S(1)} collective-permute-done((f32[8,8,128]{2,1,0:T(8,128)S(1)}, f32[8,8,128]{2,1,0:T(8,128)S(1)}, u32[]{:S(2)}, u32[]{:S(2)}) %collective-permute-start.15) | collective-permute-done | bytes 32800 | tf_op jit(solution)/shard_map/ppermute | solution.py:285
  73.3 3.1 %all-to-all-done.1 = f32[8,1,3584]{2,1,0:T(1,128)S(1)} async-done(((f32[8,1,3584]{2,1,0:T(1,128)}), f32[8,1,3584]{2,1,0:T(1,128)S(1)}, u32[]{:S(2)}, u32[]{:S(2)}) %all-to-all-start.1) | async-done | bytes 114720 | tf_op jit(solution)/shard_map/all_to_all | solution.py:300
  76.4 0.8 after_y_fold.1
  77.2 5.9 %all-to-all-start.2 = ((f32[32,1,3584]{2,1,0:T(1,128)}), f32[32,1,3584]{2,1,0:T(1,128)S(1)}, u32[]{:S(2)}, u32[]{:S(2)}) async-start(f32[32,1,3584]{2,1,0:T(1,128)} %bitcast.13), calls=%async_computation.2 | async-start | bytes 917504 | tf_op jit(solution)/shard_map/all_to_all | solution.py:300
  83.1 2.9 %collective-permute-start.16 = (f32[8,8,128]{2,1,0:T(8,128)S(1)}, f32[8,8,128]{2,1,0:T(8,128)S(1)}, u32[]{:S(2)}, u32[]{:S(2)}) collective-permute-start(f32[8,8,128]{2,1,0:T(8,128)S(1)} %get-tuple-element.95), channel_id=1, source_target_pairs={{0,16},{16,32},{32,48},{48,64},{64,80},{80,96},{96,112},{112,128},... | collective-permute-start | bytes 98312 | tf_op jit(solution)/shard_map/ppermute | solution.py:285
  86.1 2.2 %collective-permute-start.17 = (f32[8,8,128]{2,1,0:T(8,128)S(1)}, f32[8,8,128]{2,1,0:T(8,128)S(1)}, u32[]{:S(2)}, u32[]{:S(2)}) collective-permute-start(f32[8,8,128]{2,1,0:T(8,128)S(1)} %get-tuple-element.96), channel_id=1, source_target_pairs={{16,0},{32,16},{48,32},{64,48},{80,64},{96,80},{112,96},{128,112},... | collective-permute-start | bytes 98312 | tf_op jit(solution)/shard_map/ppermute | solution.py:285
  88.3 1.1 %edge_grad.1 = bf16[2048,128]{1,0:T(8,128)(2,1)} custom-call(bf16[2048,128]{1,0:T(8,128)(2,1)S(1)} %get-tuple-element.85.slopes, bf16[384,128]{1,0:T(8,128)(2,1)S(1)} %get-tuple-element.75.w_in), custom_call_target="tpu_custom_call" | custom-call | tf_op jit(solution)/shard_map/edge_grad/pallas_call | solution.py:369
  89.4 4.5 %all-to-all-done.2 = f32[32,1,3584]{2,1,0:T(1,128)S(1)} async-done(((f32[32,1,3584]{2,1,0:T(1,128)}), f32[32,1,3584]{2,1,0:T(1,128)S(1)}, u32[]{:S(2)}, u32[]{:S(2)}) %all-to-all-start.2) | async-done | bytes 458784 | tf_op jit(solution)/shard_map/all_to_all | solution.py:300
  93.9 1.0 %clip.1 = (f32[384,128]{1,0:T(8,128)}, f32[128,128]{1,0:T(8,128)}, f32[256,128]{1,0:T(8,128)}, f32[128,128]{1,0:T(8,128)}) custom-call(f32[896,128]{1,0:T(8,128)S(1)} %bitcast.18), custom_call_target="tpu_custom_call" | custom-call | tf_op jit(solution)/shard_map/clip/pallas_call | solution.py:370
  94.9 0.0 collective-permute-done.16.x0
  94.9 0.0 collective-permute-done.17.x1
  94.9 0.8 last.1
  (10 shorter events, 0.1 us)
Async XLA Ops:
  0.6 21.1 %copy-start.4 = (s32[8,8,8]{2,1,0:T(8,128)S(1)}, s32[8,8,8]{2,1,0:T(8,128)}, u32[]{:S(2)}) copy-start(s32[8,8,8]{2,1,0:T(8,128)} %param.11) | copy-start | bytes 6148
  0.6 21.1 %copy-start.1 = (bf16[8,8,8,128]{3,2,1,0:T(8,128)(2,1)S(1)}, bf16[8,8,8,128]{3,2,1,0:T(8,128)(2,1)}, u32[]{:S(2)}) copy-start(bf16[8,8,8,128]{3,2,1,0:T(8,128)(2,1)} %param.17) | copy-start | bytes 393220
  0.7 21.1 %copy-start = (bf16[256,128]{1,0:T(8,128)(2,1)S(1)}, bf16[256,128]{1,0:T(8,128)(2,1)}, u32[]{:S(2)}) copy-start(bf16[256,128]{1,0:T(8,128)(2,1)} %w_in.5) | copy-start | bytes 196612
  0.7 21.1 %copy-start.2 = (bf16[128,128]{1,0:T(8,128)(2,1)S(1)}, bf16[128,128]{1,0:T(8,128)(2,1)}, u32[]{:S(2)}) copy-start(bf16[128,128]{1,0:T(8,128)(2,1)} %w_out.1) | copy-start | bytes 98308
  3.1 10.4 %collective-permute-start = (f32[8,8,128]{2,1,0:T(8,128)S(1)}, f32[8,8,128]{2,1,0:T(8,128)S(1)}, u32[]{:S(2)}, u32[]{:S(2)}) collective-permute-start(f32[8,8,128]{2,1,0:T(8,128)S(1)} %get-tuple-element.55), channel_id=1, source_target_pairs={{0,16},{16,32},{32,48},{48,64},{64,80},{80,96},{96,112},{112,128},... | collective-permute-start | bytes 98312 | tf_op jit(solution)/shard_map/ppermute | solution.py:285
  6.9 6.6 %collective-permute-start.1 = (f32[8,8,128]{2,1,0:T(8,128)S(1)}, f32[8,8,128]{2,1,0:T(8,128)S(1)}, u32[]{:S(2)}, u32[]{:S(2)}) collective-permute-start(f32[8,8,128]{2,1,0:T(8,128)S(1)} %get-tuple-element.56), channel_id=1, source_target_pairs={{16,0},{32,16},{48,32},{64,48},{80,64},{96,80},{112,96},{128,112},... | collective-permute-start | bytes 98312 | tf_op jit(solution)/shard_map/ppermute | solution.py:285
  13.6 2.9 %collective-permute-start.2 = (f32[8,8,128]{2,1,0:T(8,128)S(1)}, f32[8,8,128]{2,1,0:T(8,128)S(1)}, u32[]{:S(2)}, u32[]{:S(2)}) collective-permute-start(f32[8,8,128]{2,1,0:T(8,128)S(1)} %get-tuple-element.57), channel_id=1, source_target_pairs={{0,4},{4,8},{8,12},{12,0},{1,5},{5,9},{9,13},{13,1},{2,6},{6,10},{... | collective-permute-start | bytes 98312 | tf_op jit(solution)/shard_map/ppermute | solution.py:285
  15.5 23.8 %copy-start.3 = (s32[4,3]{1,0:T(4,128)S(1)}, s32[4,3]{1,0:T(4,128)}, u32[]{:S(2)}) copy-start(s32[4,3]{1,0:T(4,128)} %offs.3) | copy-start | bytes 148
  15.5 3.3 %collective-permute-start.3 = (f32[8,8,128]{2,1,0:T(8,128)S(1)}, f32[8,8,128]{2,1,0:T(8,128)S(1)}, u32[]{:S(2)}, u32[]{:S(2)}) collective-permute-start(f32[8,8,128]{2,1,0:T(8,128)S(1)} %get-tuple-element.58), channel_id=1, source_target_pairs={{4,0},{8,4},{12,8},{0,12},{5,1},{9,5},{13,9},{1,13},{6,2},{10,6},{... | collective-permute-start | bytes 98312 | tf_op jit(solution)/shard_map/ppermute | solution.py:285
  18.9 4.5 %collective-permute-start.4 = (f32[8,8,128]{2,1,0:T(8,128)S(1)}, f32[8,8,128]{2,1,0:T(8,128)S(1)}, u32[]{:S(2)}, u32[]{:S(2)}) collective-permute-start(f32[8,8,128]{2,1,0:T(8,128)S(1)} %get-tuple-element.59), channel_id=1, source_target_pairs={{0,1},{1,2},{2,3},{3,0},{4,5},{5,6},{6,7},{7,4},{8,9},{9,10},{10,1... | collective-permute-start | bytes 98312 | tf_op jit(solution)/shard_map/ppermute | solution.py:285
  20.2 3.2 %collective-permute-start.5 = (f32[8,8,128]{2,1,0:T(8,128)S(1)}, f32[8,8,128]{2,1,0:T(8,128)S(1)}, u32[]{:S(2)}, u32[]{:S(2)}) collective-permute-start(f32[8,8,128]{2,1,0:T(8,128)S(1)} %get-tuple-element.60), channel_id=1, source_target_pairs={{1,0},{2,1},{3,2},{0,3},{5,4},{6,5},{7,6},{4,7},{9,8},{10,9},{11,1... | collective-permute-start | bytes 98312 | tf_op jit(solution)/shard_map/ppermute | solution.py:285
  24.0 7.3 %collective-permute-start.6 = (f32[8,8,128]{2,1,0:T(8,128)S(1)}, f32[8,8,128]{2,1,0:T(8,128)S(1)}, u32[]{:S(2)}, u32[]{:S(2)}) collective-permute-start(f32[8,8,128]{2,1,0:T(8,128)S(1)} %get-tuple-element.66), channel_id=1, source_target_pairs={{0,16},{16,32},{32,48},{48,64},{64,80},{80,96},{96,112},{112,128},... | collective-permute-start | bytes 98312 | tf_op jit(solution)/shard_map/ppermute | solution.py:285
  25.6 5.7 %collective-permute-start.7 = (f32[8,8,128]{2,1,0:T(8,128)S(1)}, f32[8,8,128]{2,1,0:T(8,128)S(1)}, u32[]{:S(2)}, u32[]{:S(2)}) collective-permute-start(f32[8,8,128]{2,1,0:T(8,128)S(1)} %get-tuple-element.67), channel_id=1, source_target_pairs={{16,0},{32,16},{48,32},{64,48},{80,64},{96,80},{112,96},{128,112},... | collective-permute-start | bytes 98312 | tf_op jit(solution)/shard_map/ppermute | solution.py:285
  31.3 2.5 %collective-permute-start.8 = (f32[8,8,128]{2,1,0:T(8,128)S(1)}, f32[8,8,128]{2,1,0:T(8,128)S(1)}, u32[]{:S(2)}, u32[]{:S(2)}) collective-permute-start(f32[8,8,128]{2,1,0:T(8,128)S(1)} %get-tuple-element.68), channel_id=1, source_target_pairs={{0,4},{4,8},{8,12},{12,0},{1,5},{5,9},{9,13},{13,1},{2,6},{6,10},{... | collective-permute-start | bytes 98312 | tf_op jit(solution)/shard_map/ppermute | solution.py:285
  32.8 3.3 %collective-permute-start.9 = (f32[8,8,128]{2,1,0:T(8,128)S(1)}, f32[8,8,128]{2,1,0:T(8,128)S(1)}, u32[]{:S(2)}, u32[]{:S(2)}) collective-permute-start(f32[8,8,128]{2,1,0:T(8,128)S(1)} %get-tuple-element.69), channel_id=1, source_target_pairs={{4,0},{8,4},{12,8},{0,12},{5,1},{9,5},{13,9},{1,13},{6,2},{10,6},{... | collective-permute-start | bytes 98312 | tf_op jit(solution)/shard_map/ppermute | solution.py:285
  36.2 4.8 %collective-permute-start.10 = (f32[8,8,128]{2,1,0:T(8,128)S(1)}, f32[8,8,128]{2,1,0:T(8,128)S(1)}, u32[]{:S(2)}, u32[]{:S(2)}) collective-permute-start(f32[8,8,128]{2,1,0:T(8,128)S(1)} %get-tuple-element.70), channel_id=1, source_target_pairs={{0,1},{1,2},{2,3},{3,0},{4,5},{5,6},{6,7},{7,4},{8,9},{9,10},{10,1... | collective-permute-start | bytes 98312 | tf_op jit(solution)/shard_map/ppermute | solution.py:285
  37.5 3.6 %collective-permute-start.11 = (f32[8,8,128]{2,1,0:T(8,128)S(1)}, f32[8,8,128]{2,1,0:T(8,128)S(1)}, u32[]{:S(2)}, u32[]{:S(2)}) collective-permute-start(f32[8,8,128]{2,1,0:T(8,128)S(1)} %get-tuple-element.71), channel_id=1, source_target_pairs={{1,0},{2,1},{3,2},{0,3},{5,4},{6,5},{7,6},{4,7},{9,8},{10,9},{11,1... | collective-permute-start | bytes 98312 | tf_op jit(solution)/shard_map/ppermute | solution.py:285
  42.8 16.8 %all-to-all-start = ((f32[32,1,3584]{2,1,0:T(1,128)}), f32[32,1,3584]{2,1,0:T(1,128)S(1)}, u32[]{:S(2)}, u32[]{:S(2)}) async-start(f32[32,1,3584]{2,1,0:T(1,128)} %bitcast.9), calls=%async_computation | async-start | bytes 917504 | tf_op jit(solution)/shard_map/all_to_all | solution.py:300
  49.9 7.7 %collective-permute-start.12 = (f32[8,8,128]{2,1,0:T(8,128)S(1)}, f32[8,8,128]{2,1,0:T(8,128)S(1)}, u32[]{:S(2)}, u32[]{:S(2)}) collective-permute-start(f32[8,8,128]{2,1,0:T(8,128)S(1)} %get-tuple-element.89), channel_id=1, source_target_pairs={{0,1},{1,2},{2,3},{3,0},{4,5},{5,6},{6,7},{7,4},{8,9},{9,10},{10,1... | collective-permute-start | bytes 98312 | tf_op jit(solution)/shard_map/ppermute | solution.py:285
  51.3 6.2 %collective-permute-start.13 = (f32[8,8,128]{2,1,0:T(8,128)S(1)}, f32[8,8,128]{2,1,0:T(8,128)S(1)}, u32[]{:S(2)}, u32[]{:S(2)}) collective-permute-start(f32[8,8,128]{2,1,0:T(8,128)S(1)} %get-tuple-element.90), channel_id=1, source_target_pairs={{1,0},{2,1},{3,2},{0,3},{5,4},{6,5},{7,6},{4,7},{9,8},{10,9},{11,1... | collective-permute-start | bytes 98312 | tf_op jit(solution)/shard_map/ppermute | solution.py:285
  60.3 16.1 %all-to-all-start.1 = ((f32[8,1,3584]{2,1,0:T(1,128)}), f32[8,1,3584]{2,1,0:T(1,128)S(1)}, u32[]{:S(2)}, u32[]{:S(2)}) async-start(f32[8,1,3584]{2,1,0:T(1,128)} %bitcast.11), calls=%async_computation.1 | async-start | bytes 229376 | tf_op jit(solution)/shard_map/all_to_all | solution.py:300
  68.6 2.3 %collective-permute-start.14 = (f32[8,8,128]{2,1,0:T(8,128)S(1)}, f32[8,8,128]{2,1,0:T(8,128)S(1)}, u32[]{:S(2)}, u32[]{:S(2)}) collective-permute-start(f32[8,8,128]{2,1,0:T(8,128)S(1)} %get-tuple-element.92), channel_id=1, source_target_pairs={{0,4},{4,8},{8,12},{12,0},{1,5},{5,9},{9,13},{13,1},{2,6},{6,10},{... | collective-permute-start | bytes 98312 | tf_op jit(solution)/shard_map/ppermute | solution.py:285
  69.9 3.3 %collective-permute-start.15 = (f32[8,8,128]{2,1,0:T(8,128)S(1)}, f32[8,8,128]{2,1,0:T(8,128)S(1)}, u32[]{:S(2)}, u32[]{:S(2)}) collective-permute-start(f32[8,8,128]{2,1,0:T(8,128)S(1)} %get-tuple-element.93), channel_id=1, source_target_pairs={{4,0},{8,4},{12,8},{0,12},{5,1},{9,5},{13,9},{1,13},{6,2},{10,6},{... | collective-permute-start | bytes 98312 | tf_op jit(solution)/shard_map/ppermute | solution.py:285
  77.2 16.7 %all-to-all-start.2 = ((f32[32,1,3584]{2,1,0:T(1,128)}), f32[32,1,3584]{2,1,0:T(1,128)S(1)}, u32[]{:S(2)}, u32[]{:S(2)}) async-start(f32[32,1,3584]{2,1,0:T(1,128)} %bitcast.13), calls=%async_computation.2 | async-start | bytes 917504 | tf_op jit(solution)/shard_map/all_to_all | solution.py:300
  83.1 11.8 %collective-permute-start.16 = (f32[8,8,128]{2,1,0:T(8,128)S(1)}, f32[8,8,128]{2,1,0:T(8,128)S(1)}, u32[]{:S(2)}, u32[]{:S(2)}) collective-permute-start(f32[8,8,128]{2,1,0:T(8,128)S(1)} %get-tuple-element.95), channel_id=1, source_target_pairs={{0,16},{16,32},{32,48},{48,64},{64,80},{80,96},{96,112},{112,128},... | collective-permute-start | bytes 98312 | tf_op jit(solution)/shard_map/ppermute | solution.py:285
  86.1 8.8 %collective-permute-start.17 = (f32[8,8,128]{2,1,0:T(8,128)S(1)}, f32[8,8,128]{2,1,0:T(8,128)S(1)}, u32[]{:S(2)}, u32[]{:S(2)}) collective-permute-start(f32[8,8,128]{2,1,0:T(8,128)S(1)} %get-tuple-element.96), channel_id=1, source_target_pairs={{16,0},{32,16},{48,32},{64,48},{80,64},{96,80},{112,96},{128,112},... | collective-permute-start | bytes 98312 | tf_op jit(solution)/shard_map/ppermute | solution.py:285

commit v4 on v3

--- a/solution.py
+++ b/solution.py
@@ -76,9 +76,21 @@
     return ok
 
 
+def fill_masks(rim):
+    for d, axis in enumerate((GX, GY, GZ)):
+        at, count = jnp.int32(0), 1
+        for name in axis:
+            size = lax.axis_size(name)
+            at, count = at * size + lax.axis_index(name), count * size
+        odd = at & 1
+        flags = (1 - odd, jnp.where(at > 0, 1 - odd, 0), jnp.where(at < count - 1, odd, 0))
+        for i, flag in enumerate(flags):
+            rim[3 * d + i] = jnp.full((B, W), flag.astype(F32))
+
+
 def forward_kernel(
     nodes_h, edges_h, w_in_h, w_out_h, offs_h,
-    local, xlo, xhi, preact, hidden, nodes, edges, w_in, w_out,
+    local, xa, xb, preact, hidden, nodes, edges, w_in, w_out, rim,
     pad, offs, sems,
 ):
     pairs = [(nodes_h, nodes), (w_in_h, w_in), (offs_h, offs), (w_out_h, w_out)]
@@ -86,6 +98,7 @@
     copies = [pltpu.make_async_copy(a, b, sems.at[i]) for i, (a, b) in enumerate(pairs)]
     for copy in copies:
         copy.start()
+    fill_masks(rim)
     for copy in copies[:3]:
         copy.wait()
     node = nodes[...]
@@ -103,8 +116,7 @@
         total = total + dot(kept, w_out[...])
     total = total.reshape(CUBE)
     local[...] = total
-    xlo[...] = total[0]
-    xhi[...] = total[B - 1]
+    send(rim, 0, total[0], total[B - 1], xa, xb)
 
 
 def prepare_node_kernel(nodes, cot, w_in, w_out, pre, upstream, w_back):
@@ -132,55 +144,69 @@
     w_back[W:] = w_in[:W].T
 
 
-def shown(rim, which, plane):
-    return jnp.where(rim[which] > 0, plane, 0.0)
+def low(rim, d, a, b):
+    return jnp.where(rim[3 * d] > 0, jnp.where(rim[3 * d + 1] > 0, b, 0.0), a)
+
+
+def high(rim, d, a, b):
+    return jnp.where(rim[3 * d] > 0, a, jnp.where(rim[3 * d + 2] > 0, b, 0.0))
+
+
+def send(rim, d, lo, hi, a, b):
+    even = rim[3 * d] > 0
+    a[...] = jnp.where(even, hi, lo)
+    b[...] = jnp.where(even, lo, hi)
 
 
 def add_x(rim, x, out):
-    out[0] = out[0] + shown(rim, 0, x[0][...])
-    out[B - 1] = out[B - 1] + shown(rim, 1, x[1][...])
+    out[0] = out[0] + low(rim, 0, x[0][...], x[1][...])
+    out[B - 1] = out[B - 1] + high(rim, 0, x[0][...], x[1][...])
 
 
 def add_y(rim, y, out):
-    out[:, 0] = out[:, 0] + shown(rim, 2, y[0][...])
-    out[:, B - 1] = out[:, B - 1] + shown(rim, 3, y[1][...])
+    out[:, 0] = out[:, 0] + low(rim, 1, y[0][...], y[1][...])
+    out[:, B - 1] = out[:, B - 1] + high(rim, 1, y[0][...], y[1][...])
 
 
 def add_z(rim, z, out):
-    out[:, :, 0, :] = out[:, :, 0, :] + shown(rim, 4, z[0][...])
-    out[:, :, B - 1, :] = out[:, :, B - 1, :] + shown(rim, 5, z[1][...])
-
-
-def y_faces_after_x(rim, field, x0, x1, lo, hi):
-    for at, out in ((0, lo), (B - 1, hi)):
-        out[...] = field[:, at]
-        out[0] = out[0] + shown(rim, 0, x0[at])
-        out[B - 1] = out[B - 1] + shown(rim, 1, x1[at])
-
-
-def z_faces_after_y(rim, field, x0, x1, y0, y1, lo, hi):
-    for at, out in ((0, lo), (B - 1, hi)):
-        out[...] = field[:, :, at, :]
-        out[0] = out[0] + shown(rim, 0, x0[:, at, :])
-        out[B - 1] = out[B - 1] + shown(rim, 1, x1[:, at, :])
-        out[:, 0, :] = out[:, 0, :] + shown(rim, 2, y0[:, at, :])
-        out[:, B - 1, :] = out[:, B - 1, :] + shown(rim, 3, y1[:, at, :])
-
-
-def y_faces_after_z(rim, field, z0, z1, lo, hi):
-    for at, out in ((0, lo), (B - 1, hi)):
-        out[...] = field[:, at]
-        out[:, 0, :] = out[:, 0, :] + shown(rim, 4, z0[:, at, :])
-        out[:, B - 1, :] = out[:, B - 1, :] + shown(rim, 5, z1[:, at, :])
-
-
-def x_faces_after_y(rim, field, z0, z1, y0, y1, lo, hi):
-    for at, out in ((0, lo), (B - 1, hi)):
-        out[...] = field[at]
-        out[:, 0, :] = out[:, 0, :] + shown(rim, 4, z0[at])
-        out[:, B - 1, :] = out[:, B - 1, :] + shown(rim, 5, z1[at])
-        out[0] = out[0] + shown(rim, 2, y0[at])
-        out[B - 1] = out[B - 1] + shown(rim, 3, y1[at])
+    out[:, :, 0, :] = out[:, :, 0, :] + low(rim, 2, z[0][...], z[1][...])
+    out[:, :, B - 1, :] = out[:, :, B - 1, :] + high(rim, 2, z[0][...], z[1][...])
+
+
+def y_faces_after_x(rim, field, x0, x1, a, b, faces):
+    for i, at in enumerate((0, B - 1)):
+        faces[i] = field[:, at]
+        faces[i, 0] = faces[i, 0] + low(rim, 0, x0[at], x1[at])
+        faces[i, B - 1] = faces[i, B - 1] + high(rim, 0, x0[at], x1[at])
+    send(rim, 1, faces[0], faces[1], a, b)
+
+
+def z_faces_after_y(rim, field, x0, x1, y0, y1, a, b, faces):
+    for i, at in enumerate((0, B - 1)):
+        faces[i] = field[:, :, at, :]
+        faces[i, 0] = faces[i, 0] + low(rim, 0, x0[:, at, :], x1[:, at, :])
+        faces[i, B - 1] = faces[i, B - 1] + high(rim, 0, x0[:, at, :], x1[:, at, :])
+        faces[i, :, 0, :] = faces[i, :, 0, :] + low(rim, 1, y0[:, at, :], y1[:, at, :])
+        faces[i, :, B - 1, :] = faces[i, :, B - 1, :] + high(rim, 1, y0[:, at, :], y1[:, at, :])
+    send(rim, 2, faces[0], faces[1], a, b)
+
+
+def y_faces_after_z(rim, field, z0, z1, a, b, faces):
+    for i, at in enumerate((0, B - 1)):
+        faces[i] = field[:, at]
+        faces[i, :, 0, :] = faces[i, :, 0, :] + low(rim, 2, z0[:, at, :], z1[:, at, :])
+        faces[i, :, B - 1, :] = faces[i, :, B - 1, :] + high(rim, 2, z0[:, at, :], z1[:, at, :])
+    send(rim, 1, faces[0], faces[1], a, b)
+
+
+def x_faces_after_y(rim, field, z0, z1, y0, y1, a, b, faces):
+    for i, at in enumerate((0, B - 1)):
+        faces[i] = field[at]
+        faces[i, :, 0, :] = faces[i, :, 0, :] + low(rim, 2, z0[at], z1[at])
+        faces[i, :, B - 1, :] = faces[i, :, B - 1, :] + high(rim, 2, z0[at], z1[at])
+        faces[i, 0] = faces[i, 0] + low(rim, 1, y0[at], y1[at])
+        faces[i, B - 1] = faces[i, B - 1] + high(rim, 1, y0[at], y1[at])
+    send(rim, 0, faces[0], faces[1], a, b)
 
 
 def whole(rim, field, x0, x1, y0, y1, z0, z1, work):
@@ -193,7 +219,7 @@
 
 def node_kernel(
     rim, field, x0, x1, y0, y1, z0, z1, inverse, begun, upstream, w_in, w_back,
-    local, xlo, xhi, gathered, slope, hidden, work,
+    local, xa, xb, gathered, slope, hidden, work,
 ):
     inv = inverse[...]
     agg = (whole(rim, field, x0, x1, y0, y1, z0, z1, work) * inv).astype(BF16)
@@ -205,8 +231,7 @@
     slope[...] = slo
     part = (dot(slo, w_back[...]) * inv).reshape(CUBE)
     local[...] = part
-    xlo[...] = part[0]
-    xhi[...] = part[B - 1]
+    send(rim, 0, part[0], part[B - 1], xa, xb)
 
 
 def node_grads_kernel(nodes, gathered, slope, hidden, cot, w_in, grads, base):
@@ -230,7 +255,7 @@
     grads[: 3 * W] = dot(left[...], slopes[...])
 
 
-def node_part_kernel(offs, slopes, base, w_back, local, zlo, zhi, pad):
+def node_part_kernel(offs, rim, slopes, base, w_back, local, za, zb, pad):
     part = base[...]
     for k in range(K):
         slo = slopes[k * N : (k + 1) * N]
@@ -238,8 +263,7 @@
         sent = ring_shift(pad, -offs[k, 0], -offs[k, 1], -offs[k, 2]).astype(BF16)
         part = part + dot(jnp.concatenate([slo, sent], axis=1), w_back[...])
     local[...] = part.reshape(CUBE)
-    zlo[...] = local[:, :, 0, :]
-    zhi[...] = local[:, :, B - 1, :]
+    send(rim, 2, local[:, :, 0, :], local[:, :, B - 1, :], za, zb)
 
 
 def edge_grad_kernel(slopes, w_in, out):
@@ -264,8 +288,8 @@
 
 
 def fold_with_faces_kernel(faces, rows, pairs, copies, arrived, *refs):
-    fold(rows, pairs, copies, arrived, refs[-1])
-    faces(*refs[:-1])
+    fold(rows, pairs, copies, arrived, refs[-2])
+    faces(*refs[:-2], refs[-1])
 
 
 def clip_kernel(grads, edge_in, edge_out, node_in, node_out):
@@ -278,65 +302,64 @@
     node_out[...] = total[6 * W :] * factor
 
 
-def exchange(lo, hi, axis):
+def exchange(a, b, axis):
     count = lax.axis_size(axis)
-    up = [(i, (i + 1) % count) for i in range(count)]
-    down = [(t, s) for s, t in up]
-    return lax.ppermute(hi, axis, up), lax.ppermute(lo, axis, down)
+    first = [(i, i ^ 1) for i in range(count)]
+    second = [(i, min(max((i + 1) ^ 1, 1) - 1, count - 1)) for i in range(count)]
+    b = lax.ppermute(b, axis, second)
+    return lax.ppermute(a, axis, first), b
 
 
 FACES = [(FACE, F32), (FACE, F32)]
-
-
-def arrivals(rim, field, xlo, xhi, tag):
-    x = exchange(xlo, xhi, GX)
-    lo, hi = call(y_faces_after_x, FACES, [VMEM] * 4, "after_x" + tag)(rim, field, *x)
-    y = exchange(lo, hi, GY)
-    lo, hi = call(z_faces_after_y, FACES, [VMEM] * 6, "after_y" + tag)(rim, field, *x, *y)
-    return (*x, *y, *exchange(lo, hi, GZ))
+BOTH = pltpu.VMEM((2, *FACE), F32)
+
+
+def arrivals(rim, field, xa, xb, tag):
+    x = exchange(xa, xb, GX)
+    a, b = call(y_faces_after_x, FACES, [VMEM] * 4, "after_x" + tag, [BOTH])(rim, field, *x)
+    y = exchange(a, b, GY)
+    a, b = call(z_faces_after_y, FACES, [VMEM] * 6, "after_y" + tag, [BOTH])(rim, field, *x, *y)
+    return (*x, *y, *exchange(a, b, GZ))
 
 
 def swap(rows, axes):
     return lax.all_to_all(rows.reshape(lax.axis_size(axes), -1), axes, 0, 0, tiled=True).reshape(-1, W)
 
 
-def arrivals_and_sum(rim, field, zlo, zhi, grads):
+def arrivals_and_sum(rim, field, za, zb, grads):
     near, far = lax.axis_size(NEAR), lax.axis_size(FAR)
     rows = grads.shape[0] // near
     got = swap(grads, NEAR)
-    z = exchange(zlo, zhi, GZ)
-    lo, hi, spread = call(
+    z = exchange(za, zb, GZ)
+    a, b, spread = call(
         functools.partial(fold_with_faces_kernel, y_faces_after_z, rows, near // 2, far // 2),
         FACES + [((rows * far, W), F32)],
         [VMEM] * 5,
         "after_z_fold",
+        [BOTH],
     )(got, rim, field, *z)
     got = swap(spread, FAR)
-    y = exchange(lo, hi, GY)
-    lo, hi, spread = call(
+    y = exchange(a, b, GY)
+    a, b, spread = call(
         functools.partial(fold_with_faces_kernel, x_faces_after_y, rows, far // 2, near // 2),
         FACES + [((rows * near, W), F32)],
         [VMEM] * 7,
         "after_y_fold",
+        [BOTH],
     )(got, rim, field, *z, *y)
     total = swap(spread, NEAR)
-    return (*z, *y, *exchange(lo, hi, GX)), total
+    return (*z, *y, *exchange(a, b, GX)), total
 
 
 def on_device(node_feat, edge_feat, copies, offsets, w_edge_in, w_edge_out, w_node_in, w_node_out, node_cot):
-    ends = []
-    for axis in (GX, GY, GZ):
-        at = lax.axis_index(axis)
-        ends += [at > 0, at < lax.axis_size(axis) - 1]
-    rim = jnp.broadcast_to(jnp.stack(ends).astype(F32)[:, None, None], (6, B, W))
     cot = node_cot.reshape(N, W)
     inverse = jnp.broadcast_to(1.0 / copies.reshape(N, 1).astype(F32), (N, W))
     square = ((W, W), BF16)
     many = ((K, N, W), BF16)
 
-    local, xlo, xhi, preact, hidden, nodes, edges, w_in, w_out = call(
+    local, xa, xb, preact, hidden, nodes, edges, w_in, w_out, rim = call(
         forward_kernel,
-        [(CUBE, F32)] + FACES + [((K, N, W), F32), many, ((N, W), BF16), many, ((3 * W, W), BF16), square],
+        [(CUBE, F32)] + FACES + [((K, N, W), F32), many, ((N, W), BF16), many, ((3 * W, W), BF16), square, ((9, B, W), F32)],
         [HBM] * 5,
         "forward",
         [PAD, pltpu.SMEM((K, 3), jnp.int32), pltpu.SemaphoreType.DMA((4 + K,))],
@@ -344,7 +367,7 @@
     begun, upstream, w_node_back = call(
         prepare_node_kernel, [((N, W), F32), ((N, W), F32), square], [VMEM] * 4, "prepare_node"
     )(nodes, cot, w_node_in, w_node_out)
-    arrived = arrivals(rim, local, xlo, xhi, "_1")
+    arrived = arrivals(rim, local, xa, xb, "_1")
     dact, hidden_t, left, w_out_t, w_back = call(
         prepare_edge_kernel,
         [((K, N, W), F32), ((K * W, N), BF16), ((3 * W, K * N), BF16), square, ((2 * W, W), BF16)],
@@ -352,20 +375,20 @@
         "prepare_edge",
         [PAD],
     )(offsets, preact, hidden, nodes, edges, w_in, w_out)
-    local, xlo, xhi, gathered, slope, node_hidden = call(
+    local, xa, xb, gathered, slope, node_hidden = call(
         node_kernel, [(CUBE, F32)] + FACES + [((N, W), BF16)] * 3, [VMEM] * 13, "node", [WORK]
     )(rim, local, *arrived, inverse, begun, upstream, w_node_in, w_node_back)
-    arrived = arrivals(rim, local, xlo, xhi, "_2")
+    arrived = arrivals(rim, local, xa, xb, "_2")
     node_grads, base = call(node_grads_kernel, [((3 * W, W), F32), ((N, W), F32)], [VMEM] * 6, "node_grads")(
         nodes, gathered, slope, node_hidden, cot, w_node_in
     )
     slopes, grads = call(
         edge_kernel, [((K * N, W), BF16), ((7 * W, W), F32)], [VMEM] * 13, "edge", [WORK]
     )(rim, local, *arrived, dact, hidden_t, left, w_out_t, node_grads)
-    local, zlo, zhi = call(
-        node_part_kernel, [(CUBE, F32)] + FACES, [SMEM] + [VMEM] * 3, "node_part", [PAD]
-    )(offsets, slopes, base, w_back)
-    arrived, total = arrivals_and_sum(rim, local, zlo, zhi, grads)
+    local, za, zb = call(
+        node_part_kernel, [(CUBE, F32)] + FACES, [SMEM] + [VMEM] * 4, "node_part", [PAD]
+    )(offsets, rim, slopes, base, w_back)
+    arrived, total = arrivals_and_sum(rim, local, za, zb, grads)
     (edge_grad,) = call(edge_grad_kernel, [((K * N, W), BF16)], [VMEM] * 2, "edge_grad")(slopes, w_in)
     clipped = call(
         clip_kernel, [((3 * W, W), F32), ((W, W), F32), ((2 * W, W), F32), ((W, W), F32)], [VMEM], "clip"

time: 96.2 us -> 107 us (1.11)
  starting transfers between devices: 53.9 us -> 65.9 us
  waiting for transfers between devices: 28.4 us -> 26.7 us
    all_to_all x3, starting transfers between devices: 20.2 us -> 32.1 us  [swap(): lax.all_to_all(rows.reshape(lax.axis_size(axes), -1), axes, 0, 0, tiled=T...]
    ppermute x18, waiting for transfers between devices: 18.7 us -> 15.9 us  [the longest x9 8.46 us: exchange(): b = lax.ppermute(b, axis, second)]
  transfers between devices with their start and end apart: 21 -> 21, of which waited for: 13 -> 10; matrix products, arithmetic and copies ran while one was open for 0% -> 0% of each run, Pallas kernels for 5% -> 5%
where the time goes in v4:
time: 107 us; the launch traced here: 106 us
  starting transfers between devices  65.9 us (62%)
  waiting for transfers between devices  26.7 us (25%)
  Pallas kernels  12.2 us (11%)
    all_to_all x3, starting transfers between devices, swap(): lax.all_to_all(rows.reshape(lax.axis_size(axes), -1), axes, 0, 0, tiled=T...  32.1 us
    ppermute x9, starting transfers between devices, exchange(): return (lax.ppermute(a, axis, first), b)  22.4 us
    ppermute x9, starting transfers between devices, exchange(): b = lax.ppermute(b, axis, second)  11.4 us
    all_to_all x3, waiting for transfers between devices, swap(): lax.all_to_all(rows.reshape(lax.axis_size(axes), -1), axes, 0, 0, tiled=T...  10.7 us
    ppermute x9, waiting for transfers between devices, exchange(): b = lax.ppermute(b, axis, second)  8.46 us
    ppermute x9, waiting for transfers between devices, exchange(): return (lax.ppermute(a, axis, first), b)  7.49 us
    pallas_call x1, Pallas kernels, on_device(): call(forward_kernel, [(CUBE, F32)] + FACES + [((K, N, W), F32), many, ((N...  2.42 us
  transfers between devices with their start and end apart: 21, of which 10 were waited for; matrix products, arithmetic and copies ran while one was open for 0% of the time, Pallas kernels for 5%

profile of v4, /device:TPU:1, one launch (start us, length us, event | category | flops | bytes accessed | tf_op | source)
XLA Modules:
  0.0 106.0 jit_solution(1640815846507929282)
XLA Ops:
  0.6 0.0 copy-start.4
  0.6 0.0 copy-start.1
  0.7 0.0 copy-start
  0.7 2.4 %forward.1 = (f32[8,8,8,128]{3,2,1,0:T(8,128)S(1)}, f32[8,8,128]{2,1,0:T(8,128)S(1)}, f32[8,8,128]{2,1,0:T(8,128)S(1)}, f32[4,512,128]{2,1,0:T(8,128)S(1)}, bf16...) custom-call(bf16[512,128]{1,0:T(8,128)(2,1)} %bitcast.18, ...), custom_call_target="tpu_custom_call" | custom-call | tf_op jit(solution)/shard_map/forward/pallas_call | solution.py:360
  3.1 3.8 %collective-permute-start = (f32[8,8,128]{2,1,0:T(8,128)S(1)}, f32[8,8,128]{2,1,0:T(8,128)S(1)}, u32[]{:S(2)}, u32[]{:S(2)}) collective-permute-start(f32[8,8,128]{2,1,0:T(8,128)S(1)} %get-tuple-element.57), channel_id=1, source_target_pairs={{0,16},{16,0},{32,48},{48,32},{64,80},{80,64},{96,112},{112,96},{1... | collective-permute-start | bytes 98312 | tf_op jit(solution)/shard_map/ppermute | solution.py:310
  6.9 0.7 collective-permute-start.1
  7.6 0.6 collective-permute-done.x0
  8.2 0.0 collective-permute-done.1.x1
  8.2 3.7 %collective-permute-start.2 = (f32[8,8,128]{2,1,0:T(8,128)S(1)}, f32[8,8,128]{2,1,0:T(8,128)S(1)}, u32[]{:S(2)}, u32[]{:S(2)}) collective-permute-start(f32[8,8,128]{2,1,0:T(8,128)S(1)} %get-tuple-element.59), channel_id=1, source_target_pairs={{0,4},{4,0},{8,12},{12,8},{1,5},{5,1},{9,13},{13,9},{2,6},{6,2},{1... | collective-permute-start | bytes 98312 | tf_op jit(solution)/shard_map/ppermute | solution.py:310
  11.9 1.9 %collective-permute-start.3 = (f32[8,8,128]{2,1,0:T(8,128)S(1)}, f32[8,8,128]{2,1,0:T(8,128)S(1)}, u32[]{:S(2)}, u32[]{:S(2)}) collective-permute-start(f32[8,8,128]{2,1,0:T(8,128)S(1)} %get-tuple-element.60), channel_id=1, source_target_pairs={{0,0},{4,8},{8,4},{12,12},{1,1},{5,9},{9,5},{13,13},{2,2},{6,10},{... | collective-permute-start | bytes 98312 | tf_op jit(solution)/shard_map/ppermute | solution.py:309
  13.8 0.0 collective-permute-done.2.y0
  13.8 3.3 %collective-permute-done.3.y1 = f32[8,8,128]{2,1,0:T(8,128)S(1)} collective-permute-done((f32[8,8,128]{2,1,0:T(8,128)S(1)}, f32[8,8,128]{2,1,0:T(8,128)S(1)}, u32[]{:S(2)}, u32[]{:S(2)}) %collective-permute-start.3) | collective-permute-done | bytes 32800 | tf_op jit(solution)/shard_map/ppermute | solution.py:309
  17.1 0.1 after_y_1.1
  17.2 0.0 copy-start.3
  17.2 0.1 collective-permute-start.4
  17.3 0.7 collective-permute-start.5
  18.0 0.0 copy-done.4
  18.0 0.1 div.16
  18.1 0.0 copy-done.1
  18.2 0.2 prepare_node.1
  18.4 1.7 %collective-permute-done.4.z0 = f32[8,8,128]{2,1,0:T(8,128)S(1)} collective-permute-done((f32[8,8,128]{2,1,0:T(8,128)S(1)}, f32[8,8,128]{2,1,0:T(8,128)S(1)}, u32[]{:S(2)}, u32[]{:S(2)}) %collective-permute-start.4) | collective-permute-done | bytes 32800 | tf_op jit(solution)/shard_map/ppermute | solution.py:310
  20.1 0.0 collective-permute-done.5.z1
  20.1 0.1 broadcast_in_dim.2.inverse
  20.2 0.4 node.1
  20.6 6.1 %collective-permute-start.6 = (f32[8,8,128]{2,1,0:T(8,128)S(1)}, f32[8,8,128]{2,1,0:T(8,128)S(1)}, u32[]{:S(2)}, u32[]{:S(2)}) collective-permute-start(f32[8,8,128]{2,1,0:T(8,128)S(1)} %get-tuple-element.68), channel_id=1, source_target_pairs={{0,16},{16,0},{32,48},{48,32},{64,80},{80,64},{96,112},{112,96},{1... | collective-permute-start | bytes 98312 | tf_op jit(solution)/shard_map/ppermute | solution.py:310
  26.8 0.7 collective-permute-start.7
  27.4 0.6 collective-permute-done.6.x0
  28.1 0.0 collective-permute-done.7.x1
  28.1 0.1 collective-permute-start.8
  28.2 3.4 %collective-permute-start.9 = (f32[8,8,128]{2,1,0:T(8,128)S(1)}, f32[8,8,128]{2,1,0:T(8,128)S(1)}, u32[]{:S(2)}, u32[]{:S(2)}) collective-permute-start(f32[8,8,128]{2,1,0:T(8,128)S(1)} %get-tuple-element.71), channel_id=1, source_target_pairs={{0,0},{4,8},{8,4},{12,12},{1,1},{5,9},{9,5},{13,13},{2,2},{6,10},{... | collective-permute-start | bytes 98312 | tf_op jit(solution)/shard_map/ppermute | solution.py:309
  31.6 0.0 collective-permute-done.8.y0
  31.6 1.8 %collective-permute-done.9.y1 = f32[8,8,128]{2,1,0:T(8,128)S(1)} collective-permute-done((f32[8,8,128]{2,1,0:T(8,128)S(1)}, f32[8,8,128]{2,1,0:T(8,128)S(1)}, u32[]{:S(2)}, u32[]{:S(2)}) %collective-permute-start.9) | collective-permute-done | bytes 32800 | tf_op jit(solution)/shard_map/ppermute | solution.py:309
  33.4 0.1 after_y_2.1
  33.5 3.6 %collective-permute-start.10 = (f32[8,8,128]{2,1,0:T(8,128)S(1)}, f32[8,8,128]{2,1,0:T(8,128)S(1)}, u32[]{:S(2)}, u32[]{:S(2)}) collective-permute-start(f32[8,8,128]{2,1,0:T(8,128)S(1)} %get-tuple-element.72), channel_id=1, source_target_pairs={{0,1},{1,0},{2,3},{3,2},{4,5},{5,4},{6,7},{7,6},{8,9},{9,8},{10,11... | collective-permute-start | bytes 98312 | tf_op jit(solution)/shard_map/ppermute | solution.py:310
  37.1 0.7 collective-permute-start.11
  37.8 1.5 %prepare_edge.1 = (f32[4,512,128]{2,1,0:T(8,128)S(1)}, bf16[512,512]{1,0:T(8,128)(2,1)S(1)}, bf16[384,2048]{1,0:T(8,128)(2,1)S(1)}, bf16[128,128]{1,0:T(8,128)(2,1)S(1)}, bf16[256,128]{1,0:T(8,128)(2,1)S(1)}) custom-call(s32[4,3]{1,0:T(4,128)S(1)} %copy-done.3, f32[4,512,128]{2,1,0:T(8,128)S(1)} %get-tuple-element.74.preact, ...), custom_call_target="tpu_custom_call" | custom-call | tf_op jit(solution)/shard_map/prepare_edge/pallas_call | solution.py:371
  39.3 0.3 node_grads.1
  39.6 0.0 collective-permute-done.10.z0
  39.6 0.0 collective-permute-done.11.z1
  39.6 1.7 %edge.1 = (bf16[2048,128]{1,0:T(8,128)(2,1)S(1)}, f32[896,128]{1,0:T(8,128)}) custom-call(f32[9,8,128]{2,1,0:T(8,128)S(1)} %get-tuple-element.55.rim.refs_0_, f32[8,8,8,128]{3,2,1,0:T(8,128)S(1)} %get-tuple-element.67.field, f32[8,8,128]{2,1,0:T(8,128)S(1)} %collective-permute-done.6.x0, f32[8,8,128]{2,1,0:T(8,128)S(1)} %collective-permute-done.7.x1, ...), custom_call_target="tpu_custom_call" | custom-call | tf_op jit(solution)/shard_map/edge/pallas_call | solution.py:385
  41.3 14.6 %all-to-all-start = ((f32[32,1,3584]{2,1,0:T(1,128)}), f32[32,1,3584]{2,1,0:T(1,128)S(1)}, u32[]{:S(2)}, u32[]{:S(2)}) async-start(f32[32,1,3584]{2,1,0:T(1,128)} %bitcast.3), calls=%async_computation | async-start | bytes 917504 | tf_op jit(solution)/shard_map/all_to_all | solution.py:326
  55.9 1.2 %node_part.1 = (f32[8,8,8,128]{3,2,1,0:T(8,128)S(1)}, f32[8,8,128]{2,1,0:T(8,128)S(1)}, f32[8,8,128]{2,1,0:T(8,128)S(1)}) custom-call(s32[4,3]{1,0:T(4,128)S(1)} %copy-done.3, f32[9,8,128]{2,1,0:T(8,128)S(1)} %get-tuple-element.55.rim.refs_0_, bf16[2048,128]{1,0:T(8,128)(2,1)S(1)} %get-tuple-element.87.slopes, f32[512,128]{1,0:T(8,128)S(1)} %get-tuple-element.88.base, ...), custom_call_target="tpu_custom_call" | custom-call | tf_op jit(solution)/shard_map/node_part/pallas_call | solution.py:388
  57.0 1.4 %collective-permute-start.12 = (f32[8,8,128]{2,1,0:T(8,128)S(1)}, f32[8,8,128]{2,1,0:T(8,128)S(1)}, u32[]{:S(2)}, u32[]{:S(2)}) collective-permute-start(f32[8,8,128]{2,1,0:T(8,128)S(1)} %get-tuple-element.91), channel_id=1, source_target_pairs={{0,1},{1,0},{2,3},{3,2},{4,5},{5,4},{6,7},{7,6},{8,9},{9,8},{10,11... | collective-permute-start | bytes 98312 | tf_op jit(solution)/shard_map/ppermute | solution.py:310
  58.5 0.7 collective-permute-start.13
  59.1 4.5 %collective-permute-done.12.refs_2_.z0 = f32[8,8,128]{2,1,0:T(8,128)S(1)} collective-permute-done((f32[8,8,128]{2,1,0:T(8,128)S(1)}, f32[8,8,128]{2,1,0:T(8,128)S(1)}, u32[]{:S(2)}, u32[]{:S(2)}) %collective-permute-start.12) | collective-permute-done | bytes 32800 | tf_op jit(solution)/shard_map/ppermute | solution.py:310
  63.6 0.0 collective-permute-done.13.refs_3_.z1
  63.6 3.1 %all-to-all-done = f32[32,1,3584]{2,1,0:T(1,128)S(1)} async-done(((f32[32,1,3584]{2,1,0:T(1,128)}), f32[32,1,3584]{2,1,0:T(1,128)S(1)}, u32[]{:S(2)}, u32[]{:S(2)}) %all-to-all-start) | async-done | bytes 458784 | tf_op jit(solution)/shard_map/all_to_all | solution.py:326
  66.8 0.7 after_z_fold.1
  67.4 11.2 %all-to-all-start.1 = ((f32[8,1,3584]{2,1,0:T(1,128)}), f32[8,1,3584]{2,1,0:T(1,128)S(1)}, u32[]{:S(2)}, u32[]{:S(2)}) async-start(f32[8,1,3584]{2,1,0:T(1,128)} %bitcast.5), calls=%async_computation.1 | async-start | bytes 229376 | tf_op jit(solution)/shard_map/all_to_all | solution.py:326
  78.7 0.6 collective-permute-start.14
  79.3 2.1 %collective-permute-start.15 = (f32[8,8,128]{2,1,0:T(8,128)S(1)}, f32[8,8,128]{2,1,0:T(8,128)S(1)}, u32[]{:S(2)}, u32[]{:S(2)}) collective-permute-start(f32[8,8,128]{2,1,0:T(8,128)S(1)} %get-tuple-element.95), channel_id=1, source_target_pairs={{0,0},{4,8},{8,4},{12,12},{1,1},{5,9},{9,5},{13,13},{2,2},{6,10},{... | collective-permute-start | bytes 98312 | tf_op jit(solution)/shard_map/ppermute | solution.py:309
  81.4 0.0 collective-permute-done.14.refs_4_.y0
  81.4 3.4 %collective-permute-done.15.refs_5_.y1 = f32[8,8,128]{2,1,0:T(8,128)S(1)} collective-permute-done((f32[8,8,128]{2,1,0:T(8,128)S(1)}, f32[8,8,128]{2,1,0:T(8,128)S(1)}, u32[]{:S(2)}, u32[]{:S(2)}) %collective-permute-start.15) | collective-permute-done | bytes 32800 | tf_op jit(solution)/shard_map/ppermute | solution.py:309
  84.8 1.5 %all-to-all-done.1 = f32[8,1,3584]{2,1,0:T(1,128)S(1)} async-done(((f32[8,1,3584]{2,1,0:T(1,128)}), f32[8,1,3584]{2,1,0:T(1,128)S(1)}, u32[]{:S(2)}, u32[]{:S(2)}) %all-to-all-start.1) | async-done | bytes 114720 | tf_op jit(solution)/shard_map/all_to_all | solution.py:326
  86.3 0.8 after_y_fold.1
  87.1 6.3 %all-to-all-start.2 = ((f32[32,1,3584]{2,1,0:T(1,128)}), f32[32,1,3584]{2,1,0:T(1,128)S(1)}, u32[]{:S(2)}, u32[]{:S(2)}) async-start(f32[32,1,3584]{2,1,0:T(1,128)} %bitcast.7), calls=%async_computation.2 | async-start | bytes 917504 | tf_op jit(solution)/shard_map/all_to_all | solution.py:326
  93.4 3.0 %collective-permute-start.16 = (f32[8,8,128]{2,1,0:T(8,128)S(1)}, f32[8,8,128]{2,1,0:T(8,128)S(1)}, u32[]{:S(2)}, u32[]{:S(2)}) collective-permute-start(f32[8,8,128]{2,1,0:T(8,128)S(1)} %get-tuple-element.97), channel_id=1, source_target_pairs={{0,16},{16,0},{32,48},{48,32},{64,80},{80,64},{96,112},{112,96},{1... | collective-permute-start | bytes 98312 | tf_op jit(solution)/shard_map/ppermute | solution.py:310
  96.4 0.7 collective-permute-start.17
  97.0 1.1 %edge_grad.1 = bf16[2048,128]{1,0:T(8,128)(2,1)} custom-call(bf16[2048,128]{1,0:T(8,128)(2,1)S(1)} %get-tuple-element.87.slopes, bf16[384,128]{1,0:T(8,128)(2,1)S(1)} %get-tuple-element.77.w_in), custom_call_target="tpu_custom_call" | custom-call | tf_op jit(solution)/shard_map/edge_grad/pallas_call | solution.py:392
  98.1 6.1 %all-to-all-done.2 = f32[32,1,3584]{2,1,0:T(1,128)S(1)} async-done(((f32[32,1,3584]{2,1,0:T(1,128)}), f32[32,1,3584]{2,1,0:T(1,128)S(1)}, u32[]{:S(2)}, u32[]{:S(2)}) %all-to-all-start.2) | async-done | bytes 458784 | tf_op jit(solution)/shard_map/all_to_all | solution.py:326
  104.2 1.0 clip.1
  105.2 0.0 collective-permute-done.16.x0
  105.2 0.0 collective-permute-done.17.x1
  105.2 0.8 last.1
  (7 shorter events, 0.0 us)
Async XLA Ops:
  0.6 17.4 %copy-start.4 = (s32[8,8,8]{2,1,0:T(8,128)S(1)}, s32[8,8,8]{2,1,0:T(8,128)}, u32[]{:S(2)}) copy-start(s32[8,8,8]{2,1,0:T(8,128)} %param.11) | copy-start | bytes 6148
  0.6 17.5 %copy-start.1 = (bf16[8,8,8,128]{3,2,1,0:T(8,128)(2,1)S(1)}, bf16[8,8,8,128]{3,2,1,0:T(8,128)(2,1)}, u32[]{:S(2)}) copy-start(bf16[8,8,8,128]{3,2,1,0:T(8,128)(2,1)} %param.17) | copy-start | bytes 393220
  0.7 17.5 %copy-start = (bf16[256,128]{1,0:T(8,128)(2,1)S(1)}, bf16[256,128]{1,0:T(8,128)(2,1)}, u32[]{:S(2)}) copy-start(bf16[256,128]{1,0:T(8,128)(2,1)} %w_in.5) | copy-start | bytes 196612
  0.7 17.5 %copy-start.2 = (bf16[128,128]{1,0:T(8,128)(2,1)S(1)}, bf16[128,128]{1,0:T(8,128)(2,1)}, u32[]{:S(2)}) copy-start(bf16[128,128]{1,0:T(8,128)(2,1)} %w_out.1) | copy-start | bytes 98308
  3.1 5.1 %collective-permute-start = (f32[8,8,128]{2,1,0:T(8,128)S(1)}, f32[8,8,128]{2,1,0:T(8,128)S(1)}, u32[]{:S(2)}, u32[]{:S(2)}) collective-permute-start(f32[8,8,128]{2,1,0:T(8,128)S(1)} %get-tuple-element.57), channel_id=1, source_target_pairs={{0,16},{16,0},{32,48},{48,32},{64,80},{80,64},{96,112},{112,96},{1... | collective-permute-start | bytes 98312 | tf_op jit(solution)/shard_map/ppermute | solution.py:310
  6.9 1.3 %collective-permute-start.1 = (f32[8,8,128]{2,1,0:T(8,128)S(1)}, f32[8,8,128]{2,1,0:T(8,128)S(1)}, u32[]{:S(2)}, u32[]{:S(2)}) collective-permute-start(f32[8,8,128]{2,1,0:T(8,128)S(1)} %get-tuple-element.58), channel_id=1, source_target_pairs={{0,0},{16,32},{32,16},{48,64},{64,48},{80,96},{96,80},{112,128},{1... | collective-permute-start | bytes 98312 | tf_op jit(solution)/shard_map/ppermute | solution.py:309
  8.2 5.6 %collective-permute-start.2 = (f32[8,8,128]{2,1,0:T(8,128)S(1)}, f32[8,8,128]{2,1,0:T(8,128)S(1)}, u32[]{:S(2)}, u32[]{:S(2)}) collective-permute-start(f32[8,8,128]{2,1,0:T(8,128)S(1)} %get-tuple-element.59), channel_id=1, source_target_pairs={{0,4},{4,0},{8,12},{12,8},{1,5},{5,1},{9,13},{13,9},{2,6},{6,2},{1... | collective-permute-start | bytes 98312 | tf_op jit(solution)/shard_map/ppermute | solution.py:310
  11.9 5.2 %collective-permute-start.3 = (f32[8,8,128]{2,1,0:T(8,128)S(1)}, f32[8,8,128]{2,1,0:T(8,128)S(1)}, u32[]{:S(2)}, u32[]{:S(2)}) collective-permute-start(f32[8,8,128]{2,1,0:T(8,128)S(1)} %get-tuple-element.60), channel_id=1, source_target_pairs={{0,0},{4,8},{8,4},{12,12},{1,1},{5,9},{9,5},{13,13},{2,2},{6,10},{... | collective-permute-start | bytes 98312 | tf_op jit(solution)/shard_map/ppermute | solution.py:309
  17.2 20.6 %copy-start.3 = (s32[4,3]{1,0:T(4,128)S(1)}, s32[4,3]{1,0:T(4,128)}, u32[]{:S(2)}) copy-start(s32[4,3]{1,0:T(4,128)} %offs.3) | copy-start | bytes 148
  17.2 2.9 %collective-permute-start.4 = (f32[8,8,128]{2,1,0:T(8,128)S(1)}, f32[8,8,128]{2,1,0:T(8,128)S(1)}, u32[]{:S(2)}, u32[]{:S(2)}) collective-permute-start(f32[8,8,128]{2,1,0:T(8,128)S(1)} %get-tuple-element.61), channel_id=1, source_target_pairs={{0,1},{1,0},{2,3},{3,2},{4,5},{5,4},{6,7},{7,6},{8,9},{9,8},{10,11... | collective-permute-start | bytes 98312 | tf_op jit(solution)/shard_map/ppermute | solution.py:310
  17.3 2.8 %collective-permute-start.5 = (f32[8,8,128]{2,1,0:T(8,128)S(1)}, f32[8,8,128]{2,1,0:T(8,128)S(1)}, u32[]{:S(2)}, u32[]{:S(2)}) collective-permute-start(f32[8,8,128]{2,1,0:T(8,128)S(1)} %get-tuple-element.62), channel_id=1, source_target_pairs={{0,0},{1,2},{2,1},{3,3},{4,4},{5,6},{6,5},{7,7},{8,8},{9,10},{10,9... | collective-permute-start | bytes 98312 | tf_op jit(solution)/shard_map/ppermute | solution.py:309
  20.6 7.4 %collective-permute-start.6 = (f32[8,8,128]{2,1,0:T(8,128)S(1)}, f32[8,8,128]{2,1,0:T(8,128)S(1)}, u32[]{:S(2)}, u32[]{:S(2)}) collective-permute-start(f32[8,8,128]{2,1,0:T(8,128)S(1)} %get-tuple-element.68), channel_id=1, source_target_pairs={{0,16},{16,0},{32,48},{48,32},{64,80},{80,64},{96,112},{112,96},{1... | collective-permute-start | bytes 98312 | tf_op jit(solution)/shard_map/ppermute | solution.py:310
  26.8 1.3 %collective-permute-start.7 = (f32[8,8,128]{2,1,0:T(8,128)S(1)}, f32[8,8,128]{2,1,0:T(8,128)S(1)}, u32[]{:S(2)}, u32[]{:S(2)}) collective-permute-start(f32[8,8,128]{2,1,0:T(8,128)S(1)} %get-tuple-element.69), channel_id=1, source_target_pairs={{0,0},{16,32},{32,16},{48,64},{64,48},{80,96},{96,80},{112,128},{1... | collective-permute-start | bytes 98312 | tf_op jit(solution)/shard_map/ppermute | solution.py:309
  28.1 3.5 %collective-permute-start.8 = (f32[8,8,128]{2,1,0:T(8,128)S(1)}, f32[8,8,128]{2,1,0:T(8,128)S(1)}, u32[]{:S(2)}, u32[]{:S(2)}) collective-permute-start(f32[8,8,128]{2,1,0:T(8,128)S(1)} %get-tuple-element.70), channel_id=1, source_target_pairs={{0,4},{4,0},{8,12},{12,8},{1,5},{5,1},{9,13},{13,9},{2,6},{6,2},{1... | collective-permute-start | bytes 98312 | tf_op jit(solution)/shard_map/ppermute | solution.py:310
  28.2 5.2 %collective-permute-start.9 = (f32[8,8,128]{2,1,0:T(8,128)S(1)}, f32[8,8,128]{2,1,0:T(8,128)S(1)}, u32[]{:S(2)}, u32[]{:S(2)}) collective-permute-start(f32[8,8,128]{2,1,0:T(8,128)S(1)} %get-tuple-element.71), channel_id=1, source_target_pairs={{0,0},{4,8},{8,4},{12,12},{1,1},{5,9},{9,5},{13,13},{2,2},{6,10},{... | collective-permute-start | bytes 98312 | tf_op jit(solution)/shard_map/ppermute | solution.py:309
  33.5 6.1 %collective-permute-start.10 = (f32[8,8,128]{2,1,0:T(8,128)S(1)}, f32[8,8,128]{2,1,0:T(8,128)S(1)}, u32[]{:S(2)}, u32[]{:S(2)}) collective-permute-start(f32[8,8,128]{2,1,0:T(8,128)S(1)} %get-tuple-element.72), channel_id=1, source_target_pairs={{0,1},{1,0},{2,3},{3,2},{4,5},{5,4},{6,7},{7,6},{8,9},{9,8},{10,11... | collective-permute-start | bytes 98312 | tf_op jit(solution)/shard_map/ppermute | solution.py:310
  37.1 2.5 %collective-permute-start.11 = (f32[8,8,128]{2,1,0:T(8,128)S(1)}, f32[8,8,128]{2,1,0:T(8,128)S(1)}, u32[]{:S(2)}, u32[]{:S(2)}) collective-permute-start(f32[8,8,128]{2,1,0:T(8,128)S(1)} %get-tuple-element.73), channel_id=1, source_target_pairs={{0,0},{1,2},{2,1},{3,3},{4,4},{5,6},{6,5},{7,7},{8,8},{9,10},{10,9... | collective-permute-start | bytes 98312 | tf_op jit(solution)/shard_map/ppermute | solution.py:309
  41.3 25.4 %all-to-all-start = ((f32[32,1,3584]{2,1,0:T(1,128)}), f32[32,1,3584]{2,1,0:T(1,128)S(1)}, u32[]{:S(2)}, u32[]{:S(2)}) async-start(f32[32,1,3584]{2,1,0:T(1,128)} %bitcast.3), calls=%async_computation | async-start | bytes 917504 | tf_op jit(solution)/shard_map/all_to_all | solution.py:326
  57.0 6.6 %collective-permute-start.12 = (f32[8,8,128]{2,1,0:T(8,128)S(1)}, f32[8,8,128]{2,1,0:T(8,128)S(1)}, u32[]{:S(2)}, u32[]{:S(2)}) collective-permute-start(f32[8,8,128]{2,1,0:T(8,128)S(1)} %get-tuple-element.91), channel_id=1, source_target_pairs={{0,1},{1,0},{2,3},{3,2},{4,5},{5,4},{6,7},{7,6},{8,9},{9,8},{10,11... | collective-permute-start | bytes 98312 | tf_op jit(solution)/shard_map/ppermute | solution.py:310
  58.5 5.1 %collective-permute-start.13 = (f32[8,8,128]{2,1,0:T(8,128)S(1)}, f32[8,8,128]{2,1,0:T(8,128)S(1)}, u32[]{:S(2)}, u32[]{:S(2)}) collective-permute-start(f32[8,8,128]{2,1,0:T(8,128)S(1)} %get-tuple-element.92), channel_id=1, source_target_pairs={{0,0},{1,2},{2,1},{3,3},{4,4},{5,6},{6,5},{7,7},{8,8},{9,10},{10,9... | collective-permute-start | bytes 98312 | tf_op jit(solution)/shard_map/ppermute | solution.py:309
  67.4 18.8 %all-to-all-start.1 = ((f32[8,1,3584]{2,1,0:T(1,128)}), f32[8,1,3584]{2,1,0:T(1,128)S(1)}, u32[]{:S(2)}, u32[]{:S(2)}) async-start(f32[8,1,3584]{2,1,0:T(1,128)} %bitcast.5), calls=%async_computation.1 | async-start | bytes 229376 | tf_op jit(solution)/shard_map/all_to_all | solution.py:326
  78.7 2.7 %collective-permute-start.14 = (f32[8,8,128]{2,1,0:T(8,128)S(1)}, f32[8,8,128]{2,1,0:T(8,128)S(1)}, u32[]{:S(2)}, u32[]{:S(2)}) collective-permute-start(f32[8,8,128]{2,1,0:T(8,128)S(1)} %get-tuple-element.94), channel_id=1, source_target_pairs={{0,4},{4,0},{8,12},{12,8},{1,5},{5,1},{9,13},{13,9},{2,6},{6,2},{1... | collective-permute-start | bytes 98312 | tf_op jit(solution)/shard_map/ppermute | solution.py:310
  79.3 5.5 %collective-permute-start.15 = (f32[8,8,128]{2,1,0:T(8,128)S(1)}, f32[8,8,128]{2,1,0:T(8,128)S(1)}, u32[]{:S(2)}, u32[]{:S(2)}) collective-permute-start(f32[8,8,128]{2,1,0:T(8,128)S(1)} %get-tuple-element.95), channel_id=1, source_target_pairs={{0,0},{4,8},{8,4},{12,12},{1,1},{5,9},{9,5},{13,13},{2,2},{6,10},{... | collective-permute-start | bytes 98312 | tf_op jit(solution)/shard_map/ppermute | solution.py:309
  87.1 17.1 %all-to-all-start.2 = ((f32[32,1,3584]{2,1,0:T(1,128)}), f32[32,1,3584]{2,1,0:T(1,128)S(1)}, u32[]{:S(2)}, u32[]{:S(2)}) async-start(f32[32,1,3584]{2,1,0:T(1,128)} %bitcast.7), calls=%async_computation.2 | async-start | bytes 917504 | tf_op jit(solution)/shard_map/all_to_all | solution.py:326
  93.4 11.8 %collective-permute-start.16 = (f32[8,8,128]{2,1,0:T(8,128)S(1)}, f32[8,8,128]{2,1,0:T(8,128)S(1)}, u32[]{:S(2)}, u32[]{:S(2)}) collective-permute-start(f32[8,8,128]{2,1,0:T(8,128)S(1)} %get-tuple-element.97), channel_id=1, source_target_pairs={{0,16},{16,0},{32,48},{48,32},{64,80},{80,64},{96,112},{112,96},{1... | collective-permute-start | bytes 98312 | tf_op jit(solution)/shard_map/ppermute | solution.py:310
  96.4 8.8 %collective-permute-start.17 = (f32[8,8,128]{2,1,0:T(8,128)S(1)}, f32[8,8,128]{2,1,0:T(8,128)S(1)}, u32[]{:S(2)}, u32[]{:S(2)}) collective-permute-start(f32[8,8,128]{2,1,0:T(8,128)S(1)} %get-tuple-element.98), channel_id=1, source_target_pairs={{0,0},{16,32},{32,16},{48,64},{64,48},{80,96},{96,80},{112,128},{1... | collective-permute-start | bytes 98312 | tf_op jit(solution)/shard_map/ppermute | solution.py:309

commit v5 on v4

--- a/solution.py
+++ b/solution.py
@@ -1,4 +1,5 @@
 import functools
+import itertools
 import math
 
 import jax
@@ -145,17 +146,17 @@
 
 
 def low(rim, d, a, b):
-    return jnp.where(rim[3 * d] > 0, jnp.where(rim[3 * d + 1] > 0, b, 0.0), a)
+    return jnp.where(rim[3 * d] > 0, jnp.where(rim[3 * d + 1] > 0, a, 0.0), b)
 
 
 def high(rim, d, a, b):
-    return jnp.where(rim[3 * d] > 0, a, jnp.where(rim[3 * d + 2] > 0, b, 0.0))
+    return jnp.where(rim[3 * d] > 0, b, jnp.where(rim[3 * d + 2] > 0, a, 0.0))
 
 
 def send(rim, d, lo, hi, a, b):
     even = rim[3 * d] > 0
-    a[...] = jnp.where(even, hi, lo)
-    b[...] = jnp.where(even, lo, hi)
+    a[...] = jnp.where(even, lo, hi)
+    b[...] = jnp.where(even, hi, lo)
 
 
 def add_x(rim, x, out):
@@ -302,12 +303,25 @@
     node_out[...] = total[6 * W :] * factor
 
 
-def exchange(a, b, axis):
-    count = lax.axis_size(axis)
-    first = [(i, i ^ 1) for i in range(count)]
-    second = [(i, min(max((i + 1) ^ 1, 1) - 1, count - 1)) for i in range(count)]
-    b = lax.ppermute(b, axis, second)
-    return lax.ppermute(a, axis, first), b
+def exchange(a, b, which):
+    sizes = [lax.axis_size(axis) for axis in (GX, GY, GZ)]
+    aside = {0: 1, 1: 2, 2: 1}[which]
+    first, second = [], []
+    for me in itertools.product(*map(range, sizes)):
+        at = ((me[which] + 1) ^ 1) - 1
+        end = at < 0 or at >= sizes[which]
+        first.append(moved_to(me, aside, me[aside] ^ 1) if end else moved_to(me, which, at))
+        second.append(moved_to(me, which, me[which] ^ 1))
+    ranks = {me: rank for rank, me in enumerate(itertools.product(*map(range, sizes)))}
+    a, b = (
+        lax.ppermute(face, GX + GY + GZ, [(rank, ranks[to]) for rank, to in enumerate(targets)])
+        for face, targets in ((a, first), (b, second))
+    )
+    return a, b
+
+
+def moved_to(me, which, at):
+    return me[:which] + (at,) + me[which + 1 :]
 
 
 FACES = [(FACE, F32), (FACE, F32)]
@@ -315,11 +329,11 @@
 
 
 def arrivals(rim, field, xa, xb, tag):
-    x = exchange(xa, xb, GX)
+    x = exchange(xa, xb, 0)
     a, b = call(y_faces_after_x, FACES, [VMEM] * 4, "after_x" + tag, [BOTH])(rim, field, *x)
-    y = exchange(a, b, GY)
+    y = exchange(a, b, 1)
     a, b = call(z_faces_after_y, FACES, [VMEM] * 6, "after_y" + tag, [BOTH])(rim, field, *x, *y)
-    return (*x, *y, *exchange(a, b, GZ))
+    return (*x, *y, *exchange(a, b, 2))
 
 
 def swap(rows, axes):
@@ -330,7 +344,7 @@
     near, far = lax.axis_size(NEAR), lax.axis_size(FAR)
     rows = grads.shape[0] // near
     got = swap(grads, NEAR)
-    z = exchange(za, zb, GZ)
+    z = exchange(za, zb, 2)
     a, b, spread = call(
         functools.partial(fold_with_faces_kernel, y_faces_after_z, rows, near // 2, far // 2),
         FACES + [((rows * far, W), F32)],
@@ -339,7 +353,7 @@
         [BOTH],
     )(got, rim, field, *z)
     got = swap(spread, FAR)
-    y = exchange(a, b, GY)
+    y = exchange(a, b, 1)
     a, b, spread = call(
         functools.partial(fold_with_faces_kernel, x_faces_after_y, rows, far // 2, near // 2),
         FACES + [((rows * near, W), F32)],
@@ -348,7 +362,7 @@
         [BOTH],
     )(got, rim, field, *z, *y)
     total = swap(spread, NEAR)
-    return (*z, *y, *exchange(a, b, GX)), total
+    return (*z, *y, *exchange(a, b, 0)), total
 
 
 def on_device(node_feat, edge_feat, copies, offsets, w_edge_in, w_edge_out, w_node_in, w_node_out, node_cot):

time: 107 us -> 94.9 us (0.89)
  starting transfers between devices: 65.9 us -> 52.3 us
  waiting for transfers between devices: 26.7 us -> 28.8 us
    all_to_all x3, starting transfers between devices: 32.1 us -> 23.9 us  [swap(): lax.all_to_all(rows.reshape(lax.axis_size(axes), -1), axes, 0, 0, tiled=T...]
    ppermute x18, starting transfers between devices: 33.8 us -> 28.5 us  [exchange(): lax.ppermute(face, GX + GY + GZ, [(rank, ranks[to]) for rank, to in enume...]
    all_to_all x3, waiting for transfers between devices: 10.7 us -> 14.1 us  [swap(): lax.all_to_all(rows.reshape(lax.axis_size(axes), -1), axes, 0, 0, tiled=T...]
    ppermute x18, waiting for transfers between devices: 15.9 us -> 14.8 us  [exchange(): lax.ppermute(face, GX + GY + GZ, [(rank, ranks[to]) for rank, to in enume...]
  transfers between devices with their start and end apart: 21 -> 21, of which waited for: 10 -> 11; matrix products, arithmetic and copies ran while one was open for 0% -> 0% of each run, Pallas kernels for 5% -> 6%
where the time goes in v5:
time: 94.9 us; the launch traced here: 94.4 us
  starting transfers between devices  52.3 us (55%)
  waiting for transfers between devices  28.8 us (30%)
  Pallas kernels  12.2 us (13%)
    ppermute x18, starting transfers between devices, exchange(): lax.ppermute(face, GX + GY + GZ, [(rank, ranks[to]) for rank, to in enume...  28.5 us
    all_to_all x3, starting transfers between devices, swap(): lax.all_to_all(rows.reshape(lax.axis_size(axes), -1), axes, 0, 0, tiled=T...  23.9 us
    ppermute x18, waiting for transfers between devices, exchange(): lax.ppermute(face, GX + GY + GZ, [(rank, ranks[to]) for rank, to in enume...  14.8 us
    all_to_all x3, waiting for transfers between devices, swap(): lax.all_to_all(rows.reshape(lax.axis_size(axes), -1), axes, 0, 0, tiled=T...  14.1 us
    pallas_call x1, Pallas kernels, on_device(): call(forward_kernel, [(CUBE, F32)] + FACES + [((K, N, W), F32), many, ((N...  2.42 us
  transfers between devices with their start and end apart: 21, of which 11 were waited for; matrix products, arithmetic and copies ran while one was open for 0% of the time, Pallas kernels for 6%

profile of v5, /device:TPU:1, one launch (start us, length us, event | category | flops | bytes accessed | tf_op | source)
XLA Modules:
  0.0 94.4 jit_solution(2824414250069365296)
XLA Ops:
  0.6 0.0 copy-start.4
  0.6 0.0 copy-start.1
  0.7 0.0 copy-start
  0.7 0.0 copy-start.2
  0.7 2.4 %forward.1 = (f32[8,8,8,128]{3,2,1,0:T(8,128)S(1)}, f32[8,8,128]{2,1,0:T(8,128)S(1)}, f32[8,8,128]{2,1,0:T(8,128)S(1)}, f32[4,512,128]{2,1,0:T(8,128)S(1)}, bf16...) custom-call(bf16[512,128]{1,0:T(8,128)(2,1)} %bitcast.18, ...), custom_call_target="tpu_custom_call" | custom-call | tf_op jit(solution)/shard_map/forward/pallas_call | solution.py:374
  3.1 3.3 %collective-permute-start = (f32[8,8,128]{2,1,0:T(8,128)S(1)}, f32[8,8,128]{2,1,0:T(8,128)S(1)}, u32[]{:S(2)}, u32[]{:S(2)}) collective-permute-start(f32[8,8,128]{2,1,0:T(8,128)S(1)} %get-tuple-element.57), channel_id=1, source_target_pairs={{0,4},{1,5},{2,6},{3,7},{4,0},{5,1},{6,2},{7,3},{8,12},{9,13},{10,... | collective-permute-start | bytes 98312 | tf_op jit(solution)/shard_map/ppermute | solution.py:317
  6.4 1.9 %collective-permute-start.1 = (f32[8,8,128]{2,1,0:T(8,128)S(1)}, f32[8,8,128]{2,1,0:T(8,128)S(1)}, u32[]{:S(2)}, u32[]{:S(2)}) collective-permute-start(f32[8,8,128]{2,1,0:T(8,128)S(1)} %get-tuple-element.58), channel_id=1, source_target_pairs={{0,16},{1,17},{2,18},{3,19},{4,20},{5,21},{6,22},{7,23},{8,24},{9,... | collective-permute-start | bytes 98312 | tf_op jit(solution)/shard_map/ppermute | solution.py:317
  8.3 0.0 collective-permute-done.x0
  8.3 2.3 %collective-permute-done.1.x1 = f32[8,8,128]{2,1,0:T(8,128)S(1)} collective-permute-done((f32[8,8,128]{2,1,0:T(8,128)S(1)}, f32[8,8,128]{2,1,0:T(8,128)S(1)}, u32[]{:S(2)}, u32[]{:S(2)}) %collective-permute-start.1) | collective-permute-done | bytes 32800 | tf_op jit(solution)/shard_map/ppermute | solution.py:317
  10.7 2.1 %collective-permute-start.2 = (f32[8,8,128]{2,1,0:T(8,128)S(1)}, f32[8,8,128]{2,1,0:T(8,128)S(1)}, u32[]{:S(2)}, u32[]{:S(2)}) collective-permute-start(f32[8,8,128]{2,1,0:T(8,128)S(1)} %get-tuple-element.59), channel_id=1, source_target_pairs={{0,1},{1,0},{2,3},{3,2},{4,8},{5,9},{6,10},{7,11},{8,4},{9,5},{10,... | collective-permute-start | bytes 98312 | tf_op jit(solution)/shard_map/ppermute | solution.py:317
  12.7 0.3 collective-permute-start.3
  13.1 1.3 %collective-permute-done.2.y0 = f32[8,8,128]{2,1,0:T(8,128)S(1)} collective-permute-done((f32[8,8,128]{2,1,0:T(8,128)S(1)}, f32[8,8,128]{2,1,0:T(8,128)S(1)}, u32[]{:S(2)}, u32[]{:S(2)}) %collective-permute-start.2) | collective-permute-done | bytes 32800 | tf_op jit(solution)/shard_map/ppermute | solution.py:317
  14.3 0.0 collective-permute-done.3.y1
  14.3 0.1 after_y_1.1
  14.4 0.0 copy-start.3
  14.5 1.7 %collective-permute-start.4 = (f32[8,8,128]{2,1,0:T(8,128)S(1)}, f32[8,8,128]{2,1,0:T(8,128)S(1)}, u32[]{:S(2)}, u32[]{:S(2)}) collective-permute-start(f32[8,8,128]{2,1,0:T(8,128)S(1)} %get-tuple-element.61), channel_id=1, source_target_pairs={{0,4},{1,2},{2,1},{3,7},{4,0},{5,6},{6,5},{7,3},{8,12},{9,10},{10,... | collective-permute-start | bytes 98312 | tf_op jit(solution)/shard_map/ppermute | solution.py:317
  16.1 0.8 collective-permute-start.5
  17.0 0.1 div.16
  17.1 0.0 copy-done.1
  17.1 0.2 prepare_node.1
  17.3 0.0 collective-permute-done.4.z0
  17.3 1.6 %collective-permute-done.5.z1 = f32[8,8,128]{2,1,0:T(8,128)S(1)} collective-permute-done((f32[8,8,128]{2,1,0:T(8,128)S(1)}, f32[8,8,128]{2,1,0:T(8,128)S(1)}, u32[]{:S(2)}, u32[]{:S(2)}) %collective-permute-start.5) | collective-permute-done | bytes 32800 | tf_op jit(solution)/shard_map/ppermute | solution.py:317
  18.9 0.1 broadcast_in_dim.2.inverse
  19.0 0.4 node.1
  19.4 1.7 %collective-permute-start.6 = (f32[8,8,128]{2,1,0:T(8,128)S(1)}, f32[8,8,128]{2,1,0:T(8,128)S(1)}, u32[]{:S(2)}, u32[]{:S(2)}) collective-permute-start(f32[8,8,128]{2,1,0:T(8,128)S(1)} %get-tuple-element.68), channel_id=1, source_target_pairs={{0,4},{1,5},{2,6},{3,7},{4,0},{5,1},{6,2},{7,3},{8,12},{9,13},{10,... | collective-permute-start | bytes 98312 | tf_op jit(solution)/shard_map/ppermute | solution.py:317
  21.2 3.6 %collective-permute-start.7 = (f32[8,8,128]{2,1,0:T(8,128)S(1)}, f32[8,8,128]{2,1,0:T(8,128)S(1)}, u32[]{:S(2)}, u32[]{:S(2)}) collective-permute-start(f32[8,8,128]{2,1,0:T(8,128)S(1)} %get-tuple-element.69), channel_id=1, source_target_pairs={{0,16},{1,17},{2,18},{3,19},{4,20},{5,21},{6,22},{7,23},{8,24},{9,... | collective-permute-start | bytes 98312 | tf_op jit(solution)/shard_map/ppermute | solution.py:317
  24.8 0.0 collective-permute-done.6.x0
  24.8 1.3 %collective-permute-done.7.x1 = f32[8,8,128]{2,1,0:T(8,128)S(1)} collective-permute-done((f32[8,8,128]{2,1,0:T(8,128)S(1)}, f32[8,8,128]{2,1,0:T(8,128)S(1)}, u32[]{:S(2)}, u32[]{:S(2)}) %collective-permute-start.7) | collective-permute-done | bytes 32800 | tf_op jit(solution)/shard_map/ppermute | solution.py:317
  26.1 3.1 %collective-permute-start.8 = (f32[8,8,128]{2,1,0:T(8,128)S(1)}, f32[8,8,128]{2,1,0:T(8,128)S(1)}, u32[]{:S(2)}, u32[]{:S(2)}) collective-permute-start(f32[8,8,128]{2,1,0:T(8,128)S(1)} %get-tuple-element.70), channel_id=1, source_target_pairs={{0,1},{1,0},{2,3},{3,2},{4,8},{5,9},{6,10},{7,11},{8,4},{9,5},{10,... | collective-permute-start | bytes 98312 | tf_op jit(solution)/shard_map/ppermute | solution.py:317
  29.1 2.3 %collective-permute-start.9 = (f32[8,8,128]{2,1,0:T(8,128)S(1)}, f32[8,8,128]{2,1,0:T(8,128)S(1)}, u32[]{:S(2)}, u32[]{:S(2)}) collective-permute-start(f32[8,8,128]{2,1,0:T(8,128)S(1)} %get-tuple-element.71), channel_id=1, source_target_pairs={{0,4},{1,5},{2,6},{3,7},{4,0},{5,1},{6,2},{7,3},{8,12},{9,13},{10,... | collective-permute-start | bytes 98312 | tf_op jit(solution)/shard_map/ppermute | solution.py:317
  31.5 0.0 collective-permute-done.8.y0
  31.5 0.9 collective-permute-done.9.y1
  32.3 0.1 after_y_2.1
  32.4 1.1 %collective-permute-start.10 = (f32[8,8,128]{2,1,0:T(8,128)S(1)}, f32[8,8,128]{2,1,0:T(8,128)S(1)}, u32[]{:S(2)}, u32[]{:S(2)}) collective-permute-start(f32[8,8,128]{2,1,0:T(8,128)S(1)} %get-tuple-element.72), channel_id=1, source_target_pairs={{0,4},{1,2},{2,1},{3,7},{4,0},{5,6},{6,5},{7,3},{8,12},{9,10},{10,... | collective-permute-start | bytes 98312 | tf_op jit(solution)/shard_map/ppermute | solution.py:317
  33.5 0.0 collective-permute-start.11
  33.5 1.5 %prepare_edge.1 = (f32[4,512,128]{2,1,0:T(8,128)S(1)}, bf16[512,512]{1,0:T(8,128)(2,1)S(1)}, bf16[384,2048]{1,0:T(8,128)(2,1)S(1)}, bf16[128,128]{1,0:T(8,128)(2,1)S(1)}, bf16[256,128]{1,0:T(8,128)(2,1)S(1)}) custom-call(s32[4,3]{1,0:T(4,128)S(1)} %copy-done.3, f32[4,512,128]{2,1,0:T(8,128)S(1)} %get-tuple-element.74.preact, ...), custom_call_target="tpu_custom_call" | custom-call | tf_op jit(solution)/shard_map/prepare_edge/pallas_call | solution.py:385
  35.0 0.3 node_grads.1
  35.4 0.0 collective-permute-done.10.z0
  35.4 0.9 collective-permute-done.11.z1
  36.3 1.7 %edge.1 = (bf16[2048,128]{1,0:T(8,128)(2,1)S(1)}, f32[896,128]{1,0:T(8,128)}) custom-call(f32[9,8,128]{2,1,0:T(8,128)S(1)} %get-tuple-element.55.rim.refs_0_, f32[8,8,8,128]{3,2,1,0:T(8,128)S(1)} %get-tuple-element.67.field, f32[8,8,128]{2,1,0:T(8,128)S(1)} %collective-permute-done.6.x0, f32[8,8,128]{2,1,0:T(8,128)S(1)} %collective-permute-done.7.x1, ...), custom_call_target="tpu_custom_call" | custom-call | tf_op jit(solution)/shard_map/edge/pallas_call | solution.py:399
  38.0 9.6 %all-to-all-start = ((f32[32,1,3584]{2,1,0:T(1,128)}), f32[32,1,3584]{2,1,0:T(1,128)S(1)}, u32[]{:S(2)}, u32[]{:S(2)}) async-start(f32[32,1,3584]{2,1,0:T(1,128)} %bitcast.3), calls=%async_computation | async-start | bytes 917504 | tf_op jit(solution)/shard_map/all_to_all | solution.py:340
  47.6 1.2 %node_part.1 = (f32[8,8,8,128]{3,2,1,0:T(8,128)S(1)}, f32[8,8,128]{2,1,0:T(8,128)S(1)}, f32[8,8,128]{2,1,0:T(8,128)S(1)}) custom-call(s32[4,3]{1,0:T(4,128)S(1)} %copy-done.3, f32[9,8,128]{2,1,0:T(8,128)S(1)} %get-tuple-element.55.rim.refs_0_, bf16[2048,128]{1,0:T(8,128)(2,1)S(1)} %get-tuple-element.87.slopes, f32[512,128]{1,0:T(8,128)S(1)} %get-tuple-element.88.base, ...), custom_call_target="tpu_custom_call" | custom-call | tf_op jit(solution)/shard_map/node_part/pallas_call | solution.py:402
  48.8 0.3 collective-permute-start.12
  49.1 2.3 %collective-permute-start.13 = (f32[8,8,128]{2,1,0:T(8,128)S(1)}, f32[8,8,128]{2,1,0:T(8,128)S(1)}, u32[]{:S(2)}, u32[]{:S(2)}) collective-permute-start(f32[8,8,128]{2,1,0:T(8,128)S(1)} %get-tuple-element.92), channel_id=1, source_target_pairs={{0,1},{1,0},{2,3},{3,2},{4,5},{5,4},{6,7},{7,6},{8,9},{9,8},{10,11... | collective-permute-start | bytes 98312 | tf_op jit(solution)/shard_map/ppermute | solution.py:317
  51.4 0.0 collective-permute-done.12.refs_2_.z0
  51.4 3.9 %collective-permute-done.13.refs_3_.z1 = f32[8,8,128]{2,1,0:T(8,128)S(1)} collective-permute-done((f32[8,8,128]{2,1,0:T(8,128)S(1)}, f32[8,8,128]{2,1,0:T(8,128)S(1)}, u32[]{:S(2)}, u32[]{:S(2)}) %collective-permute-start.13) | collective-permute-done | bytes 32800 | tf_op jit(solution)/shard_map/ppermute | solution.py:317
  55.3 3.1 %all-to-all-done = f32[32,1,3584]{2,1,0:T(1,128)S(1)} async-done(((f32[32,1,3584]{2,1,0:T(1,128)}), f32[32,1,3584]{2,1,0:T(1,128)S(1)}, u32[]{:S(2)}, u32[]{:S(2)}) %all-to-all-start) | async-done | bytes 458784 | tf_op jit(solution)/shard_map/all_to_all | solution.py:340
  58.5 0.7 after_z_fold.1
  59.2 8.2 %all-to-all-start.1 = ((f32[8,1,3584]{2,1,0:T(1,128)}), f32[8,1,3584]{2,1,0:T(1,128)S(1)}, u32[]{:S(2)}, u32[]{:S(2)}) async-start(f32[8,1,3584]{2,1,0:T(1,128)} %bitcast.5), calls=%async_computation.1 | async-start | bytes 229376 | tf_op jit(solution)/shard_map/all_to_all | solution.py:340
  67.4 0.8 collective-permute-start.14
  68.2 0.0 collective-permute-start.15
  68.2 2.5 %collective-permute-done.14.refs_4_.y0 = f32[8,8,128]{2,1,0:T(8,128)S(1)} collective-permute-done((f32[8,8,128]{2,1,0:T(8,128)S(1)}, f32[8,8,128]{2,1,0:T(8,128)S(1)}, u32[]{:S(2)}, u32[]{:S(2)}) %collective-permute-start.14) | collective-permute-done | bytes 32800 | tf_op jit(solution)/shard_map/ppermute | solution.py:317
  70.7 0.0 collective-permute-done.15.refs_5_.y1
  70.7 4.3 %all-to-all-done.1 = f32[8,1,3584]{2,1,0:T(1,128)S(1)} async-done(((f32[8,1,3584]{2,1,0:T(1,128)}), f32[8,1,3584]{2,1,0:T(1,128)S(1)}, u32[]{:S(2)}, u32[]{:S(2)}) %all-to-all-start.1) | async-done | bytes 114720 | tf_op jit(solution)/shard_map/all_to_all | solution.py:340
  75.0 0.8 after_y_fold.1
  75.8 6.1 %all-to-all-start.2 = ((f32[32,1,3584]{2,1,0:T(1,128)}), f32[32,1,3584]{2,1,0:T(1,128)S(1)}, u32[]{:S(2)}, u32[]{:S(2)}) async-start(f32[32,1,3584]{2,1,0:T(1,128)} %bitcast.7), calls=%async_computation.2 | async-start | bytes 917504 | tf_op jit(solution)/shard_map/all_to_all | solution.py:340
  81.9 0.3 collective-permute-start.16
  82.2 2.7 %collective-permute-start.17 = (f32[8,8,128]{2,1,0:T(8,128)S(1)}, f32[8,8,128]{2,1,0:T(8,128)S(1)}, u32[]{:S(2)}, u32[]{:S(2)}) collective-permute-start(f32[8,8,128]{2,1,0:T(8,128)S(1)} %get-tuple-element.98), channel_id=1, source_target_pairs={{0,16},{1,17},{2,18},{3,19},{4,20},{5,21},{6,22},{7,23},{8,24},{9,... | collective-permute-start | bytes 98312 | tf_op jit(solution)/shard_map/ppermute | solution.py:317
  84.9 1.1 %edge_grad.1 = bf16[2048,128]{1,0:T(8,128)(2,1)} custom-call(bf16[2048,128]{1,0:T(8,128)(2,1)S(1)} %get-tuple-element.87.slopes, bf16[384,128]{1,0:T(8,128)(2,1)S(1)} %get-tuple-element.77.w_in), custom_call_target="tpu_custom_call" | custom-call | tf_op jit(solution)/shard_map/edge_grad/pallas_call | solution.py:406
  86.0 6.6 %all-to-all-done.2 = f32[32,1,3584]{2,1,0:T(1,128)S(1)} async-done(((f32[32,1,3584]{2,1,0:T(1,128)}), f32[32,1,3584]{2,1,0:T(1,128)S(1)}, u32[]{:S(2)}, u32[]{:S(2)}) %all-to-all-start.2) | async-done | bytes 458784 | tf_op jit(solution)/shard_map/all_to_all | solution.py:340
  92.7 1.0 %clip.1 = (f32[384,128]{1,0:T(8,128)}, f32[128,128]{1,0:T(8,128)}, f32[256,128]{1,0:T(8,128)}, f32[128,128]{1,0:T(8,128)}) custom-call(f32[896,128]{1,0:T(8,128)S(1)} %bitcast.12), custom_call_target="tpu_custom_call" | custom-call | tf_op jit(solution)/shard_map/clip/pallas_call | solution.py:407
  93.6 0.0 collective-permute-done.16.x0
  93.7 0.0 collective-permute-done.17.x1
  93.7 0.8 last.1
  (7 shorter events, 0.0 us)
Async XLA Ops:
  0.6 16.3 %copy-start.4 = (s32[8,8,8]{2,1,0:T(8,128)S(1)}, s32[8,8,8]{2,1,0:T(8,128)}, u32[]{:S(2)}) copy-start(s32[8,8,8]{2,1,0:T(8,128)} %param.11) | copy-start | bytes 6148
  0.6 16.4 %copy-start.1 = (bf16[8,8,8,128]{3,2,1,0:T(8,128)(2,1)S(1)}, bf16[8,8,8,128]{3,2,1,0:T(8,128)(2,1)}, u32[]{:S(2)}) copy-start(bf16[8,8,8,128]{3,2,1,0:T(8,128)(2,1)} %param.17) | copy-start | bytes 393220
  0.7 16.4 %copy-start = (bf16[256,128]{1,0:T(8,128)(2,1)S(1)}, bf16[256,128]{1,0:T(8,128)(2,1)}, u32[]{:S(2)}) copy-start(bf16[256,128]{1,0:T(8,128)(2,1)} %w_in.5) | copy-start | bytes 196612
  0.7 16.4 %copy-start.2 = (bf16[128,128]{1,0:T(8,128)(2,1)S(1)}, bf16[128,128]{1,0:T(8,128)(2,1)}, u32[]{:S(2)}) copy-start(bf16[128,128]{1,0:T(8,128)(2,1)} %w_out.1) | copy-start | bytes 98308
  3.1 5.2 %collective-permute-start = (f32[8,8,128]{2,1,0:T(8,128)S(1)}, f32[8,8,128]{2,1,0:T(8,128)S(1)}, u32[]{:S(2)}, u32[]{:S(2)}) collective-permute-start(f32[8,8,128]{2,1,0:T(8,128)S(1)} %get-tuple-element.57), channel_id=1, source_target_pairs={{0,4},{1,5},{2,6},{3,7},{4,0},{5,1},{6,2},{7,3},{8,12},{9,13},{10,... | collective-permute-start | bytes 98312 | tf_op jit(solution)/shard_map/ppermute | solution.py:317
  6.4 4.3 %collective-permute-start.1 = (f32[8,8,128]{2,1,0:T(8,128)S(1)}, f32[8,8,128]{2,1,0:T(8,128)S(1)}, u32[]{:S(2)}, u32[]{:S(2)}) collective-permute-start(f32[8,8,128]{2,1,0:T(8,128)S(1)} %get-tuple-element.58), channel_id=1, source_target_pairs={{0,16},{1,17},{2,18},{3,19},{4,20},{5,21},{6,22},{7,23},{8,24},{9,... | collective-permute-start | bytes 98312 | tf_op jit(solution)/shard_map/ppermute | solution.py:317
  10.7 3.7 %collective-permute-start.2 = (f32[8,8,128]{2,1,0:T(8,128)S(1)}, f32[8,8,128]{2,1,0:T(8,128)S(1)}, u32[]{:S(2)}, u32[]{:S(2)}) collective-permute-start(f32[8,8,128]{2,1,0:T(8,128)S(1)} %get-tuple-element.59), channel_id=1, source_target_pairs={{0,1},{1,0},{2,3},{3,2},{4,8},{5,9},{6,10},{7,11},{8,4},{9,5},{10,... | collective-permute-start | bytes 98312 | tf_op jit(solution)/shard_map/ppermute | solution.py:317
  12.7 1.6 %collective-permute-start.3 = (f32[8,8,128]{2,1,0:T(8,128)S(1)}, f32[8,8,128]{2,1,0:T(8,128)S(1)}, u32[]{:S(2)}, u32[]{:S(2)}) collective-permute-start(f32[8,8,128]{2,1,0:T(8,128)S(1)} %get-tuple-element.60), channel_id=1, source_target_pairs={{0,4},{1,5},{2,6},{3,7},{4,0},{5,1},{6,2},{7,3},{8,12},{9,13},{10,... | collective-permute-start | bytes 98312 | tf_op jit(solution)/shard_map/ppermute | solution.py:317
  14.4 19.1 %copy-start.3 = (s32[4,3]{1,0:T(4,128)S(1)}, s32[4,3]{1,0:T(4,128)}, u32[]{:S(2)}) copy-start(s32[4,3]{1,0:T(4,128)} %offs.3) | copy-start | bytes 148
  14.5 2.9 %collective-permute-start.4 = (f32[8,8,128]{2,1,0:T(8,128)S(1)}, f32[8,8,128]{2,1,0:T(8,128)S(1)}, u32[]{:S(2)}, u32[]{:S(2)}) collective-permute-start(f32[8,8,128]{2,1,0:T(8,128)S(1)} %get-tuple-element.61), channel_id=1, source_target_pairs={{0,4},{1,2},{2,1},{3,7},{4,0},{5,6},{6,5},{7,3},{8,12},{9,10},{10,... | collective-permute-start | bytes 98312 | tf_op jit(solution)/shard_map/ppermute | solution.py:317
  16.1 2.8 %collective-permute-start.5 = (f32[8,8,128]{2,1,0:T(8,128)S(1)}, f32[8,8,128]{2,1,0:T(8,128)S(1)}, u32[]{:S(2)}, u32[]{:S(2)}) collective-permute-start(f32[8,8,128]{2,1,0:T(8,128)S(1)} %get-tuple-element.62), channel_id=1, source_target_pairs={{0,1},{1,0},{2,3},{3,2},{4,5},{5,4},{6,7},{7,6},{8,9},{9,8},{10,11... | collective-permute-start | bytes 98312 | tf_op jit(solution)/shard_map/ppermute | solution.py:317
  19.4 5.3 %collective-permute-start.6 = (f32[8,8,128]{2,1,0:T(8,128)S(1)}, f32[8,8,128]{2,1,0:T(8,128)S(1)}, u32[]{:S(2)}, u32[]{:S(2)}) collective-permute-start(f32[8,8,128]{2,1,0:T(8,128)S(1)} %get-tuple-element.68), channel_id=1, source_target_pairs={{0,4},{1,5},{2,6},{3,7},{4,0},{5,1},{6,2},{7,3},{8,12},{9,13},{10,... | collective-permute-start | bytes 98312 | tf_op jit(solution)/shard_map/ppermute | solution.py:317
  21.2 4.9 %collective-permute-start.7 = (f32[8,8,128]{2,1,0:T(8,128)S(1)}, f32[8,8,128]{2,1,0:T(8,128)S(1)}, u32[]{:S(2)}, u32[]{:S(2)}) collective-permute-start(f32[8,8,128]{2,1,0:T(8,128)S(1)} %get-tuple-element.69), channel_id=1, source_target_pairs={{0,16},{1,17},{2,18},{3,19},{4,20},{5,21},{6,22},{7,23},{8,24},{9,... | collective-permute-start | bytes 98312 | tf_op jit(solution)/shard_map/ppermute | solution.py:317
  26.1 5.4 %collective-permute-start.8 = (f32[8,8,128]{2,1,0:T(8,128)S(1)}, f32[8,8,128]{2,1,0:T(8,128)S(1)}, u32[]{:S(2)}, u32[]{:S(2)}) collective-permute-start(f32[8,8,128]{2,1,0:T(8,128)S(1)} %get-tuple-element.70), channel_id=1, source_target_pairs={{0,1},{1,0},{2,3},{3,2},{4,8},{5,9},{6,10},{7,11},{8,4},{9,5},{10,... | collective-permute-start | bytes 98312 | tf_op jit(solution)/shard_map/ppermute | solution.py:317
  29.1 3.2 %collective-permute-start.9 = (f32[8,8,128]{2,1,0:T(8,128)S(1)}, f32[8,8,128]{2,1,0:T(8,128)S(1)}, u32[]{:S(2)}, u32[]{:S(2)}) collective-permute-start(f32[8,8,128]{2,1,0:T(8,128)S(1)} %get-tuple-element.71), channel_id=1, source_target_pairs={{0,4},{1,5},{2,6},{3,7},{4,0},{5,1},{6,2},{7,3},{8,12},{9,13},{10,... | collective-permute-start | bytes 98312 | tf_op jit(solution)/shard_map/ppermute | solution.py:317
  32.4 2.9 %collective-permute-start.10 = (f32[8,8,128]{2,1,0:T(8,128)S(1)}, f32[8,8,128]{2,1,0:T(8,128)S(1)}, u32[]{:S(2)}, u32[]{:S(2)}) collective-permute-start(f32[8,8,128]{2,1,0:T(8,128)S(1)} %get-tuple-element.72), channel_id=1, source_target_pairs={{0,4},{1,2},{2,1},{3,7},{4,0},{5,6},{6,5},{7,3},{8,12},{9,10},{10,... | collective-permute-start | bytes 98312 | tf_op jit(solution)/shard_map/ppermute | solution.py:317
  33.5 2.8 %collective-permute-start.11 = (f32[8,8,128]{2,1,0:T(8,128)S(1)}, f32[8,8,128]{2,1,0:T(8,128)S(1)}, u32[]{:S(2)}, u32[]{:S(2)}) collective-permute-start(f32[8,8,128]{2,1,0:T(8,128)S(1)} %get-tuple-element.73), channel_id=1, source_target_pairs={{0,1},{1,0},{2,3},{3,2},{4,5},{5,4},{6,7},{7,6},{8,9},{9,8},{10,11... | collective-permute-start | bytes 98312 | tf_op jit(solution)/shard_map/ppermute | solution.py:317
  38.0 20.5 %all-to-all-start = ((f32[32,1,3584]{2,1,0:T(1,128)}), f32[32,1,3584]{2,1,0:T(1,128)S(1)}, u32[]{:S(2)}, u32[]{:S(2)}) async-start(f32[32,1,3584]{2,1,0:T(1,128)} %bitcast.3), calls=%async_computation | async-start | bytes 917504 | tf_op jit(solution)/shard_map/all_to_all | solution.py:340
  48.8 2.6 %collective-permute-start.12 = (f32[8,8,128]{2,1,0:T(8,128)S(1)}, f32[8,8,128]{2,1,0:T(8,128)S(1)}, u32[]{:S(2)}, u32[]{:S(2)}) collective-permute-start(f32[8,8,128]{2,1,0:T(8,128)S(1)} %get-tuple-element.91), channel_id=1, source_target_pairs={{0,4},{1,2},{2,1},{3,7},{4,0},{5,6},{6,5},{7,3},{8,12},{9,10},{10,... | collective-permute-start | bytes 98312 | tf_op jit(solution)/shard_map/ppermute | solution.py:317
  49.1 6.2 %collective-permute-start.13 = (f32[8,8,128]{2,1,0:T(8,128)S(1)}, f32[8,8,128]{2,1,0:T(8,128)S(1)}, u32[]{:S(2)}, u32[]{:S(2)}) collective-permute-start(f32[8,8,128]{2,1,0:T(8,128)S(1)} %get-tuple-element.92), channel_id=1, source_target_pairs={{0,1},{1,0},{2,3},{3,2},{4,5},{5,4},{6,7},{7,6},{8,9},{9,8},{10,11... | collective-permute-start | bytes 98312 | tf_op jit(solution)/shard_map/ppermute | solution.py:317
  59.2 15.8 %all-to-all-start.1 = ((f32[8,1,3584]{2,1,0:T(1,128)}), f32[8,1,3584]{2,1,0:T(1,128)S(1)}, u32[]{:S(2)}, u32[]{:S(2)}) async-start(f32[8,1,3584]{2,1,0:T(1,128)} %bitcast.5), calls=%async_computation.1 | async-start | bytes 229376 | tf_op jit(solution)/shard_map/all_to_all | solution.py:340
  67.4 3.3 %collective-permute-start.14 = (f32[8,8,128]{2,1,0:T(8,128)S(1)}, f32[8,8,128]{2,1,0:T(8,128)S(1)}, u32[]{:S(2)}, u32[]{:S(2)}) collective-permute-start(f32[8,8,128]{2,1,0:T(8,128)S(1)} %get-tuple-element.94), channel_id=1, source_target_pairs={{0,1},{1,0},{2,3},{3,2},{4,8},{5,9},{6,10},{7,11},{8,4},{9,5},{10,... | collective-permute-start | bytes 98312 | tf_op jit(solution)/shard_map/ppermute | solution.py:317
  68.2 2.5 %collective-permute-start.15 = (f32[8,8,128]{2,1,0:T(8,128)S(1)}, f32[8,8,128]{2,1,0:T(8,128)S(1)}, u32[]{:S(2)}, u32[]{:S(2)}) collective-permute-start(f32[8,8,128]{2,1,0:T(8,128)S(1)} %get-tuple-element.95), channel_id=1, source_target_pairs={{0,4},{1,5},{2,6},{3,7},{4,0},{5,1},{6,2},{7,3},{8,12},{9,13},{10,... | collective-permute-start | bytes 98312 | tf_op jit(solution)/shard_map/ppermute | solution.py:317
  75.8 16.9 %all-to-all-start.2 = ((f32[32,1,3584]{2,1,0:T(1,128)}), f32[32,1,3584]{2,1,0:T(1,128)S(1)}, u32[]{:S(2)}, u32[]{:S(2)}) async-start(f32[32,1,3584]{2,1,0:T(1,128)} %bitcast.7), calls=%async_computation.2 | async-start | bytes 917504 | tf_op jit(solution)/shard_map/all_to_all | solution.py:340
  81.9 11.8 %collective-permute-start.16 = (f32[8,8,128]{2,1,0:T(8,128)S(1)}, f32[8,8,128]{2,1,0:T(8,128)S(1)}, u32[]{:S(2)}, u32[]{:S(2)}) collective-permute-start(f32[8,8,128]{2,1,0:T(8,128)S(1)} %get-tuple-element.97), channel_id=1, source_target_pairs={{0,4},{1,5},{2,6},{3,7},{4,0},{5,1},{6,2},{7,3},{8,12},{9,13},{10,... | collective-permute-start | bytes 98312 | tf_op jit(solution)/shard_map/ppermute | solution.py:317
  82.2 11.5 %collective-permute-start.17 = (f32[8,8,128]{2,1,0:T(8,128)S(1)}, f32[8,8,128]{2,1,0:T(8,128)S(1)}, u32[]{:S(2)}, u32[]{:S(2)}) collective-permute-start(f32[8,8,128]{2,1,0:T(8,128)S(1)} %get-tuple-element.98), channel_id=1, source_target_pairs={{0,16},{1,17},{2,18},{3,19},{4,20},{5,21},{6,22},{7,23},{8,24},{9,... | collective-permute-start | bytes 98312 | tf_op jit(solution)/shard_map/ppermute | solution.py:317

commit v6 on v5

--- a/solution.py
+++ b/solution.py
@@ -27,7 +27,7 @@
 WORK = pltpu.VMEM(CUBE, F32)
 
 GX, GY, GZ = ("z", "yh"), ("yl", "c"), ("x",)
-NEAR, FAR = ("yh", "yl", "c", "x"), ("z",)
+NEAR, FAR = ("yh", "yl", "x"), ("z",)
 
 
 def call(body, outs, specs, name, scratch=()):
@@ -159,6 +159,15 @@
     b[...] = jnp.where(even, hi, lo)
 
 
+def own(rim, top, bottom):
+    first = jnp.broadcast_to(rim[3, :1, :], top.shape) > 0
+    return jnp.where(first, top, bottom)
+
+
+def add_kernel(keep, got, after, out):
+    out[...] = keep[...] + got[...]
+
+
 def add_x(rim, x, out):
     out[0] = out[0] + low(rim, 0, x[0][...], x[1][...])
     out[B - 1] = out[B - 1] + high(rim, 0, x[0][...], x[1][...])
@@ -244,7 +253,7 @@
 
 
 def edge_kernel(
-    rim, field, x0, x1, y0, y1, z0, z1, dact, hidden_t, left, w_out_t, node_grads, slopes, grads, work
+    rim, field, x0, x1, y0, y1, z0, z1, dact, hidden_t, left, w_out_t, node_grads, slopes, keep, give, work, grads
 ):
     agg = whole(rim, field, x0, x1, y0, y1, z0, z1, work).astype(BF16)
     back = dot(agg, w_out_t[...])
@@ -254,6 +263,9 @@
     grads[3 * W : 4 * W] = (outer[:W] + outer[W : 2 * W]) + (outer[2 * W : 3 * W] + outer[3 * W :])
     grads[4 * W :] = node_grads[...]
     grads[: 3 * W] = dot(left[...], slopes[...])
+    half = keep.shape[0]
+    keep[...] = own(rim, grads[:half], grads[half:])
+    give[...] = own(rim, grads[half:], grads[:half])
 
 
 def node_part_kernel(offs, rim, slopes, base, w_back, local, za, zb, pad):
@@ -271,7 +283,7 @@
     out[...] = dot_t(slopes[...], w_in[2 * W :]).astype(BF16)
 
 
-def last_kernel(rim, field, z0, z1, y0, y1, x0, x1, clipped, out, work):
+def last_kernel(rim, field, z0, z1, y0, y1, x0, x1, out, work):
     work[...] = field[...]
     add_z(rim, (z0, z1), work)
     add_y(rim, (y0, y1), work)
@@ -293,8 +305,8 @@
     faces(*refs[:-2], refs[-1])
 
 
-def clip_kernel(grads, edge_in, edge_out, node_in, node_out):
-    total = grads[...]
+def clip_kernel(rim, mine, other, edge_in, edge_out, node_in, node_out):
+    total = jnp.concatenate([own(rim, mine[...], other[...]), own(rim, other[...], mine[...])], axis=0)
     squares = jnp.sum(jnp.sum(total * total, axis=0, keepdims=True), axis=1, keepdims=True)
     factor = math.sqrt(7 * W * W) / jnp.sqrt(squares)
     edge_in[...] = total[: 3 * W] * factor
@@ -320,6 +332,12 @@
     return a, b
 
 
+def other_core(half):
+    count = math.prod(lax.axis_size(axis) for axis in (GX, GY, GZ))
+    step = lax.axis_size(GZ)
+    return lax.ppermute(half, GX + GY + GZ, [(rank, rank ^ step) for rank in range(count)])
+
+
 def moved_to(me, which, at):
     return me[:which] + (at,) + me[which + 1 :]
 
@@ -340,10 +358,11 @@
     return lax.all_to_all(rows.reshape(lax.axis_size(axes), -1), axes, 0, 0, tiled=True).reshape(-1, W)
 
 
-def arrivals_and_sum(rim, field, za, zb, grads):
+def arrivals_and_sum(rim, field, za, zb, keep, give, edge_grad):
     near, far = lax.axis_size(NEAR), lax.axis_size(FAR)
-    rows = grads.shape[0] // near
-    got = swap(grads, NEAR)
+    rows = keep.shape[0] // near
+    (half,) = call(add_kernel, [(keep.shape, F32)], [VMEM] * 3, "add_core")(keep, other_core(give), za)
+    got = swap(half, NEAR)
     z = exchange(za, zb, 2)
     a, b, spread = call(
         functools.partial(fold_with_faces_kernel, y_faces_after_z, rows, near // 2, far // 2),
@@ -361,8 +380,10 @@
         "after_y_fold",
         [BOTH],
     )(got, rim, field, *z, *y)
-    total = swap(spread, NEAR)
-    return (*z, *y, *exchange(a, b, 0)), total
+    mine = swap(spread, NEAR)
+    x = exchange(a, b, 0)
+    mine, edge_grad, *x = lax.optimization_barrier((mine, edge_grad, *x))
+    return (*z, *y, *x), (mine, other_core(mine)), edge_grad
 
 
 def on_device(node_feat, edge_feat, copies, offsets, w_edge_in, w_edge_out, w_node_in, w_node_out, node_cot):
@@ -396,20 +417,23 @@
     node_grads, base = call(node_grads_kernel, [((3 * W, W), F32), ((N, W), F32)], [VMEM] * 6, "node_grads")(
         nodes, gathered, slope, node_hidden, cot, w_node_in
     )
-    slopes, grads = call(
-        edge_kernel, [((K * N, W), BF16), ((7 * W, W), F32)], [VMEM] * 13, "edge", [WORK]
+    half = ((7 * W // 2, W), F32)
+    slopes, keep, give = call(
+        edge_kernel,
+        [((K * N, W), BF16), half, half],
+        [VMEM] * 13,
+        "edge",
+        [WORK, pltpu.VMEM((7 * W, W), F32)],
     )(rim, local, *arrived, dact, hidden_t, left, w_out_t, node_grads)
     local, za, zb = call(
         node_part_kernel, [(CUBE, F32)] + FACES, [SMEM] + [VMEM] * 4, "node_part", [PAD]
     )(offsets, rim, slopes, base, w_back)
-    arrived, total = arrivals_and_sum(rim, local, za, zb, grads)
     (edge_grad,) = call(edge_grad_kernel, [((K * N, W), BF16)], [VMEM] * 2, "edge_grad")(slopes, w_in)
+    arrived, halves, edge_grad = arrivals_and_sum(rim, local, za, zb, keep, give, edge_grad)
     clipped = call(
-        clip_kernel, [((3 * W, W), F32), ((W, W), F32), ((2 * W, W), F32), ((W, W), F32)], [VMEM], "clip"
-    )(total)
-    (node_grad,) = call(last_kernel, [((N, W), BF16)], [VMEM] * 8 + [HBM], "last", [WORK])(
-        rim, local, *arrived, in_hbm(clipped[1])
-    )
+        clip_kernel, [((3 * W, W), F32), ((W, W), F32), ((2 * W, W), F32), ((W, W), F32)], [VMEM] * 3, "clip"
+    )(rim, *halves)
+    (node_grad,) = call(last_kernel, [((N, W), BF16)], [VMEM] * 8, "last", [WORK])(rim, local, *arrived)
     return (node_grad.reshape(node_feat.shape), edge_grad.reshape(edge_feat.shape), *clipped)
 
 

time: 94.9 us -> 91.5 us (0.964)
  waiting for transfers between devices: 28.8 us -> 22.5 us
  starting transfers between devices: 52.3 us -> 55.4 us
    all_to_all x3, waiting for transfers between devices: 14.1 us -> 7.25 us  [swap(): lax.all_to_all(rows.reshape(lax.axis_size(axes), -1), axes, 0, 0, tiled=T...]
    ppermute x0 -> x2, starting transfers between devices: none -> 5.69 us  [other_core(): lax.ppermute(half, GX + GY + GZ, [(rank, rank ^ step) for rank in range(c...]
    all_to_all x3, starting transfers between devices: 23.9 us -> 19.3 us  [swap(): lax.all_to_all(rows.reshape(lax.axis_size(axes), -1), axes, 0, 0, tiled=T...]
    ppermute x18, starting transfers between devices: 28.5 us -> 30.4 us  [exchange(): lax.ppermute(face, GX + GY + GZ, [(rank, ranks[to]) for rank, to in enume...]
    pallas_call x2 -> x3, Pallas kernels: 2.45 us -> 2.39 us  [the longest x1 0.9 us: on_device(): call(edge_kernel, [((K * N, W), BF16), half, half], [VMEM] * 13, 'edge',...]
  transfers between devices with their start and end apart: 21 -> 23, of which waited for: 11 -> 13; matrix products, arithmetic and copies ran while one was open for 0% -> 0% of each run, Pallas kernels for 6% -> 6%
where the time goes in v6:
time: 91.5 us; the launch traced here: 91 us
  starting transfers between devices  55.4 us (61%)
  waiting for transfers between devices  22.5 us (25%)
  Pallas kernels  12.1 us (13%)
    ppermute x18, starting transfers between devices, exchange(): lax.ppermute(face, GX + GY + GZ, [(rank, ranks[to]) for rank, to in enume...  30.4 us
    all_to_all x3, starting transfers between devices, swap(): lax.all_to_all(rows.reshape(lax.axis_size(axes), -1), axes, 0, 0, tiled=T...  19.3 us
    ppermute x18, waiting for transfers between devices, exchange(): lax.ppermute(face, GX + GY + GZ, [(rank, ranks[to]) for rank, to in enume...  14.9 us
    all_to_all x3, waiting for transfers between devices, swap(): lax.all_to_all(rows.reshape(lax.axis_size(axes), -1), axes, 0, 0, tiled=T...  7.25 us
    ppermute x2, starting transfers between devices, other_core(): lax.ppermute(half, GX + GY + GZ, [(rank, rank ^ step) for rank in range(c...  5.69 us
    pallas_call x1, Pallas kernels, on_device(): call(forward_kernel, [(CUBE, F32)] + FACES + [((K, N, W), F32), many, ((N...  2.42 us
  transfers between devices with their start and end apart: 23, of which 13 were waited for; matrix products, arithmetic and copies ran while one was open for 0% of the time, Pallas kernels for 6%

profile of v6, /device:TPU:1, one launch (start us, length us, event | category | flops | bytes accessed | tf_op | source)
XLA Modules:
  0.0 91.0 jit_solution(7120403721609407218)
XLA Ops:
  0.7 2.4 %forward.1 = (f32[8,8,8,128]{3,2,1,0:T(8,128)S(1)}, f32[8,8,128]{2,1,0:T(8,128)S(1)}, f32[8,8,128]{2,1,0:T(8,128)S(1)}, f32[4,512,128]{2,1,0:T(8,128)S(1)}, bf16...) custom-call(bf16[512,128]{1,0:T(8,128)(2,1)} %bitcast.20, ...), custom_call_target="tpu_custom_call" | custom-call | tf_op jit(solution)/shard_map/forward/pallas_call | solution.py:395
  3.1 3.3 %collective-permute-start = (f32[8,8,128]{2,1,0:T(8,128)S(1)}, f32[8,8,128]{2,1,0:T(8,128)S(1)}, u32[]{:S(2)}, u32[]{:S(2)}) collective-permute-start(f32[8,8,128]{2,1,0:T(8,128)S(1)} %get-tuple-element.62), channel_id=1, source_target_pairs={{0,4},{1,5},{2,6},{3,7},{4,0},{5,1},{6,2},{7,3},{8,12},{9,13},{10,... | collective-permute-start | bytes 98312 | tf_op jit(solution)/shard_map/ppermute | solution.py:329
  6.4 1.9 %collective-permute-start.1 = (f32[8,8,128]{2,1,0:T(8,128)S(1)}, f32[8,8,128]{2,1,0:T(8,128)S(1)}, u32[]{:S(2)}, u32[]{:S(2)}) collective-permute-start(f32[8,8,128]{2,1,0:T(8,128)S(1)} %get-tuple-element.63), channel_id=1, source_target_pairs={{0,16},{1,17},{2,18},{3,19},{4,20},{5,21},{6,22},{7,23},{8,24},{9,... | collective-permute-start | bytes 98312 | tf_op jit(solution)/shard_map/ppermute | solution.py:329
  8.3 0.0 collective-permute-done.x0
  8.3 2.3 %collective-permute-done.1.x1 = f32[8,8,128]{2,1,0:T(8,128)S(1)} collective-permute-done((f32[8,8,128]{2,1,0:T(8,128)S(1)}, f32[8,8,128]{2,1,0:T(8,128)S(1)}, u32[]{:S(2)}, u32[]{:S(2)}) %collective-permute-start.1) | collective-permute-done | bytes 32800 | tf_op jit(solution)/shard_map/ppermute | solution.py:329
  10.7 2.1 %collective-permute-start.2 = (f32[8,8,128]{2,1,0:T(8,128)S(1)}, f32[8,8,128]{2,1,0:T(8,128)S(1)}, u32[]{:S(2)}, u32[]{:S(2)}) collective-permute-start(f32[8,8,128]{2,1,0:T(8,128)S(1)} %get-tuple-element.64), channel_id=1, source_target_pairs={{0,1},{1,0},{2,3},{3,2},{4,8},{5,9},{6,10},{7,11},{8,4},{9,5},{10,... | collective-permute-start | bytes 98312 | tf_op jit(solution)/shard_map/ppermute | solution.py:329
  12.7 0.3 collective-permute-start.3
  13.0 1.3 %collective-permute-done.2.y0 = f32[8,8,128]{2,1,0:T(8,128)S(1)} collective-permute-done((f32[8,8,128]{2,1,0:T(8,128)S(1)}, f32[8,8,128]{2,1,0:T(8,128)S(1)}, u32[]{:S(2)}, u32[]{:S(2)}) %collective-permute-start.2) | collective-permute-done | bytes 32800 | tf_op jit(solution)/shard_map/ppermute | solution.py:329
  14.3 0.0 collective-permute-done.3.y1
  14.3 0.1 after_y_1.1
  14.4 0.0 copy-start.3
  14.4 1.7 %collective-permute-start.4 = (f32[8,8,128]{2,1,0:T(8,128)S(1)}, f32[8,8,128]{2,1,0:T(8,128)S(1)}, u32[]{:S(2)}, u32[]{:S(2)}) collective-permute-start(f32[8,8,128]{2,1,0:T(8,128)S(1)} %get-tuple-element.66), channel_id=1, source_target_pairs={{0,4},{1,2},{2,1},{3,7},{4,0},{5,6},{6,5},{7,3},{8,12},{9,10},{10,... | collective-permute-start | bytes 98312 | tf_op jit(solution)/shard_map/ppermute | solution.py:329
  16.1 0.8 collective-permute-start.5
  17.0 0.1 div.16
  17.1 0.2 prepare_node.1
  17.3 0.0 collective-permute-done.4.z0
  17.3 1.6 %collective-permute-done.5.z1 = f32[8,8,128]{2,1,0:T(8,128)S(1)} collective-permute-done((f32[8,8,128]{2,1,0:T(8,128)S(1)}, f32[8,8,128]{2,1,0:T(8,128)S(1)}, u32[]{:S(2)}, u32[]{:S(2)}) %collective-permute-start.5) | collective-permute-done | bytes 32800 | tf_op jit(solution)/shard_map/ppermute | solution.py:329
  18.9 0.1 broadcast_in_dim.2.inverse
  19.0 0.4 node.1
  19.4 1.7 %collective-permute-start.6 = (f32[8,8,128]{2,1,0:T(8,128)S(1)}, f32[8,8,128]{2,1,0:T(8,128)S(1)}, u32[]{:S(2)}, u32[]{:S(2)}) collective-permute-start(f32[8,8,128]{2,1,0:T(8,128)S(1)} %get-tuple-element.73), channel_id=1, source_target_pairs={{0,4},{1,5},{2,6},{3,7},{4,0},{5,1},{6,2},{7,3},{8,12},{9,13},{10,... | collective-permute-start | bytes 98312 | tf_op jit(solution)/shard_map/ppermute | solution.py:329
  21.2 3.6 %collective-permute-start.7 = (f32[8,8,128]{2,1,0:T(8,128)S(1)}, f32[8,8,128]{2,1,0:T(8,128)S(1)}, u32[]{:S(2)}, u32[]{:S(2)}) collective-permute-start(f32[8,8,128]{2,1,0:T(8,128)S(1)} %get-tuple-element.74), channel_id=1, source_target_pairs={{0,16},{1,17},{2,18},{3,19},{4,20},{5,21},{6,22},{7,23},{8,24},{9,... | collective-permute-start | bytes 98312 | tf_op jit(solution)/shard_map/ppermute | solution.py:329
  24.8 0.0 collective-permute-done.6.x0
  24.8 1.3 %collective-permute-done.7.x1 = f32[8,8,128]{2,1,0:T(8,128)S(1)} collective-permute-done((f32[8,8,128]{2,1,0:T(8,128)S(1)}, f32[8,8,128]{2,1,0:T(8,128)S(1)}, u32[]{:S(2)}, u32[]{:S(2)}) %collective-permute-start.7) | collective-permute-done | bytes 32800 | tf_op jit(solution)/shard_map/ppermute | solution.py:329
  26.1 3.1 %collective-permute-start.8 = (f32[8,8,128]{2,1,0:T(8,128)S(1)}, f32[8,8,128]{2,1,0:T(8,128)S(1)}, u32[]{:S(2)}, u32[]{:S(2)}) collective-permute-start(f32[8,8,128]{2,1,0:T(8,128)S(1)} %get-tuple-element.75), channel_id=1, source_target_pairs={{0,1},{1,0},{2,3},{3,2},{4,8},{5,9},{6,10},{7,11},{8,4},{9,5},{10,... | collective-permute-start | bytes 98312 | tf_op jit(solution)/shard_map/ppermute | solution.py:329
  29.1 2.3 %collective-permute-start.9 = (f32[8,8,128]{2,1,0:T(8,128)S(1)}, f32[8,8,128]{2,1,0:T(8,128)S(1)}, u32[]{:S(2)}, u32[]{:S(2)}) collective-permute-start(f32[8,8,128]{2,1,0:T(8,128)S(1)} %get-tuple-element.76), channel_id=1, source_target_pairs={{0,4},{1,5},{2,6},{3,7},{4,0},{5,1},{6,2},{7,3},{8,12},{9,13},{10,... | collective-permute-start | bytes 98312 | tf_op jit(solution)/shard_map/ppermute | solution.py:329
  31.5 0.0 collective-permute-done.8.y0
  31.5 0.9 collective-permute-done.9.y1
  32.3 0.1 after_y_2.1
  32.4 1.1 %collective-permute-start.10 = (f32[8,8,128]{2,1,0:T(8,128)S(1)}, f32[8,8,128]{2,1,0:T(8,128)S(1)}, u32[]{:S(2)}, u32[]{:S(2)}) collective-permute-start(f32[8,8,128]{2,1,0:T(8,128)S(1)} %get-tuple-element.77), channel_id=1, source_target_pairs={{0,4},{1,2},{2,1},{3,7},{4,0},{5,6},{6,5},{7,3},{8,12},{9,10},{10,... | collective-permute-start | bytes 98312 | tf_op jit(solution)/shard_map/ppermute | solution.py:329
  33.5 0.0 collective-permute-start.11
  33.5 1.5 %prepare_edge.1 = (f32[4,512,128]{2,1,0:T(8,128)S(1)}, bf16[512,512]{1,0:T(8,128)(2,1)S(1)}, bf16[384,2048]{1,0:T(8,128)(2,1)S(1)}, bf16[128,128]{1,0:T(8,128)(2,1)S(1)}, bf16[256,128]{1,0:T(8,128)(2,1)S(1)}) custom-call(s32[4,3]{1,0:T(4,128)S(1)} %copy-done.3, f32[4,512,128]{2,1,0:T(8,128)S(1)} %get-tuple-element.79.preact, ...), custom_call_target="tpu_custom_call" | custom-call | tf_op jit(solution)/shard_map/prepare_edge/pallas_call | solution.py:406
  35.0 0.3 node_grads.1
  35.4 0.0 collective-permute-done.10.z0
  35.4 0.9 %collective-permute-done.11.z1 = f32[8,8,128]{2,1,0:T(8,128)S(1)} collective-permute-done((f32[8,8,128]{2,1,0:T(8,128)S(1)}, f32[8,8,128]{2,1,0:T(8,128)S(1)}, u32[]{:S(2)}, u32[]{:S(2)}) %collective-permute-start.11) | collective-permute-done | bytes 32800 | tf_op jit(solution)/shard_map/ppermute | solution.py:329
  36.3 0.9 edge.1
  37.2 1.8 %collective-permute-start.14 = (f32[448,128]{1,0:T(8,128)S(1)}, f32[448,128]{1,0:T(8,128)S(1)}, u32[]{:S(2)}, u32[]{:S(2)}) collective-permute-start(f32[448,128]{1,0:T(8,128)S(1)} %get-tuple-element.99), channel_id=1, source_target_pairs={{0,4},{1,5},{2,6},{3,7},{4,0},{5,1},{6,2},{7,3},{8,12},{9,13},{10,... | collective-permute-start | bytes 688136 | tf_op jit(solution)/shard_map/ppermute | solution.py:338
  39.0 1.2 %node_part.1 = (f32[8,8,8,128]{3,2,1,0:T(8,128)S(1)}, f32[8,8,128]{2,1,0:T(8,128)S(1)}, f32[8,8,128]{2,1,0:T(8,128)S(1)}) custom-call(s32[4,3]{1,0:T(4,128)S(1)} %copy-done.3, f32[9,8,128]{2,1,0:T(8,128)S(1)} %get-tuple-element.60.rim.refs_0_, bf16[2048,128]{1,0:T(8,128)(2,1)S(1)} %get-tuple-element.92.slopes, f32[512,128]{1,0:T(8,128)S(1)} %get-tuple-element.93.base, ...), custom_call_target="tpu_custom_call" | custom-call | tf_op jit(solution)/shard_map/node_part/pallas_call | solution.py:428
  40.1 0.0 collective-permute-done.14.got
  40.1 0.7 add_core.1
  40.9 7.6 %all-to-all-start = ((f32[16,1,3584]{2,1,0:T(1,128)}), f32[16,1,3584]{2,1,0:T(1,128)S(1)}, u32[]{:S(2)}, u32[]{:S(2)}) async-start(f32[16,1,3584]{2,1,0:T(1,128)} %bitcast.3), calls=%async_computation | async-start | bytes 458752 | tf_op jit(solution)/shard_map/all_to_all | solution.py:358
  48.5 0.9 collective-permute-start.12
  49.4 1.7 %collective-permute-start.13 = (f32[8,8,128]{2,1,0:T(8,128)S(1)}, f32[8,8,128]{2,1,0:T(8,128)S(1)}, u32[]{:S(2)}, u32[]{:S(2)}) collective-permute-start(f32[8,8,128]{2,1,0:T(8,128)S(1)} %get-tuple-element.97), channel_id=1, source_target_pairs={{0,1},{1,0},{2,3},{3,2},{4,5},{5,4},{6,7},{7,6},{8,9},{9,8},{10,11... | collective-permute-start | bytes 98312 | tf_op jit(solution)/shard_map/ppermute | solution.py:329
  51.0 0.0 collective-permute-done.12.refs_2_.z0
  51.0 2.4 %collective-permute-done.13.refs_3_.z1 = f32[8,8,128]{2,1,0:T(8,128)S(1)} collective-permute-done((f32[8,8,128]{2,1,0:T(8,128)S(1)}, f32[8,8,128]{2,1,0:T(8,128)S(1)}, u32[]{:S(2)}, u32[]{:S(2)}) %collective-permute-start.13) | collective-permute-done | bytes 32800 | tf_op jit(solution)/shard_map/ppermute | solution.py:329
  53.4 2.9 %all-to-all-done = f32[16,1,3584]{2,1,0:T(1,128)S(1)} async-done(((f32[16,1,3584]{2,1,0:T(1,128)}), f32[16,1,3584]{2,1,0:T(1,128)S(1)}, u32[]{:S(2)}, u32[]{:S(2)}) %all-to-all-start) | async-done | bytes 229408 | tf_op jit(solution)/shard_map/all_to_all | solution.py:358
  56.3 0.7 after_z_fold.1
  57.0 8.2 %all-to-all-start.1 = ((f32[8,1,3584]{2,1,0:T(1,128)}), f32[8,1,3584]{2,1,0:T(1,128)S(1)}, u32[]{:S(2)}, u32[]{:S(2)}) async-start(f32[8,1,3584]{2,1,0:T(1,128)} %bitcast.5), calls=%async_computation.1 | async-start | bytes 229376 | tf_op jit(solution)/shard_map/all_to_all | solution.py:358
  65.2 1.4 %collective-permute-start.15 = (f32[8,8,128]{2,1,0:T(8,128)S(1)}, f32[8,8,128]{2,1,0:T(8,128)S(1)}, u32[]{:S(2)}, u32[]{:S(2)}) collective-permute-start(f32[8,8,128]{2,1,0:T(8,128)S(1)} %get-tuple-element.100), channel_id=1, source_target_pairs={{0,1},{1,0},{2,3},{3,2},{4,8},{5,9},{6,10},{7,11},{8,4},{9,5},{10,... | collective-permute-start | bytes 98312 | tf_op jit(solution)/shard_map/ppermute | solution.py:329
  66.5 1.3 %collective-permute-start.16 = (f32[8,8,128]{2,1,0:T(8,128)S(1)}, f32[8,8,128]{2,1,0:T(8,128)S(1)}, u32[]{:S(2)}, u32[]{:S(2)}) collective-permute-start(f32[8,8,128]{2,1,0:T(8,128)S(1)} %get-tuple-element.101), channel_id=1, source_target_pairs={{0,4},{1,5},{2,6},{3,7},{4,0},{5,1},{6,2},{7,3},{8,12},{9,13},{10,... | collective-permute-start | bytes 98312 | tf_op jit(solution)/shard_map/ppermute | solution.py:329
  67.8 0.7 collective-permute-done.15.refs_4_.y0
  68.5 0.2 collective-permute-done.16.refs_5_.y1
  68.7 4.3 %all-to-all-done.1 = f32[8,1,3584]{2,1,0:T(1,128)S(1)} async-done(((f32[8,1,3584]{2,1,0:T(1,128)}), f32[8,1,3584]{2,1,0:T(1,128)S(1)}, u32[]{:S(2)}, u32[]{:S(2)}) %all-to-all-start.1) | async-done | bytes 114720 | tf_op jit(solution)/shard_map/all_to_all | solution.py:358
  73.0 0.7 after_y_fold.1
  73.7 3.5 %all-to-all-start.2 = ((f32[16,1,3584]{2,1,0:T(1,128)}), f32[16,1,3584]{2,1,0:T(1,128)S(1)}, u32[]{:S(2)}, u32[]{:S(2)}) async-start(f32[16,1,3584]{2,1,0:T(1,128)} %bitcast.7), calls=%async_computation.2 | async-start | bytes 458752 | tf_op jit(solution)/shard_map/all_to_all | solution.py:358
  77.3 3.2 %collective-permute-start.17 = (f32[8,8,128]{2,1,0:T(8,128)S(1)}, f32[8,8,128]{2,1,0:T(8,128)S(1)}, u32[]{:S(2)}, u32[]{:S(2)}) collective-permute-start(f32[8,8,128]{2,1,0:T(8,128)S(1)} %get-tuple-element.104), channel_id=1, source_target_pairs={{0,4},{1,5},{2,6},{3,7},{4,0},{5,1},{6,2},{7,3},{8,12},{9,13},{10,... | collective-permute-start | bytes 98312 | tf_op jit(solution)/shard_map/ppermute | solution.py:329
  80.5 0.0 collective-permute-start.18
  80.5 1.1 %edge_grad.1 = bf16[2048,128]{1,0:T(8,128)(2,1)} custom-call(bf16[2048,128]{1,0:T(8,128)(2,1)S(1)} %get-tuple-element.92.slopes, bf16[384,128]{1,0:T(8,128)(2,1)S(1)} %get-tuple-element.82.w_in), custom_call_target="tpu_custom_call" | custom-call | tf_op jit(solution)/shard_map/edge_grad/pallas_call | solution.py:431
  81.6 0.0 collective-permute-done.17.x0
  81.6 3.4 %collective-permute-done.18.x1 = f32[8,8,128]{2,1,0:T(8,128)S(1)} collective-permute-done((f32[8,8,128]{2,1,0:T(8,128)S(1)}, f32[8,8,128]{2,1,0:T(8,128)S(1)}, u32[]{:S(2)}, u32[]{:S(2)}) %collective-permute-start.18) | collective-permute-done | bytes 32800 | tf_op jit(solution)/shard_map/ppermute | solution.py:329
  85.0 0.0 all-to-all-done.2
  85.0 3.9 %collective-permute-start.19 = (f32[448,128]{1,0:T(8,128)S(1)}, f32[448,128]{1,0:T(8,128)S(1)}, u32[]{:S(2)}, u32[]{:S(2)}) collective-permute-start(f32[448,128]{1,0:T(8,128)S(1)} %bitcast.12), channel_id=1, source_target_pairs={{0,4},{1,5},{2,6},{3,7},{4,0},{5,1},{6,2},{7,3},{8,12},{9,13},{10,... | collective-permute-start | bytes 688136 | tf_op jit(solution)/shard_map/ppermute | solution.py:338
  88.9 0.8 last.1
  89.7 0.3 collective-permute-done.19.other
  90.0 1.0 %clip.1 = (f32[384,128]{1,0:T(8,128)}, f32[128,128]{1,0:T(8,128)}, f32[256,128]{1,0:T(8,128)}, f32[128,128]{1,0:T(8,128)}) custom-call(f32[9,8,128]{2,1,0:T(8,128)S(1)} %get-tuple-element.60.rim.refs_0_, f32[448,128]{1,0:T(8,128)S(1)} %bitcast.13, f32[448,128]{1,0:T(8,128)S(1)} %collective-permute-done.19.other), custom_call_target="tpu_custom_call" | custom-call | tf_op jit(solution)/shard_map/clip/pallas_call | solution.py:433
  (12 shorter events, 0.0 us)
Async XLA Ops:
  0.6 16.3 %copy-start.4 = (s32[8,8,8]{2,1,0:T(8,128)S(1)}, s32[8,8,8]{2,1,0:T(8,128)}, u32[]{:S(2)}) copy-start(s32[8,8,8]{2,1,0:T(8,128)} %param.11) | copy-start | bytes 6148
  0.6 16.4 %copy-start.1 = (bf16[8,8,8,128]{3,2,1,0:T(8,128)(2,1)S(1)}, bf16[8,8,8,128]{3,2,1,0:T(8,128)(2,1)}, u32[]{:S(2)}) copy-start(bf16[8,8,8,128]{3,2,1,0:T(8,128)(2,1)} %param.17) | copy-start | bytes 393220
  0.7 16.4 %copy-start = (bf16[256,128]{1,0:T(8,128)(2,1)S(1)}, bf16[256,128]{1,0:T(8,128)(2,1)}, u32[]{:S(2)}) copy-start(bf16[256,128]{1,0:T(8,128)(2,1)} %w_in.5) | copy-start | bytes 196612
  0.7 16.4 %copy-start.2 = (bf16[128,128]{1,0:T(8,128)(2,1)S(1)}, bf16[128,128]{1,0:T(8,128)(2,1)}, u32[]{:S(2)}) copy-start(bf16[128,128]{1,0:T(8,128)(2,1)} %w_out.1) | copy-start | bytes 98308
  3.1 5.2 %collective-permute-start = (f32[8,8,128]{2,1,0:T(8,128)S(1)}, f32[8,8,128]{2,1,0:T(8,128)S(1)}, u32[]{:S(2)}, u32[]{:S(2)}) collective-permute-start(f32[8,8,128]{2,1,0:T(8,128)S(1)} %get-tuple-element.62), channel_id=1, source_target_pairs={{0,4},{1,5},{2,6},{3,7},{4,0},{5,1},{6,2},{7,3},{8,12},{9,13},{10,... | collective-permute-start | bytes 98312 | tf_op jit(solution)/shard_map/ppermute | solution.py:329
  6.4 4.3 %collective-permute-start.1 = (f32[8,8,128]{2,1,0:T(8,128)S(1)}, f32[8,8,128]{2,1,0:T(8,128)S(1)}, u32[]{:S(2)}, u32[]{:S(2)}) collective-permute-start(f32[8,8,128]{2,1,0:T(8,128)S(1)} %get-tuple-element.63), channel_id=1, source_target_pairs={{0,16},{1,17},{2,18},{3,19},{4,20},{5,21},{6,22},{7,23},{8,24},{9,... | collective-permute-start | bytes 98312 | tf_op jit(solution)/shard_map/ppermute | solution.py:329
  10.7 3.7 %collective-permute-start.2 = (f32[8,8,128]{2,1,0:T(8,128)S(1)}, f32[8,8,128]{2,1,0:T(8,128)S(1)}, u32[]{:S(2)}, u32[]{:S(2)}) collective-permute-start(f32[8,8,128]{2,1,0:T(8,128)S(1)} %get-tuple-element.64), channel_id=1, source_target_pairs={{0,1},{1,0},{2,3},{3,2},{4,8},{5,9},{6,10},{7,11},{8,4},{9,5},{10,... | collective-permute-start | bytes 98312 | tf_op jit(solution)/shard_map/ppermute | solution.py:329
  12.7 1.6 %collective-permute-start.3 = (f32[8,8,128]{2,1,0:T(8,128)S(1)}, f32[8,8,128]{2,1,0:T(8,128)S(1)}, u32[]{:S(2)}, u32[]{:S(2)}) collective-permute-start(f32[8,8,128]{2,1,0:T(8,128)S(1)} %get-tuple-element.65), channel_id=1, source_target_pairs={{0,4},{1,5},{2,6},{3,7},{4,0},{5,1},{6,2},{7,3},{8,12},{9,13},{10,... | collective-permute-start | bytes 98312 | tf_op jit(solution)/shard_map/ppermute | solution.py:329
  14.4 19.1 %copy-start.3 = (s32[4,3]{1,0:T(4,128)S(1)}, s32[4,3]{1,0:T(4,128)}, u32[]{:S(2)}) copy-start(s32[4,3]{1,0:T(4,128)} %offs.3) | copy-start | bytes 148
  14.4 2.9 %collective-permute-start.4 = (f32[8,8,128]{2,1,0:T(8,128)S(1)}, f32[8,8,128]{2,1,0:T(8,128)S(1)}, u32[]{:S(2)}, u32[]{:S(2)}) collective-permute-start(f32[8,8,128]{2,1,0:T(8,128)S(1)} %get-tuple-element.66), channel_id=1, source_target_pairs={{0,4},{1,2},{2,1},{3,7},{4,0},{5,6},{6,5},{7,3},{8,12},{9,10},{10,... | collective-permute-start | bytes 98312 | tf_op jit(solution)/shard_map/ppermute | solution.py:329
  16.1 2.8 %collective-permute-start.5 = (f32[8,8,128]{2,1,0:T(8,128)S(1)}, f32[8,8,128]{2,1,0:T(8,128)S(1)}, u32[]{:S(2)}, u32[]{:S(2)}) collective-permute-start(f32[8,8,128]{2,1,0:T(8,128)S(1)} %get-tuple-element.67), channel_id=1, source_target_pairs={{0,1},{1,0},{2,3},{3,2},{4,5},{5,4},{6,7},{7,6},{8,9},{9,8},{10,11... | collective-permute-start | bytes 98312 | tf_op jit(solution)/shard_map/ppermute | solution.py:329
  19.4 5.3 %collective-permute-start.6 = (f32[8,8,128]{2,1,0:T(8,128)S(1)}, f32[8,8,128]{2,1,0:T(8,128)S(1)}, u32[]{:S(2)}, u32[]{:S(2)}) collective-permute-start(f32[8,8,128]{2,1,0:T(8,128)S(1)} %get-tuple-element.73), channel_id=1, source_target_pairs={{0,4},{1,5},{2,6},{3,7},{4,0},{5,1},{6,2},{7,3},{8,12},{9,13},{10,... | collective-permute-start | bytes 98312 | tf_op jit(solution)/shard_map/ppermute | solution.py:329
  21.2 4.9 %collective-permute-start.7 = (f32[8,8,128]{2,1,0:T(8,128)S(1)}, f32[8,8,128]{2,1,0:T(8,128)S(1)}, u32[]{:S(2)}, u32[]{:S(2)}) collective-permute-start(f32[8,8,128]{2,1,0:T(8,128)S(1)} %get-tuple-element.74), channel_id=1, source_target_pairs={{0,16},{1,17},{2,18},{3,19},{4,20},{5,21},{6,22},{7,23},{8,24},{9,... | collective-permute-start | bytes 98312 | tf_op jit(solution)/shard_map/ppermute | solution.py:329
  26.1 5.4 %collective-permute-start.8 = (f32[8,8,128]{2,1,0:T(8,128)S(1)}, f32[8,8,128]{2,1,0:T(8,128)S(1)}, u32[]{:S(2)}, u32[]{:S(2)}) collective-permute-start(f32[8,8,128]{2,1,0:T(8,128)S(1)} %get-tuple-element.75), channel_id=1, source_target_pairs={{0,1},{1,0},{2,3},{3,2},{4,8},{5,9},{6,10},{7,11},{8,4},{9,5},{10,... | collective-permute-start | bytes 98312 | tf_op jit(solution)/shard_map/ppermute | solution.py:329
  29.1 3.2 %collective-permute-start.9 = (f32[8,8,128]{2,1,0:T(8,128)S(1)}, f32[8,8,128]{2,1,0:T(8,128)S(1)}, u32[]{:S(2)}, u32[]{:S(2)}) collective-permute-start(f32[8,8,128]{2,1,0:T(8,128)S(1)} %get-tuple-element.76), channel_id=1, source_target_pairs={{0,4},{1,5},{2,6},{3,7},{4,0},{5,1},{6,2},{7,3},{8,12},{9,13},{10,... | collective-permute-start | bytes 98312 | tf_op jit(solution)/shard_map/ppermute | solution.py:329
  32.4 2.9 %collective-permute-start.10 = (f32[8,8,128]{2,1,0:T(8,128)S(1)}, f32[8,8,128]{2,1,0:T(8,128)S(1)}, u32[]{:S(2)}, u32[]{:S(2)}) collective-permute-start(f32[8,8,128]{2,1,0:T(8,128)S(1)} %get-tuple-element.77), channel_id=1, source_target_pairs={{0,4},{1,2},{2,1},{3,7},{4,0},{5,6},{6,5},{7,3},{8,12},{9,10},{10,... | collective-permute-start | bytes 98312 | tf_op jit(solution)/shard_map/ppermute | solution.py:329
  33.5 2.8 %collective-permute-start.11 = (f32[8,8,128]{2,1,0:T(8,128)S(1)}, f32[8,8,128]{2,1,0:T(8,128)S(1)}, u32[]{:S(2)}, u32[]{:S(2)}) collective-permute-start(f32[8,8,128]{2,1,0:T(8,128)S(1)} %get-tuple-element.78), channel_id=1, source_target_pairs={{0,1},{1,0},{2,3},{3,2},{4,5},{5,4},{6,7},{7,6},{8,9},{9,8},{10,11... | collective-permute-start | bytes 98312 | tf_op jit(solution)/shard_map/ppermute | solution.py:329
  37.2 2.9 %collective-permute-start.14 = (f32[448,128]{1,0:T(8,128)S(1)}, f32[448,128]{1,0:T(8,128)S(1)}, u32[]{:S(2)}, u32[]{:S(2)}) collective-permute-start(f32[448,128]{1,0:T(8,128)S(1)} %get-tuple-element.99), channel_id=1, source_target_pairs={{0,4},{1,5},{2,6},{3,7},{4,0},{5,1},{6,2},{7,3},{8,12},{9,13},{10,... | collective-permute-start | bytes 688136 | tf_op jit(solution)/shard_map/ppermute | solution.py:338
  40.9 15.5 %all-to-all-start = ((f32[16,1,3584]{2,1,0:T(1,128)}), f32[16,1,3584]{2,1,0:T(1,128)S(1)}, u32[]{:S(2)}, u32[]{:S(2)}) async-start(f32[16,1,3584]{2,1,0:T(1,128)} %bitcast.3), calls=%async_computation | async-start | bytes 458752 | tf_op jit(solution)/shard_map/all_to_all | solution.py:358
  48.5 2.6 %collective-permute-start.12 = (f32[8,8,128]{2,1,0:T(8,128)S(1)}, f32[8,8,128]{2,1,0:T(8,128)S(1)}, u32[]{:S(2)}, u32[]{:S(2)}) collective-permute-start(f32[8,8,128]{2,1,0:T(8,128)S(1)} %get-tuple-element.96.after), channel_id=1, source_target_pairs={{0,4},{1,2},{2,1},{3,7},{4,0},{5,6},{6,5},{7,3},{8,12},{9,10},{10,... | collective-permute-start | bytes 98312 | tf_op jit(solution)/shard_map/ppermute | solution.py:329
  49.4 4.0 %collective-permute-start.13 = (f32[8,8,128]{2,1,0:T(8,128)S(1)}, f32[8,8,128]{2,1,0:T(8,128)S(1)}, u32[]{:S(2)}, u32[]{:S(2)}) collective-permute-start(f32[8,8,128]{2,1,0:T(8,128)S(1)} %get-tuple-element.97), channel_id=1, source_target_pairs={{0,1},{1,0},{2,3},{3,2},{4,5},{5,4},{6,7},{7,6},{8,9},{9,8},{10,11... | collective-permute-start | bytes 98312 | tf_op jit(solution)/shard_map/ppermute | solution.py:329
  57.0 16.0 %all-to-all-start.1 = ((f32[8,1,3584]{2,1,0:T(1,128)}), f32[8,1,3584]{2,1,0:T(1,128)S(1)}, u32[]{:S(2)}, u32[]{:S(2)}) async-start(f32[8,1,3584]{2,1,0:T(1,128)} %bitcast.5), calls=%async_computation.1 | async-start | bytes 229376 | tf_op jit(solution)/shard_map/all_to_all | solution.py:358
  65.2 3.3 %collective-permute-start.15 = (f32[8,8,128]{2,1,0:T(8,128)S(1)}, f32[8,8,128]{2,1,0:T(8,128)S(1)}, u32[]{:S(2)}, u32[]{:S(2)}) collective-permute-start(f32[8,8,128]{2,1,0:T(8,128)S(1)} %get-tuple-element.100), channel_id=1, source_target_pairs={{0,1},{1,0},{2,3},{3,2},{4,8},{5,9},{6,10},{7,11},{8,4},{9,5},{10,... | collective-permute-start | bytes 98312 | tf_op jit(solution)/shard_map/ppermute | solution.py:329
  66.5 2.2 %collective-permute-start.16 = (f32[8,8,128]{2,1,0:T(8,128)S(1)}, f32[8,8,128]{2,1,0:T(8,128)S(1)}, u32[]{:S(2)}, u32[]{:S(2)}) collective-permute-start(f32[8,8,128]{2,1,0:T(8,128)S(1)} %get-tuple-element.101), channel_id=1, source_target_pairs={{0,4},{1,5},{2,6},{3,7},{4,0},{5,1},{6,2},{7,3},{8,12},{9,13},{10,... | collective-permute-start | bytes 98312 | tf_op jit(solution)/shard_map/ppermute | solution.py:329
  73.7 11.2 %all-to-all-start.2 = ((f32[16,1,3584]{2,1,0:T(1,128)}), f32[16,1,3584]{2,1,0:T(1,128)S(1)}, u32[]{:S(2)}, u32[]{:S(2)}) async-start(f32[16,1,3584]{2,1,0:T(1,128)} %bitcast.7), calls=%async_computation.2 | async-start | bytes 458752 | tf_op jit(solution)/shard_map/all_to_all | solution.py:358
  77.3 4.3 %collective-permute-start.17 = (f32[8,8,128]{2,1,0:T(8,128)S(1)}, f32[8,8,128]{2,1,0:T(8,128)S(1)}, u32[]{:S(2)}, u32[]{:S(2)}) collective-permute-start(f32[8,8,128]{2,1,0:T(8,128)S(1)} %get-tuple-element.104), channel_id=1, source_target_pairs={{0,4},{1,5},{2,6},{3,7},{4,0},{5,1},{6,2},{7,3},{8,12},{9,13},{10,... | collective-permute-start | bytes 98312 | tf_op jit(solution)/shard_map/ppermute | solution.py:329
  80.5 4.5 %collective-permute-start.18 = (f32[8,8,128]{2,1,0:T(8,128)S(1)}, f32[8,8,128]{2,1,0:T(8,128)S(1)}, u32[]{:S(2)}, u32[]{:S(2)}) collective-permute-start(f32[8,8,128]{2,1,0:T(8,128)S(1)} %get-tuple-element.105), channel_id=1, source_target_pairs={{0,16},{1,17},{2,18},{3,19},{4,20},{5,21},{6,22},{7,23},{8,24},{9,... | collective-permute-start | bytes 98312 | tf_op jit(solution)/shard_map/ppermute | solution.py:329
  85.0 5.0 %collective-permute-start.19 = (f32[448,128]{1,0:T(8,128)S(1)}, f32[448,128]{1,0:T(8,128)S(1)}, u32[]{:S(2)}, u32[]{:S(2)}) collective-permute-start(f32[448,128]{1,0:T(8,128)S(1)} %bitcast.12), channel_id=1, source_target_pairs={{0,4},{1,5},{2,6},{3,7},{4,0},{5,1},{6,2},{7,3},{8,12},{9,13},{10,... | collective-permute-start | bytes 688136 | tf_op jit(solution)/shard_map/ppermute | solution.py:338

commit v7 on v6

--- a/solution.py
+++ b/solution.py
@@ -48,6 +48,10 @@
 
 def dot(a, b):
     return jnp.dot(a, b, preferred_element_type=F32)
+
+
+def sigmoid(v):
+    return 0.5 + 0.5 * jnp.tanh(0.5 * v)
 
 
 def dot_t(a, b):
@@ -111,7 +115,7 @@
         copies[4 + k].wait()
         pre = ring_shift(pad, offs[k, 0], offs[k, 1], offs[k, 2]) + receiver + dot(edges[k], w_in[2 * W :])
         preact[k] = pre
-        act = (pre * jax.nn.sigmoid(pre)).reshape(CUBE)
+        act = (pre * sigmoid(pre)).reshape(CUBE)
         kept = jnp.where(inside(offs, k), act, 0.0).reshape(N, W).astype(BF16)
         hidden[k] = kept
         total = total + dot(kept, w_out[...])
@@ -132,7 +136,7 @@
     fill_ring(pad, node.astype(F32).reshape(CUBE))
     for k in range(K):
         pre = preact[k]
-        sigma = jax.nn.sigmoid(pre)
+        sigma = sigmoid(pre)
         rate = (sigma * (1.0 + pre * (1.0 - sigma))).reshape(CUBE)
         dact[k] = jnp.where(inside(offs, k), rate, 0.0).reshape(N, W)
         hidden_t[k * W : (k + 1) * W] = hidden[k].T
@@ -201,24 +205,6 @@
     send(rim, 2, faces[0], faces[1], a, b)
 
 
-def y_faces_after_z(rim, field, z0, z1, a, b, faces):
-    for i, at in enumerate((0, B - 1)):
-        faces[i] = field[:, at]
-        faces[i, :, 0, :] = faces[i, :, 0, :] + low(rim, 2, z0[:, at, :], z1[:, at, :])
-        faces[i, :, B - 1, :] = faces[i, :, B - 1, :] + high(rim, 2, z0[:, at, :], z1[:, at, :])
-    send(rim, 1, faces[0], faces[1], a, b)
-
-
-def x_faces_after_y(rim, field, z0, z1, y0, y1, a, b, faces):
-    for i, at in enumerate((0, B - 1)):
-        faces[i] = field[at]
-        faces[i, :, 0, :] = faces[i, :, 0, :] + low(rim, 2, z0[at], z1[at])
-        faces[i, :, B - 1, :] = faces[i, :, B - 1, :] + high(rim, 2, z0[at], z1[at])
-        faces[i, 0] = faces[i, 0] + low(rim, 1, y0[at], y1[at])
-        faces[i, B - 1] = faces[i, B - 1] + high(rim, 1, y0[at], y1[at])
-    send(rim, 0, faces[0], faces[1], a, b)
-
-
 def whole(rim, field, x0, x1, y0, y1, z0, z1, work):
     work[...] = field[...]
     add_x(rim, (x0, x1), work)
@@ -235,7 +221,7 @@
     agg = (whole(rim, field, x0, x1, y0, y1, z0, z1, work) * inv).astype(BF16)
     gathered[...] = agg
     pre = begun[...] + dot(agg, w_in[W:])
-    sigma = jax.nn.sigmoid(pre)
+    sigma = sigmoid(pre)
     hidden[...] = (pre * sigma).astype(BF16)
     slo = (upstream[...] * (sigma * (1.0 + pre * (1.0 - sigma)))).astype(BF16)
     slope[...] = slo
@@ -268,7 +254,7 @@
     give[...] = own(rim, grads[half:], grads[:half])
 
 
-def node_part_kernel(offs, rim, slopes, base, w_back, local, za, zb, pad):
+def node_part_kernel(offs, rim, slopes, base, w_back, local, xa, xb, pad):
     part = base[...]
     for k in range(K):
         slo = slopes[k * N : (k + 1) * N]
@@ -276,19 +262,15 @@
         sent = ring_shift(pad, -offs[k, 0], -offs[k, 1], -offs[k, 2]).astype(BF16)
         part = part + dot(jnp.concatenate([slo, sent], axis=1), w_back[...])
     local[...] = part.reshape(CUBE)
-    send(rim, 2, local[:, :, 0, :], local[:, :, B - 1, :], za, zb)
+    send(rim, 0, local[0], local[B - 1], xa, xb)
 
 
 def edge_grad_kernel(slopes, w_in, out):
     out[...] = dot_t(slopes[...], w_in[2 * W :]).astype(BF16)
 
 
-def last_kernel(rim, field, z0, z1, y0, y1, x0, x1, out, work):
-    work[...] = field[...]
-    add_z(rim, (z0, z1), work)
-    add_y(rim, (y0, y1), work)
-    add_x(rim, (x0, x1), work)
-    out[...] = work[...].reshape(N, W).astype(BF16)
+def last_kernel(rim, field, x0, x1, y0, y1, z0, z1, out, work):
+    out[...] = whole(rim, field, x0, x1, y0, y1, z0, z1, work).astype(BF16)
 
 
 def fold(rows, pairs, copies, arrived, out):
@@ -358,32 +340,32 @@
     return lax.all_to_all(rows.reshape(lax.axis_size(axes), -1), axes, 0, 0, tiled=True).reshape(-1, W)
 
 
-def arrivals_and_sum(rim, field, za, zb, keep, give, edge_grad):
+def arrivals_and_sum(rim, field, xa, xb, keep, give, edge_grad):
     near, far = lax.axis_size(NEAR), lax.axis_size(FAR)
     rows = keep.shape[0] // near
-    (half,) = call(add_kernel, [(keep.shape, F32)], [VMEM] * 3, "add_core")(keep, other_core(give), za)
+    (half,) = call(add_kernel, [(keep.shape, F32)], [VMEM] * 3, "add_core")(keep, other_core(give), xa)
     got = swap(half, NEAR)
-    z = exchange(za, zb, 2)
+    x = exchange(xa, xb, 0)
     a, b, spread = call(
-        functools.partial(fold_with_faces_kernel, y_faces_after_z, rows, near // 2, far // 2),
+        functools.partial(fold_with_faces_kernel, y_faces_after_x, rows, near // 2, far // 2),
         FACES + [((rows * far, W), F32)],
         [VMEM] * 5,
-        "after_z_fold",
+        "after_x_fold",
         [BOTH],
-    )(got, rim, field, *z)
+    )(got, rim, field, *x)
     got = swap(spread, FAR)
     y = exchange(a, b, 1)
     a, b, spread = call(
-        functools.partial(fold_with_faces_kernel, x_faces_after_y, rows, far // 2, near // 2),
+        functools.partial(fold_with_faces_kernel, z_faces_after_y, rows, far // 2, near // 2),
         FACES + [((rows * near, W), F32)],
         [VMEM] * 7,
         "after_y_fold",
         [BOTH],
-    )(got, rim, field, *z, *y)
+    )(got, rim, field, *x, *y)
     mine = swap(spread, NEAR)
-    x = exchange(a, b, 0)
-    mine, edge_grad, *x = lax.optimization_barrier((mine, edge_grad, *x))
-    return (*z, *y, *x), (mine, other_core(mine)), edge_grad
+    z = exchange(a, b, 2)
+    mine, edge_grad, *z = lax.optimization_barrier((mine, edge_grad, *z))
+    return (*x, *y, *z), (mine, other_core(mine)), edge_grad
 
 
 def on_device(node_feat, edge_feat, copies, offsets, w_edge_in, w_edge_out, w_node_in, w_node_out, node_cot):
@@ -425,11 +407,11 @@
         "edge",
         [WORK, pltpu.VMEM((7 * W, W), F32)],
     )(rim, local, *arrived, dact, hidden_t, left, w_out_t, node_grads)
-    local, za, zb = call(
+    local, xa, xb = call(
         node_part_kernel, [(CUBE, F32)] + FACES, [SMEM] + [VMEM] * 4, "node_part", [PAD]
     )(offsets, rim, slopes, base, w_back)
     (edge_grad,) = call(edge_grad_kernel, [((K * N, W), BF16)], [VMEM] * 2, "edge_grad")(slopes, w_in)
-    arrived, halves, edge_grad = arrivals_and_sum(rim, local, za, zb, keep, give, edge_grad)
+    arrived, halves, edge_grad = arrivals_and_sum(rim, local, xa, xb, keep, give, edge_grad)
     clipped = call(
         clip_kernel, [((3 * W, W), F32), ((W, W), F32), ((2 * W, W), F32), ((W, W), F32)], [VMEM] * 3, "clip"
     )(rim, *halves)

time: 91.5 us -> 93.7 us (1.024)
  starting transfers between devices: 55.4 us -> 61.3 us
  waiting for transfers between devices: 22.5 us -> 18.6 us
    ppermute x18, starting transfers between devices: 30.4 us -> 33.7 us  [exchange(): lax.ppermute(face, GX + GY + GZ, [(rank, ranks[to]) for rank, to in enume...]
    ppermute x18, waiting for transfers between devices: 14.9 us -> 12.6 us  [exchange(): lax.ppermute(face, GX + GY + GZ, [(rank, ranks[to]) for rank, to in enume...]
    all_to_all x3, waiting for transfers between devices: 7.25 us -> 5.71 us  [swap(): lax.all_to_all(rows.reshape(lax.axis_size(axes), -1), axes, 0, 0, tiled=T...]
    ppermute x2, starting transfers between devices: 5.69 us -> 7.2 us  [other_core(): lax.ppermute(half, GX + GY + GZ, [(rank, rank ^ step) for rank in range(c...]
    all_to_all x3, starting transfers between devices: 19.3 us -> 20.5 us  [swap(): lax.all_to_all(rows.reshape(lax.axis_size(axes), -1), axes, 0, 0, tiled=T...]
  transfers between devices with their start and end apart: 23 -> 23, of which waited for: 13 -> 14; matrix products, arithmetic and copies ran while one was open for 0% -> 0% of each run, Pallas kernels for 6% -> 5%
where the time goes in v7:
time: 93.7 us; the launch traced here: 93.3 us
  starting transfers between devices  61.3 us (65%)
  waiting for transfers between devices  18.6 us (20%)
  Pallas kernels  12.2 us (13%)
    ppermute x18, starting transfers between devices, exchange(): lax.ppermute(face, GX + GY + GZ, [(rank, ranks[to]) for rank, to in enume...  33.7 us
    all_to_all x3, starting transfers between devices, swap(): lax.all_to_all(rows.reshape(lax.axis_size(axes), -1), axes, 0, 0, tiled=T...  20.5 us
    ppermute x18, waiting for transfers between devices, exchange(): lax.ppermute(face, GX + GY + GZ, [(rank, ranks[to]) for rank, to in enume...  12.6 us
    ppermute x2, starting transfers between devices, other_core(): lax.ppermute(half, GX + GY + GZ, [(rank, rank ^ step) for rank in range(c...  7.2 us
    all_to_all x3, waiting for transfers between devices, swap(): lax.all_to_all(rows.reshape(lax.axis_size(axes), -1), axes, 0, 0, tiled=T...  5.71 us
    pallas_call x1, Pallas kernels, on_device(): call(forward_kernel, [(CUBE, F32)] + FACES + [((K, N, W), F32), many, ((N...  2.52 us
  transfers between devices with their start and end apart: 23, of which 14 were waited for; matrix products, arithmetic and copies ran while one was open for 0% of the time, Pallas kernels for 5%

profile of v7, /device:TPU:1, one launch (start us, length us, event | category | flops | bytes accessed | tf_op | source)
XLA Modules:
  0.0 93.3 jit_solution(12784362752346902139)
XLA Ops:
  0.7 2.5 %forward.1 = (f32[8,8,8,128]{3,2,1,0:T(8,128)S(1)}, f32[8,8,128]{2,1,0:T(8,128)S(1)}, f32[8,8,128]{2,1,0:T(8,128)S(1)}, f32[4,512,128]{2,1,0:T(8,128)S(1)}, bf16...) custom-call(bf16[512,128]{1,0:T(8,128)(2,1)} %bitcast.20, ...), custom_call_target="tpu_custom_call" | custom-call | tf_op jit(solution)/shard_map/forward/pallas_call | solution.py:377
  3.2 3.3 %collective-permute-start = (f32[8,8,128]{2,1,0:T(8,128)S(1)}, f32[8,8,128]{2,1,0:T(8,128)S(1)}, u32[]{:S(2)}, u32[]{:S(2)}) collective-permute-start(f32[8,8,128]{2,1,0:T(8,128)S(1)} %get-tuple-element.62), channel_id=1, source_target_pairs={{0,4},{1,5},{2,6},{3,7},{4,0},{5,1},{6,2},{7,3},{8,12},{9,13},{10,... | collective-permute-start | bytes 98312 | tf_op jit(solution)/shard_map/ppermute | solution.py:311
  6.5 1.9 %collective-permute-start.1 = (f32[8,8,128]{2,1,0:T(8,128)S(1)}, f32[8,8,128]{2,1,0:T(8,128)S(1)}, u32[]{:S(2)}, u32[]{:S(2)}) collective-permute-start(f32[8,8,128]{2,1,0:T(8,128)S(1)} %get-tuple-element.63), channel_id=1, source_target_pairs={{0,16},{1,17},{2,18},{3,19},{4,20},{5,21},{6,22},{7,23},{8,24},{9,... | collective-permute-start | bytes 98312 | tf_op jit(solution)/shard_map/ppermute | solution.py:311
  8.4 0.0 collective-permute-done.x0
  8.4 2.3 %collective-permute-done.1.x1 = f32[8,8,128]{2,1,0:T(8,128)S(1)} collective-permute-done((f32[8,8,128]{2,1,0:T(8,128)S(1)}, f32[8,8,128]{2,1,0:T(8,128)S(1)}, u32[]{:S(2)}, u32[]{:S(2)}) %collective-permute-start.1) | collective-permute-done | bytes 32800 | tf_op jit(solution)/shard_map/ppermute | solution.py:311
  10.8 2.1 %collective-permute-start.2 = (f32[8,8,128]{2,1,0:T(8,128)S(1)}, f32[8,8,128]{2,1,0:T(8,128)S(1)}, u32[]{:S(2)}, u32[]{:S(2)}) collective-permute-start(f32[8,8,128]{2,1,0:T(8,128)S(1)} %get-tuple-element.64), channel_id=1, source_target_pairs={{0,1},{1,0},{2,3},{3,2},{4,8},{5,9},{6,10},{7,11},{8,4},{9,5},{10,... | collective-permute-start | bytes 98312 | tf_op jit(solution)/shard_map/ppermute | solution.py:311
  12.8 0.3 collective-permute-start.3
  13.1 1.3 %collective-permute-done.2.y0 = f32[8,8,128]{2,1,0:T(8,128)S(1)} collective-permute-done((f32[8,8,128]{2,1,0:T(8,128)S(1)}, f32[8,8,128]{2,1,0:T(8,128)S(1)}, u32[]{:S(2)}, u32[]{:S(2)}) %collective-permute-start.2) | collective-permute-done | bytes 32800 | tf_op jit(solution)/shard_map/ppermute | solution.py:311
  14.4 0.0 collective-permute-done.3.y1
  14.4 0.1 after_y_1.1
  14.5 0.0 copy-start.3
  14.5 1.7 %collective-permute-start.4 = (f32[8,8,128]{2,1,0:T(8,128)S(1)}, f32[8,8,128]{2,1,0:T(8,128)S(1)}, u32[]{:S(2)}, u32[]{:S(2)}) collective-permute-start(f32[8,8,128]{2,1,0:T(8,128)S(1)} %get-tuple-element.66), channel_id=1, source_target_pairs={{0,4},{1,2},{2,1},{3,7},{4,0},{5,6},{6,5},{7,3},{8,12},{9,10},{10,... | collective-permute-start | bytes 98312 | tf_op jit(solution)/shard_map/ppermute | solution.py:311
  16.2 0.8 collective-permute-start.5
  17.1 0.1 div.16
  17.2 0.2 prepare_node.1
  17.4 0.0 collective-permute-done.4.z0
  17.4 1.6 %collective-permute-done.5.z1 = f32[8,8,128]{2,1,0:T(8,128)S(1)} collective-permute-done((f32[8,8,128]{2,1,0:T(8,128)S(1)}, f32[8,8,128]{2,1,0:T(8,128)S(1)}, u32[]{:S(2)}, u32[]{:S(2)}) %collective-permute-start.5) | collective-permute-done | bytes 32800 | tf_op jit(solution)/shard_map/ppermute | solution.py:311
  19.0 0.1 broadcast_in_dim.2.inverse
  19.1 0.4 node.1
  19.5 1.7 %collective-permute-start.6 = (f32[8,8,128]{2,1,0:T(8,128)S(1)}, f32[8,8,128]{2,1,0:T(8,128)S(1)}, u32[]{:S(2)}, u32[]{:S(2)}) collective-permute-start(f32[8,8,128]{2,1,0:T(8,128)S(1)} %get-tuple-element.73), channel_id=1, source_target_pairs={{0,4},{1,5},{2,6},{3,7},{4,0},{5,1},{6,2},{7,3},{8,12},{9,13},{10,... | collective-permute-start | bytes 98312 | tf_op jit(solution)/shard_map/ppermute | solution.py:311
  21.3 3.6 %collective-permute-start.7 = (f32[8,8,128]{2,1,0:T(8,128)S(1)}, f32[8,8,128]{2,1,0:T(8,128)S(1)}, u32[]{:S(2)}, u32[]{:S(2)}) collective-permute-start(f32[8,8,128]{2,1,0:T(8,128)S(1)} %get-tuple-element.74), channel_id=1, source_target_pairs={{0,16},{1,17},{2,18},{3,19},{4,20},{5,21},{6,22},{7,23},{8,24},{9,... | collective-permute-start | bytes 98312 | tf_op jit(solution)/shard_map/ppermute | solution.py:311
  24.9 0.0 collective-permute-done.6.x0
  24.9 1.3 %collective-permute-done.7.x1 = f32[8,8,128]{2,1,0:T(8,128)S(1)} collective-permute-done((f32[8,8,128]{2,1,0:T(8,128)S(1)}, f32[8,8,128]{2,1,0:T(8,128)S(1)}, u32[]{:S(2)}, u32[]{:S(2)}) %collective-permute-start.7) | collective-permute-done | bytes 32800 | tf_op jit(solution)/shard_map/ppermute | solution.py:311
  26.2 3.1 %collective-permute-start.8 = (f32[8,8,128]{2,1,0:T(8,128)S(1)}, f32[8,8,128]{2,1,0:T(8,128)S(1)}, u32[]{:S(2)}, u32[]{:S(2)}) collective-permute-start(f32[8,8,128]{2,1,0:T(8,128)S(1)} %get-tuple-element.75), channel_id=1, source_target_pairs={{0,1},{1,0},{2,3},{3,2},{4,8},{5,9},{6,10},{7,11},{8,4},{9,5},{10,... | collective-permute-start | bytes 98312 | tf_op jit(solution)/shard_map/ppermute | solution.py:311
  29.3 2.3 %collective-permute-start.9 = (f32[8,8,128]{2,1,0:T(8,128)S(1)}, f32[8,8,128]{2,1,0:T(8,128)S(1)}, u32[]{:S(2)}, u32[]{:S(2)}) collective-permute-start(f32[8,8,128]{2,1,0:T(8,128)S(1)} %get-tuple-element.76), channel_id=1, source_target_pairs={{0,4},{1,5},{2,6},{3,7},{4,0},{5,1},{6,2},{7,3},{8,12},{9,13},{10,... | collective-permute-start | bytes 98312 | tf_op jit(solution)/shard_map/ppermute | solution.py:311
  31.6 0.0 collective-permute-done.8.y0
  31.6 0.9 collective-permute-done.9.y1
  32.4 0.1 after_y_2.1
  32.5 1.1 %collective-permute-start.10 = (f32[8,8,128]{2,1,0:T(8,128)S(1)}, f32[8,8,128]{2,1,0:T(8,128)S(1)}, u32[]{:S(2)}, u32[]{:S(2)}) collective-permute-start(f32[8,8,128]{2,1,0:T(8,128)S(1)} %get-tuple-element.77), channel_id=1, source_target_pairs={{0,4},{1,2},{2,1},{3,7},{4,0},{5,6},{6,5},{7,3},{8,12},{9,10},{10,... | collective-permute-start | bytes 98312 | tf_op jit(solution)/shard_map/ppermute | solution.py:311
  33.6 0.0 collective-permute-start.11
  33.7 1.5 %prepare_edge.1 = (f32[4,512,128]{2,1,0:T(8,128)S(1)}, bf16[512,512]{1,0:T(8,128)(2,1)S(1)}, bf16[384,2048]{1,0:T(8,128)(2,1)S(1)}, bf16[128,128]{1,0:T(8,128)(2,1)S(1)}, bf16[256,128]{1,0:T(8,128)(2,1)S(1)}) custom-call(s32[4,3]{1,0:T(4,128)S(1)} %copy-done.3, f32[4,512,128]{2,1,0:T(8,128)S(1)} %get-tuple-element.79.preact, ...), custom_call_target="tpu_custom_call" | custom-call | tf_op jit(solution)/shard_map/prepare_edge/pallas_call | solution.py:388
  35.2 0.3 node_grads.1
  35.5 0.0 collective-permute-done.10.z0
  35.5 0.9 collective-permute-done.11.z1
  36.4 0.9 edge.1
  37.3 1.8 %collective-permute-start.14 = (f32[448,128]{1,0:T(8,128)S(1)}, f32[448,128]{1,0:T(8,128)S(1)}, u32[]{:S(2)}, u32[]{:S(2)}) collective-permute-start(f32[448,128]{1,0:T(8,128)S(1)} %get-tuple-element.99), channel_id=1, source_target_pairs={{0,4},{1,5},{2,6},{3,7},{4,0},{5,1},{6,2},{7,3},{8,12},{9,13},{10,... | collective-permute-start | bytes 688136 | tf_op jit(solution)/shard_map/ppermute | solution.py:320
  39.1 1.1 %node_part.1 = (f32[8,8,8,128]{3,2,1,0:T(8,128)S(1)}, f32[8,8,128]{2,1,0:T(8,128)S(1)}, f32[8,8,128]{2,1,0:T(8,128)S(1)}) custom-call(s32[4,3]{1,0:T(4,128)S(1)} %copy-done.3, f32[9,8,128]{2,1,0:T(8,128)S(1)} %get-tuple-element.60.rim.refs_0_, bf16[2048,128]{1,0:T(8,128)(2,1)S(1)} %get-tuple-element.92.slopes, f32[512,128]{1,0:T(8,128)S(1)} %get-tuple-element.93.base, ...), custom_call_target="tpu_custom_call" | custom-call | tf_op jit(solution)/shard_map/node_part/pallas_call | solution.py:410
  40.2 0.0 collective-permute-done.14.got
  40.2 0.7 add_core.1
  40.9 7.6 %all-to-all-start = ((f32[16,1,3584]{2,1,0:T(1,128)}), f32[16,1,3584]{2,1,0:T(1,128)S(1)}, u32[]{:S(2)}, u32[]{:S(2)}) async-start(f32[16,1,3584]{2,1,0:T(1,128)} %bitcast.3), calls=%async_computation | async-start | bytes 458752 | tf_op jit(solution)/shard_map/all_to_all | solution.py:340
  48.5 0.9 collective-permute-start.12
  49.5 3.7 %collective-permute-start.13 = (f32[8,8,128]{2,1,0:T(8,128)S(1)}, f32[8,8,128]{2,1,0:T(8,128)S(1)}, u32[]{:S(2)}, u32[]{:S(2)}) collective-permute-start(f32[8,8,128]{2,1,0:T(8,128)S(1)} %get-tuple-element.97), channel_id=1, source_target_pairs={{0,16},{1,17},{2,18},{3,19},{4,20},{5,21},{6,22},{7,23},{8,24},{9,... | collective-permute-start | bytes 98312 | tf_op jit(solution)/shard_map/ppermute | solution.py:311
  53.1 0.0 collective-permute-done.12.refs_2_.x0
  53.1 1.8 %collective-permute-done.13.refs_3_.x1 = f32[8,8,128]{2,1,0:T(8,128)S(1)} collective-permute-done((f32[8,8,128]{2,1,0:T(8,128)S(1)}, f32[8,8,128]{2,1,0:T(8,128)S(1)}, u32[]{:S(2)}, u32[]{:S(2)}) %collective-permute-start.13) | collective-permute-done | bytes 32800 | tf_op jit(solution)/shard_map/ppermute | solution.py:311
  54.9 1.4 %all-to-all-done = f32[16,1,3584]{2,1,0:T(1,128)S(1)} async-done(((f32[16,1,3584]{2,1,0:T(1,128)}), f32[16,1,3584]{2,1,0:T(1,128)S(1)}, u32[]{:S(2)}, u32[]{:S(2)}) %all-to-all-start) | async-done | bytes 229408 | tf_op jit(solution)/shard_map/all_to_all | solution.py:340
  56.3 0.7 after_x_fold.1
  57.0 9.3 %all-to-all-start.1 = ((f32[8,1,3584]{2,1,0:T(1,128)}), f32[8,1,3584]{2,1,0:T(1,128)S(1)}, u32[]{:S(2)}, u32[]{:S(2)}) async-start(f32[8,1,3584]{2,1,0:T(1,128)} %bitcast.5), calls=%async_computation.1 | async-start | bytes 229376 | tf_op jit(solution)/shard_map/all_to_all | solution.py:340
  66.3 1.8 %collective-permute-start.15 = (f32[8,8,128]{2,1,0:T(8,128)S(1)}, f32[8,8,128]{2,1,0:T(8,128)S(1)}, u32[]{:S(2)}, u32[]{:S(2)}) collective-permute-start(f32[8,8,128]{2,1,0:T(8,128)S(1)} %get-tuple-element.100), channel_id=1, source_target_pairs={{0,1},{1,0},{2,3},{3,2},{4,8},{5,9},{6,10},{7,11},{8,4},{9,5},{10,... | collective-permute-start | bytes 98312 | tf_op jit(solution)/shard_map/ppermute | solution.py:311
  68.1 1.3 %collective-permute-start.16 = (f32[8,8,128]{2,1,0:T(8,128)S(1)}, f32[8,8,128]{2,1,0:T(8,128)S(1)}, u32[]{:S(2)}, u32[]{:S(2)}) collective-permute-start(f32[8,8,128]{2,1,0:T(8,128)S(1)} %get-tuple-element.101), channel_id=1, source_target_pairs={{0,4},{1,5},{2,6},{3,7},{4,0},{5,1},{6,2},{7,3},{8,12},{9,13},{10,... | collective-permute-start | bytes 98312 | tf_op jit(solution)/shard_map/ppermute | solution.py:311
  69.4 0.3 collective-permute-done.15.refs_4_.y0
  69.7 0.6 collective-permute-done.16.refs_5_.y1
  70.3 3.8 %all-to-all-done.1 = f32[8,1,3584]{2,1,0:T(1,128)S(1)} async-done(((f32[8,1,3584]{2,1,0:T(1,128)}), f32[8,1,3584]{2,1,0:T(1,128)S(1)}, u32[]{:S(2)}, u32[]{:S(2)}) %all-to-all-start.1) | async-done | bytes 114720 | tf_op jit(solution)/shard_map/all_to_all | solution.py:340
  74.0 0.7 after_y_fold.1
  74.8 3.6 %all-to-all-start.2 = ((f32[16,1,3584]{2,1,0:T(1,128)}), f32[16,1,3584]{2,1,0:T(1,128)S(1)}, u32[]{:S(2)}, u32[]{:S(2)}) async-start(f32[16,1,3584]{2,1,0:T(1,128)} %bitcast.7), calls=%async_computation.2 | async-start | bytes 458752 | tf_op jit(solution)/shard_map/all_to_all | solution.py:340
  78.3 4.0 %collective-permute-start.17 = (f32[8,8,128]{2,1,0:T(8,128)S(1)}, f32[8,8,128]{2,1,0:T(8,128)S(1)}, u32[]{:S(2)}, u32[]{:S(2)}) collective-permute-start(f32[8,8,128]{2,1,0:T(8,128)S(1)} %get-tuple-element.104), channel_id=1, source_target_pairs={{0,4},{1,2},{2,1},{3,7},{4,0},{5,6},{6,5},{7,3},{8,12},{9,10},{10,... | collective-permute-start | bytes 98312 | tf_op jit(solution)/shard_map/ppermute | solution.py:311
  82.3 0.0 collective-permute-start.18
  82.3 1.1 %edge_grad.1 = bf16[2048,128]{1,0:T(8,128)(2,1)} custom-call(bf16[2048,128]{1,0:T(8,128)(2,1)S(1)} %get-tuple-element.92.slopes, bf16[384,128]{1,0:T(8,128)(2,1)S(1)} %get-tuple-element.82.w_in), custom_call_target="tpu_custom_call" | custom-call | tf_op jit(solution)/shard_map/edge_grad/pallas_call | solution.py:413
  83.4 0.0 collective-permute-done.17.z0
  83.4 1.7 %collective-permute-done.18.z1 = f32[8,8,128]{2,1,0:T(8,128)S(1)} collective-permute-done((f32[8,8,128]{2,1,0:T(8,128)S(1)}, f32[8,8,128]{2,1,0:T(8,128)S(1)}, u32[]{:S(2)}, u32[]{:S(2)}) %collective-permute-start.18) | collective-permute-done | bytes 32800 | tf_op jit(solution)/shard_map/ppermute | solution.py:311
  85.1 0.6 all-to-all-done.2
  85.7 5.4 %collective-permute-start.19 = (f32[448,128]{1,0:T(8,128)S(1)}, f32[448,128]{1,0:T(8,128)S(1)}, u32[]{:S(2)}, u32[]{:S(2)}) collective-permute-start(f32[448,128]{1,0:T(8,128)S(1)} %bitcast.12), channel_id=1, source_target_pairs={{0,4},{1,5},{2,6},{3,7},{4,0},{5,1},{6,2},{7,3},{8,12},{9,13},{10,... | collective-permute-start | bytes 688136 | tf_op jit(solution)/shard_map/ppermute | solution.py:320
  91.1 0.8 last.1
  91.9 0.3 collective-permute-done.19.other
  92.2 1.0 %clip.1 = (f32[384,128]{1,0:T(8,128)}, f32[128,128]{1,0:T(8,128)}, f32[256,128]{1,0:T(8,128)}, f32[128,128]{1,0:T(8,128)}) custom-call(f32[9,8,128]{2,1,0:T(8,128)S(1)} %get-tuple-element.60.rim.refs_0_, f32[448,128]{1,0:T(8,128)S(1)} %bitcast.13, f32[448,128]{1,0:T(8,128)S(1)} %collective-permute-done.19.other), custom_call_target="tpu_custom_call" | custom-call | tf_op jit(solution)/shard_map/clip/pallas_call | solution.py:415
  (12 shorter events, 0.0 us)
Async XLA Ops:
  0.6 16.4 %copy-start.4 = (s32[8,8,8]{2,1,0:T(8,128)S(1)}, s32[8,8,8]{2,1,0:T(8,128)}, u32[]{:S(2)}) copy-start(s32[8,8,8]{2,1,0:T(8,128)} %param.11) | copy-start | bytes 6148
  0.6 16.5 %copy-start.1 = (bf16[8,8,8,128]{3,2,1,0:T(8,128)(2,1)S(1)}, bf16[8,8,8,128]{3,2,1,0:T(8,128)(2,1)}, u32[]{:S(2)}) copy-start(bf16[8,8,8,128]{3,2,1,0:T(8,128)(2,1)} %param.17) | copy-start | bytes 393220
  0.7 16.5 %copy-start = (bf16[256,128]{1,0:T(8,128)(2,1)S(1)}, bf16[256,128]{1,0:T(8,128)(2,1)}, u32[]{:S(2)}) copy-start(bf16[256,128]{1,0:T(8,128)(2,1)} %w_in.5) | copy-start | bytes 196612
  0.7 16.5 %copy-start.2 = (bf16[128,128]{1,0:T(8,128)(2,1)S(1)}, bf16[128,128]{1,0:T(8,128)(2,1)}, u32[]{:S(2)}) copy-start(bf16[128,128]{1,0:T(8,128)(2,1)} %w_out.1) | copy-start | bytes 98308
  3.2 5.2 %collective-permute-start = (f32[8,8,128]{2,1,0:T(8,128)S(1)}, f32[8,8,128]{2,1,0:T(8,128)S(1)}, u32[]{:S(2)}, u32[]{:S(2)}) collective-permute-start(f32[8,8,128]{2,1,0:T(8,128)S(1)} %get-tuple-element.62), channel_id=1, source_target_pairs={{0,4},{1,5},{2,6},{3,7},{4,0},{5,1},{6,2},{7,3},{8,12},{9,13},{10,... | collective-permute-start | bytes 98312 | tf_op jit(solution)/shard_map/ppermute | solution.py:311
  6.5 4.3 %collective-permute-start.1 = (f32[8,8,128]{2,1,0:T(8,128)S(1)}, f32[8,8,128]{2,1,0:T(8,128)S(1)}, u32[]{:S(2)}, u32[]{:S(2)}) collective-permute-start(f32[8,8,128]{2,1,0:T(8,128)S(1)} %get-tuple-element.63), channel_id=1, source_target_pairs={{0,16},{1,17},{2,18},{3,19},{4,20},{5,21},{6,22},{7,23},{8,24},{9,... | collective-permute-start | bytes 98312 | tf_op jit(solution)/shard_map/ppermute | solution.py:311
  10.8 3.7 %collective-permute-start.2 = (f32[8,8,128]{2,1,0:T(8,128)S(1)}, f32[8,8,128]{2,1,0:T(8,128)S(1)}, u32[]{:S(2)}, u32[]{:S(2)}) collective-permute-start(f32[8,8,128]{2,1,0:T(8,128)S(1)} %get-tuple-element.64), channel_id=1, source_target_pairs={{0,1},{1,0},{2,3},{3,2},{4,8},{5,9},{6,10},{7,11},{8,4},{9,5},{10,... | collective-permute-start | bytes 98312 | tf_op jit(solution)/shard_map/ppermute | solution.py:311
  12.8 1.6 %collective-permute-start.3 = (f32[8,8,128]{2,1,0:T(8,128)S(1)}, f32[8,8,128]{2,1,0:T(8,128)S(1)}, u32[]{:S(2)}, u32[]{:S(2)}) collective-permute-start(f32[8,8,128]{2,1,0:T(8,128)S(1)} %get-tuple-element.65), channel_id=1, source_target_pairs={{0,4},{1,5},{2,6},{3,7},{4,0},{5,1},{6,2},{7,3},{8,12},{9,13},{10,... | collective-permute-start | bytes 98312 | tf_op jit(solution)/shard_map/ppermute | solution.py:311
  14.5 19.1 %copy-start.3 = (s32[4,3]{1,0:T(4,128)S(1)}, s32[4,3]{1,0:T(4,128)}, u32[]{:S(2)}) copy-start(s32[4,3]{1,0:T(4,128)} %offs.3) | copy-start | bytes 148
  14.5 2.9 %collective-permute-start.4 = (f32[8,8,128]{2,1,0:T(8,128)S(1)}, f32[8,8,128]{2,1,0:T(8,128)S(1)}, u32[]{:S(2)}, u32[]{:S(2)}) collective-permute-start(f32[8,8,128]{2,1,0:T(8,128)S(1)} %get-tuple-element.66), channel_id=1, source_target_pairs={{0,4},{1,2},{2,1},{3,7},{4,0},{5,6},{6,5},{7,3},{8,12},{9,10},{10,... | collective-permute-start | bytes 98312 | tf_op jit(solution)/shard_map/ppermute | solution.py:311
  16.2 2.8 %collective-permute-start.5 = (f32[8,8,128]{2,1,0:T(8,128)S(1)}, f32[8,8,128]{2,1,0:T(8,128)S(1)}, u32[]{:S(2)}, u32[]{:S(2)}) collective-permute-start(f32[8,8,128]{2,1,0:T(8,128)S(1)} %get-tuple-element.67), channel_id=1, source_target_pairs={{0,1},{1,0},{2,3},{3,2},{4,5},{5,4},{6,7},{7,6},{8,9},{9,8},{10,11... | collective-permute-start | bytes 98312 | tf_op jit(solution)/shard_map/ppermute | solution.py:311
  19.5 5.3 %collective-permute-start.6 = (f32[8,8,128]{2,1,0:T(8,128)S(1)}, f32[8,8,128]{2,1,0:T(8,128)S(1)}, u32[]{:S(2)}, u32[]{:S(2)}) collective-permute-start(f32[8,8,128]{2,1,0:T(8,128)S(1)} %get-tuple-element.73), channel_id=1, source_target_pairs={{0,4},{1,5},{2,6},{3,7},{4,0},{5,1},{6,2},{7,3},{8,12},{9,13},{10,... | collective-permute-start | bytes 98312 | tf_op jit(solution)/shard_map/ppermute | solution.py:311
  21.3 4.9 %collective-permute-start.7 = (f32[8,8,128]{2,1,0:T(8,128)S(1)}, f32[8,8,128]{2,1,0:T(8,128)S(1)}, u32[]{:S(2)}, u32[]{:S(2)}) collective-permute-start(f32[8,8,128]{2,1,0:T(8,128)S(1)} %get-tuple-element.74), channel_id=1, source_target_pairs={{0,16},{1,17},{2,18},{3,19},{4,20},{5,21},{6,22},{7,23},{8,24},{9,... | collective-permute-start | bytes 98312 | tf_op jit(solution)/shard_map/ppermute | solution.py:311
  26.2 5.4 %collective-permute-start.8 = (f32[8,8,128]{2,1,0:T(8,128)S(1)}, f32[8,8,128]{2,1,0:T(8,128)S(1)}, u32[]{:S(2)}, u32[]{:S(2)}) collective-permute-start(f32[8,8,128]{2,1,0:T(8,128)S(1)} %get-tuple-element.75), channel_id=1, source_target_pairs={{0,1},{1,0},{2,3},{3,2},{4,8},{5,9},{6,10},{7,11},{8,4},{9,5},{10,... | collective-permute-start | bytes 98312 | tf_op jit(solution)/shard_map/ppermute | solution.py:311
  29.3 3.2 %collective-permute-start.9 = (f32[8,8,128]{2,1,0:T(8,128)S(1)}, f32[8,8,128]{2,1,0:T(8,128)S(1)}, u32[]{:S(2)}, u32[]{:S(2)}) collective-permute-start(f32[8,8,128]{2,1,0:T(8,128)S(1)} %get-tuple-element.76), channel_id=1, source_target_pairs={{0,4},{1,5},{2,6},{3,7},{4,0},{5,1},{6,2},{7,3},{8,12},{9,13},{10,... | collective-permute-start | bytes 98312 | tf_op jit(solution)/shard_map/ppermute | solution.py:311
  32.5 3.0 %collective-permute-start.10 = (f32[8,8,128]{2,1,0:T(8,128)S(1)}, f32[8,8,128]{2,1,0:T(8,128)S(1)}, u32[]{:S(2)}, u32[]{:S(2)}) collective-permute-start(f32[8,8,128]{2,1,0:T(8,128)S(1)} %get-tuple-element.77), channel_id=1, source_target_pairs={{0,4},{1,2},{2,1},{3,7},{4,0},{5,6},{6,5},{7,3},{8,12},{9,10},{10,... | collective-permute-start | bytes 98312 | tf_op jit(solution)/shard_map/ppermute | solution.py:311
  33.6 2.8 %collective-permute-start.11 = (f32[8,8,128]{2,1,0:T(8,128)S(1)}, f32[8,8,128]{2,1,0:T(8,128)S(1)}, u32[]{:S(2)}, u32[]{:S(2)}) collective-permute-start(f32[8,8,128]{2,1,0:T(8,128)S(1)} %get-tuple-element.78), channel_id=1, source_target_pairs={{0,1},{1,0},{2,3},{3,2},{4,5},{5,4},{6,7},{7,6},{8,9},{9,8},{10,11... | collective-permute-start | bytes 98312 | tf_op jit(solution)/shard_map/ppermute | solution.py:311
  37.3 2.9 %collective-permute-start.14 = (f32[448,128]{1,0:T(8,128)S(1)}, f32[448,128]{1,0:T(8,128)S(1)}, u32[]{:S(2)}, u32[]{:S(2)}) collective-permute-start(f32[448,128]{1,0:T(8,128)S(1)} %get-tuple-element.99), channel_id=1, source_target_pairs={{0,4},{1,5},{2,6},{3,7},{4,0},{5,1},{6,2},{7,3},{8,12},{9,13},{10,... | collective-permute-start | bytes 688136 | tf_op jit(solution)/shard_map/ppermute | solution.py:320
  40.9 15.4 %all-to-all-start = ((f32[16,1,3584]{2,1,0:T(1,128)}), f32[16,1,3584]{2,1,0:T(1,128)S(1)}, u32[]{:S(2)}, u32[]{:S(2)}) async-start(f32[16,1,3584]{2,1,0:T(1,128)} %bitcast.3), calls=%async_computation | async-start | bytes 458752 | tf_op jit(solution)/shard_map/all_to_all | solution.py:340
  48.5 4.6 %collective-permute-start.12 = (f32[8,8,128]{2,1,0:T(8,128)S(1)}, f32[8,8,128]{2,1,0:T(8,128)S(1)}, u32[]{:S(2)}, u32[]{:S(2)}) collective-permute-start(f32[8,8,128]{2,1,0:T(8,128)S(1)} %get-tuple-element.96.after), channel_id=1, source_target_pairs={{0,4},{1,5},{2,6},{3,7},{4,0},{5,1},{6,2},{7,3},{8,12},{9,13},{10,... | collective-permute-start | bytes 98312 | tf_op jit(solution)/shard_map/ppermute | solution.py:311
  49.5 5.5 %collective-permute-start.13 = (f32[8,8,128]{2,1,0:T(8,128)S(1)}, f32[8,8,128]{2,1,0:T(8,128)S(1)}, u32[]{:S(2)}, u32[]{:S(2)}) collective-permute-start(f32[8,8,128]{2,1,0:T(8,128)S(1)} %get-tuple-element.97), channel_id=1, source_target_pairs={{0,16},{1,17},{2,18},{3,19},{4,20},{5,21},{6,22},{7,23},{8,24},{9,... | collective-permute-start | bytes 98312 | tf_op jit(solution)/shard_map/ppermute | solution.py:311
  57.0 17.0 %all-to-all-start.1 = ((f32[8,1,3584]{2,1,0:T(1,128)}), f32[8,1,3584]{2,1,0:T(1,128)S(1)}, u32[]{:S(2)}, u32[]{:S(2)}) async-start(f32[8,1,3584]{2,1,0:T(1,128)} %bitcast.5), calls=%async_computation.1 | async-start | bytes 229376 | tf_op jit(solution)/shard_map/all_to_all | solution.py:340
  66.3 3.4 %collective-permute-start.15 = (f32[8,8,128]{2,1,0:T(8,128)S(1)}, f32[8,8,128]{2,1,0:T(8,128)S(1)}, u32[]{:S(2)}, u32[]{:S(2)}) collective-permute-start(f32[8,8,128]{2,1,0:T(8,128)S(1)} %get-tuple-element.100), channel_id=1, source_target_pairs={{0,1},{1,0},{2,3},{3,2},{4,8},{5,9},{6,10},{7,11},{8,4},{9,5},{10,... | collective-permute-start | bytes 98312 | tf_op jit(solution)/shard_map/ppermute | solution.py:311
  68.1 2.2 %collective-permute-start.16 = (f32[8,8,128]{2,1,0:T(8,128)S(1)}, f32[8,8,128]{2,1,0:T(8,128)S(1)}, u32[]{:S(2)}, u32[]{:S(2)}) collective-permute-start(f32[8,8,128]{2,1,0:T(8,128)S(1)} %get-tuple-element.101), channel_id=1, source_target_pairs={{0,4},{1,5},{2,6},{3,7},{4,0},{5,1},{6,2},{7,3},{8,12},{9,13},{10,... | collective-permute-start | bytes 98312 | tf_op jit(solution)/shard_map/ppermute | solution.py:311
  74.8 10.9 %all-to-all-start.2 = ((f32[16,1,3584]{2,1,0:T(1,128)}), f32[16,1,3584]{2,1,0:T(1,128)S(1)}, u32[]{:S(2)}, u32[]{:S(2)}) async-start(f32[16,1,3584]{2,1,0:T(1,128)} %bitcast.7), calls=%async_computation.2 | async-start | bytes 458752 | tf_op jit(solution)/shard_map/all_to_all | solution.py:340
  78.3 5.1 %collective-permute-start.17 = (f32[8,8,128]{2,1,0:T(8,128)S(1)}, f32[8,8,128]{2,1,0:T(8,128)S(1)}, u32[]{:S(2)}, u32[]{:S(2)}) collective-permute-start(f32[8,8,128]{2,1,0:T(8,128)S(1)} %get-tuple-element.104), channel_id=1, source_target_pairs={{0,4},{1,2},{2,1},{3,7},{4,0},{5,6},{6,5},{7,3},{8,12},{9,10},{10,... | collective-permute-start | bytes 98312 | tf_op jit(solution)/shard_map/ppermute | solution.py:311
  82.3 2.8 %collective-permute-start.18 = (f32[8,8,128]{2,1,0:T(8,128)S(1)}, f32[8,8,128]{2,1,0:T(8,128)S(1)}, u32[]{:S(2)}, u32[]{:S(2)}) collective-permute-start(f32[8,8,128]{2,1,0:T(8,128)S(1)} %get-tuple-element.105), channel_id=1, source_target_pairs={{0,1},{1,0},{2,3},{3,2},{4,5},{5,4},{6,7},{7,6},{8,9},{9,8},{10,11... | collective-permute-start | bytes 98312 | tf_op jit(solution)/shard_map/ppermute | solution.py:311
  85.7 6.5 %collective-permute-start.19 = (f32[448,128]{1,0:T(8,128)S(1)}, f32[448,128]{1,0:T(8,128)S(1)}, u32[]{:S(2)}, u32[]{:S(2)}) collective-permute-start(f32[448,128]{1,0:T(8,128)S(1)} %bitcast.12), channel_id=1, source_target_pairs={{0,4},{1,5},{2,6},{3,7},{4,0},{5,1},{6,2},{7,3},{8,12},{9,13},{10,... | collective-permute-start | bytes 688136 | tf_op jit(solution)/shard_map/ppermute | solution.py:320

commit v8 on v6

--- a/solution.py
+++ b/solution.py
@@ -9,6 +9,7 @@
 from jax.experimental.pallas import tpu as pltpu
 from jax.sharding import Mesh
 from jax.sharding import PartitionSpec as P
+
 
 B = 8
 W = 128
@@ -30,7 +31,7 @@
 NEAR, FAR = ("yh", "yl", "x"), ("z",)
 
 
-def call(body, outs, specs, name, scratch=()):
+def call(body, outs, specs, scratch=()):
     return pl.pallas_call(
         body,
         out_shape=[jax.ShapeDtypeStruct(s, t) for s, t in outs],
@@ -38,7 +39,6 @@
         out_specs=[VMEM] * len(outs),
         scratch_shapes=list(scratch),
         compiler_params=pltpu.CompilerParams(vmem_limit_bytes=GRANT),
-        name=name,
     )
 
 
@@ -283,7 +283,7 @@
     out[...] = dot_t(slopes[...], w_in[2 * W :]).astype(BF16)
 
 
-def last_kernel(rim, field, z0, z1, y0, y1, x0, x1, out, work):
+def last_kernel(rim, field, z0, z1, y0, y1, x0, x1, clipped, out, work):
     work[...] = field[...]
     add_z(rim, (z0, z1), work)
     add_y(rim, (y0, y1), work)
@@ -346,11 +346,11 @@
 BOTH = pltpu.VMEM((2, *FACE), F32)
 
 
-def arrivals(rim, field, xa, xb, tag):
+def arrivals(rim, field, xa, xb):
     x = exchange(xa, xb, 0)
-    a, b = call(y_faces_after_x, FACES, [VMEM] * 4, "after_x" + tag, [BOTH])(rim, field, *x)
+    a, b = call(y_faces_after_x, FACES, [VMEM] * 4, [BOTH])(rim, field, *x)
     y = exchange(a, b, 1)
-    a, b = call(z_faces_after_y, FACES, [VMEM] * 6, "after_y" + tag, [BOTH])(rim, field, *x, *y)
+    a, b = call(z_faces_after_y, FACES, [VMEM] * 6, [BOTH])(rim, field, *x, *y)
     return (*x, *y, *exchange(a, b, 2))
 
 
@@ -358,17 +358,16 @@
     return lax.all_to_all(rows.reshape(lax.axis_size(axes), -1), axes, 0, 0, tiled=True).reshape(-1, W)
 
 
-def arrivals_and_sum(rim, field, za, zb, keep, give, edge_grad):
+def arrivals_and_sum(rim, field, za, zb, keep, give):
     near, far = lax.axis_size(NEAR), lax.axis_size(FAR)
     rows = keep.shape[0] // near
-    (half,) = call(add_kernel, [(keep.shape, F32)], [VMEM] * 3, "add_core")(keep, other_core(give), za)
+    (half,) = call(add_kernel, [(keep.shape, F32)], [VMEM] * 3)(keep, other_core(give), za)
     got = swap(half, NEAR)
     z = exchange(za, zb, 2)
     a, b, spread = call(
         functools.partial(fold_with_faces_kernel, y_faces_after_z, rows, near // 2, far // 2),
         FACES + [((rows * far, W), F32)],
         [VMEM] * 5,
-        "after_z_fold",
         [BOTH],
     )(got, rim, field, *z)
     got = swap(spread, FAR)
@@ -377,13 +376,11 @@
         functools.partial(fold_with_faces_kernel, x_faces_after_y, rows, far // 2, near // 2),
         FACES + [((rows * near, W), F32)],
         [VMEM] * 7,
-        "after_y_fold",
         [BOTH],
     )(got, rim, field, *z, *y)
     mine = swap(spread, NEAR)
     x = exchange(a, b, 0)
-    mine, edge_grad, *x = lax.optimization_barrier((mine, edge_grad, *x))
-    return (*z, *y, *x), (mine, other_core(mine)), edge_grad
+    return (*z, *y, *x), (mine, other_core(mine))
 
 
 def on_device(node_feat, edge_feat, copies, offsets, w_edge_in, w_edge_out, w_node_in, w_node_out, node_cot):
@@ -396,44 +393,40 @@
         forward_kernel,
         [(CUBE, F32)] + FACES + [((K, N, W), F32), many, ((N, W), BF16), many, ((3 * W, W), BF16), square, ((9, B, W), F32)],
         [HBM] * 5,
-        "forward",
         [PAD, pltpu.SMEM((K, 3), jnp.int32), pltpu.SemaphoreType.DMA((4 + K,))],
     )(*map(in_hbm, (node_feat.reshape(N, W), edge_feat.reshape(K, N, W), w_edge_in, w_edge_out, offsets)))
     begun, upstream, w_node_back = call(
-        prepare_node_kernel, [((N, W), F32), ((N, W), F32), square], [VMEM] * 4, "prepare_node"
+        prepare_node_kernel, [((N, W), F32), ((N, W), F32), square], [VMEM] * 4
     )(nodes, cot, w_node_in, w_node_out)
-    arrived = arrivals(rim, local, xa, xb, "_1")
+    arrived = arrivals(rim, local, xa, xb)
     dact, hidden_t, left, w_out_t, w_back = call(
         prepare_edge_kernel,
         [((K, N, W), F32), ((K * W, N), BF16), ((3 * W, K * N), BF16), square, ((2 * W, W), BF16)],
         [SMEM] + [VMEM] * 6,
-        "prepare_edge",
         [PAD],
     )(offsets, preact, hidden, nodes, edges, w_in, w_out)
     local, xa, xb, gathered, slope, node_hidden = call(
-        node_kernel, [(CUBE, F32)] + FACES + [((N, W), BF16)] * 3, [VMEM] * 13, "node", [WORK]
+        node_kernel, [(CUBE, F32)] + FACES + [((N, W), BF16)] * 3, [VMEM] * 13, [WORK]
     )(rim, local, *arrived, inverse, begun, upstream, w_node_in, w_node_back)
-    arrived = arrivals(rim, local, xa, xb, "_2")
-    node_grads, base = call(node_grads_kernel, [((3 * W, W), F32), ((N, W), F32)], [VMEM] * 6, "node_grads")(
+    arrived = arrivals(rim, local, xa, xb)
+    node_grads, base = call(node_grads_kernel, [((3 * W, W), F32), ((N, W), F32)], [VMEM] * 6)(
         nodes, gathered, slope, node_hidden, cot, w_node_in
     )
     half = ((7 * W // 2, W), F32)
     slopes, keep, give = call(
-        edge_kernel,
-        [((K * N, W), BF16), half, half],
-        [VMEM] * 13,
-        "edge",
-        [WORK, pltpu.VMEM((7 * W, W), F32)],
+        edge_kernel, [((K * N, W), BF16), half, half], [VMEM] * 13, [WORK, pltpu.VMEM((7 * W, W), F32)]
     )(rim, local, *arrived, dact, hidden_t, left, w_out_t, node_grads)
     local, za, zb = call(
-        node_part_kernel, [(CUBE, F32)] + FACES, [SMEM] + [VMEM] * 4, "node_part", [PAD]
+        node_part_kernel, [(CUBE, F32)] + FACES, [SMEM] + [VMEM] * 4, [PAD]
     )(offsets, rim, slopes, base, w_back)
-    (edge_grad,) = call(edge_grad_kernel, [((K * N, W), BF16)], [VMEM] * 2, "edge_grad")(slopes, w_in)
-    arrived, halves, edge_grad = arrivals_and_sum(rim, local, za, zb, keep, give, edge_grad)
+    (edge_grad,) = call(edge_grad_kernel, [((K * N, W), BF16)], [VMEM] * 2)(slopes, w_in)
+    arrived, halves = arrivals_and_sum(rim, local, za, zb, keep, give)
     clipped = call(
-        clip_kernel, [((3 * W, W), F32), ((W, W), F32), ((2 * W, W), F32), ((W, W), F32)], [VMEM] * 3, "clip"
+        clip_kernel, [((3 * W, W), F32), ((W, W), F32), ((2 * W, W), F32), ((W, W), F32)], [VMEM] * 3
     )(rim, *halves)
-    (node_grad,) = call(last_kernel, [((N, W), BF16)], [VMEM] * 8, "last", [WORK])(rim, local, *arrived)
+    (node_grad,) = call(last_kernel, [((N, W), BF16)], [VMEM] * 8 + [HBM], [WORK])(
+        rim, local, *arrived, in_hbm(clipped[1])
+    )
     return (node_grad.reshape(node_feat.shape), edge_grad.reshape(edge_feat.shape), *clipped)
 
 
@@ -451,6 +444,7 @@
         P(),
         P(*place, None),
     )
+
     return jax.shard_map(
         on_device,
         mesh=split,

time: 91.5 us -> 94 us (1.027)
  blocking collectives: 0 us -> 10.3 us
  waiting for transfers between devices: 22.5 us -> 18.8 us
  starting transfers between devices: 55.4 us -> 52 us
    all_to_all x0 -> x1, blocking collectives: none -> 10.3 us  [swap(): lax.all_to_all(rows.reshape(lax.axis_size(axes), -1), axes, 0, 0, tiled=T...]
    all_to_all x3 -> x2, starting transfers between devices: 19.3 us -> 15.8 us  [swap(): lax.all_to_all(rows.reshape(lax.axis_size(axes), -1), axes, 0, 0, tiled=T...]
    ppermute x18, waiting for transfers between devices: 14.9 us -> 11.5 us  [exchange(): lax.ppermute(face, GX + GY + GZ, [(rank, ranks[to]) for rank, to in enume...]
    all_to_all x3 -> x2, waiting for transfers between devices: 7.25 us -> 7.26 us  [swap(): lax.all_to_all(rows.reshape(lax.axis_size(axes), -1), axes, 0, 0, tiled=T...]
  transfers between devices with their start and end apart: 23 -> 22, of which waited for: 13 -> 11; matrix products, arithmetic and copies ran while one was open for 0% -> 0% of each run, Pallas kernels for 6% -> 6%
where the time goes in v8:
time: 94 us; the launch traced here: 93.6 us
  starting transfers between devices  52 us (55%)
  waiting for transfers between devices  18.8 us (20%)
  Pallas kernels  11.4 us (12%)
  blocking collectives  10.3 us (11%)
    ppermute x18, starting transfers between devices, exchange(): lax.ppermute(face, GX + GY + GZ, [(rank, ranks[to]) for rank, to in enume...  30.1 us
    all_to_all x2, starting transfers between devices, swap(): lax.all_to_all(rows.reshape(lax.axis_size(axes), -1), axes, 0, 0, tiled=T...  15.8 us
    ppermute x18, waiting for transfers between devices, exchange(): lax.ppermute(face, GX + GY + GZ, [(rank, ranks[to]) for rank, to in enume...  11.5 us
    all_to_all x1, blocking collectives, swap(): lax.all_to_all(rows.reshape(lax.axis_size(axes), -1), axes, 0, 0, tiled=T...  10.3 us
    all_to_all x2, waiting for transfers between devices, swap(): lax.all_to_all(rows.reshape(lax.axis_size(axes), -1), axes, 0, 0, tiled=T...  7.26 us
    ppermute x2, starting transfers between devices, other_core(): lax.ppermute(half, GX + GY + GZ, [(rank, rank ^ step) for rank in range(c...  6.09 us
    pallas_call x1, Pallas kernels, on_device(): call(forward_kernel, [(CUBE, F32)] + FACES + [((K, N, W), F32), many, ((N...  2.42 us
  transfers between devices with their start and end apart: 22, of which 11 were waited for; matrix products, arithmetic and copies ran while one was open for 0% of the time, Pallas kernels for 6%

profile of v8, /device:TPU:1, one launch (start us, length us, event | category | flops | bytes accessed | tf_op | source)
XLA Modules:
  0.0 93.6 jit_solution(17733770399019495069)
XLA Ops:
  0.6 0.0 copy-start.4
  0.7 2.4 %shard_map.136 = (f32[8,8,8,128]{3,2,1,0:T(8,128)S(1)}, f32[8,8,128]{2,1,0:T(8,128)S(1)}, f32[8,8,128]{2,1,0:T(8,128)S(1)}, f32[4,512,128]{2,1,0:T(8,128)S(1)}, ...) custom-call(bf16[512,128]{1,0:T(8,128)(2,1)} %bitcast.20, ...), custom_call_target="tpu_custom_call" | custom-call | tf_op jit(solution)/shard_map/pallas_call | solution.py:392
  3.1 3.3 %collective-permute-start = (f32[8,8,128]{2,1,0:T(8,128)S(1)}, f32[8,8,128]{2,1,0:T(8,128)S(1)}, u32[]{:S(2)}, u32[]{:S(2)}) collective-permute-start(f32[8,8,128]{2,1,0:T(8,128)S(1)} %get-tuple-element.58), channel_id=1, source_target_pairs={{0,4},{1,5},{2,6},{3,7},{4,0},{5,1},{6,2},{7,3},{8,12},{9,13},{10,... | collective-permute-start | bytes 98312 | tf_op jit(solution)/shard_map/ppermute | solution.py:329
  6.4 1.9 %collective-permute-start.1 = (f32[8,8,128]{2,1,0:T(8,128)S(1)}, f32[8,8,128]{2,1,0:T(8,128)S(1)}, u32[]{:S(2)}, u32[]{:S(2)}) collective-permute-start(f32[8,8,128]{2,1,0:T(8,128)S(1)} %get-tuple-element.59), channel_id=1, source_target_pairs={{0,16},{1,17},{2,18},{3,19},{4,20},{5,21},{6,22},{7,23},{8,24},{9,... | collective-permute-start | bytes 98312 | tf_op jit(solution)/shard_map/ppermute | solution.py:329
  8.3 0.0 collective-permute-done.x0
  8.3 2.3 %collective-permute-done.1.x1 = f32[8,8,128]{2,1,0:T(8,128)S(1)} collective-permute-done((f32[8,8,128]{2,1,0:T(8,128)S(1)}, f32[8,8,128]{2,1,0:T(8,128)S(1)}, u32[]{:S(2)}, u32[]{:S(2)}) %collective-permute-start.1) | collective-permute-done | bytes 32800 | tf_op jit(solution)/shard_map/ppermute | solution.py:329
  10.7 2.1 %collective-permute-start.2 = (f32[8,8,128]{2,1,0:T(8,128)S(1)}, f32[8,8,128]{2,1,0:T(8,128)S(1)}, u32[]{:S(2)}, u32[]{:S(2)}) collective-permute-start(f32[8,8,128]{2,1,0:T(8,128)S(1)} %get-tuple-element.60), channel_id=1, source_target_pairs={{0,1},{1,0},{2,3},{3,2},{4,8},{5,9},{6,10},{7,11},{8,4},{9,5},{10,... | collective-permute-start | bytes 98312 | tf_op jit(solution)/shard_map/ppermute | solution.py:329
  12.7 0.3 collective-permute-start.3
  13.1 1.3 %collective-permute-done.2.y0 = f32[8,8,128]{2,1,0:T(8,128)S(1)} collective-permute-done((f32[8,8,128]{2,1,0:T(8,128)S(1)}, f32[8,8,128]{2,1,0:T(8,128)S(1)}, u32[]{:S(2)}, u32[]{:S(2)}) %collective-permute-start.2) | collective-permute-done | bytes 32800 | tf_op jit(solution)/shard_map/ppermute | solution.py:329
  14.3 0.0 collective-permute-done.3.y1
  14.3 0.1 shard_map.138
  14.4 0.0 copy-start.3
  14.5 1.7 %collective-permute-start.4 = (f32[8,8,128]{2,1,0:T(8,128)S(1)}, f32[8,8,128]{2,1,0:T(8,128)S(1)}, u32[]{:S(2)}, u32[]{:S(2)}) collective-permute-start(f32[8,8,128]{2,1,0:T(8,128)S(1)} %get-tuple-element.62), channel_id=1, source_target_pairs={{0,4},{1,2},{2,1},{3,7},{4,0},{5,6},{6,5},{7,3},{8,12},{9,10},{10,... | collective-permute-start | bytes 98312 | tf_op jit(solution)/shard_map/ppermute | solution.py:329
  16.1 0.8 collective-permute-start.5
  17.0 0.1 div.16
  17.1 0.2 shard_map.139
  17.3 0.0 collective-permute-done.4.z0
  17.3 1.6 %collective-permute-done.5.z1 = f32[8,8,128]{2,1,0:T(8,128)S(1)} collective-permute-done((f32[8,8,128]{2,1,0:T(8,128)S(1)}, f32[8,8,128]{2,1,0:T(8,128)S(1)}, u32[]{:S(2)}, u32[]{:S(2)}) %collective-permute-start.5) | collective-permute-done | bytes 32800 | tf_op jit(solution)/shard_map/ppermute | solution.py:329
  18.9 0.1 broadcast_in_dim.2.inverse
  19.0 0.4 shard_map.140
  19.4 1.7 %collective-permute-start.6 = (f32[8,8,128]{2,1,0:T(8,128)S(1)}, f32[8,8,128]{2,1,0:T(8,128)S(1)}, u32[]{:S(2)}, u32[]{:S(2)}) collective-permute-start(f32[8,8,128]{2,1,0:T(8,128)S(1)} %get-tuple-element.69), channel_id=1, source_target_pairs={{0,4},{1,5},{2,6},{3,7},{4,0},{5,1},{6,2},{7,3},{8,12},{9,13},{10,... | collective-permute-start | bytes 98312 | tf_op jit(solution)/shard_map/ppermute | solution.py:329
  21.2 3.6 %collective-permute-start.7 = (f32[8,8,128]{2,1,0:T(8,128)S(1)}, f32[8,8,128]{2,1,0:T(8,128)S(1)}, u32[]{:S(2)}, u32[]{:S(2)}) collective-permute-start(f32[8,8,128]{2,1,0:T(8,128)S(1)} %get-tuple-element.70), channel_id=1, source_target_pairs={{0,16},{1,17},{2,18},{3,19},{4,20},{5,21},{6,22},{7,23},{8,24},{9,... | collective-permute-start | bytes 98312 | tf_op jit(solution)/shard_map/ppermute | solution.py:329
  24.8 0.0 collective-permute-done.6.x0
  24.8 1.3 %collective-permute-done.7.x1 = f32[8,8,128]{2,1,0:T(8,128)S(1)} collective-permute-done((f32[8,8,128]{2,1,0:T(8,128)S(1)}, f32[8,8,128]{2,1,0:T(8,128)S(1)}, u32[]{:S(2)}, u32[]{:S(2)}) %collective-permute-start.7) | collective-permute-done | bytes 32800 | tf_op jit(solution)/shard_map/ppermute | solution.py:329
  26.1 3.1 %collective-permute-start.8 = (f32[8,8,128]{2,1,0:T(8,128)S(1)}, f32[8,8,128]{2,1,0:T(8,128)S(1)}, u32[]{:S(2)}, u32[]{:S(2)}) collective-permute-start(f32[8,8,128]{2,1,0:T(8,128)S(1)} %get-tuple-element.71), channel_id=1, source_target_pairs={{0,1},{1,0},{2,3},{3,2},{4,8},{5,9},{6,10},{7,11},{8,4},{9,5},{10,... | collective-permute-start | bytes 98312 | tf_op jit(solution)/shard_map/ppermute | solution.py:329
  29.1 2.3 %collective-permute-start.9 = (f32[8,8,128]{2,1,0:T(8,128)S(1)}, f32[8,8,128]{2,1,0:T(8,128)S(1)}, u32[]{:S(2)}, u32[]{:S(2)}) collective-permute-start(f32[8,8,128]{2,1,0:T(8,128)S(1)} %get-tuple-element.72), channel_id=1, source_target_pairs={{0,4},{1,5},{2,6},{3,7},{4,0},{5,1},{6,2},{7,3},{8,12},{9,13},{10,... | collective-permute-start | bytes 98312 | tf_op jit(solution)/shard_map/ppermute | solution.py:329
  31.5 0.0 collective-permute-done.8.y0
  31.5 0.9 collective-permute-done.9.y1
  32.3 0.1 shard_map.142
  32.4 1.1 %collective-permute-start.10 = (f32[8,8,128]{2,1,0:T(8,128)S(1)}, f32[8,8,128]{2,1,0:T(8,128)S(1)}, u32[]{:S(2)}, u32[]{:S(2)}) collective-permute-start(f32[8,8,128]{2,1,0:T(8,128)S(1)} %get-tuple-element.73), channel_id=1, source_target_pairs={{0,4},{1,2},{2,1},{3,7},{4,0},{5,6},{6,5},{7,3},{8,12},{9,10},{10,... | collective-permute-start | bytes 98312 | tf_op jit(solution)/shard_map/ppermute | solution.py:329
  33.5 0.0 collective-permute-start.11
  33.5 1.5 %shard_map.143 = (f32[4,512,128]{2,1,0:T(8,128)S(1)}, bf16[512,512]{1,0:T(8,128)(2,1)S(1)}, bf16[384,2048]{1,0:T(8,128)(2,1)S(1)}, bf16[128,128]{1,0:T(8,128)(2,1)S(1)}, bf16[256,128]{1,0:T(8,128)(2,1)S(1)}) custom-call(s32[4,3]{1,0:T(4,128)S(1)} %copy-done.3, f32[4,512,128]{2,1,0:T(8,128)S(1)} %get-tuple-element.75.preact, ...), custom_call_target="tpu_custom_call" | custom-call | tf_op jit(solution)/shard_map/pallas_call | solution.py:402
  35.0 0.3 shard_map.144
  35.4 0.0 collective-permute-done.10.z0
  35.4 0.9 %collective-permute-done.11.z1 = f32[8,8,128]{2,1,0:T(8,128)S(1)} collective-permute-done((f32[8,8,128]{2,1,0:T(8,128)S(1)}, f32[8,8,128]{2,1,0:T(8,128)S(1)}, u32[]{:S(2)}, u32[]{:S(2)}) %collective-permute-start.11) | collective-permute-done | bytes 32800 | tf_op jit(solution)/shard_map/ppermute | solution.py:329
  36.3 0.9 shard_map.145
  37.2 1.8 %collective-permute-start.14 = (f32[448,128]{1,0:T(8,128)S(1)}, f32[448,128]{1,0:T(8,128)S(1)}, u32[]{:S(2)}, u32[]{:S(2)}) collective-permute-start(f32[448,128]{1,0:T(8,128)S(1)} %get-tuple-element.95), channel_id=1, source_target_pairs={{0,4},{1,5},{2,6},{3,7},{4,0},{5,1},{6,2},{7,3},{8,12},{9,13},{10,... | collective-permute-start | bytes 688136 | tf_op jit(solution)/shard_map/ppermute | solution.py:338
  39.0 1.2 %shard_map.146 = (f32[8,8,8,128]{3,2,1,0:T(8,128)S(1)}, f32[8,8,128]{2,1,0:T(8,128)S(1)}, f32[8,8,128]{2,1,0:T(8,128)S(1)}) custom-call(s32[4,3]{1,0:T(4,128)S(1)} %copy-done.3, f32[9,8,128]{2,1,0:T(8,128)S(1)} %get-tuple-element.56.rim.refs_0_, bf16[2048,128]{1,0:T(8,128)(2,1)S(1)} %get-tuple-element.88.slopes, f32[512,128]{1,0:T(8,128)S(1)} %get-tuple-element.89.base, ...), custom_call_target="tpu_custom_call" | custom-call | tf_op jit(solution)/shard_map/pallas_call | solution.py:419
  40.1 0.0 collective-permute-done.14.got
  40.1 0.7 shard_map.147
  40.9 7.6 %all-to-all-start = ((f32[16,1,3584]{2,1,0:T(1,128)}), f32[16,1,3584]{2,1,0:T(1,128)S(1)}, u32[]{:S(2)}, u32[]{:S(2)}) async-start(f32[16,1,3584]{2,1,0:T(1,128)} %bitcast.3), calls=%async_computation | async-start | bytes 458752 | tf_op jit(solution)/shard_map/all_to_all | solution.py:358
  48.5 0.9 collective-permute-start.12
  49.4 1.7 %collective-permute-start.13 = (f32[8,8,128]{2,1,0:T(8,128)S(1)}, f32[8,8,128]{2,1,0:T(8,128)S(1)}, u32[]{:S(2)}, u32[]{:S(2)}) collective-permute-start(f32[8,8,128]{2,1,0:T(8,128)S(1)} %get-tuple-element.93), channel_id=1, source_target_pairs={{0,1},{1,0},{2,3},{3,2},{4,5},{5,4},{6,7},{7,6},{8,9},{9,8},{10,11... | collective-permute-start | bytes 98312 | tf_op jit(solution)/shard_map/ppermute | solution.py:329
  51.0 0.0 collective-permute-done.12.refs_2_.z0
  51.0 2.4 %collective-permute-done.13.refs_3_.z1 = f32[8,8,128]{2,1,0:T(8,128)S(1)} collective-permute-done((f32[8,8,128]{2,1,0:T(8,128)S(1)}, f32[8,8,128]{2,1,0:T(8,128)S(1)}, u32[]{:S(2)}, u32[]{:S(2)}) %collective-permute-start.13) | collective-permute-done | bytes 32800 | tf_op jit(solution)/shard_map/ppermute | solution.py:329
  53.4 2.9 %all-to-all-done = f32[16,1,3584]{2,1,0:T(1,128)S(1)} async-done(((f32[16,1,3584]{2,1,0:T(1,128)}), f32[16,1,3584]{2,1,0:T(1,128)S(1)}, u32[]{:S(2)}, u32[]{:S(2)}) %all-to-all-start) | async-done | bytes 229408 | tf_op jit(solution)/shard_map/all_to_all | solution.py:358
  56.3 0.7 shard_map.148
  57.0 8.2 %all-to-all-start.1 = ((f32[8,1,3584]{2,1,0:T(1,128)}), f32[8,1,3584]{2,1,0:T(1,128)S(1)}, u32[]{:S(2)}, u32[]{:S(2)}) async-start(f32[8,1,3584]{2,1,0:T(1,128)} %bitcast.5), calls=%async_computation.1 | async-start | bytes 229376 | tf_op jit(solution)/shard_map/all_to_all | solution.py:358
  65.2 1.3 %collective-permute-start.15 = (f32[8,8,128]{2,1,0:T(8,128)S(1)}, f32[8,8,128]{2,1,0:T(8,128)S(1)}, u32[]{:S(2)}, u32[]{:S(2)}) collective-permute-start(f32[8,8,128]{2,1,0:T(8,128)S(1)} %get-tuple-element.96), channel_id=1, source_target_pairs={{0,1},{1,0},{2,3},{3,2},{4,8},{5,9},{6,10},{7,11},{8,4},{9,5},{10,... | collective-permute-start | bytes 98312 | tf_op jit(solution)/shard_map/ppermute | solution.py:329
  66.5 1.3 %collective-permute-start.16 = (f32[8,8,128]{2,1,0:T(8,128)S(1)}, f32[8,8,128]{2,1,0:T(8,128)S(1)}, u32[]{:S(2)}, u32[]{:S(2)}) collective-permute-start(f32[8,8,128]{2,1,0:T(8,128)S(1)} %get-tuple-element.97), channel_id=1, source_target_pairs={{0,4},{1,5},{2,6},{3,7},{4,0},{5,1},{6,2},{7,3},{8,12},{9,13},{10,... | collective-permute-start | bytes 98312 | tf_op jit(solution)/shard_map/ppermute | solution.py:329
  67.8 0.7 collective-permute-done.15.refs_4_.y0
  68.5 0.2 collective-permute-done.16.refs_5_.y1
  68.7 4.3 %all-to-all-done.1 = f32[8,1,3584]{2,1,0:T(1,128)S(1)} async-done(((f32[8,1,3584]{2,1,0:T(1,128)}), f32[8,1,3584]{2,1,0:T(1,128)S(1)}, u32[]{:S(2)}, u32[]{:S(2)}) %all-to-all-start.1) | async-done | bytes 114720 | tf_op jit(solution)/shard_map/all_to_all | solution.py:358
  73.0 0.1 shard_map.149
  73.1 10.3 %all_to_all.27 = f32[16,1,3584]{2,1,0:T(1,128)S(1)} all-to-all(f32[16,1,3584]{2,1,0:T(1,128)S(1)} %bitcast.17), channel_id=1, replica_groups=mesh['z'=8,'yh'=2,'yl'=2,'c'=2,'x'=4] {'yh','yl','x'}, dimensions={0} | all-to-all | bytes 458752 | tf_op jit(solution)/shard_map/all_to_all | solution.py:358
  83.4 4.3 %collective-permute-start.19 = (f32[448,128]{1,0:T(8,128)S(1)}, f32[448,128]{1,0:T(8,128)S(1)}, u32[]{:S(2)}, u32[]{:S(2)}) collective-permute-start(f32[448,128]{1,0:T(8,128)S(1)} %bitcast.12), channel_id=1, source_target_pairs={{0,4},{1,5},{2,6},{3,7},{4,0},{5,1},{6,2},{7,3},{8,12},{9,13},{10,... | collective-permute-start | bytes 688136 | tf_op jit(solution)/shard_map/ppermute | solution.py:338
  87.7 0.0 collective-permute-start.17
  87.7 3.0 %collective-permute-start.18 = (f32[8,8,128]{2,1,0:T(8,128)S(1)}, f32[8,8,128]{2,1,0:T(8,128)S(1)}, u32[]{:S(2)}, u32[]{:S(2)}) collective-permute-start(f32[8,8,128]{2,1,0:T(8,128)S(1)} %get-tuple-element.100), channel_id=1, source_target_pairs={{0,16},{1,17},{2,18},{3,19},{4,20},{5,21},{6,22},{7,23},{8,24},{9,... | collective-permute-start | bytes 98312 | tf_op jit(solution)/shard_map/ppermute | solution.py:329
  90.7 1.1 %shard_map.152 = bf16[2048,128]{1,0:T(8,128)(2,1)} custom-call(bf16[2048,128]{1,0:T(8,128)(2,1)S(1)} %get-tuple-element.88.slopes, bf16[384,128]{1,0:T(8,128)(2,1)S(1)} %get-tuple-element.78.w_in), custom_call_target="tpu_custom_call" | custom-call | tf_op jit(solution)/shard_map/pallas_call | solution.py:422
  91.8 0.0 collective-permute-done.19.other
  91.8 1.0 %shard_map.150 = (f32[384,128]{1,0:T(8,128)}, f32[128,128]{1,0:T(8,128)}, f32[256,128]{1,0:T(8,128)}, f32[128,128]{1,0:T(8,128)}) custom-call(f32[9,8,128]{2,1,0:T(8,128)S(1)} %get-tuple-element.56.rim.refs_0_, f32[448,128]{1,0:T(8,128)S(1)} %bitcast.13, f32[448,128]{1,0:T(8,128)S(1)} %collective-permute-done.19.other), custom_call_target="tpu_custom_call" | custom-call | tf_op jit(solution)/shard_map/pallas_call | solution.py:424
  92.8 0.0 collective-permute-done.17.x0
  92.8 0.0 collective-permute-done.18.x1
  92.8 0.8 shard_map.151
  (11 shorter events, 0.0 us)
Async XLA Ops:
  0.6 16.3 %copy-start.4 = (s32[8,8,8]{2,1,0:T(8,128)S(1)}, s32[8,8,8]{2,1,0:T(8,128)}, u32[]{:S(2)}) copy-start(s32[8,8,8]{2,1,0:T(8,128)} %param.11) | copy-start | bytes 6148
  0.6 16.4 %copy-start.1 = (bf16[8,8,8,128]{3,2,1,0:T(8,128)(2,1)S(1)}, bf16[8,8,8,128]{3,2,1,0:T(8,128)(2,1)}, u32[]{:S(2)}) copy-start(bf16[8,8,8,128]{3,2,1,0:T(8,128)(2,1)} %param.17) | copy-start | bytes 393220
  0.7 16.4 %copy-start = (bf16[256,128]{1,0:T(8,128)(2,1)S(1)}, bf16[256,128]{1,0:T(8,128)(2,1)}, u32[]{:S(2)}) copy-start(bf16[256,128]{1,0:T(8,128)(2,1)} %w_in.5) | copy-start | bytes 196612
  0.7 16.4 %copy-start.2 = (bf16[128,128]{1,0:T(8,128)(2,1)S(1)}, bf16[128,128]{1,0:T(8,128)(2,1)}, u32[]{:S(2)}) copy-start(bf16[128,128]{1,0:T(8,128)(2,1)} %w_out.1) | copy-start | bytes 98308
  3.1 5.2 %collective-permute-start = (f32[8,8,128]{2,1,0:T(8,128)S(1)}, f32[8,8,128]{2,1,0:T(8,128)S(1)}, u32[]{:S(2)}, u32[]{:S(2)}) collective-permute-start(f32[8,8,128]{2,1,0:T(8,128)S(1)} %get-tuple-element.58), channel_id=1, source_target_pairs={{0,4},{1,5},{2,6},{3,7},{4,0},{5,1},{6,2},{7,3},{8,12},{9,13},{10,... | collective-permute-start | bytes 98312 | tf_op jit(solution)/shard_map/ppermute | solution.py:329
  6.4 4.3 %collective-permute-start.1 = (f32[8,8,128]{2,1,0:T(8,128)S(1)}, f32[8,8,128]{2,1,0:T(8,128)S(1)}, u32[]{:S(2)}, u32[]{:S(2)}) collective-permute-start(f32[8,8,128]{2,1,0:T(8,128)S(1)} %get-tuple-element.59), channel_id=1, source_target_pairs={{0,16},{1,17},{2,18},{3,19},{4,20},{5,21},{6,22},{7,23},{8,24},{9,... | collective-permute-start | bytes 98312 | tf_op jit(solution)/shard_map/ppermute | solution.py:329
  10.7 3.7 %collective-permute-start.2 = (f32[8,8,128]{2,1,0:T(8,128)S(1)}, f32[8,8,128]{2,1,0:T(8,128)S(1)}, u32[]{:S(2)}, u32[]{:S(2)}) collective-permute-start(f32[8,8,128]{2,1,0:T(8,128)S(1)} %get-tuple-element.60), channel_id=1, source_target_pairs={{0,1},{1,0},{2,3},{3,2},{4,8},{5,9},{6,10},{7,11},{8,4},{9,5},{10,... | collective-permute-start | bytes 98312 | tf_op jit(solution)/shard_map/ppermute | solution.py:329
  12.7 1.6 %collective-permute-start.3 = (f32[8,8,128]{2,1,0:T(8,128)S(1)}, f32[8,8,128]{2,1,0:T(8,128)S(1)}, u32[]{:S(2)}, u32[]{:S(2)}) collective-permute-start(f32[8,8,128]{2,1,0:T(8,128)S(1)} %get-tuple-element.61), channel_id=1, source_target_pairs={{0,4},{1,5},{2,6},{3,7},{4,0},{5,1},{6,2},{7,3},{8,12},{9,13},{10,... | collective-permute-start | bytes 98312 | tf_op jit(solution)/shard_map/ppermute | solution.py:329
  14.4 19.1 %copy-start.3 = (s32[4,3]{1,0:T(4,128)S(1)}, s32[4,3]{1,0:T(4,128)}, u32[]{:S(2)}) copy-start(s32[4,3]{1,0:T(4,128)} %offs.3) | copy-start | bytes 148
  14.5 2.9 %collective-permute-start.4 = (f32[8,8,128]{2,1,0:T(8,128)S(1)}, f32[8,8,128]{2,1,0:T(8,128)S(1)}, u32[]{:S(2)}, u32[]{:S(2)}) collective-permute-start(f32[8,8,128]{2,1,0:T(8,128)S(1)} %get-tuple-element.62), channel_id=1, source_target_pairs={{0,4},{1,2},{2,1},{3,7},{4,0},{5,6},{6,5},{7,3},{8,12},{9,10},{10,... | collective-permute-start | bytes 98312 | tf_op jit(solution)/shard_map/ppermute | solution.py:329
  16.1 2.8 %collective-permute-start.5 = (f32[8,8,128]{2,1,0:T(8,128)S(1)}, f32[8,8,128]{2,1,0:T(8,128)S(1)}, u32[]{:S(2)}, u32[]{:S(2)}) collective-permute-start(f32[8,8,128]{2,1,0:T(8,128)S(1)} %get-tuple-element.63), channel_id=1, source_target_pairs={{0,1},{1,0},{2,3},{3,2},{4,5},{5,4},{6,7},{7,6},{8,9},{9,8},{10,11... | collective-permute-start | bytes 98312 | tf_op jit(solution)/shard_map/ppermute | solution.py:329
  19.4 5.3 %collective-permute-start.6 = (f32[8,8,128]{2,1,0:T(8,128)S(1)}, f32[8,8,128]{2,1,0:T(8,128)S(1)}, u32[]{:S(2)}, u32[]{:S(2)}) collective-permute-start(f32[8,8,128]{2,1,0:T(8,128)S(1)} %get-tuple-element.69), channel_id=1, source_target_pairs={{0,4},{1,5},{2,6},{3,7},{4,0},{5,1},{6,2},{7,3},{8,12},{9,13},{10,... | collective-permute-start | bytes 98312 | tf_op jit(solution)/shard_map/ppermute | solution.py:329
  21.2 4.9 %collective-permute-start.7 = (f32[8,8,128]{2,1,0:T(8,128)S(1)}, f32[8,8,128]{2,1,0:T(8,128)S(1)}, u32[]{:S(2)}, u32[]{:S(2)}) collective-permute-start(f32[8,8,128]{2,1,0:T(8,128)S(1)} %get-tuple-element.70), channel_id=1, source_target_pairs={{0,16},{1,17},{2,18},{3,19},{4,20},{5,21},{6,22},{7,23},{8,24},{9,... | collective-permute-start | bytes 98312 | tf_op jit(solution)/shard_map/ppermute | solution.py:329
  26.1 5.4 %collective-permute-start.8 = (f32[8,8,128]{2,1,0:T(8,128)S(1)}, f32[8,8,128]{2,1,0:T(8,128)S(1)}, u32[]{:S(2)}, u32[]{:S(2)}) collective-permute-start(f32[8,8,128]{2,1,0:T(8,128)S(1)} %get-tuple-element.71), channel_id=1, source_target_pairs={{0,1},{1,0},{2,3},{3,2},{4,8},{5,9},{6,10},{7,11},{8,4},{9,5},{10,... | collective-permute-start | bytes 98312 | tf_op jit(solution)/shard_map/ppermute | solution.py:329
  29.1 3.2 %collective-permute-start.9 = (f32[8,8,128]{2,1,0:T(8,128)S(1)}, f32[8,8,128]{2,1,0:T(8,128)S(1)}, u32[]{:S(2)}, u32[]{:S(2)}) collective-permute-start(f32[8,8,128]{2,1,0:T(8,128)S(1)} %get-tuple-element.72), channel_id=1, source_target_pairs={{0,4},{1,5},{2,6},{3,7},{4,0},{5,1},{6,2},{7,3},{8,12},{9,13},{10,... | collective-permute-start | bytes 98312 | tf_op jit(solution)/shard_map/ppermute | solution.py:329
  32.4 2.9 %collective-permute-start.10 = (f32[8,8,128]{2,1,0:T(8,128)S(1)}, f32[8,8,128]{2,1,0:T(8,128)S(1)}, u32[]{:S(2)}, u32[]{:S(2)}) collective-permute-start(f32[8,8,128]{2,1,0:T(8,128)S(1)} %get-tuple-element.73), channel_id=1, source_target_pairs={{0,4},{1,2},{2,1},{3,7},{4,0},{5,6},{6,5},{7,3},{8,12},{9,10},{10,... | collective-permute-start | bytes 98312 | tf_op jit(solution)/shard_map/ppermute | solution.py:329
  33.5 2.8 %collective-permute-start.11 = (f32[8,8,128]{2,1,0:T(8,128)S(1)}, f32[8,8,128]{2,1,0:T(8,128)S(1)}, u32[]{:S(2)}, u32[]{:S(2)}) collective-permute-start(f32[8,8,128]{2,1,0:T(8,128)S(1)} %get-tuple-element.74), channel_id=1, source_target_pairs={{0,1},{1,0},{2,3},{3,2},{4,5},{5,4},{6,7},{7,6},{8,9},{9,8},{10,11... | collective-permute-start | bytes 98312 | tf_op jit(solution)/shard_map/ppermute | solution.py:329
  37.2 2.9 %collective-permute-start.14 = (f32[448,128]{1,0:T(8,128)S(1)}, f32[448,128]{1,0:T(8,128)S(1)}, u32[]{:S(2)}, u32[]{:S(2)}) collective-permute-start(f32[448,128]{1,0:T(8,128)S(1)} %get-tuple-element.95), channel_id=1, source_target_pairs={{0,4},{1,5},{2,6},{3,7},{4,0},{5,1},{6,2},{7,3},{8,12},{9,13},{10,... | collective-permute-start | bytes 688136 | tf_op jit(solution)/shard_map/ppermute | solution.py:338
  40.9 15.5 %all-to-all-start = ((f32[16,1,3584]{2,1,0:T(1,128)}), f32[16,1,3584]{2,1,0:T(1,128)S(1)}, u32[]{:S(2)}, u32[]{:S(2)}) async-start(f32[16,1,3584]{2,1,0:T(1,128)} %bitcast.3), calls=%async_computation | async-start | bytes 458752 | tf_op jit(solution)/shard_map/all_to_all | solution.py:358
  48.5 2.6 %collective-permute-start.12 = (f32[8,8,128]{2,1,0:T(8,128)S(1)}, f32[8,8,128]{2,1,0:T(8,128)S(1)}, u32[]{:S(2)}, u32[]{:S(2)}) collective-permute-start(f32[8,8,128]{2,1,0:T(8,128)S(1)} %get-tuple-element.92.after), channel_id=1, source_target_pairs={{0,4},{1,2},{2,1},{3,7},{4,0},{5,6},{6,5},{7,3},{8,12},{9,10},{10,... | collective-permute-start | bytes 98312 | tf_op jit(solution)/shard_map/ppermute | solution.py:329
  49.4 4.0 %collective-permute-start.13 = (f32[8,8,128]{2,1,0:T(8,128)S(1)}, f32[8,8,128]{2,1,0:T(8,128)S(1)}, u32[]{:S(2)}, u32[]{:S(2)}) collective-permute-start(f32[8,8,128]{2,1,0:T(8,128)S(1)} %get-tuple-element.93), channel_id=1, source_target_pairs={{0,1},{1,0},{2,3},{3,2},{4,5},{5,4},{6,7},{7,6},{8,9},{9,8},{10,11... | collective-permute-start | bytes 98312 | tf_op jit(solution)/shard_map/ppermute | solution.py:329
  57.0 16.0 %all-to-all-start.1 = ((f32[8,1,3584]{2,1,0:T(1,128)}), f32[8,1,3584]{2,1,0:T(1,128)S(1)}, u32[]{:S(2)}, u32[]{:S(2)}) async-start(f32[8,1,3584]{2,1,0:T(1,128)} %bitcast.5), calls=%async_computation.1 | async-start | bytes 229376 | tf_op jit(solution)/shard_map/all_to_all | solution.py:358
  65.2 3.3 %collective-permute-start.15 = (f32[8,8,128]{2,1,0:T(8,128)S(1)}, f32[8,8,128]{2,1,0:T(8,128)S(1)}, u32[]{:S(2)}, u32[]{:S(2)}) collective-permute-start(f32[8,8,128]{2,1,0:T(8,128)S(1)} %get-tuple-element.96), channel_id=1, source_target_pairs={{0,1},{1,0},{2,3},{3,2},{4,8},{5,9},{6,10},{7,11},{8,4},{9,5},{10,... | collective-permute-start | bytes 98312 | tf_op jit(solution)/shard_map/ppermute | solution.py:329
  66.5 2.2 %collective-permute-start.16 = (f32[8,8,128]{2,1,0:T(8,128)S(1)}, f32[8,8,128]{2,1,0:T(8,128)S(1)}, u32[]{:S(2)}, u32[]{:S(2)}) collective-permute-start(f32[8,8,128]{2,1,0:T(8,128)S(1)} %get-tuple-element.97), channel_id=1, source_target_pairs={{0,4},{1,5},{2,6},{3,7},{4,0},{5,1},{6,2},{7,3},{8,12},{9,13},{10,... | collective-permute-start | bytes 98312 | tf_op jit(solution)/shard_map/ppermute | solution.py:329
  83.4 8.4 %collective-permute-start.19 = (f32[448,128]{1,0:T(8,128)S(1)}, f32[448,128]{1,0:T(8,128)S(1)}, u32[]{:S(2)}, u32[]{:S(2)}) collective-permute-start(f32[448,128]{1,0:T(8,128)S(1)} %bitcast.12), channel_id=1, source_target_pairs={{0,4},{1,5},{2,6},{3,7},{4,0},{5,1},{6,2},{7,3},{8,12},{9,13},{10,... | collective-permute-start | bytes 688136 | tf_op jit(solution)/shard_map/ppermute | solution.py:338
  87.7 5.1 %collective-permute-start.17 = (f32[8,8,128]{2,1,0:T(8,128)S(1)}, f32[8,8,128]{2,1,0:T(8,128)S(1)}, u32[]{:S(2)}, u32[]{:S(2)}) collective-permute-start(f32[8,8,128]{2,1,0:T(8,128)S(1)} %get-tuple-element.99), channel_id=1, source_target_pairs={{0,4},{1,5},{2,6},{3,7},{4,0},{5,1},{6,2},{7,3},{8,12},{9,13},{10,... | collective-permute-start | bytes 98312 | tf_op jit(solution)/shard_map/ppermute | solution.py:329
  87.7 5.1 %collective-permute-start.18 = (f32[8,8,128]{2,1,0:T(8,128)S(1)}, f32[8,8,128]{2,1,0:T(8,128)S(1)}, u32[]{:S(2)}, u32[]{:S(2)}) collective-permute-start(f32[8,8,128]{2,1,0:T(8,128)S(1)} %get-tuple-element.100), channel_id=1, source_target_pairs={{0,16},{1,17},{2,18},{3,19},{4,20},{5,21},{6,22},{7,23},{8,24},{9,... | collective-permute-start | bytes 98312 | tf_op jit(solution)/shard_map/ppermute | solution.py:329

commit v9 on v6

--- a/solution.py
+++ b/solution.py
@@ -27,7 +27,8 @@
 WORK = pltpu.VMEM(CUBE, F32)
 
 GX, GY, GZ = ("z", "yh"), ("yl", "c"), ("x",)
-NEAR, FAR = ("yh", "yl", "x"), ("z",)
+NEAR, FAR, BACK = ("yh", "yl", "x"), ("z",), ("yh", "yl", "c", "x")
+GROUPS = 4
 
 
 def call(body, outs, specs, name, scratch=()):
@@ -68,10 +69,12 @@
     return moved.reshape(N, W)
 
 
-def inside(offs, k):
+def inside(offs, k, rims=False):
     ok = None
+    shape = (2, *FACE) if rims else CUBE
     for which in range(3):
-        at = lax.broadcasted_iota(jnp.int32, CUBE, which) + offs[k, which]
+        at = lax.broadcasted_iota(jnp.int32, shape, which)
+        at = (at * (B - 1) if rims and which == 0 else at) + offs[k, which]
         one = (at >= 0) & (at < B)
         ok = one if ok is None else ok & one
     return ok
@@ -89,11 +92,13 @@
             rim[3 * d + i] = jnp.full((B, W), flag.astype(F32))
 
 
-def forward_kernel(
-    nodes_h, edges_h, w_in_h, w_out_h, offs_h,
-    local, xa, xb, preact, hidden, nodes, edges, w_in, w_out, rim,
-    pad, offs, sems,
+RIMS = (0, (B - 1) * B * B)
+
+
+def first_rims_kernel(
+    nodes_h, edges_h, w_in_h, w_out_h, offs_h, xa, xb, rim, nodes, edges, w_in, w_out, pad, offs, sems
 ):
+    plane = B * B
     pairs = [(nodes_h, nodes), (w_in_h, w_in), (offs_h, offs), (w_out_h, w_out)]
     pairs += [(edges_h.at[k], edges.at[k]) for k in range(K)]
     copies = [pltpu.make_async_copy(a, b, sems.at[i]) for i, (a, b) in enumerate(pairs)]
@@ -104,23 +109,40 @@
         copy.wait()
     node = nodes[...]
     fill_ring(pad, dot(node, w_in[:W]).reshape(CUBE))
+    rims = jnp.concatenate([node[at : at + plane] for at in RIMS], axis=0)
+    receiver = dot(rims, w_in[W : 2 * W])
+    copies[3].wait()
+    total = jnp.zeros((2 * plane, W), F32)
+    for k in range(K):
+        copies[4 + k].wait()
+        o0, o1, o2 = offs[k, 0], offs[k, 1], offs[k, 2]
+        sent = jnp.concatenate([pad[pl.ds(1 + at + o0, 1), pl.ds(1 + o1, B)] for at in (0, B - 1)], axis=0)
+        sent = pltpu.roll(sent.reshape(2 * B, B, W), lax.rem(B - o2, B), 1).reshape(2 * plane, W)
+        edge = jnp.concatenate([edges[k, at : at + plane] for at in RIMS], axis=0)
+        pre = sent + receiver + dot(edge, w_in[2 * W :])
+        act = (pre * jax.nn.sigmoid(pre)).reshape(2, B, B, W)
+        kept = jnp.where(inside(offs, k, True), act, 0.0).reshape(2 * plane, W).astype(BF16)
+        total = total + dot(kept, w_out[...])
+    total = total.reshape(2, B, B, W)
+    send(rim, 0, total[0], total[1], xa, xb)
+
+
+def forward_kernel(offs, nodes, edges, w_in, w_out, after, local, preact, hidden, pad):
+    node = nodes[...]
+    fill_ring(pad, dot(node, w_in[:W]).reshape(CUBE))
     receiver = dot(node, w_in[W : 2 * W])
-    copies[3].wait()
     total = jnp.zeros((N, W), F32)
     for k in range(K):
-        copies[4 + k].wait()
         pre = ring_shift(pad, offs[k, 0], offs[k, 1], offs[k, 2]) + receiver + dot(edges[k], w_in[2 * W :])
         preact[k] = pre
         act = (pre * jax.nn.sigmoid(pre)).reshape(CUBE)
         kept = jnp.where(inside(offs, k), act, 0.0).reshape(N, W).astype(BF16)
         hidden[k] = kept
         total = total + dot(kept, w_out[...])
-    total = total.reshape(CUBE)
-    local[...] = total
-    send(rim, 0, total[0], total[B - 1], xa, xb)
-
-
-def prepare_node_kernel(nodes, cot, w_in, w_out, pre, upstream, w_back):
+    local[...] = total.reshape(CUBE)
+
+
+def prepare_node_kernel(nodes, cot, w_in, w_out, after, pre, upstream, w_back):
     pre[...] = dot(nodes[...], w_in[:W])
     upstream[...] = dot_t(cot[...], w_out[...])
     w_back[...] = w_in[W:].T
@@ -159,9 +181,12 @@
     b[...] = jnp.where(even, hi, lo)
 
 
-def own(rim, top, bottom):
-    first = jnp.broadcast_to(rim[3, :1, :], top.shape) > 0
-    return jnp.where(first, top, bottom)
+def own(rim, grads, out, first):
+    step = grads.shape[0] // (2 * GROUPS)
+    mask = jnp.broadcast_to(rim[3, :1, :], (step, W)) > 0
+    for g in range(GROUPS):
+        even, odd = grads[2 * g * step : (2 * g + 1) * step], grads[(2 * g + 1) * step : (2 * g + 2) * step]
+        out[g * step : (g + 1) * step] = jnp.where(mask, even, odd) if first else jnp.where(mask, odd, even)
 
 
 def add_kernel(keep, got, after, out):
@@ -263,9 +288,8 @@
     grads[3 * W : 4 * W] = (outer[:W] + outer[W : 2 * W]) + (outer[2 * W : 3 * W] + outer[3 * W :])
     grads[4 * W :] = node_grads[...]
     grads[: 3 * W] = dot(left[...], slopes[...])
-    half = keep.shape[0]
-    keep[...] = own(rim, grads[:half], grads[half:])
-    give[...] = own(rim, grads[half:], grads[:half])
+    own(rim, grads, keep, True)
+    own(rim, grads, give, False)
 
 
 def node_part_kernel(offs, rim, slopes, base, w_back, local, za, zb, pad):
@@ -305,8 +329,8 @@
     faces(*refs[:-2], refs[-1])
 
 
-def clip_kernel(rim, mine, other, edge_in, edge_out, node_in, node_out):
-    total = jnp.concatenate([own(rim, mine[...], other[...]), own(rim, other[...], mine[...])], axis=0)
+def clip_kernel(grads, edge_in, edge_out, node_in, node_out):
+    total = grads[...]
     squares = jnp.sum(jnp.sum(total * total, axis=0, keepdims=True), axis=1, keepdims=True)
     factor = math.sqrt(7 * W * W) / jnp.sqrt(squares)
     edge_in[...] = total[: 3 * W] * factor
@@ -358,7 +382,7 @@
     return lax.all_to_all(rows.reshape(lax.axis_size(axes), -1), axes, 0, 0, tiled=True).reshape(-1, W)
 
 
-def arrivals_and_sum(rim, field, za, zb, keep, give, edge_grad):
+def arrivals_and_sum(rim, field, za, zb, keep, give):
     near, far = lax.axis_size(NEAR), lax.axis_size(FAR)
     rows = keep.shape[0] // near
     (half,) = call(add_kernel, [(keep.shape, F32)], [VMEM] * 3, "add_core")(keep, other_core(give), za)
@@ -374,16 +398,14 @@
     got = swap(spread, FAR)
     y = exchange(a, b, 1)
     a, b, spread = call(
-        functools.partial(fold_with_faces_kernel, x_faces_after_y, rows, far // 2, near // 2),
-        FACES + [((rows * near, W), F32)],
+        functools.partial(fold_with_faces_kernel, x_faces_after_y, rows, far // 2, near),
+        FACES + [((2 * rows * near, W), F32)],
         [VMEM] * 7,
         "after_y_fold",
         [BOTH],
     )(got, rim, field, *z, *y)
-    mine = swap(spread, NEAR)
-    x = exchange(a, b, 0)
-    mine, edge_grad, *x = lax.optimization_barrier((mine, edge_grad, *x))
-    return (*z, *y, *x), (mine, other_core(mine)), edge_grad
+    total = swap(spread, BACK)
+    return (*z, *y, *exchange(a, b, 0)), total
 
 
 def on_device(node_feat, edge_feat, copies, offsets, w_edge_in, w_edge_out, w_node_in, w_node_out, node_cot):
@@ -392,16 +414,19 @@
     square = ((W, W), BF16)
     many = ((K, N, W), BF16)
 
-    local, xa, xb, preact, hidden, nodes, edges, w_in, w_out, rim = call(
-        forward_kernel,
-        [(CUBE, F32)] + FACES + [((K, N, W), F32), many, ((N, W), BF16), many, ((3 * W, W), BF16), square, ((9, B, W), F32)],
+    xa, xb, rim, nodes, edges, w_in, w_out = call(
+        first_rims_kernel,
+        FACES + [((9, B, W), F32), ((N, W), BF16), many, ((3 * W, W), BF16), square],
         [HBM] * 5,
-        "forward",
+        "first_rims",
         [PAD, pltpu.SMEM((K, 3), jnp.int32), pltpu.SemaphoreType.DMA((4 + K,))],
     )(*map(in_hbm, (node_feat.reshape(N, W), edge_feat.reshape(K, N, W), w_edge_in, w_edge_out, offsets)))
+    local, preact, hidden = call(
+        forward_kernel, [(CUBE, F32), ((K, N, W), F32), many], [SMEM] + [VMEM] * 5, "forward", [PAD]
+    )(offsets, nodes, edges, w_in, w_out, rim)
     begun, upstream, w_node_back = call(
-        prepare_node_kernel, [((N, W), F32), ((N, W), F32), square], [VMEM] * 4, "prepare_node"
-    )(nodes, cot, w_node_in, w_node_out)
+        prepare_node_kernel, [((N, W), F32), ((N, W), F32), square], [VMEM] * 5, "prepare_node"
+    )(nodes, cot, w_node_in, w_node_out, local)
     arrived = arrivals(rim, local, xa, xb, "_1")
     dact, hidden_t, left, w_out_t, w_back = call(
         prepare_edge_kernel,
@@ -429,10 +454,10 @@
         node_part_kernel, [(CUBE, F32)] + FACES, [SMEM] + [VMEM] * 4, "node_part", [PAD]
     )(offsets, rim, slopes, base, w_back)
     (edge_grad,) = call(edge_grad_kernel, [((K * N, W), BF16)], [VMEM] * 2, "edge_grad")(slopes, w_in)
-    arrived, halves, edge_grad = arrivals_and_sum(rim, local, za, zb, keep, give, edge_grad)
+    arrived, total = arrivals_and_sum(rim, local, za, zb, keep, give)
     clipped = call(
-        clip_kernel, [((3 * W, W), F32), ((W, W), F32), ((2 * W, W), F32), ((W, W), F32)], [VMEM] * 3, "clip"
-    )(rim, *halves)
+        clip_kernel, [((3 * W, W), F32), ((W, W), F32), ((2 * W, W), F32), ((W, W), F32)], [VMEM], "clip"
+    )(total)
     (node_grad,) = call(last_kernel, [((N, W), BF16)], [VMEM] * 8, "last", [WORK])(rim, local, *arrived)
     return (node_grad.reshape(node_feat.shape), edge_grad.reshape(edge_feat.shape), *clipped)
 

time: 91.5 us -> 92.6 us (1.012)
  Pallas kernels: 12.1 us -> 13.2 us
    all_to_all x3, waiting for transfers between devices: 7.25 us -> 11.4 us  [swap(): lax.all_to_all(rows.reshape(lax.axis_size(axes), -1), axes, 0, 0, tiled=T...]
    ppermute x18, waiting for transfers between devices: 14.9 us -> 10.9 us  [exchange(): lax.ppermute(face, GX + GY + GZ, [(rank, ranks[to]) for rank, to in enume...]
    ppermute x2 -> x1, starting transfers between devices: 5.69 us -> 1.77 us  [other_core(): lax.ppermute(half, GX + GY + GZ, [(rank, rank ^ step) for rank in range(c...]
    all_to_all x3, starting transfers between devices: 19.3 us -> 22.5 us  [swap(): lax.all_to_all(rows.reshape(lax.axis_size(axes), -1), axes, 0, 0, tiled=T...]
    pallas_call x1 -> x2, Pallas kernels: 2.42 us -> 3.53 us  [the longest x1 2.17 us: on_device(): call(first_rims_kernel, FACES + [((9, B, W), F32), ((N, W), BF16), many,...]
  transfers between devices with their start and end apart: 23 -> 22, of which waited for: 13 -> 13; matrix products, arithmetic and copies ran while one was open for 0% -> 0% of each run, Pallas kernels for 6% -> 7%
where the time goes in v9:
time: 92.6 us; the launch traced here: 92.1 us
  starting transfers between devices  54.8 us (59%)
  waiting for transfers between devices  22.3 us (24%)
  Pallas kernels  13.2 us (14%)
    ppermute x18, starting transfers between devices, exchange(): lax.ppermute(face, GX + GY + GZ, [(rank, ranks[to]) for rank, to in enume...  30.5 us
    all_to_all x3, starting transfers between devices, swap(): lax.all_to_all(rows.reshape(lax.axis_size(axes), -1), axes, 0, 0, tiled=T...  22.5 us
    all_to_all x3, waiting for transfers between devices, swap(): lax.all_to_all(rows.reshape(lax.axis_size(axes), -1), axes, 0, 0, tiled=T...  11.4 us
    ppermute x18, waiting for transfers between devices, exchange(): lax.ppermute(face, GX + GY + GZ, [(rank, ranks[to]) for rank, to in enume...  10.9 us
    pallas_call x1, Pallas kernels, on_device(): call(first_rims_kernel, FACES + [((9, B, W), F32), ((N, W), BF16), many,...  2.17 us
  transfers between devices with their start and end apart: 22, of which 13 were waited for; matrix products, arithmetic and copies ran while one was open for 0% of the time, Pallas kernels for 7%

profile of v9, /device:TPU:1, one launch (start us, length us, event | category | flops | bytes accessed | tf_op | source)
XLA Modules:
  0.0 92.1 jit_solution(10433177165258606559)
XLA Ops:
  0.7 2.2 %first_rims.1 = (f32[8,8,128]{2,1,0:T(8,128)S(1)}, f32[8,8,128]{2,1,0:T(8,128)S(1)}, f32[9,8,128]{2,1,0:T(8,128)S(1)}, bf16[512,128]{1,0:T(8,128)(2,1)S(1)}, bf1...) custom-call(bf16[512,128]{1,0:T(8,128)(2,1)} %bitcast.19, ...), custom_call_target="tpu_custom_call" | custom-call | tf_op jit(solution)/shard_map/first_rims/pallas_call | solution.py:417
  2.8 3.3 %collective-permute-start = (f32[8,8,128]{2,1,0:T(8,128)S(1)}, f32[8,8,128]{2,1,0:T(8,128)S(1)}, u32[]{:S(2)}, u32[]{:S(2)}) collective-permute-start(f32[8,8,128]{2,1,0:T(8,128)S(1)} %get-tuple-element.62), channel_id=1, source_target_pairs={{0,4},{1,5},{2,6},{3,7},{4,0},{5,1},{6,2},{7,3},{8,12},{9,13},{10,... | collective-permute-start | bytes 98312 | tf_op jit(solution)/shard_map/ppermute | solution.py:353
  6.1 1.9 %collective-permute-start.1 = (f32[8,8,128]{2,1,0:T(8,128)S(1)}, f32[8,8,128]{2,1,0:T(8,128)S(1)}, u32[]{:S(2)}, u32[]{:S(2)}) collective-permute-start(f32[8,8,128]{2,1,0:T(8,128)S(1)} %get-tuple-element.63), channel_id=1, source_target_pairs={{0,16},{1,17},{2,18},{3,19},{4,20},{5,21},{6,22},{7,23},{8,24},{9,... | collective-permute-start | bytes 98312 | tf_op jit(solution)/shard_map/ppermute | solution.py:353
  8.1 0.7 copy-done.3
  8.8 1.4 %forward.1 = (f32[8,8,8,128]{3,2,1,0:T(8,128)S(1)}, f32[4,512,128]{2,1,0:T(8,128)S(1)}, bf16[4,512,128]{2,1,0:T(8,128)(2,1)S(1)}) custom-call(s32[4,3]{1,0:T(4,128)S(1)} %copy-done.3, bf16[512,128]{1,0:T(8,128)(2,1)S(1)} %get-tuple-element.57.nodes, bf16[4,512,128]{2,1,0:T(8,128)(2,1)S(1)} %get-tuple-element.58.edges, ...), custom_call_target="tpu_custom_call" | custom-call | tf_op jit(solution)/shard_map/forward/pallas_call | solution.py:424
  10.1 0.0 collective-permute-done.x0
  10.1 0.3 collective-permute-done.1.x1
  10.4 2.3 %collective-permute-start.2 = (f32[8,8,128]{2,1,0:T(8,128)S(1)}, f32[8,8,128]{2,1,0:T(8,128)S(1)}, u32[]{:S(2)}, u32[]{:S(2)}) collective-permute-start(f32[8,8,128]{2,1,0:T(8,128)S(1)} %get-tuple-element.64), channel_id=1, source_target_pairs={{0,1},{1,0},{2,3},{3,2},{4,8},{5,9},{6,10},{7,11},{8,4},{9,5},{10,... | collective-permute-start | bytes 98312 | tf_op jit(solution)/shard_map/ppermute | solution.py:353
  12.7 0.3 collective-permute-start.3
  13.0 1.3 %collective-permute-done.2.y0 = f32[8,8,128]{2,1,0:T(8,128)S(1)} collective-permute-done((f32[8,8,128]{2,1,0:T(8,128)S(1)}, f32[8,8,128]{2,1,0:T(8,128)S(1)}, u32[]{:S(2)}, u32[]{:S(2)}) %collective-permute-start.2) | collective-permute-done | bytes 32800 | tf_op jit(solution)/shard_map/ppermute | solution.py:353
  14.3 0.0 collective-permute-done.3.y1
  14.3 0.1 after_y_1.1
  14.4 1.5 %collective-permute-start.4 = (f32[8,8,128]{2,1,0:T(8,128)S(1)}, f32[8,8,128]{2,1,0:T(8,128)S(1)}, u32[]{:S(2)}, u32[]{:S(2)}) collective-permute-start(f32[8,8,128]{2,1,0:T(8,128)S(1)} %get-tuple-element.66), channel_id=1, source_target_pairs={{0,4},{1,2},{2,1},{3,7},{4,0},{5,6},{6,5},{7,3},{8,12},{9,10},{10,... | collective-permute-start | bytes 98312 | tf_op jit(solution)/shard_map/ppermute | solution.py:353
  15.9 1.0 %collective-permute-start.5 = (f32[8,8,128]{2,1,0:T(8,128)S(1)}, f32[8,8,128]{2,1,0:T(8,128)S(1)}, u32[]{:S(2)}, u32[]{:S(2)}) collective-permute-start(f32[8,8,128]{2,1,0:T(8,128)S(1)} %get-tuple-element.67), channel_id=1, source_target_pairs={{0,1},{1,0},{2,3},{3,2},{4,5},{5,4},{6,7},{7,6},{8,9},{9,8},{10,11... | collective-permute-start | bytes 98312 | tf_op jit(solution)/shard_map/ppermute | solution.py:353
  16.9 0.0 copy-start.4
  16.9 0.1 div.16
  17.0 0.2 prepare_node.1
  17.3 0.0 collective-permute-done.4.z0
  17.3 1.4 %collective-permute-done.5.z1 = f32[8,8,128]{2,1,0:T(8,128)S(1)} collective-permute-done((f32[8,8,128]{2,1,0:T(8,128)S(1)}, f32[8,8,128]{2,1,0:T(8,128)S(1)}, u32[]{:S(2)}, u32[]{:S(2)}) %collective-permute-start.5) | collective-permute-done | bytes 32800 | tf_op jit(solution)/shard_map/ppermute | solution.py:353
  18.6 0.1 broadcast_in_dim.2.inverse
  18.7 0.4 node.1
  19.2 1.9 %collective-permute-start.6 = (f32[8,8,128]{2,1,0:T(8,128)S(1)}, f32[8,8,128]{2,1,0:T(8,128)S(1)}, u32[]{:S(2)}, u32[]{:S(2)}) collective-permute-start(f32[8,8,128]{2,1,0:T(8,128)S(1)} %get-tuple-element.72), channel_id=1, source_target_pairs={{0,4},{1,5},{2,6},{3,7},{4,0},{5,1},{6,2},{7,3},{8,12},{9,13},{10,... | collective-permute-start | bytes 98312 | tf_op jit(solution)/shard_map/ppermute | solution.py:353
  21.1 3.4 %collective-permute-start.7 = (f32[8,8,128]{2,1,0:T(8,128)S(1)}, f32[8,8,128]{2,1,0:T(8,128)S(1)}, u32[]{:S(2)}, u32[]{:S(2)}) collective-permute-start(f32[8,8,128]{2,1,0:T(8,128)S(1)} %get-tuple-element.73), channel_id=1, source_target_pairs={{0,16},{1,17},{2,18},{3,19},{4,20},{5,21},{6,22},{7,23},{8,24},{9,... | collective-permute-start | bytes 98312 | tf_op jit(solution)/shard_map/ppermute | solution.py:353
  24.5 0.0 collective-permute-done.6.x0
  24.5 1.3 %collective-permute-done.7.x1 = f32[8,8,128]{2,1,0:T(8,128)S(1)} collective-permute-done((f32[8,8,128]{2,1,0:T(8,128)S(1)}, f32[8,8,128]{2,1,0:T(8,128)S(1)}, u32[]{:S(2)}, u32[]{:S(2)}) %collective-permute-start.7) | collective-permute-done | bytes 32800 | tf_op jit(solution)/shard_map/ppermute | solution.py:353
  25.8 3.1 %collective-permute-start.8 = (f32[8,8,128]{2,1,0:T(8,128)S(1)}, f32[8,8,128]{2,1,0:T(8,128)S(1)}, u32[]{:S(2)}, u32[]{:S(2)}) collective-permute-start(f32[8,8,128]{2,1,0:T(8,128)S(1)} %get-tuple-element.74), channel_id=1, source_target_pairs={{0,1},{1,0},{2,3},{3,2},{4,8},{5,9},{6,10},{7,11},{8,4},{9,5},{10,... | collective-permute-start | bytes 98312 | tf_op jit(solution)/shard_map/ppermute | solution.py:353
  28.9 2.3 %collective-permute-start.9 = (f32[8,8,128]{2,1,0:T(8,128)S(1)}, f32[8,8,128]{2,1,0:T(8,128)S(1)}, u32[]{:S(2)}, u32[]{:S(2)}) collective-permute-start(f32[8,8,128]{2,1,0:T(8,128)S(1)} %get-tuple-element.75), channel_id=1, source_target_pairs={{0,4},{1,5},{2,6},{3,7},{4,0},{5,1},{6,2},{7,3},{8,12},{9,13},{10,... | collective-permute-start | bytes 98312 | tf_op jit(solution)/shard_map/ppermute | solution.py:353
  31.2 0.0 collective-permute-done.8.y0
  31.2 0.9 collective-permute-done.9.y1
  32.1 0.1 after_y_2.1
  32.1 1.1 %collective-permute-start.10 = (f32[8,8,128]{2,1,0:T(8,128)S(1)}, f32[8,8,128]{2,1,0:T(8,128)S(1)}, u32[]{:S(2)}, u32[]{:S(2)}) collective-permute-start(f32[8,8,128]{2,1,0:T(8,128)S(1)} %get-tuple-element.76), channel_id=1, source_target_pairs={{0,4},{1,2},{2,1},{3,7},{4,0},{5,6},{6,5},{7,3},{8,12},{9,10},{10,... | collective-permute-start | bytes 98312 | tf_op jit(solution)/shard_map/ppermute | solution.py:353
  33.3 0.0 collective-permute-start.11
  33.3 1.5 %prepare_edge.1 = (f32[4,512,128]{2,1,0:T(8,128)S(1)}, bf16[512,512]{1,0:T(8,128)(2,1)S(1)}, bf16[384,2048]{1,0:T(8,128)(2,1)S(1)}, bf16[128,128]{1,0:T(8,128)(2,1)S(1)}, bf16[256,128]{1,0:T(8,128)(2,1)S(1)}) custom-call(s32[4,3]{1,0:T(4,128)S(1)} %copy-done.4, f32[4,512,128]{2,1,0:T(8,128)S(1)} %get-tuple-element.78.preact, ...), custom_call_target="tpu_custom_call" | custom-call | tf_op jit(solution)/shard_map/prepare_edge/pallas_call | solution.py:431
  34.7 0.3 node_grads.1
  35.1 0.0 collective-permute-done.10.z0
  35.1 0.9 %collective-permute-done.11.z1 = f32[8,8,128]{2,1,0:T(8,128)S(1)} collective-permute-done((f32[8,8,128]{2,1,0:T(8,128)S(1)}, f32[8,8,128]{2,1,0:T(8,128)S(1)}, u32[]{:S(2)}, u32[]{:S(2)}) %collective-permute-start.11) | collective-permute-done | bytes 32800 | tf_op jit(solution)/shard_map/ppermute | solution.py:353
  36.0 0.9 edge.1
  36.9 1.8 %collective-permute-start.14 = (f32[448,128]{1,0:T(8,128)S(1)}, f32[448,128]{1,0:T(8,128)S(1)}, u32[]{:S(2)}, u32[]{:S(2)}) collective-permute-start(f32[448,128]{1,0:T(8,128)S(1)} %get-tuple-element.95), channel_id=1, source_target_pairs={{0,4},{1,5},{2,6},{3,7},{4,0},{5,1},{6,2},{7,3},{8,12},{9,13},{10,... | collective-permute-start | bytes 688136 | tf_op jit(solution)/shard_map/ppermute | solution.py:362
  38.7 1.1 %node_part.1 = (f32[8,8,8,128]{3,2,1,0:T(8,128)S(1)}, f32[8,8,128]{2,1,0:T(8,128)S(1)}, f32[8,8,128]{2,1,0:T(8,128)S(1)}) custom-call(s32[4,3]{1,0:T(4,128)S(1)} %copy-done.4, f32[9,8,128]{2,1,0:T(8,128)S(1)} %get-tuple-element.56.after.rim.refs_0_, bf16[2048,128]{1,0:T(8,128)(2,1)S(1)} %get-tuple-element.88.slopes, f32[512,128]{1,0:T(8,128)S(1)} %get-tuple-element.89.base, ...), custom_call_target="tpu_custom_call" | custom-call | tf_op jit(solution)/shard_map/node_part/pallas_call | solution.py:453
  39.9 0.0 collective-permute-done.14.got
  39.9 0.7 add_core.1
  40.6 7.6 %all-to-all-start = ((f32[16,1,3584]{2,1,0:T(1,128)}), f32[16,1,3584]{2,1,0:T(1,128)S(1)}, u32[]{:S(2)}, u32[]{:S(2)}) async-start(f32[16,1,3584]{2,1,0:T(1,128)} %bitcast.3), calls=%async_computation | async-start | bytes 458752 | tf_op jit(solution)/shard_map/all_to_all | solution.py:382
  48.2 0.9 collective-permute-start.12
  49.1 1.7 %collective-permute-start.13 = (f32[8,8,128]{2,1,0:T(8,128)S(1)}, f32[8,8,128]{2,1,0:T(8,128)S(1)}, u32[]{:S(2)}, u32[]{:S(2)}) collective-permute-start(f32[8,8,128]{2,1,0:T(8,128)S(1)} %get-tuple-element.93), channel_id=1, source_target_pairs={{0,1},{1,0},{2,3},{3,2},{4,5},{5,4},{6,7},{7,6},{8,9},{9,8},{10,11... | collective-permute-start | bytes 98312 | tf_op jit(solution)/shard_map/ppermute | solution.py:353
  50.8 0.0 collective-permute-done.12.refs_2_.z0
  50.8 2.3 %collective-permute-done.13.refs_3_.z1 = f32[8,8,128]{2,1,0:T(8,128)S(1)} collective-permute-done((f32[8,8,128]{2,1,0:T(8,128)S(1)}, f32[8,8,128]{2,1,0:T(8,128)S(1)}, u32[]{:S(2)}, u32[]{:S(2)}) %collective-permute-start.13) | collective-permute-done | bytes 32800 | tf_op jit(solution)/shard_map/ppermute | solution.py:353
  53.1 2.9 %all-to-all-done = f32[16,1,3584]{2,1,0:T(1,128)S(1)} async-done(((f32[16,1,3584]{2,1,0:T(1,128)}), f32[16,1,3584]{2,1,0:T(1,128)S(1)}, u32[]{:S(2)}, u32[]{:S(2)}) %all-to-all-start) | async-done | bytes 229408 | tf_op jit(solution)/shard_map/all_to_all | solution.py:382
  56.0 0.7 after_z_fold.1
  56.7 8.2 %all-to-all-start.1 = ((f32[8,1,3584]{2,1,0:T(1,128)}), f32[8,1,3584]{2,1,0:T(1,128)S(1)}, u32[]{:S(2)}, u32[]{:S(2)}) async-start(f32[8,1,3584]{2,1,0:T(1,128)} %bitcast.5), calls=%async_computation.1 | async-start | bytes 229376 | tf_op jit(solution)/shard_map/all_to_all | solution.py:382
  64.9 1.4 %collective-permute-start.15 = (f32[8,8,128]{2,1,0:T(8,128)S(1)}, f32[8,8,128]{2,1,0:T(8,128)S(1)}, u32[]{:S(2)}, u32[]{:S(2)}) collective-permute-start(f32[8,8,128]{2,1,0:T(8,128)S(1)} %get-tuple-element.96), channel_id=1, source_target_pairs={{0,1},{1,0},{2,3},{3,2},{4,8},{5,9},{6,10},{7,11},{8,4},{9,5},{10,... | collective-permute-start | bytes 98312 | tf_op jit(solution)/shard_map/ppermute | solution.py:353
  66.2 1.3 %collective-permute-start.16 = (f32[8,8,128]{2,1,0:T(8,128)S(1)}, f32[8,8,128]{2,1,0:T(8,128)S(1)}, u32[]{:S(2)}, u32[]{:S(2)}) collective-permute-start(f32[8,8,128]{2,1,0:T(8,128)S(1)} %get-tuple-element.97), channel_id=1, source_target_pairs={{0,4},{1,5},{2,6},{3,7},{4,0},{5,1},{6,2},{7,3},{8,12},{9,13},{10,... | collective-permute-start | bytes 98312 | tf_op jit(solution)/shard_map/ppermute | solution.py:353
  67.6 0.7 collective-permute-done.15.refs_4_.y0
  68.2 0.2 collective-permute-done.16.refs_5_.y1
  68.4 4.3 %all-to-all-done.1 = f32[8,1,3584]{2,1,0:T(1,128)S(1)} async-done(((f32[8,1,3584]{2,1,0:T(1,128)}), f32[8,1,3584]{2,1,0:T(1,128)S(1)}, u32[]{:S(2)}, u32[]{:S(2)}) %all-to-all-start.1) | async-done | bytes 114720 | tf_op jit(solution)/shard_map/all_to_all | solution.py:382
  72.7 0.8 after_y_fold.1
  73.5 6.7 %all-to-all-start.2 = ((f32[32,1,3584]{2,1,0:T(1,128)}), f32[32,1,3584]{2,1,0:T(1,128)S(1)}, u32[]{:S(2)}, u32[]{:S(2)}) async-start(f32[32,1,3584]{2,1,0:T(1,128)} %bitcast.9), calls=%async_computation.2 | async-start | bytes 917504 | tf_op jit(solution)/shard_map/all_to_all | solution.py:382
  80.3 0.4 collective-permute-start.17
  80.7 2.7 %collective-permute-start.18 = (f32[8,8,128]{2,1,0:T(8,128)S(1)}, f32[8,8,128]{2,1,0:T(8,128)S(1)}, u32[]{:S(2)}, u32[]{:S(2)}) collective-permute-start(f32[8,8,128]{2,1,0:T(8,128)S(1)} %get-tuple-element.100), channel_id=1, source_target_pairs={{0,16},{1,17},{2,18},{3,19},{4,20},{5,21},{6,22},{7,23},{8,24},{9,... | collective-permute-start | bytes 98312 | tf_op jit(solution)/shard_map/ppermute | solution.py:353
  83.4 1.1 %edge_grad.1 = bf16[2048,128]{1,0:T(8,128)(2,1)} custom-call(bf16[2048,128]{1,0:T(8,128)(2,1)S(1)} %get-tuple-element.88.slopes, bf16[384,128]{1,0:T(8,128)(2,1)S(1)} %get-tuple-element.59.w_in), custom_call_target="tpu_custom_call" | custom-call | tf_op jit(solution)/shard_map/edge_grad/pallas_call | solution.py:456
  84.5 0.0 collective-permute-done.17.x0
  84.5 1.7 %collective-permute-done.18.x1 = f32[8,8,128]{2,1,0:T(8,128)S(1)} collective-permute-done((f32[8,8,128]{2,1,0:T(8,128)S(1)}, f32[8,8,128]{2,1,0:T(8,128)S(1)}, u32[]{:S(2)}, u32[]{:S(2)}) %collective-permute-start.18) | collective-permute-done | bytes 32800 | tf_op jit(solution)/shard_map/ppermute | solution.py:353
  86.2 0.8 last.1
  87.0 4.2 %all-to-all-done.2 = f32[32,1,3584]{2,1,0:T(1,128)S(1)} async-done(((f32[32,1,3584]{2,1,0:T(1,128)}), f32[32,1,3584]{2,1,0:T(1,128)S(1)}, u32[]{:S(2)}, u32[]{:S(2)}) %all-to-all-start.2) | async-done | bytes 458784 | tf_op jit(solution)/shard_map/all_to_all | solution.py:382
  91.1 1.0 %clip.1 = (f32[384,128]{1,0:T(8,128)}, f32[128,128]{1,0:T(8,128)}, f32[256,128]{1,0:T(8,128)}, f32[128,128]{1,0:T(8,128)}) custom-call(f32[896,128]{1,0:T(8,128)S(1)} %bitcast.11), custom_call_target="tpu_custom_call" | custom-call | tf_op jit(solution)/shard_map/clip/pallas_call | solution.py:458
  (13 shorter events, 0.0 us)
Async XLA Ops:
  0.6 16.3 %copy-start.5 = (s32[8,8,8]{2,1,0:T(8,128)S(1)}, s32[8,8,8]{2,1,0:T(8,128)}, u32[]{:S(2)}) copy-start(s32[8,8,8]{2,1,0:T(8,128)} %param.11) | copy-start | bytes 6148
  0.6 16.4 %copy-start.1 = (bf16[8,8,8,128]{3,2,1,0:T(8,128)(2,1)S(1)}, bf16[8,8,8,128]{3,2,1,0:T(8,128)(2,1)}, u32[]{:S(2)}) copy-start(bf16[8,8,8,128]{3,2,1,0:T(8,128)(2,1)} %param.17) | copy-start | bytes 393220
  0.7 16.4 %copy-start = (bf16[256,128]{1,0:T(8,128)(2,1)S(1)}, bf16[256,128]{1,0:T(8,128)(2,1)}, u32[]{:S(2)}) copy-start(bf16[256,128]{1,0:T(8,128)(2,1)} %w_in.5) | copy-start | bytes 196612
  0.7 16.4 %copy-start.2 = (bf16[128,128]{1,0:T(8,128)(2,1)S(1)}, bf16[128,128]{1,0:T(8,128)(2,1)}, u32[]{:S(2)}) copy-start(bf16[128,128]{1,0:T(8,128)(2,1)} %w_out.1) | copy-start | bytes 98308
  2.8 7.3 %collective-permute-start = (f32[8,8,128]{2,1,0:T(8,128)S(1)}, f32[8,8,128]{2,1,0:T(8,128)S(1)}, u32[]{:S(2)}, u32[]{:S(2)}) collective-permute-start(f32[8,8,128]{2,1,0:T(8,128)S(1)} %get-tuple-element.62), channel_id=1, source_target_pairs={{0,4},{1,5},{2,6},{3,7},{4,0},{5,1},{6,2},{7,3},{8,12},{9,13},{10,... | collective-permute-start | bytes 98312 | tf_op jit(solution)/shard_map/ppermute | solution.py:353
  6.1 4.3 %collective-permute-start.1 = (f32[8,8,128]{2,1,0:T(8,128)S(1)}, f32[8,8,128]{2,1,0:T(8,128)S(1)}, u32[]{:S(2)}, u32[]{:S(2)}) collective-permute-start(f32[8,8,128]{2,1,0:T(8,128)S(1)} %get-tuple-element.63), channel_id=1, source_target_pairs={{0,16},{1,17},{2,18},{3,19},{4,20},{5,21},{6,22},{7,23},{8,24},{9,... | collective-permute-start | bytes 98312 | tf_op jit(solution)/shard_map/ppermute | solution.py:353
  8.1 0.7 copy-start.3
  10.4 3.9 %collective-permute-start.2 = (f32[8,8,128]{2,1,0:T(8,128)S(1)}, f32[8,8,128]{2,1,0:T(8,128)S(1)}, u32[]{:S(2)}, u32[]{:S(2)}) collective-permute-start(f32[8,8,128]{2,1,0:T(8,128)S(1)} %get-tuple-element.64), channel_id=1, source_target_pairs={{0,1},{1,0},{2,3},{3,2},{4,8},{5,9},{6,10},{7,11},{8,4},{9,5},{10,... | collective-permute-start | bytes 98312 | tf_op jit(solution)/shard_map/ppermute | solution.py:353
  12.7 1.6 %collective-permute-start.3 = (f32[8,8,128]{2,1,0:T(8,128)S(1)}, f32[8,8,128]{2,1,0:T(8,128)S(1)}, u32[]{:S(2)}, u32[]{:S(2)}) collective-permute-start(f32[8,8,128]{2,1,0:T(8,128)S(1)} %get-tuple-element.65), channel_id=1, source_target_pairs={{0,4},{1,5},{2,6},{3,7},{4,0},{5,1},{6,2},{7,3},{8,12},{9,13},{10,... | collective-permute-start | bytes 98312 | tf_op jit(solution)/shard_map/ppermute | solution.py:353
  14.4 2.9 %collective-permute-start.4 = (f32[8,8,128]{2,1,0:T(8,128)S(1)}, f32[8,8,128]{2,1,0:T(8,128)S(1)}, u32[]{:S(2)}, u32[]{:S(2)}) collective-permute-start(f32[8,8,128]{2,1,0:T(8,128)S(1)} %get-tuple-element.66), channel_id=1, source_target_pairs={{0,4},{1,2},{2,1},{3,7},{4,0},{5,6},{6,5},{7,3},{8,12},{9,10},{10,... | collective-permute-start | bytes 98312 | tf_op jit(solution)/shard_map/ppermute | solution.py:353
  15.9 2.8 %collective-permute-start.5 = (f32[8,8,128]{2,1,0:T(8,128)S(1)}, f32[8,8,128]{2,1,0:T(8,128)S(1)}, u32[]{:S(2)}, u32[]{:S(2)}) collective-permute-start(f32[8,8,128]{2,1,0:T(8,128)S(1)} %get-tuple-element.67), channel_id=1, source_target_pairs={{0,1},{1,0},{2,3},{3,2},{4,5},{5,4},{6,7},{7,6},{8,9},{9,8},{10,11... | collective-permute-start | bytes 98312 | tf_op jit(solution)/shard_map/ppermute | solution.py:353
  16.9 16.4 %copy-start.4 = (s32[4,3]{1,0:T(4,128)S(1)}, s32[4,3]{1,0:T(4,128)}, u32[]{:S(2)}) copy-start(s32[4,3]{1,0:T(4,128)} %offs.5) | copy-start | bytes 148
  19.2 5.3 %collective-permute-start.6 = (f32[8,8,128]{2,1,0:T(8,128)S(1)}, f32[8,8,128]{2,1,0:T(8,128)S(1)}, u32[]{:S(2)}, u32[]{:S(2)}) collective-permute-start(f32[8,8,128]{2,1,0:T(8,128)S(1)} %get-tuple-element.72), channel_id=1, source_target_pairs={{0,4},{1,5},{2,6},{3,7},{4,0},{5,1},{6,2},{7,3},{8,12},{9,13},{10,... | collective-permute-start | bytes 98312 | tf_op jit(solution)/shard_map/ppermute | solution.py:353
  21.1 4.7 %collective-permute-start.7 = (f32[8,8,128]{2,1,0:T(8,128)S(1)}, f32[8,8,128]{2,1,0:T(8,128)S(1)}, u32[]{:S(2)}, u32[]{:S(2)}) collective-permute-start(f32[8,8,128]{2,1,0:T(8,128)S(1)} %get-tuple-element.73), channel_id=1, source_target_pairs={{0,16},{1,17},{2,18},{3,19},{4,20},{5,21},{6,22},{7,23},{8,24},{9,... | collective-permute-start | bytes 98312 | tf_op jit(solution)/shard_map/ppermute | solution.py:353
  25.8 5.4 %collective-permute-start.8 = (f32[8,8,128]{2,1,0:T(8,128)S(1)}, f32[8,8,128]{2,1,0:T(8,128)S(1)}, u32[]{:S(2)}, u32[]{:S(2)}) collective-permute-start(f32[8,8,128]{2,1,0:T(8,128)S(1)} %get-tuple-element.74), channel_id=1, source_target_pairs={{0,1},{1,0},{2,3},{3,2},{4,8},{5,9},{6,10},{7,11},{8,4},{9,5},{10,... | collective-permute-start | bytes 98312 | tf_op jit(solution)/shard_map/ppermute | solution.py:353
  28.9 3.2 %collective-permute-start.9 = (f32[8,8,128]{2,1,0:T(8,128)S(1)}, f32[8,8,128]{2,1,0:T(8,128)S(1)}, u32[]{:S(2)}, u32[]{:S(2)}) collective-permute-start(f32[8,8,128]{2,1,0:T(8,128)S(1)} %get-tuple-element.75), channel_id=1, source_target_pairs={{0,4},{1,5},{2,6},{3,7},{4,0},{5,1},{6,2},{7,3},{8,12},{9,13},{10,... | collective-permute-start | bytes 98312 | tf_op jit(solution)/shard_map/ppermute | solution.py:353
  32.1 2.9 %collective-permute-start.10 = (f32[8,8,128]{2,1,0:T(8,128)S(1)}, f32[8,8,128]{2,1,0:T(8,128)S(1)}, u32[]{:S(2)}, u32[]{:S(2)}) collective-permute-start(f32[8,8,128]{2,1,0:T(8,128)S(1)} %get-tuple-element.76), channel_id=1, source_target_pairs={{0,4},{1,2},{2,1},{3,7},{4,0},{5,6},{6,5},{7,3},{8,12},{9,10},{10,... | collective-permute-start | bytes 98312 | tf_op jit(solution)/shard_map/ppermute | solution.py:353
  33.3 2.8 %collective-permute-start.11 = (f32[8,8,128]{2,1,0:T(8,128)S(1)}, f32[8,8,128]{2,1,0:T(8,128)S(1)}, u32[]{:S(2)}, u32[]{:S(2)}) collective-permute-start(f32[8,8,128]{2,1,0:T(8,128)S(1)} %get-tuple-element.77), channel_id=1, source_target_pairs={{0,1},{1,0},{2,3},{3,2},{4,5},{5,4},{6,7},{7,6},{8,9},{9,8},{10,11... | collective-permute-start | bytes 98312 | tf_op jit(solution)/shard_map/ppermute | solution.py:353
  36.9 2.9 %collective-permute-start.14 = (f32[448,128]{1,0:T(8,128)S(1)}, f32[448,128]{1,0:T(8,128)S(1)}, u32[]{:S(2)}, u32[]{:S(2)}) collective-permute-start(f32[448,128]{1,0:T(8,128)S(1)} %get-tuple-element.95), channel_id=1, source_target_pairs={{0,4},{1,5},{2,6},{3,7},{4,0},{5,1},{6,2},{7,3},{8,12},{9,13},{10,... | collective-permute-start | bytes 688136 | tf_op jit(solution)/shard_map/ppermute | solution.py:362
  40.6 15.4 %all-to-all-start = ((f32[16,1,3584]{2,1,0:T(1,128)}), f32[16,1,3584]{2,1,0:T(1,128)S(1)}, u32[]{:S(2)}, u32[]{:S(2)}) async-start(f32[16,1,3584]{2,1,0:T(1,128)} %bitcast.3), calls=%async_computation | async-start | bytes 458752 | tf_op jit(solution)/shard_map/all_to_all | solution.py:382
  48.2 2.6 %collective-permute-start.12 = (f32[8,8,128]{2,1,0:T(8,128)S(1)}, f32[8,8,128]{2,1,0:T(8,128)S(1)}, u32[]{:S(2)}, u32[]{:S(2)}) collective-permute-start(f32[8,8,128]{2,1,0:T(8,128)S(1)} %get-tuple-element.92.after), channel_id=1, source_target_pairs={{0,4},{1,2},{2,1},{3,7},{4,0},{5,6},{6,5},{7,3},{8,12},{9,10},{10,... | collective-permute-start | bytes 98312 | tf_op jit(solution)/shard_map/ppermute | solution.py:353
  49.1 4.0 %collective-permute-start.13 = (f32[8,8,128]{2,1,0:T(8,128)S(1)}, f32[8,8,128]{2,1,0:T(8,128)S(1)}, u32[]{:S(2)}, u32[]{:S(2)}) collective-permute-start(f32[8,8,128]{2,1,0:T(8,128)S(1)} %get-tuple-element.93), channel_id=1, source_target_pairs={{0,1},{1,0},{2,3},{3,2},{4,5},{5,4},{6,7},{7,6},{8,9},{9,8},{10,11... | collective-permute-start | bytes 98312 | tf_op jit(solution)/shard_map/ppermute | solution.py:353
  56.7 16.0 %all-to-all-start.1 = ((f32[8,1,3584]{2,1,0:T(1,128)}), f32[8,1,3584]{2,1,0:T(1,128)S(1)}, u32[]{:S(2)}, u32[]{:S(2)}) async-start(f32[8,1,3584]{2,1,0:T(1,128)} %bitcast.5), calls=%async_computation.1 | async-start | bytes 229376 | tf_op jit(solution)/shard_map/all_to_all | solution.py:382
  64.9 3.3 %collective-permute-start.15 = (f32[8,8,128]{2,1,0:T(8,128)S(1)}, f32[8,8,128]{2,1,0:T(8,128)S(1)}, u32[]{:S(2)}, u32[]{:S(2)}) collective-permute-start(f32[8,8,128]{2,1,0:T(8,128)S(1)} %get-tuple-element.96), channel_id=1, source_target_pairs={{0,1},{1,0},{2,3},{3,2},{4,8},{5,9},{6,10},{7,11},{8,4},{9,5},{10,... | collective-permute-start | bytes 98312 | tf_op jit(solution)/shard_map/ppermute | solution.py:353
  66.2 2.2 %collective-permute-start.16 = (f32[8,8,128]{2,1,0:T(8,128)S(1)}, f32[8,8,128]{2,1,0:T(8,128)S(1)}, u32[]{:S(2)}, u32[]{:S(2)}) collective-permute-start(f32[8,8,128]{2,1,0:T(8,128)S(1)} %get-tuple-element.97), channel_id=1, source_target_pairs={{0,4},{1,5},{2,6},{3,7},{4,0},{5,1},{6,2},{7,3},{8,12},{9,13},{10,... | collective-permute-start | bytes 98312 | tf_op jit(solution)/shard_map/ppermute | solution.py:353
  73.5 17.6 %all-to-all-start.2 = ((f32[32,1,3584]{2,1,0:T(1,128)}), f32[32,1,3584]{2,1,0:T(1,128)S(1)}, u32[]{:S(2)}, u32[]{:S(2)}) async-start(f32[32,1,3584]{2,1,0:T(1,128)} %bitcast.9), calls=%async_computation.2 | async-start | bytes 917504 | tf_op jit(solution)/shard_map/all_to_all | solution.py:382
  80.3 4.3 %collective-permute-start.17 = (f32[8,8,128]{2,1,0:T(8,128)S(1)}, f32[8,8,128]{2,1,0:T(8,128)S(1)}, u32[]{:S(2)}, u32[]{:S(2)}) collective-permute-start(f32[8,8,128]{2,1,0:T(8,128)S(1)} %get-tuple-element.99), channel_id=1, source_target_pairs={{0,4},{1,5},{2,6},{3,7},{4,0},{5,1},{6,2},{7,3},{8,12},{9,13},{10,... | collective-permute-start | bytes 98312 | tf_op jit(solution)/shard_map/ppermute | solution.py:353
  80.7 5.5 %collective-permute-start.18 = (f32[8,8,128]{2,1,0:T(8,128)S(1)}, f32[8,8,128]{2,1,0:T(8,128)S(1)}, u32[]{:S(2)}, u32[]{:S(2)}) collective-permute-start(f32[8,8,128]{2,1,0:T(8,128)S(1)} %get-tuple-element.100), channel_id=1, source_target_pairs={{0,16},{1,17},{2,18},{3,19},{4,20},{5,21},{6,22},{7,23},{8,24},{9,... | collective-permute-start | bytes 98312 | tf_op jit(solution)/shard_map/ppermute | solution.py:353

commit v10 on v8

--- a/solution.py
+++ b/solution.py
@@ -68,10 +68,12 @@
     return moved.reshape(N, W)
 
 
-def inside(offs, k):
+def inside(offs, k, rims=False):
     ok = None
+    shape = (2, *FACE) if rims else CUBE
     for which in range(3):
-        at = lax.broadcasted_iota(jnp.int32, CUBE, which) + offs[k, which]
+        at = lax.broadcasted_iota(jnp.int32, shape, which)
+        at = (at * (B - 1) if rims and which == 0 else at) + offs[k, which]
         one = (at >= 0) & (at < B)
         ok = one if ok is None else ok & one
     return ok
@@ -89,13 +91,17 @@
             rim[3 * d + i] = jnp.full((B, W), flag.astype(F32))
 
 
-def forward_kernel(
-    nodes_h, edges_h, w_in_h, w_out_h, offs_h,
-    local, xa, xb, preact, hidden, nodes, edges, w_in, w_out, rim,
-    pad, offs, sems,
+RIMS = (0, (B - 1) * B * B)
+
+
+def first_rims_kernel(
+    nodes_h, edges_h, w_in_h, w_out_h, offs_h, xa, xb, rim, nodes, w_in, w_out, edges, pad, offs, sems
 ):
+    plane = B * B
     pairs = [(nodes_h, nodes), (w_in_h, w_in), (offs_h, offs), (w_out_h, w_out)]
-    pairs += [(edges_h.at[k], edges.at[k]) for k in range(K)]
+    for k in range(K):
+        for i, at in enumerate(RIMS):
+            pairs.append((edges_h.at[k, pl.ds(at, plane)], edges.at[k, pl.ds(i * plane, plane)]))
     copies = [pltpu.make_async_copy(a, b, sems.at[i]) for i, (a, b) in enumerate(pairs)]
     for copy in copies:
         copy.start()
@@ -104,23 +110,44 @@
         copy.wait()
     node = nodes[...]
     fill_ring(pad, dot(node, w_in[:W]).reshape(CUBE))
+    rims = jnp.concatenate([node[at : at + plane] for at in RIMS], axis=0)
+    receiver = dot(rims, w_in[W : 2 * W])
+    copies[3].wait()
+    total = jnp.zeros((2 * plane, W), F32)
+    for k in range(K):
+        copies[4 + 2 * k].wait()
+        copies[5 + 2 * k].wait()
+        o0, o1, o2 = offs[k, 0], offs[k, 1], offs[k, 2]
+        sent = jnp.concatenate([pad[pl.ds(1 + at + o0, 1), pl.ds(1 + o1, B)] for at in (0, B - 1)], axis=0)
+        sent = pltpu.roll(sent.reshape(2 * B, B, W), lax.rem(B - o2, B), 1).reshape(2 * plane, W)
+        pre = sent + receiver + dot(edges[k], w_in[2 * W :])
+        act = (pre * jax.nn.sigmoid(pre)).reshape(2, B, B, W)
+        kept = jnp.where(inside(offs, k, True), act, 0.0).reshape(2 * plane, W).astype(BF16)
+        total = total + dot(kept, w_out[...])
+    total = total.reshape(2, B, B, W)
+    send(rim, 0, total[0], total[1], xa, xb)
+
+
+def forward_kernel(edges_h, offs, nodes, w_in, w_out, after, local, preact, hidden, edges, pad, sems):
+    copies = [pltpu.make_async_copy(edges_h.at[k], edges.at[k], sems.at[k]) for k in range(K)]
+    for copy in copies:
+        copy.start()
+    node = nodes[...]
+    fill_ring(pad, dot(node, w_in[:W]).reshape(CUBE))
     receiver = dot(node, w_in[W : 2 * W])
-    copies[3].wait()
     total = jnp.zeros((N, W), F32)
     for k in range(K):
-        copies[4 + k].wait()
+        copies[k].wait()
         pre = ring_shift(pad, offs[k, 0], offs[k, 1], offs[k, 2]) + receiver + dot(edges[k], w_in[2 * W :])
         preact[k] = pre
         act = (pre * jax.nn.sigmoid(pre)).reshape(CUBE)
         kept = jnp.where(inside(offs, k), act, 0.0).reshape(N, W).astype(BF16)
         hidden[k] = kept
         total = total + dot(kept, w_out[...])
-    total = total.reshape(CUBE)
-    local[...] = total
-    send(rim, 0, total[0], total[B - 1], xa, xb)
-
-
-def prepare_node_kernel(nodes, cot, w_in, w_out, pre, upstream, w_back):
+    local[...] = total.reshape(CUBE)
+
+
+def prepare_node_kernel(nodes, cot, w_in, w_out, after, pre, upstream, w_back):
     pre[...] = dot(nodes[...], w_in[:W])
     upstream[...] = dot_t(cot[...], w_out[...])
     w_back[...] = w_in[W:].T
@@ -283,7 +310,7 @@
     out[...] = dot_t(slopes[...], w_in[2 * W :]).astype(BF16)
 
 
-def last_kernel(rim, field, z0, z1, y0, y1, x0, x1, clipped, out, work):
+def last_kernel(rim, field, z0, z1, y0, y1, x0, x1, out, work):
     work[...] = field[...]
     add_z(rim, (z0, z1), work)
     add_y(rim, (y0, y1), work)
@@ -389,15 +416,27 @@
     square = ((W, W), BF16)
     many = ((K, N, W), BF16)
 
-    local, xa, xb, preact, hidden, nodes, edges, w_in, w_out, rim = call(
+    edges_all = in_hbm(edge_feat.reshape(K, N, W))
+    xa, xb, rim, nodes, w_in, w_out = call(
+        first_rims_kernel,
+        FACES + [((9, B, W), F32), ((N, W), BF16), ((3 * W, W), BF16), square],
+        [HBM] * 5,
+        [
+            pltpu.VMEM((K, 2 * B * B, W), BF16),
+            PAD,
+            pltpu.SMEM((K, 3), jnp.int32),
+            pltpu.SemaphoreType.DMA((4 + 2 * K,)),
+        ],
+    )(in_hbm(node_feat.reshape(N, W)), edges_all, in_hbm(w_edge_in), in_hbm(w_edge_out), in_hbm(offsets))
+    local, preact, hidden, edges = call(
         forward_kernel,
-        [(CUBE, F32)] + FACES + [((K, N, W), F32), many, ((N, W), BF16), many, ((3 * W, W), BF16), square, ((9, B, W), F32)],
-        [HBM] * 5,
-        [PAD, pltpu.SMEM((K, 3), jnp.int32), pltpu.SemaphoreType.DMA((4 + K,))],
-    )(*map(in_hbm, (node_feat.reshape(N, W), edge_feat.reshape(K, N, W), w_edge_in, w_edge_out, offsets)))
+        [(CUBE, F32), ((K, N, W), F32), many, many],
+        [HBM, SMEM] + [VMEM] * 4,
+        [PAD, pltpu.SemaphoreType.DMA((K,))],
+    )(edges_all, offsets, nodes, w_in, w_out, rim)
     begun, upstream, w_node_back = call(
-        prepare_node_kernel, [((N, W), F32), ((N, W), F32), square], [VMEM] * 4
-    )(nodes, cot, w_node_in, w_node_out)
+        prepare_node_kernel, [((N, W), F32), ((N, W), F32), square], [VMEM] * 5
+    )(nodes, cot, w_node_in, w_node_out, local)
     arrived = arrivals(rim, local, xa, xb)
     dact, hidden_t, left, w_out_t, w_back = call(
         prepare_edge_kernel,
@@ -424,9 +463,7 @@
     clipped = call(
         clip_kernel, [((3 * W, W), F32), ((W, W), F32), ((2 * W, W), F32), ((W, W), F32)], [VMEM] * 3
     )(rim, *halves)
-    (node_grad,) = call(last_kernel, [((N, W), BF16)], [VMEM] * 8 + [HBM], [WORK])(
-        rim, local, *arrived, in_hbm(clipped[1])
-    )
+    (node_grad,) = call(last_kernel, [((N, W), BF16)], [VMEM] * 8, [WORK])(rim, local, *arrived)
     return (node_grad.reshape(node_feat.shape), edge_grad.reshape(edge_feat.shape), *clipped)
 
 

time: 94 us -> 94.1 us (level)
  Pallas kernels: 11.4 us -> 13.8 us
  waiting for transfers between devices: 18.8 us -> 16.7 us
  starting transfers between devices: 52 us -> 51 us
    pallas_call x2 -> x3, Pallas kernels: 3.21 us -> 5.56 us  [the longest x1 2.57 us: on_device(): call(forward_kernel, [(CUBE, F32), ((K, N, W), F32), many, many], [HBM, S...]
    ppermute x18, waiting for transfers between devices: 11.5 us -> 9.4 us  [exchange(): lax.ppermute(face, GX + GY + GZ, [(rank, ranks[to]) for rank, to in enume...]
    ppermute x18, starting transfers between devices: 30.1 us -> 29.2 us  [exchange(): lax.ppermute(face, GX + GY + GZ, [(rank, ranks[to]) for rank, to in enume...]
  transfers between devices with their start and end apart: 22 -> 22, of which waited for: 11 -> 12; matrix products, arithmetic and copies ran while one was open for 0% -> 0% of each run, Pallas kernels for 6% -> 8%
where the time goes in v10:
time: 94.1 us; the launch traced here: 93.6 us
  starting transfers between devices  51 us (54%)
  waiting for transfers between devices  16.7 us (18%)
  Pallas kernels  13.8 us (15%)
  blocking collectives  10.3 us (11%)
    ppermute x18, starting transfers between devices, exchange(): lax.ppermute(face, GX + GY + GZ, [(rank, ranks[to]) for rank, to in enume...  29.2 us
    all_to_all x2, starting transfers between devices, swap(): lax.all_to_all(rows.reshape(lax.axis_size(axes), -1), axes, 0, 0, tiled=T...  15.8 us
    all_to_all x1, blocking collectives, swap(): lax.all_to_all(rows.reshape(lax.axis_size(axes), -1), axes, 0, 0, tiled=T...  10.3 us
    ppermute x18, waiting for transfers between devices, exchange(): lax.ppermute(face, GX + GY + GZ, [(rank, ranks[to]) for rank, to in enume...  9.4 us
    all_to_all x2, waiting for transfers between devices, swap(): lax.all_to_all(rows.reshape(lax.axis_size(axes), -1), axes, 0, 0, tiled=T...  7.26 us
    ppermute x2, starting transfers between devices, other_core(): lax.ppermute(half, GX + GY + GZ, [(rank, rank ^ step) for rank in range(c...  6.09 us
    pallas_call x1, Pallas kernels, on_device(): call(forward_kernel, [(CUBE, F32), ((K, N, W), F32), many, many], [HBM, S...  2.57 us
    pallas_call x1, Pallas kernels, on_device(): call(first_rims_kernel, FACES + [((9, B, W), F32), ((N, W), BF16), ((3 *...  2.21 us
  transfers between devices with their start and end apart: 22, of which 12 were waited for; matrix products, arithmetic and copies ran while one was open for 0% of the time, Pallas kernels for 8%

profile of v10, /device:TPU:1, one launch (start us, length us, event | category | flops | bytes accessed | tf_op | source)
XLA Modules:
  0.0 93.6 jit_solution(7551557807567900782)
XLA Ops:
  0.7 2.2 %shard_map.136 = (f32[8,8,128]{2,1,0:T(8,128)S(1)}, f32[8,8,128]{2,1,0:T(8,128)S(1)}, f32[9,8,128]{2,1,0:T(8,128)S(1)}, bf16[512,128]{1,0:T(8,128)(2,1)S(1)}, bf...) custom-call(bf16[512,128]{1,0:T(8,128)(2,1)} %bitcast.22, bf16[4,512,128]{2,1,0:T(8,128)(2,1)} %bitcast.18, ...), custom_call_target="tpu_custom_call" | custom-call | tf_op jit(solution)/shard_map/pallas_call | solution.py:420
  2.9 3.3 %collective-permute-start = (f32[8,8,128]{2,1,0:T(8,128)S(1)}, f32[8,8,128]{2,1,0:T(8,128)S(1)}, u32[]{:S(2)}, u32[]{:S(2)}) collective-permute-start(f32[8,8,128]{2,1,0:T(8,128)S(1)} %get-tuple-element.61), channel_id=1, source_target_pairs={{0,4},{1,5},{2,6},{3,7},{4,0},{5,1},{6,2},{7,3},{8,12},{9,13},{10,... | collective-permute-start | bytes 98312 | tf_op jit(solution)/shard_map/ppermute | solution.py:356
  6.2 1.9 %collective-permute-start.1 = (f32[8,8,128]{2,1,0:T(8,128)S(1)}, f32[8,8,128]{2,1,0:T(8,128)S(1)}, u32[]{:S(2)}, u32[]{:S(2)}) collective-permute-start(f32[8,8,128]{2,1,0:T(8,128)S(1)} %get-tuple-element.62), channel_id=1, source_target_pairs={{0,16},{1,17},{2,18},{3,19},{4,20},{5,21},{6,22},{7,23},{8,24},{9,... | collective-permute-start | bytes 98312 | tf_op jit(solution)/shard_map/ppermute | solution.py:356
  8.1 0.7 copy-done.3
  8.8 2.6 %shard_map.137 = (f32[8,8,8,128]{3,2,1,0:T(8,128)S(1)}, f32[4,512,128]{2,1,0:T(8,128)S(1)}, bf16[4,512,128]{2,1,0:T(8,128)(2,1)S(1)}, bf16[4,512,128]{2,1,0:T(8,128)(2,1)S(1)}) custom-call(bf16[4,512,128]{2,1,0:T(8,128)(2,1)} %bitcast.19, s32[4,3]{1,0:T(4,128)S(1)} %copy-done.3, bf16[512,128]{1,0:T(8,128)(2,1)S(1)} %get-tuple-element.57.nodes, ...), custom_call_target="tpu_custom_call" | custom-call | tf_op jit(solution)/shard_map/pallas_call | solution.py:431
  11.4 0.0 collective-permute-done.x0
  11.4 0.0 collective-permute-done.1.x1
  11.4 2.5 %collective-permute-start.2 = (f32[8,8,128]{2,1,0:T(8,128)S(1)}, f32[8,8,128]{2,1,0:T(8,128)S(1)}, u32[]{:S(2)}, u32[]{:S(2)}) collective-permute-start(f32[8,8,128]{2,1,0:T(8,128)S(1)} %get-tuple-element.63), channel_id=1, source_target_pairs={{0,1},{1,0},{2,3},{3,2},{4,8},{5,9},{6,10},{7,11},{8,4},{9,5},{10,... | collective-permute-start | bytes 98312 | tf_op jit(solution)/shard_map/ppermute | solution.py:356
  13.9 0.3 collective-permute-start.3
  14.2 1.3 %collective-permute-done.2.y0 = f32[8,8,128]{2,1,0:T(8,128)S(1)} collective-permute-done((f32[8,8,128]{2,1,0:T(8,128)S(1)}, f32[8,8,128]{2,1,0:T(8,128)S(1)}, u32[]{:S(2)}, u32[]{:S(2)}) %collective-permute-start.2) | collective-permute-done | bytes 32800 | tf_op jit(solution)/shard_map/ppermute | solution.py:356
  15.5 0.0 collective-permute-done.3.y1
  15.5 0.1 shard_map.139
  15.6 1.2 %collective-permute-start.4 = (f32[8,8,128]{2,1,0:T(8,128)S(1)}, f32[8,8,128]{2,1,0:T(8,128)S(1)}, u32[]{:S(2)}, u32[]{:S(2)}) collective-permute-start(f32[8,8,128]{2,1,0:T(8,128)S(1)} %get-tuple-element.65), channel_id=1, source_target_pairs={{0,4},{1,2},{2,1},{3,7},{4,0},{5,6},{6,5},{7,3},{8,12},{9,10},{10,... | collective-permute-start | bytes 98312 | tf_op jit(solution)/shard_map/ppermute | solution.py:356
  16.8 1.3 %collective-permute-start.5 = (f32[8,8,128]{2,1,0:T(8,128)S(1)}, f32[8,8,128]{2,1,0:T(8,128)S(1)}, u32[]{:S(2)}, u32[]{:S(2)}) collective-permute-start(f32[8,8,128]{2,1,0:T(8,128)S(1)} %get-tuple-element.66), channel_id=1, source_target_pairs={{0,1},{1,0},{2,3},{3,2},{4,5},{5,4},{6,7},{7,6},{8,9},{9,8},{10,11... | collective-permute-start | bytes 98312 | tf_op jit(solution)/shard_map/ppermute | solution.py:356
  18.1 0.0 copy-start.4
  18.2 0.1 div.16
  18.3 0.2 shard_map.140
  18.5 0.0 collective-permute-done.4.z0
  18.5 1.1 %collective-permute-done.5.z1 = f32[8,8,128]{2,1,0:T(8,128)S(1)} collective-permute-done((f32[8,8,128]{2,1,0:T(8,128)S(1)}, f32[8,8,128]{2,1,0:T(8,128)S(1)}, u32[]{:S(2)}, u32[]{:S(2)}) %collective-permute-start.5) | collective-permute-done | bytes 32800 | tf_op jit(solution)/shard_map/ppermute | solution.py:356
  19.6 0.1 broadcast_in_dim.2.inverse
  19.7 0.4 shard_map.141
  20.2 2.2 %collective-permute-start.6 = (f32[8,8,128]{2,1,0:T(8,128)S(1)}, f32[8,8,128]{2,1,0:T(8,128)S(1)}, u32[]{:S(2)}, u32[]{:S(2)}) collective-permute-start(f32[8,8,128]{2,1,0:T(8,128)S(1)} %get-tuple-element.71), channel_id=1, source_target_pairs={{0,4},{1,5},{2,6},{3,7},{4,0},{5,1},{6,2},{7,3},{8,12},{9,13},{10,... | collective-permute-start | bytes 98312 | tf_op jit(solution)/shard_map/ppermute | solution.py:356
  22.4 2.2 %collective-permute-start.7 = (f32[8,8,128]{2,1,0:T(8,128)S(1)}, f32[8,8,128]{2,1,0:T(8,128)S(1)}, u32[]{:S(2)}, u32[]{:S(2)}) collective-permute-start(f32[8,8,128]{2,1,0:T(8,128)S(1)} %get-tuple-element.72), channel_id=1, source_target_pairs={{0,16},{1,17},{2,18},{3,19},{4,20},{5,21},{6,22},{7,23},{8,24},{9,... | collective-permute-start | bytes 98312 | tf_op jit(solution)/shard_map/ppermute | solution.py:356
  24.6 0.0 collective-permute-done.6.x0
  24.6 2.1 %collective-permute-done.7.x1 = f32[8,8,128]{2,1,0:T(8,128)S(1)} collective-permute-done((f32[8,8,128]{2,1,0:T(8,128)S(1)}, f32[8,8,128]{2,1,0:T(8,128)S(1)}, u32[]{:S(2)}, u32[]{:S(2)}) %collective-permute-start.7) | collective-permute-done | bytes 32800 | tf_op jit(solution)/shard_map/ppermute | solution.py:356
  26.6 3.2 %collective-permute-start.8 = (f32[8,8,128]{2,1,0:T(8,128)S(1)}, f32[8,8,128]{2,1,0:T(8,128)S(1)}, u32[]{:S(2)}, u32[]{:S(2)}) collective-permute-start(f32[8,8,128]{2,1,0:T(8,128)S(1)} %get-tuple-element.73), channel_id=1, source_target_pairs={{0,1},{1,0},{2,3},{3,2},{4,8},{5,9},{6,10},{7,11},{8,4},{9,5},{10,... | collective-permute-start | bytes 98312 | tf_op jit(solution)/shard_map/ppermute | solution.py:356
  29.8 1.4 %collective-permute-start.9 = (f32[8,8,128]{2,1,0:T(8,128)S(1)}, f32[8,8,128]{2,1,0:T(8,128)S(1)}, u32[]{:S(2)}, u32[]{:S(2)}) collective-permute-start(f32[8,8,128]{2,1,0:T(8,128)S(1)} %get-tuple-element.74), channel_id=1, source_target_pairs={{0,4},{1,5},{2,6},{3,7},{4,0},{5,1},{6,2},{7,3},{8,12},{9,13},{10,... | collective-permute-start | bytes 98312 | tf_op jit(solution)/shard_map/ppermute | solution.py:356
  31.3 0.2 collective-permute-done.8.y0
  31.4 0.7 collective-permute-done.9.y1
  32.1 0.1 shard_map.143
  32.2 1.1 %collective-permute-start.10 = (f32[8,8,128]{2,1,0:T(8,128)S(1)}, f32[8,8,128]{2,1,0:T(8,128)S(1)}, u32[]{:S(2)}, u32[]{:S(2)}) collective-permute-start(f32[8,8,128]{2,1,0:T(8,128)S(1)} %get-tuple-element.75), channel_id=1, source_target_pairs={{0,4},{1,2},{2,1},{3,7},{4,0},{5,6},{6,5},{7,3},{8,12},{9,10},{10,... | collective-permute-start | bytes 98312 | tf_op jit(solution)/shard_map/ppermute | solution.py:356
  33.3 0.3 collective-permute-start.11
  33.6 1.5 %shard_map.144 = (f32[4,512,128]{2,1,0:T(8,128)S(1)}, bf16[512,512]{1,0:T(8,128)(2,1)S(1)}, bf16[384,2048]{1,0:T(8,128)(2,1)S(1)}, bf16[128,128]{1,0:T(8,128)(2,1)S(1)}, bf16[256,128]{1,0:T(8,128)(2,1)S(1)}) custom-call(s32[4,3]{1,0:T(4,128)S(1)} %copy-done.4, f32[4,512,128]{2,1,0:T(8,128)S(1)} %get-tuple-element.77.preact, ...), custom_call_target="tpu_custom_call" | custom-call | tf_op jit(solution)/shard_map/pallas_call | solution.py:441
  35.1 0.3 shard_map.145
  35.4 0.0 collective-permute-done.10.z0
  35.4 0.7 collective-permute-done.11.z1
  36.1 0.9 shard_map.146
  37.0 1.8 %collective-permute-start.14 = (f32[448,128]{1,0:T(8,128)S(1)}, f32[448,128]{1,0:T(8,128)S(1)}, u32[]{:S(2)}, u32[]{:S(2)}) collective-permute-start(f32[448,128]{1,0:T(8,128)S(1)} %get-tuple-element.95), channel_id=1, source_target_pairs={{0,4},{1,5},{2,6},{3,7},{4,0},{5,1},{6,2},{7,3},{8,12},{9,13},{10,... | collective-permute-start | bytes 688136 | tf_op jit(solution)/shard_map/ppermute | solution.py:365
  38.8 1.2 %shard_map.147 = (f32[8,8,8,128]{3,2,1,0:T(8,128)S(1)}, f32[8,8,128]{2,1,0:T(8,128)S(1)}, f32[8,8,128]{2,1,0:T(8,128)S(1)}) custom-call(s32[4,3]{1,0:T(4,128)S(1)} %copy-done.4, f32[9,8,128]{2,1,0:T(8,128)S(1)} %get-tuple-element.56.after.rim.refs_0_, bf16[2048,128]{1,0:T(8,128)(2,1)S(1)} %get-tuple-element.88.slopes, ...), custom_call_target="tpu_custom_call" | custom-call | tf_op jit(solution)/shard_map/pallas_call | solution.py:458
  39.9 0.0 collective-permute-done.14.got
  39.9 0.7 shard_map.148
  40.6 7.6 %all-to-all-start = ((f32[16,1,3584]{2,1,0:T(1,128)}), f32[16,1,3584]{2,1,0:T(1,128)S(1)}, u32[]{:S(2)}, u32[]{:S(2)}) async-start(f32[16,1,3584]{2,1,0:T(1,128)} %bitcast.3), calls=%async_computation | async-start | bytes 458752 | tf_op jit(solution)/shard_map/all_to_all | solution.py:385
  48.3 0.9 collective-permute-start.12
  49.1 1.7 %collective-permute-start.13 = (f32[8,8,128]{2,1,0:T(8,128)S(1)}, f32[8,8,128]{2,1,0:T(8,128)S(1)}, u32[]{:S(2)}, u32[]{:S(2)}) collective-permute-start(f32[8,8,128]{2,1,0:T(8,128)S(1)} %get-tuple-element.93), channel_id=1, source_target_pairs={{0,1},{1,0},{2,3},{3,2},{4,5},{5,4},{6,7},{7,6},{8,9},{9,8},{10,11... | collective-permute-start | bytes 98312 | tf_op jit(solution)/shard_map/ppermute | solution.py:356
  50.8 2.4 %collective-permute-done.13.refs_3_.z1 = f32[8,8,128]{2,1,0:T(8,128)S(1)} collective-permute-done((f32[8,8,128]{2,1,0:T(8,128)S(1)}, f32[8,8,128]{2,1,0:T(8,128)S(1)}, u32[]{:S(2)}, u32[]{:S(2)}) %collective-permute-start.13) | collective-permute-done | bytes 32800 | tf_op jit(solution)/shard_map/ppermute | solution.py:356
  53.2 2.9 %all-to-all-done = f32[16,1,3584]{2,1,0:T(1,128)S(1)} async-done(((f32[16,1,3584]{2,1,0:T(1,128)}), f32[16,1,3584]{2,1,0:T(1,128)S(1)}, u32[]{:S(2)}, u32[]{:S(2)}) %all-to-all-start) | async-done | bytes 229408 | tf_op jit(solution)/shard_map/all_to_all | solution.py:385
  56.1 0.7 shard_map.149
  56.8 8.2 %all-to-all-start.1 = ((f32[8,1,3584]{2,1,0:T(1,128)}), f32[8,1,3584]{2,1,0:T(1,128)S(1)}, u32[]{:S(2)}, u32[]{:S(2)}) async-start(f32[8,1,3584]{2,1,0:T(1,128)} %bitcast.5), calls=%async_computation.1 | async-start | bytes 229376 | tf_op jit(solution)/shard_map/all_to_all | solution.py:385
  65.0 1.4 %collective-permute-start.15 = (f32[8,8,128]{2,1,0:T(8,128)S(1)}, f32[8,8,128]{2,1,0:T(8,128)S(1)}, u32[]{:S(2)}, u32[]{:S(2)}) collective-permute-start(f32[8,8,128]{2,1,0:T(8,128)S(1)} %get-tuple-element.96), channel_id=1, source_target_pairs={{0,1},{1,0},{2,3},{3,2},{4,8},{5,9},{6,10},{7,11},{8,4},{9,5},{10,... | collective-permute-start | bytes 98312 | tf_op jit(solution)/shard_map/ppermute | solution.py:356
  66.4 1.2 %collective-permute-start.16 = (f32[8,8,128]{2,1,0:T(8,128)S(1)}, f32[8,8,128]{2,1,0:T(8,128)S(1)}, u32[]{:S(2)}, u32[]{:S(2)}) collective-permute-start(f32[8,8,128]{2,1,0:T(8,128)S(1)} %get-tuple-element.97), channel_id=1, source_target_pairs={{0,4},{1,5},{2,6},{3,7},{4,0},{5,1},{6,2},{7,3},{8,12},{9,13},{10,... | collective-permute-start | bytes 98312 | tf_op jit(solution)/shard_map/ppermute | solution.py:356
  67.6 0.7 collective-permute-done.15.refs_4_.y0
  68.3 0.2 collective-permute-done.16.refs_5_.y1
  68.5 4.3 %all-to-all-done.1 = f32[8,1,3584]{2,1,0:T(1,128)S(1)} async-done(((f32[8,1,3584]{2,1,0:T(1,128)}), f32[8,1,3584]{2,1,0:T(1,128)S(1)}, u32[]{:S(2)}, u32[]{:S(2)}) %all-to-all-start.1) | async-done | bytes 114720 | tf_op jit(solution)/shard_map/all_to_all | solution.py:385
  72.8 0.1 shard_map.150
  72.9 10.3 %all_to_all.27 = f32[16,1,3584]{2,1,0:T(1,128)S(1)} all-to-all(f32[16,1,3584]{2,1,0:T(1,128)S(1)} %bitcast.17), channel_id=1, replica_groups=mesh['z'=8,'yh'=2,'yl'=2,'c'=2,'x'=4] {'yh','yl','x'}, dimensions={0} | all-to-all | bytes 458752 | tf_op jit(solution)/shard_map/all_to_all | solution.py:385
  83.2 4.3 %collective-permute-start.19 = (f32[448,128]{1,0:T(8,128)S(1)}, f32[448,128]{1,0:T(8,128)S(1)}, u32[]{:S(2)}, u32[]{:S(2)}) collective-permute-start(f32[448,128]{1,0:T(8,128)S(1)} %bitcast.12), channel_id=1, source_target_pairs={{0,4},{1,5},{2,6},{3,7},{4,0},{5,1},{6,2},{7,3},{8,12},{9,13},{10,... | collective-permute-start | bytes 688136 | tf_op jit(solution)/shard_map/ppermute | solution.py:365
  87.5 0.0 collective-permute-start.17
  87.5 3.0 %collective-permute-start.18 = (f32[8,8,128]{2,1,0:T(8,128)S(1)}, f32[8,8,128]{2,1,0:T(8,128)S(1)}, u32[]{:S(2)}, u32[]{:S(2)}) collective-permute-start(f32[8,8,128]{2,1,0:T(8,128)S(1)} %get-tuple-element.100), channel_id=1, source_target_pairs={{0,16},{1,17},{2,18},{3,19},{4,20},{5,21},{6,22},{7,23},{8,24},{9,... | collective-permute-start | bytes 98312 | tf_op jit(solution)/shard_map/ppermute | solution.py:356
  90.5 1.1 %shard_map.152 = bf16[2048,128]{1,0:T(8,128)(2,1)} custom-call(bf16[2048,128]{1,0:T(8,128)(2,1)S(1)} %get-tuple-element.88.slopes, bf16[384,128]{1,0:T(8,128)(2,1)S(1)} %get-tuple-element.58.w_in), custom_call_target="tpu_custom_call" | custom-call | tf_op jit(solution)/shard_map/pallas_call | solution.py:461
  91.6 0.0 collective-permute-done.17.x0
  91.6 0.2 collective-permute-done.18.x1
  91.8 0.8 shard_map.151
  92.6 0.0 collective-permute-done.19.other
  92.6 1.0 %shard_map.153 = (f32[384,128]{1,0:T(8,128)}, f32[128,128]{1,0:T(8,128)}, f32[256,128]{1,0:T(8,128)}, f32[128,128]{1,0:T(8,128)}) custom-call(f32[9,8,128]{2,1,0:T(8,128)S(1)} %get-tuple-element.56.after.rim.refs_0_, f32[448,128]{1,0:T(8,128)S(1)} %bitcast.13, f32[448,128]{1,0:T(8,128)S(1)} %collective-permute-done.19.other), custom_call_target="tpu_custom_call" | custom-call | tf_op jit(solution)/shard_map/pallas_call | solution.py:463
  (14 shorter events, 0.1 us)
Async XLA Ops:
  0.6 17.5 %copy-start.5 = (s32[8,8,8]{2,1,0:T(8,128)S(1)}, s32[8,8,8]{2,1,0:T(8,128)}, u32[]{:S(2)}) copy-start(s32[8,8,8]{2,1,0:T(8,128)} %param.11) | copy-start | bytes 6148
  0.6 17.6 %copy-start.1 = (bf16[8,8,8,128]{3,2,1,0:T(8,128)(2,1)S(1)}, bf16[8,8,8,128]{3,2,1,0:T(8,128)(2,1)}, u32[]{:S(2)}) copy-start(bf16[8,8,8,128]{3,2,1,0:T(8,128)(2,1)} %param.17) | copy-start | bytes 393220
  0.7 17.6 %copy-start = (bf16[256,128]{1,0:T(8,128)(2,1)S(1)}, bf16[256,128]{1,0:T(8,128)(2,1)}, u32[]{:S(2)}) copy-start(bf16[256,128]{1,0:T(8,128)(2,1)} %w_in.5) | copy-start | bytes 196612
  0.7 17.6 %copy-start.2 = (bf16[128,128]{1,0:T(8,128)(2,1)S(1)}, bf16[128,128]{1,0:T(8,128)(2,1)}, u32[]{:S(2)}) copy-start(bf16[128,128]{1,0:T(8,128)(2,1)} %w_out.1) | copy-start | bytes 98308
  2.9 8.5 %collective-permute-start = (f32[8,8,128]{2,1,0:T(8,128)S(1)}, f32[8,8,128]{2,1,0:T(8,128)S(1)}, u32[]{:S(2)}, u32[]{:S(2)}) collective-permute-start(f32[8,8,128]{2,1,0:T(8,128)S(1)} %get-tuple-element.61), channel_id=1, source_target_pairs={{0,4},{1,5},{2,6},{3,7},{4,0},{5,1},{6,2},{7,3},{8,12},{9,13},{10,... | collective-permute-start | bytes 98312 | tf_op jit(solution)/shard_map/ppermute | solution.py:356
  6.2 5.2 %collective-permute-start.1 = (f32[8,8,128]{2,1,0:T(8,128)S(1)}, f32[8,8,128]{2,1,0:T(8,128)S(1)}, u32[]{:S(2)}, u32[]{:S(2)}) collective-permute-start(f32[8,8,128]{2,1,0:T(8,128)S(1)} %get-tuple-element.62), channel_id=1, source_target_pairs={{0,16},{1,17},{2,18},{3,19},{4,20},{5,21},{6,22},{7,23},{8,24},{9,... | collective-permute-start | bytes 98312 | tf_op jit(solution)/shard_map/ppermute | solution.py:356
  8.1 0.7 copy-start.3
  11.4 4.1 %collective-permute-start.2 = (f32[8,8,128]{2,1,0:T(8,128)S(1)}, f32[8,8,128]{2,1,0:T(8,128)S(1)}, u32[]{:S(2)}, u32[]{:S(2)}) collective-permute-start(f32[8,8,128]{2,1,0:T(8,128)S(1)} %get-tuple-element.63), channel_id=1, source_target_pairs={{0,1},{1,0},{2,3},{3,2},{4,8},{5,9},{6,10},{7,11},{8,4},{9,5},{10,... | collective-permute-start | bytes 98312 | tf_op jit(solution)/shard_map/ppermute | solution.py:356
  13.9 1.6 %collective-permute-start.3 = (f32[8,8,128]{2,1,0:T(8,128)S(1)}, f32[8,8,128]{2,1,0:T(8,128)S(1)}, u32[]{:S(2)}, u32[]{:S(2)}) collective-permute-start(f32[8,8,128]{2,1,0:T(8,128)S(1)} %get-tuple-element.64), channel_id=1, source_target_pairs={{0,4},{1,5},{2,6},{3,7},{4,0},{5,1},{6,2},{7,3},{8,12},{9,13},{10,... | collective-permute-start | bytes 98312 | tf_op jit(solution)/shard_map/ppermute | solution.py:356
  15.6 2.9 %collective-permute-start.4 = (f32[8,8,128]{2,1,0:T(8,128)S(1)}, f32[8,8,128]{2,1,0:T(8,128)S(1)}, u32[]{:S(2)}, u32[]{:S(2)}) collective-permute-start(f32[8,8,128]{2,1,0:T(8,128)S(1)} %get-tuple-element.65), channel_id=1, source_target_pairs={{0,4},{1,2},{2,1},{3,7},{4,0},{5,6},{6,5},{7,3},{8,12},{9,10},{10,... | collective-permute-start | bytes 98312 | tf_op jit(solution)/shard_map/ppermute | solution.py:356
  16.8 2.8 %collective-permute-start.5 = (f32[8,8,128]{2,1,0:T(8,128)S(1)}, f32[8,8,128]{2,1,0:T(8,128)S(1)}, u32[]{:S(2)}, u32[]{:S(2)}) collective-permute-start(f32[8,8,128]{2,1,0:T(8,128)S(1)} %get-tuple-element.66), channel_id=1, source_target_pairs={{0,1},{1,0},{2,3},{3,2},{4,5},{5,4},{6,7},{7,6},{8,9},{9,8},{10,11... | collective-permute-start | bytes 98312 | tf_op jit(solution)/shard_map/ppermute | solution.py:356
  18.1 15.5 %copy-start.4 = (s32[4,3]{1,0:T(4,128)S(1)}, s32[4,3]{1,0:T(4,128)}, u32[]{:S(2)}) copy-start(s32[4,3]{1,0:T(4,128)} %offs.5) | copy-start | bytes 148
  20.2 4.4 %collective-permute-start.6 = (f32[8,8,128]{2,1,0:T(8,128)S(1)}, f32[8,8,128]{2,1,0:T(8,128)S(1)}, u32[]{:S(2)}, u32[]{:S(2)}) collective-permute-start(f32[8,8,128]{2,1,0:T(8,128)S(1)} %get-tuple-element.71), channel_id=1, source_target_pairs={{0,4},{1,5},{2,6},{3,7},{4,0},{5,1},{6,2},{7,3},{8,12},{9,13},{10,... | collective-permute-start | bytes 98312 | tf_op jit(solution)/shard_map/ppermute | solution.py:356
  22.4 4.3 %collective-permute-start.7 = (f32[8,8,128]{2,1,0:T(8,128)S(1)}, f32[8,8,128]{2,1,0:T(8,128)S(1)}, u32[]{:S(2)}, u32[]{:S(2)}) collective-permute-start(f32[8,8,128]{2,1,0:T(8,128)S(1)} %get-tuple-element.72), channel_id=1, source_target_pairs={{0,16},{1,17},{2,18},{3,19},{4,20},{5,21},{6,22},{7,23},{8,24},{9,... | collective-permute-start | bytes 98312 | tf_op jit(solution)/shard_map/ppermute | solution.py:356
  26.6 4.8 %collective-permute-start.8 = (f32[8,8,128]{2,1,0:T(8,128)S(1)}, f32[8,8,128]{2,1,0:T(8,128)S(1)}, u32[]{:S(2)}, u32[]{:S(2)}) collective-permute-start(f32[8,8,128]{2,1,0:T(8,128)S(1)} %get-tuple-element.73), channel_id=1, source_target_pairs={{0,1},{1,0},{2,3},{3,2},{4,8},{5,9},{6,10},{7,11},{8,4},{9,5},{10,... | collective-permute-start | bytes 98312 | tf_op jit(solution)/shard_map/ppermute | solution.py:356
  29.8 2.3 %collective-permute-start.9 = (f32[8,8,128]{2,1,0:T(8,128)S(1)}, f32[8,8,128]{2,1,0:T(8,128)S(1)}, u32[]{:S(2)}, u32[]{:S(2)}) collective-permute-start(f32[8,8,128]{2,1,0:T(8,128)S(1)} %get-tuple-element.74), channel_id=1, source_target_pairs={{0,4},{1,5},{2,6},{3,7},{4,0},{5,1},{6,2},{7,3},{8,12},{9,13},{10,... | collective-permute-start | bytes 98312 | tf_op jit(solution)/shard_map/ppermute | solution.py:356
  32.2 3.2 %collective-permute-start.10 = (f32[8,8,128]{2,1,0:T(8,128)S(1)}, f32[8,8,128]{2,1,0:T(8,128)S(1)}, u32[]{:S(2)}, u32[]{:S(2)}) collective-permute-start(f32[8,8,128]{2,1,0:T(8,128)S(1)} %get-tuple-element.75), channel_id=1, source_target_pairs={{0,4},{1,2},{2,1},{3,7},{4,0},{5,6},{6,5},{7,3},{8,12},{9,10},{10,... | collective-permute-start | bytes 98312 | tf_op jit(solution)/shard_map/ppermute | solution.py:356
  33.3 2.8 %collective-permute-start.11 = (f32[8,8,128]{2,1,0:T(8,128)S(1)}, f32[8,8,128]{2,1,0:T(8,128)S(1)}, u32[]{:S(2)}, u32[]{:S(2)}) collective-permute-start(f32[8,8,128]{2,1,0:T(8,128)S(1)} %get-tuple-element.76), channel_id=1, source_target_pairs={{0,1},{1,0},{2,3},{3,2},{4,5},{5,4},{6,7},{7,6},{8,9},{9,8},{10,11... | collective-permute-start | bytes 98312 | tf_op jit(solution)/shard_map/ppermute | solution.py:356
  37.0 2.9 %collective-permute-start.14 = (f32[448,128]{1,0:T(8,128)S(1)}, f32[448,128]{1,0:T(8,128)S(1)}, u32[]{:S(2)}, u32[]{:S(2)}) collective-permute-start(f32[448,128]{1,0:T(8,128)S(1)} %get-tuple-element.95), channel_id=1, source_target_pairs={{0,4},{1,5},{2,6},{3,7},{4,0},{5,1},{6,2},{7,3},{8,12},{9,13},{10,... | collective-permute-start | bytes 688136 | tf_op jit(solution)/shard_map/ppermute | solution.py:365
  40.6 15.5 %all-to-all-start = ((f32[16,1,3584]{2,1,0:T(1,128)}), f32[16,1,3584]{2,1,0:T(1,128)S(1)}, u32[]{:S(2)}, u32[]{:S(2)}) async-start(f32[16,1,3584]{2,1,0:T(1,128)} %bitcast.3), calls=%async_computation | async-start | bytes 458752 | tf_op jit(solution)/shard_map/all_to_all | solution.py:385
  48.3 2.6 %collective-permute-start.12 = (f32[8,8,128]{2,1,0:T(8,128)S(1)}, f32[8,8,128]{2,1,0:T(8,128)S(1)}, u32[]{:S(2)}, u32[]{:S(2)}) collective-permute-start(f32[8,8,128]{2,1,0:T(8,128)S(1)} %get-tuple-element.92.after), channel_id=1, source_target_pairs={{0,4},{1,2},{2,1},{3,7},{4,0},{5,6},{6,5},{7,3},{8,12},{9,10},{10,... | collective-permute-start | bytes 98312 | tf_op jit(solution)/shard_map/ppermute | solution.py:356
  49.1 4.0 %collective-permute-start.13 = (f32[8,8,128]{2,1,0:T(8,128)S(1)}, f32[8,8,128]{2,1,0:T(8,128)S(1)}, u32[]{:S(2)}, u32[]{:S(2)}) collective-permute-start(f32[8,8,128]{2,1,0:T(8,128)S(1)} %get-tuple-element.93), channel_id=1, source_target_pairs={{0,1},{1,0},{2,3},{3,2},{4,5},{5,4},{6,7},{7,6},{8,9},{9,8},{10,11... | collective-permute-start | bytes 98312 | tf_op jit(solution)/shard_map/ppermute | solution.py:356
  56.8 16.0 %all-to-all-start.1 = ((f32[8,1,3584]{2,1,0:T(1,128)}), f32[8,1,3584]{2,1,0:T(1,128)S(1)}, u32[]{:S(2)}, u32[]{:S(2)}) async-start(f32[8,1,3584]{2,1,0:T(1,128)} %bitcast.5), calls=%async_computation.1 | async-start | bytes 229376 | tf_op jit(solution)/shard_map/all_to_all | solution.py:385
  65.0 3.3 %collective-permute-start.15 = (f32[8,8,128]{2,1,0:T(8,128)S(1)}, f32[8,8,128]{2,1,0:T(8,128)S(1)}, u32[]{:S(2)}, u32[]{:S(2)}) collective-permute-start(f32[8,8,128]{2,1,0:T(8,128)S(1)} %get-tuple-element.96), channel_id=1, source_target_pairs={{0,1},{1,0},{2,3},{3,2},{4,8},{5,9},{6,10},{7,11},{8,4},{9,5},{10,... | collective-permute-start | bytes 98312 | tf_op jit(solution)/shard_map/ppermute | solution.py:356
  66.4 2.1 %collective-permute-start.16 = (f32[8,8,128]{2,1,0:T(8,128)S(1)}, f32[8,8,128]{2,1,0:T(8,128)S(1)}, u32[]{:S(2)}, u32[]{:S(2)}) collective-permute-start(f32[8,8,128]{2,1,0:T(8,128)S(1)} %get-tuple-element.97), channel_id=1, source_target_pairs={{0,4},{1,5},{2,6},{3,7},{4,0},{5,1},{6,2},{7,3},{8,12},{9,13},{10,... | collective-permute-start | bytes 98312 | tf_op jit(solution)/shard_map/ppermute | solution.py:356
  83.2 9.4 %collective-permute-start.19 = (f32[448,128]{1,0:T(8,128)S(1)}, f32[448,128]{1,0:T(8,128)S(1)}, u32[]{:S(2)}, u32[]{:S(2)}) collective-permute-start(f32[448,128]{1,0:T(8,128)S(1)} %bitcast.12), channel_id=1, source_target_pairs={{0,4},{1,5},{2,6},{3,7},{4,0},{5,1},{6,2},{7,3},{8,12},{9,13},{10,... | collective-permute-start | bytes 688136 | tf_op jit(solution)/shard_map/ppermute | solution.py:365
  87.5 4.1 %collective-permute-start.17 = (f32[8,8,128]{2,1,0:T(8,128)S(1)}, f32[8,8,128]{2,1,0:T(8,128)S(1)}, u32[]{:S(2)}, u32[]{:S(2)}) collective-permute-start(f32[8,8,128]{2,1,0:T(8,128)S(1)} %get-tuple-element.99), channel_id=1, source_target_pairs={{0,4},{1,5},{2,6},{3,7},{4,0},{5,1},{6,2},{7,3},{8,12},{9,13},{10,... | collective-permute-start | bytes 98312 | tf_op jit(solution)/shard_map/ppermute | solution.py:356
  87.5 4.3 %collective-permute-start.18 = (f32[8,8,128]{2,1,0:T(8,128)S(1)}, f32[8,8,128]{2,1,0:T(8,128)S(1)}, u32[]{:S(2)}, u32[]{:S(2)}) collective-permute-start(f32[8,8,128]{2,1,0:T(8,128)S(1)} %get-tuple-element.100), channel_id=1, source_target_pairs={{0,16},{1,17},{2,18},{3,19},{4,20},{5,21},{6,22},{7,23},{8,24},{9,... | collective-permute-start | bytes 98312 | tf_op jit(solution)/shard_map/ppermute | solution.py:356

commit v11 on v10

--- a/solution.py
+++ b/solution.py
@@ -95,13 +95,11 @@
 
 
 def first_rims_kernel(
-    nodes_h, edges_h, w_in_h, w_out_h, offs_h, xa, xb, rim, nodes, w_in, w_out, edges, pad, offs, sems
+    nodes_h, edges_h, w_in_h, w_out_h, offs_h, xa, xb, rim, nodes, edges, w_in, w_out, pad, offs, sems
 ):
     plane = B * B
     pairs = [(nodes_h, nodes), (w_in_h, w_in), (offs_h, offs), (w_out_h, w_out)]
-    for k in range(K):
-        for i, at in enumerate(RIMS):
-            pairs.append((edges_h.at[k, pl.ds(at, plane)], edges.at[k, pl.ds(i * plane, plane)]))
+    pairs += [(edges_h.at[k], edges.at[k]) for k in range(K)]
     copies = [pltpu.make_async_copy(a, b, sems.at[i]) for i, (a, b) in enumerate(pairs)]
     for copy in copies:
         copy.start()
@@ -115,12 +113,12 @@
     copies[3].wait()
     total = jnp.zeros((2 * plane, W), F32)
     for k in range(K):
-        copies[4 + 2 * k].wait()
-        copies[5 + 2 * k].wait()
+        copies[4 + k].wait()
         o0, o1, o2 = offs[k, 0], offs[k, 1], offs[k, 2]
         sent = jnp.concatenate([pad[pl.ds(1 + at + o0, 1), pl.ds(1 + o1, B)] for at in (0, B - 1)], axis=0)
         sent = pltpu.roll(sent.reshape(2 * B, B, W), lax.rem(B - o2, B), 1).reshape(2 * plane, W)
-        pre = sent + receiver + dot(edges[k], w_in[2 * W :])
+        edge = jnp.concatenate([edges[k, at : at + plane] for at in RIMS], axis=0)
+        pre = sent + receiver + dot(edge, w_in[2 * W :])
         act = (pre * jax.nn.sigmoid(pre)).reshape(2, B, B, W)
         kept = jnp.where(inside(offs, k, True), act, 0.0).reshape(2 * plane, W).astype(BF16)
         total = total + dot(kept, w_out[...])
@@ -128,16 +126,12 @@
     send(rim, 0, total[0], total[1], xa, xb)
 
 
-def forward_kernel(edges_h, offs, nodes, w_in, w_out, after, local, preact, hidden, edges, pad, sems):
-    copies = [pltpu.make_async_copy(edges_h.at[k], edges.at[k], sems.at[k]) for k in range(K)]
-    for copy in copies:
-        copy.start()
+def forward_kernel(offs, nodes, edges, w_in, w_out, after, local, preact, hidden, pad):
     node = nodes[...]
     fill_ring(pad, dot(node, w_in[:W]).reshape(CUBE))
     receiver = dot(node, w_in[W : 2 * W])
     total = jnp.zeros((N, W), F32)
     for k in range(K):
-        copies[k].wait()
         pre = ring_shift(pad, offs[k, 0], offs[k, 1], offs[k, 2]) + receiver + dot(edges[k], w_in[2 * W :])
         preact[k] = pre
         act = (pre * jax.nn.sigmoid(pre)).reshape(CUBE)
@@ -416,24 +410,15 @@
     square = ((W, W), BF16)
     many = ((K, N, W), BF16)
 
-    edges_all = in_hbm(edge_feat.reshape(K, N, W))
-    xa, xb, rim, nodes, w_in, w_out = call(
+    xa, xb, rim, nodes, edges, w_in, w_out = call(
         first_rims_kernel,
-        FACES + [((9, B, W), F32), ((N, W), BF16), ((3 * W, W), BF16), square],
+        FACES + [((9, B, W), F32), ((N, W), BF16), many, ((3 * W, W), BF16), square],
         [HBM] * 5,
-        [
-            pltpu.VMEM((K, 2 * B * B, W), BF16),
-            PAD,
-            pltpu.SMEM((K, 3), jnp.int32),
-            pltpu.SemaphoreType.DMA((4 + 2 * K,)),
-        ],
-    )(in_hbm(node_feat.reshape(N, W)), edges_all, in_hbm(w_edge_in), in_hbm(w_edge_out), in_hbm(offsets))
-    local, preact, hidden, edges = call(
-        forward_kernel,
-        [(CUBE, F32), ((K, N, W), F32), many, many],
-        [HBM, SMEM] + [VMEM] * 4,
-        [PAD, pltpu.SemaphoreType.DMA((K,))],
-    )(edges_all, offsets, nodes, w_in, w_out, rim)
+        [PAD, pltpu.SMEM((K, 3), jnp.int32), pltpu.SemaphoreType.DMA((4 + K,))],
+    )(*map(in_hbm, (node_feat.reshape(N, W), edge_feat.reshape(K, N, W), w_edge_in, w_edge_out, offsets)))
+    local, preact, hidden = call(
+        forward_kernel, [(CUBE, F32), ((K, N, W), F32), many], [SMEM] + [VMEM] * 5, [PAD]
+    )(offsets, nodes, edges, w_in, w_out, rim)
     begun, upstream, w_node_back = call(
         prepare_node_kernel, [((N, W), F32), ((N, W), F32), square], [VMEM] * 5
     )(nodes, cot, w_node_in, w_node_out, local)

time: 94.1 us -> 94 us (level)
  Pallas kernels: 13.8 us -> 12.5 us
  starting transfers between devices: 51 us -> 52.2 us
    pallas_call x2, Pallas kernels: 4.78 us -> 3.53 us  [the longest x1 2.17 us: on_device(): call(first_rims_kernel, FACES + [((9, B, W), F32), ((N, W), BF16), many,...]
    ppermute x18, starting transfers between devices: 29.2 us -> 30.3 us  [exchange(): lax.ppermute(face, GX + GY + GZ, [(rank, ranks[to]) for rank, to in enume...]
  transfers between devices with their start and end apart: 22 -> 22, of which waited for: 12 -> 12; matrix products, arithmetic and copies ran while one was open for 0% -> 0% of each run, Pallas kernels for 8% -> 7%
where the time goes in v11:
time: 94 us; the launch traced here: 93.5 us
  starting transfers between devices  52.2 us (56%)
  waiting for transfers between devices  16.7 us (18%)
  Pallas kernels  12.5 us (13%)
  blocking collectives  10.3 us (11%)
    ppermute x18, starting transfers between devices, exchange(): lax.ppermute(face, GX + GY + GZ, [(rank, ranks[to]) for rank, to in enume...  30.3 us
    all_to_all x2, starting transfers between devices, swap(): lax.all_to_all(rows.reshape(lax.axis_size(axes), -1), axes, 0, 0, tiled=T...  15.8 us
    all_to_all x1, blocking collectives, swap(): lax.all_to_all(rows.reshape(lax.axis_size(axes), -1), axes, 0, 0, tiled=T...  10.3 us
    ppermute x18, waiting for transfers between devices, exchange(): lax.ppermute(face, GX + GY + GZ, [(rank, ranks[to]) for rank, to in enume...  9.45 us
    all_to_all x2, waiting for transfers between devices, swap(): lax.all_to_all(rows.reshape(lax.axis_size(axes), -1), axes, 0, 0, tiled=T...  7.26 us
    ppermute x2, starting transfers between devices, other_core(): lax.ppermute(half, GX + GY + GZ, [(rank, rank ^ step) for rank in range(c...  6.09 us
    pallas_call x1, Pallas kernels, on_device(): call(first_rims_kernel, FACES + [((9, B, W), F32), ((N, W), BF16), many,...  2.17 us
  transfers between devices with their start and end apart: 22, of which 12 were waited for; matrix products, arithmetic and copies ran while one was open for 0% of the time, Pallas kernels for 7%

profile of v11, /device:TPU:1, one launch (start us, length us, event | category | flops | bytes accessed | tf_op | source)
XLA Modules:
  0.0 93.5 jit_solution(6809347069683723753)
XLA Ops:
  0.7 2.2 %shard_map.136 = (f32[8,8,128]{2,1,0:T(8,128)S(1)}, f32[8,8,128]{2,1,0:T(8,128)S(1)}, f32[9,8,128]{2,1,0:T(8,128)S(1)}, bf16[512,128]{1,0:T(8,128)(2,1)S(1)}, bf...) custom-call(bf16[512,128]{1,0:T(8,128)(2,1)} %bitcast.21, ...), custom_call_target="tpu_custom_call" | custom-call | tf_op jit(solution)/shard_map/pallas_call | solution.py:413
  2.8 3.3 %collective-permute-start = (f32[8,8,128]{2,1,0:T(8,128)S(1)}, f32[8,8,128]{2,1,0:T(8,128)S(1)}, u32[]{:S(2)}, u32[]{:S(2)}) collective-permute-start(f32[8,8,128]{2,1,0:T(8,128)S(1)} %get-tuple-element.62), channel_id=1, source_target_pairs={{0,4},{1,5},{2,6},{3,7},{4,0},{5,1},{6,2},{7,3},{8,12},{9,13},{10,... | collective-permute-start | bytes 98312 | tf_op jit(solution)/shard_map/ppermute | solution.py:350
  6.1 1.9 %collective-permute-start.1 = (f32[8,8,128]{2,1,0:T(8,128)S(1)}, f32[8,8,128]{2,1,0:T(8,128)S(1)}, u32[]{:S(2)}, u32[]{:S(2)}) collective-permute-start(f32[8,8,128]{2,1,0:T(8,128)S(1)} %get-tuple-element.63), channel_id=1, source_target_pairs={{0,16},{1,17},{2,18},{3,19},{4,20},{5,21},{6,22},{7,23},{8,24},{9,... | collective-permute-start | bytes 98312 | tf_op jit(solution)/shard_map/ppermute | solution.py:350
  8.1 0.7 copy-done.3
  8.8 1.4 %shard_map.137 = (f32[8,8,8,128]{3,2,1,0:T(8,128)S(1)}, f32[4,512,128]{2,1,0:T(8,128)S(1)}, bf16[4,512,128]{2,1,0:T(8,128)(2,1)S(1)}) custom-call(s32[4,3]{1,0:T(4,128)S(1)} %copy-done.3, bf16[512,128]{1,0:T(8,128)(2,1)S(1)} %get-tuple-element.57.nodes, bf16[4,512,128]{2,1,0:T(8,128)(2,1)S(1)} %get-tuple-element.58.edges, ...), custom_call_target="tpu_custom_call" | custom-call | tf_op jit(solution)/shard_map/pallas_call | solution.py:419
  10.1 0.0 collective-permute-done.x0
  10.1 0.3 collective-permute-done.1.x1
  10.4 2.3 %collective-permute-start.2 = (f32[8,8,128]{2,1,0:T(8,128)S(1)}, f32[8,8,128]{2,1,0:T(8,128)S(1)}, u32[]{:S(2)}, u32[]{:S(2)}) collective-permute-start(f32[8,8,128]{2,1,0:T(8,128)S(1)} %get-tuple-element.64), channel_id=1, source_target_pairs={{0,1},{1,0},{2,3},{3,2},{4,8},{5,9},{6,10},{7,11},{8,4},{9,5},{10,... | collective-permute-start | bytes 98312 | tf_op jit(solution)/shard_map/ppermute | solution.py:350
  12.7 0.3 collective-permute-start.3
  13.0 1.3 %collective-permute-done.2.y0 = f32[8,8,128]{2,1,0:T(8,128)S(1)} collective-permute-done((f32[8,8,128]{2,1,0:T(8,128)S(1)}, f32[8,8,128]{2,1,0:T(8,128)S(1)}, u32[]{:S(2)}, u32[]{:S(2)}) %collective-permute-start.2) | collective-permute-done | bytes 32800 | tf_op jit(solution)/shard_map/ppermute | solution.py:350
  14.3 0.0 collective-permute-done.3.y1
  14.3 0.1 shard_map.139
  14.4 1.5 %collective-permute-start.4 = (f32[8,8,128]{2,1,0:T(8,128)S(1)}, f32[8,8,128]{2,1,0:T(8,128)S(1)}, u32[]{:S(2)}, u32[]{:S(2)}) collective-permute-start(f32[8,8,128]{2,1,0:T(8,128)S(1)} %get-tuple-element.66), channel_id=1, source_target_pairs={{0,4},{1,2},{2,1},{3,7},{4,0},{5,6},{6,5},{7,3},{8,12},{9,10},{10,... | collective-permute-start | bytes 98312 | tf_op jit(solution)/shard_map/ppermute | solution.py:350
  15.9 1.0 %collective-permute-start.5 = (f32[8,8,128]{2,1,0:T(8,128)S(1)}, f32[8,8,128]{2,1,0:T(8,128)S(1)}, u32[]{:S(2)}, u32[]{:S(2)}) collective-permute-start(f32[8,8,128]{2,1,0:T(8,128)S(1)} %get-tuple-element.67), channel_id=1, source_target_pairs={{0,1},{1,0},{2,3},{3,2},{4,5},{5,4},{6,7},{7,6},{8,9},{9,8},{10,11... | collective-permute-start | bytes 98312 | tf_op jit(solution)/shard_map/ppermute | solution.py:350
  16.9 0.0 copy-start.4
  16.9 0.1 div.16
  17.0 0.2 shard_map.140
  17.2 0.0 collective-permute-done.4.z0
  17.3 1.4 %collective-permute-done.5.z1 = f32[8,8,128]{2,1,0:T(8,128)S(1)} collective-permute-done((f32[8,8,128]{2,1,0:T(8,128)S(1)}, f32[8,8,128]{2,1,0:T(8,128)S(1)}, u32[]{:S(2)}, u32[]{:S(2)}) %collective-permute-start.5) | collective-permute-done | bytes 32800 | tf_op jit(solution)/shard_map/ppermute | solution.py:350
  18.6 0.1 broadcast_in_dim.2.inverse
  18.7 0.4 shard_map.141
  19.2 1.9 %collective-permute-start.6 = (f32[8,8,128]{2,1,0:T(8,128)S(1)}, f32[8,8,128]{2,1,0:T(8,128)S(1)}, u32[]{:S(2)}, u32[]{:S(2)}) collective-permute-start(f32[8,8,128]{2,1,0:T(8,128)S(1)} %get-tuple-element.72), channel_id=1, source_target_pairs={{0,4},{1,5},{2,6},{3,7},{4,0},{5,1},{6,2},{7,3},{8,12},{9,13},{10,... | collective-permute-start | bytes 98312 | tf_op jit(solution)/shard_map/ppermute | solution.py:350
  21.1 3.4 %collective-permute-start.7 = (f32[8,8,128]{2,1,0:T(8,128)S(1)}, f32[8,8,128]{2,1,0:T(8,128)S(1)}, u32[]{:S(2)}, u32[]{:S(2)}) collective-permute-start(f32[8,8,128]{2,1,0:T(8,128)S(1)} %get-tuple-element.73), channel_id=1, source_target_pairs={{0,16},{1,17},{2,18},{3,19},{4,20},{5,21},{6,22},{7,23},{8,24},{9,... | collective-permute-start | bytes 98312 | tf_op jit(solution)/shard_map/ppermute | solution.py:350
  24.5 0.0 collective-permute-done.6.x0
  24.5 1.3 %collective-permute-done.7.x1 = f32[8,8,128]{2,1,0:T(8,128)S(1)} collective-permute-done((f32[8,8,128]{2,1,0:T(8,128)S(1)}, f32[8,8,128]{2,1,0:T(8,128)S(1)}, u32[]{:S(2)}, u32[]{:S(2)}) %collective-permute-start.7) | collective-permute-done | bytes 32800 | tf_op jit(solution)/shard_map/ppermute | solution.py:350
  25.8 3.1 %collective-permute-start.8 = (f32[8,8,128]{2,1,0:T(8,128)S(1)}, f32[8,8,128]{2,1,0:T(8,128)S(1)}, u32[]{:S(2)}, u32[]{:S(2)}) collective-permute-start(f32[8,8,128]{2,1,0:T(8,128)S(1)} %get-tuple-element.74), channel_id=1, source_target_pairs={{0,1},{1,0},{2,3},{3,2},{4,8},{5,9},{6,10},{7,11},{8,4},{9,5},{10,... | collective-permute-start | bytes 98312 | tf_op jit(solution)/shard_map/ppermute | solution.py:350
  28.9 2.3 %collective-permute-start.9 = (f32[8,8,128]{2,1,0:T(8,128)S(1)}, f32[8,8,128]{2,1,0:T(8,128)S(1)}, u32[]{:S(2)}, u32[]{:S(2)}) collective-permute-start(f32[8,8,128]{2,1,0:T(8,128)S(1)} %get-tuple-element.75), channel_id=1, source_target_pairs={{0,4},{1,5},{2,6},{3,7},{4,0},{5,1},{6,2},{7,3},{8,12},{9,13},{10,... | collective-permute-start | bytes 98312 | tf_op jit(solution)/shard_map/ppermute | solution.py:350
  31.2 0.9 collective-permute-done.9.y1
  32.1 0.1 shard_map.143
  32.1 1.1 %collective-permute-start.10 = (f32[8,8,128]{2,1,0:T(8,128)S(1)}, f32[8,8,128]{2,1,0:T(8,128)S(1)}, u32[]{:S(2)}, u32[]{:S(2)}) collective-permute-start(f32[8,8,128]{2,1,0:T(8,128)S(1)} %get-tuple-element.76), channel_id=1, source_target_pairs={{0,4},{1,2},{2,1},{3,7},{4,0},{5,6},{6,5},{7,3},{8,12},{9,10},{10,... | collective-permute-start | bytes 98312 | tf_op jit(solution)/shard_map/ppermute | solution.py:350
  33.3 0.0 collective-permute-start.11
  33.3 1.5 %shard_map.144 = (f32[4,512,128]{2,1,0:T(8,128)S(1)}, bf16[512,512]{1,0:T(8,128)(2,1)S(1)}, bf16[384,2048]{1,0:T(8,128)(2,1)S(1)}, bf16[128,128]{1,0:T(8,128)(2,1)S(1)}, bf16[256,128]{1,0:T(8,128)(2,1)S(1)}) custom-call(s32[4,3]{1,0:T(4,128)S(1)} %copy-done.4, f32[4,512,128]{2,1,0:T(8,128)S(1)} %get-tuple-element.78.preact, ...), custom_call_target="tpu_custom_call" | custom-call | tf_op jit(solution)/shard_map/pallas_call | solution.py:426
  34.7 0.3 shard_map.145
  35.1 0.0 collective-permute-done.10.z0
  35.1 0.9 %collective-permute-done.11.z1 = f32[8,8,128]{2,1,0:T(8,128)S(1)} collective-permute-done((f32[8,8,128]{2,1,0:T(8,128)S(1)}, f32[8,8,128]{2,1,0:T(8,128)S(1)}, u32[]{:S(2)}, u32[]{:S(2)}) %collective-permute-start.11) | collective-permute-done | bytes 32800 | tf_op jit(solution)/shard_map/ppermute | solution.py:350
  36.0 0.9 shard_map.146
  36.9 1.8 %collective-permute-start.14 = (f32[448,128]{1,0:T(8,128)S(1)}, f32[448,128]{1,0:T(8,128)S(1)}, u32[]{:S(2)}, u32[]{:S(2)}) collective-permute-start(f32[448,128]{1,0:T(8,128)S(1)} %get-tuple-element.95), channel_id=1, source_target_pairs={{0,4},{1,5},{2,6},{3,7},{4,0},{5,1},{6,2},{7,3},{8,12},{9,13},{10,... | collective-permute-start | bytes 688136 | tf_op jit(solution)/shard_map/ppermute | solution.py:359
  38.7 1.2 %shard_map.147 = (f32[8,8,8,128]{3,2,1,0:T(8,128)S(1)}, f32[8,8,128]{2,1,0:T(8,128)S(1)}, f32[8,8,128]{2,1,0:T(8,128)S(1)}) custom-call(s32[4,3]{1,0:T(4,128)S(1)} %copy-done.4, f32[9,8,128]{2,1,0:T(8,128)S(1)} %get-tuple-element.56.after.rim.refs_0_, bf16[2048,128]{1,0:T(8,128)(2,1)S(1)} %get-tuple-element.88.slopes, ...), custom_call_target="tpu_custom_call" | custom-call | tf_op jit(solution)/shard_map/pallas_call | solution.py:443
  39.9 0.0 collective-permute-done.14.got
  39.9 0.7 shard_map.148
  40.6 7.6 %all-to-all-start = ((f32[16,1,3584]{2,1,0:T(1,128)}), f32[16,1,3584]{2,1,0:T(1,128)S(1)}, u32[]{:S(2)}, u32[]{:S(2)}) async-start(f32[16,1,3584]{2,1,0:T(1,128)} %bitcast.3), calls=%async_computation | async-start | bytes 458752 | tf_op jit(solution)/shard_map/all_to_all | solution.py:379
  48.2 0.9 collective-permute-start.12
  49.1 1.7 %collective-permute-start.13 = (f32[8,8,128]{2,1,0:T(8,128)S(1)}, f32[8,8,128]{2,1,0:T(8,128)S(1)}, u32[]{:S(2)}, u32[]{:S(2)}) collective-permute-start(f32[8,8,128]{2,1,0:T(8,128)S(1)} %get-tuple-element.93), channel_id=1, source_target_pairs={{0,1},{1,0},{2,3},{3,2},{4,5},{5,4},{6,7},{7,6},{8,9},{9,8},{10,11... | collective-permute-start | bytes 98312 | tf_op jit(solution)/shard_map/ppermute | solution.py:350
  50.8 0.0 collective-permute-done.12.refs_2_.z0
  50.8 2.4 %collective-permute-done.13.refs_3_.z1 = f32[8,8,128]{2,1,0:T(8,128)S(1)} collective-permute-done((f32[8,8,128]{2,1,0:T(8,128)S(1)}, f32[8,8,128]{2,1,0:T(8,128)S(1)}, u32[]{:S(2)}, u32[]{:S(2)}) %collective-permute-start.13) | collective-permute-done | bytes 32800 | tf_op jit(solution)/shard_map/ppermute | solution.py:350
  53.1 2.9 %all-to-all-done = f32[16,1,3584]{2,1,0:T(1,128)S(1)} async-done(((f32[16,1,3584]{2,1,0:T(1,128)}), f32[16,1,3584]{2,1,0:T(1,128)S(1)}, u32[]{:S(2)}, u32[]{:S(2)}) %all-to-all-start) | async-done | bytes 229408 | tf_op jit(solution)/shard_map/all_to_all | solution.py:379
  56.0 0.7 shard_map.149
  56.7 8.2 %all-to-all-start.1 = ((f32[8,1,3584]{2,1,0:T(1,128)}), f32[8,1,3584]{2,1,0:T(1,128)S(1)}, u32[]{:S(2)}, u32[]{:S(2)}) async-start(f32[8,1,3584]{2,1,0:T(1,128)} %bitcast.5), calls=%async_computation.1 | async-start | bytes 229376 | tf_op jit(solution)/shard_map/all_to_all | solution.py:379
  64.9 1.3 %collective-permute-start.15 = (f32[8,8,128]{2,1,0:T(8,128)S(1)}, f32[8,8,128]{2,1,0:T(8,128)S(1)}, u32[]{:S(2)}, u32[]{:S(2)}) collective-permute-start(f32[8,8,128]{2,1,0:T(8,128)S(1)} %get-tuple-element.96), channel_id=1, source_target_pairs={{0,1},{1,0},{2,3},{3,2},{4,8},{5,9},{6,10},{7,11},{8,4},{9,5},{10,... | collective-permute-start | bytes 98312 | tf_op jit(solution)/shard_map/ppermute | solution.py:350
  66.2 1.3 %collective-permute-start.16 = (f32[8,8,128]{2,1,0:T(8,128)S(1)}, f32[8,8,128]{2,1,0:T(8,128)S(1)}, u32[]{:S(2)}, u32[]{:S(2)}) collective-permute-start(f32[8,8,128]{2,1,0:T(8,128)S(1)} %get-tuple-element.97), channel_id=1, source_target_pairs={{0,4},{1,5},{2,6},{3,7},{4,0},{5,1},{6,2},{7,3},{8,12},{9,13},{10,... | collective-permute-start | bytes 98312 | tf_op jit(solution)/shard_map/ppermute | solution.py:350
  67.6 0.7 collective-permute-done.15.refs_4_.y0
  68.2 0.2 collective-permute-done.16.refs_5_.y1
  68.4 4.3 %all-to-all-done.1 = f32[8,1,3584]{2,1,0:T(1,128)S(1)} async-done(((f32[8,1,3584]{2,1,0:T(1,128)}), f32[8,1,3584]{2,1,0:T(1,128)S(1)}, u32[]{:S(2)}, u32[]{:S(2)}) %all-to-all-start.1) | async-done | bytes 114720 | tf_op jit(solution)/shard_map/all_to_all | solution.py:379
  72.8 0.1 shard_map.150
  72.8 10.3 %all_to_all.27 = f32[16,1,3584]{2,1,0:T(1,128)S(1)} all-to-all(f32[16,1,3584]{2,1,0:T(1,128)S(1)} %bitcast.17), channel_id=1, replica_groups=mesh['z'=8,'yh'=2,'yl'=2,'c'=2,'x'=4] {'yh','yl','x'}, dimensions={0} | all-to-all | bytes 458752 | tf_op jit(solution)/shard_map/all_to_all | solution.py:379
  83.2 4.3 %collective-permute-start.19 = (f32[448,128]{1,0:T(8,128)S(1)}, f32[448,128]{1,0:T(8,128)S(1)}, u32[]{:S(2)}, u32[]{:S(2)}) collective-permute-start(f32[448,128]{1,0:T(8,128)S(1)} %bitcast.12), channel_id=1, source_target_pairs={{0,4},{1,5},{2,6},{3,7},{4,0},{5,1},{6,2},{7,3},{8,12},{9,13},{10,... | collective-permute-start | bytes 688136 | tf_op jit(solution)/shard_map/ppermute | solution.py:359
  87.5 0.0 collective-permute-start.17
  87.5 3.0 %collective-permute-start.18 = (f32[8,8,128]{2,1,0:T(8,128)S(1)}, f32[8,8,128]{2,1,0:T(8,128)S(1)}, u32[]{:S(2)}, u32[]{:S(2)}) collective-permute-start(f32[8,8,128]{2,1,0:T(8,128)S(1)} %get-tuple-element.100), channel_id=1, source_target_pairs={{0,16},{1,17},{2,18},{3,19},{4,20},{5,21},{6,22},{7,23},{8,24},{9,... | collective-permute-start | bytes 98312 | tf_op jit(solution)/shard_map/ppermute | solution.py:350
  90.4 1.1 %shard_map.152 = bf16[2048,128]{1,0:T(8,128)(2,1)} custom-call(bf16[2048,128]{1,0:T(8,128)(2,1)S(1)} %get-tuple-element.88.slopes, bf16[384,128]{1,0:T(8,128)(2,1)S(1)} %get-tuple-element.59.w_in), custom_call_target="tpu_custom_call" | custom-call | tf_op jit(solution)/shard_map/pallas_call | solution.py:446
  91.5 0.0 collective-permute-done.17.x0
  91.5 0.2 collective-permute-done.18.x1
  91.7 0.8 shard_map.151
  92.5 0.0 collective-permute-done.19.other
  92.5 1.0 %shard_map.153 = (f32[384,128]{1,0:T(8,128)}, f32[128,128]{1,0:T(8,128)}, f32[256,128]{1,0:T(8,128)}, f32[128,128]{1,0:T(8,128)}) custom-call(f32[9,8,128]{2,1,0:T(8,128)S(1)} %get-tuple-element.56.after.rim.refs_0_, f32[448,128]{1,0:T(8,128)S(1)} %bitcast.13, f32[448,128]{1,0:T(8,128)S(1)} %collective-permute-done.19.other), custom_call_target="tpu_custom_call" | custom-call | tf_op jit(solution)/shard_map/pallas_call | solution.py:448
  (14 shorter events, 0.1 us)
Async XLA Ops:
  0.6 16.2 %copy-start.5 = (s32[8,8,8]{2,1,0:T(8,128)S(1)}, s32[8,8,8]{2,1,0:T(8,128)}, u32[]{:S(2)}) copy-start(s32[8,8,8]{2,1,0:T(8,128)} %param.11) | copy-start | bytes 6148
  0.6 16.4 %copy-start.1 = (bf16[8,8,8,128]{3,2,1,0:T(8,128)(2,1)S(1)}, bf16[8,8,8,128]{3,2,1,0:T(8,128)(2,1)}, u32[]{:S(2)}) copy-start(bf16[8,8,8,128]{3,2,1,0:T(8,128)(2,1)} %param.17) | copy-start | bytes 393220
  0.7 16.4 %copy-start = (bf16[256,128]{1,0:T(8,128)(2,1)S(1)}, bf16[256,128]{1,0:T(8,128)(2,1)}, u32[]{:S(2)}) copy-start(bf16[256,128]{1,0:T(8,128)(2,1)} %w_in.5) | copy-start | bytes 196612
  0.7 16.4 %copy-start.2 = (bf16[128,128]{1,0:T(8,128)(2,1)S(1)}, bf16[128,128]{1,0:T(8,128)(2,1)}, u32[]{:S(2)}) copy-start(bf16[128,128]{1,0:T(8,128)(2,1)} %w_out.1) | copy-start | bytes 98308
  2.8 7.3 %collective-permute-start = (f32[8,8,128]{2,1,0:T(8,128)S(1)}, f32[8,8,128]{2,1,0:T(8,128)S(1)}, u32[]{:S(2)}, u32[]{:S(2)}) collective-permute-start(f32[8,8,128]{2,1,0:T(8,128)S(1)} %get-tuple-element.62), channel_id=1, source_target_pairs={{0,4},{1,5},{2,6},{3,7},{4,0},{5,1},{6,2},{7,3},{8,12},{9,13},{10,... | collective-permute-start | bytes 98312 | tf_op jit(solution)/shard_map/ppermute | solution.py:350
  6.1 4.3 %collective-permute-start.1 = (f32[8,8,128]{2,1,0:T(8,128)S(1)}, f32[8,8,128]{2,1,0:T(8,128)S(1)}, u32[]{:S(2)}, u32[]{:S(2)}) collective-permute-start(f32[8,8,128]{2,1,0:T(8,128)S(1)} %get-tuple-element.63), channel_id=1, source_target_pairs={{0,16},{1,17},{2,18},{3,19},{4,20},{5,21},{6,22},{7,23},{8,24},{9,... | collective-permute-start | bytes 98312 | tf_op jit(solution)/shard_map/ppermute | solution.py:350
  8.1 0.7 copy-start.3
  10.4 3.9 %collective-permute-start.2 = (f32[8,8,128]{2,1,0:T(8,128)S(1)}, f32[8,8,128]{2,1,0:T(8,128)S(1)}, u32[]{:S(2)}, u32[]{:S(2)}) collective-permute-start(f32[8,8,128]{2,1,0:T(8,128)S(1)} %get-tuple-element.64), channel_id=1, source_target_pairs={{0,1},{1,0},{2,3},{3,2},{4,8},{5,9},{6,10},{7,11},{8,4},{9,5},{10,... | collective-permute-start | bytes 98312 | tf_op jit(solution)/shard_map/ppermute | solution.py:350
  12.7 1.6 %collective-permute-start.3 = (f32[8,8,128]{2,1,0:T(8,128)S(1)}, f32[8,8,128]{2,1,0:T(8,128)S(1)}, u32[]{:S(2)}, u32[]{:S(2)}) collective-permute-start(f32[8,8,128]{2,1,0:T(8,128)S(1)} %get-tuple-element.65), channel_id=1, source_target_pairs={{0,4},{1,5},{2,6},{3,7},{4,0},{5,1},{6,2},{7,3},{8,12},{9,13},{10,... | collective-permute-start | bytes 98312 | tf_op jit(solution)/shard_map/ppermute | solution.py:350
  14.4 2.9 %collective-permute-start.4 = (f32[8,8,128]{2,1,0:T(8,128)S(1)}, f32[8,8,128]{2,1,0:T(8,128)S(1)}, u32[]{:S(2)}, u32[]{:S(2)}) collective-permute-start(f32[8,8,128]{2,1,0:T(8,128)S(1)} %get-tuple-element.66), channel_id=1, source_target_pairs={{0,4},{1,2},{2,1},{3,7},{4,0},{5,6},{6,5},{7,3},{8,12},{9,10},{10,... | collective-permute-start | bytes 98312 | tf_op jit(solution)/shard_map/ppermute | solution.py:350
  15.9 2.8 %collective-permute-start.5 = (f32[8,8,128]{2,1,0:T(8,128)S(1)}, f32[8,8,128]{2,1,0:T(8,128)S(1)}, u32[]{:S(2)}, u32[]{:S(2)}) collective-permute-start(f32[8,8,128]{2,1,0:T(8,128)S(1)} %get-tuple-element.67), channel_id=1, source_target_pairs={{0,1},{1,0},{2,3},{3,2},{4,5},{5,4},{6,7},{7,6},{8,9},{9,8},{10,11... | collective-permute-start | bytes 98312 | tf_op jit(solution)/shard_map/ppermute | solution.py:350
  16.9 16.4 %copy-start.4 = (s32[4,3]{1,0:T(4,128)S(1)}, s32[4,3]{1,0:T(4,128)}, u32[]{:S(2)}) copy-start(s32[4,3]{1,0:T(4,128)} %offs.5) | copy-start | bytes 148
  19.2 5.3 %collective-permute-start.6 = (f32[8,8,128]{2,1,0:T(8,128)S(1)}, f32[8,8,128]{2,1,0:T(8,128)S(1)}, u32[]{:S(2)}, u32[]{:S(2)}) collective-permute-start(f32[8,8,128]{2,1,0:T(8,128)S(1)} %get-tuple-element.72), channel_id=1, source_target_pairs={{0,4},{1,5},{2,6},{3,7},{4,0},{5,1},{6,2},{7,3},{8,12},{9,13},{10,... | collective-permute-start | bytes 98312 | tf_op jit(solution)/shard_map/ppermute | solution.py:350
  21.1 4.7 %collective-permute-start.7 = (f32[8,8,128]{2,1,0:T(8,128)S(1)}, f32[8,8,128]{2,1,0:T(8,128)S(1)}, u32[]{:S(2)}, u32[]{:S(2)}) collective-permute-start(f32[8,8,128]{2,1,0:T(8,128)S(1)} %get-tuple-element.73), channel_id=1, source_target_pairs={{0,16},{1,17},{2,18},{3,19},{4,20},{5,21},{6,22},{7,23},{8,24},{9,... | collective-permute-start | bytes 98312 | tf_op jit(solution)/shard_map/ppermute | solution.py:350
  25.8 5.4 %collective-permute-start.8 = (f32[8,8,128]{2,1,0:T(8,128)S(1)}, f32[8,8,128]{2,1,0:T(8,128)S(1)}, u32[]{:S(2)}, u32[]{:S(2)}) collective-permute-start(f32[8,8,128]{2,1,0:T(8,128)S(1)} %get-tuple-element.74), channel_id=1, source_target_pairs={{0,1},{1,0},{2,3},{3,2},{4,8},{5,9},{6,10},{7,11},{8,4},{9,5},{10,... | collective-permute-start | bytes 98312 | tf_op jit(solution)/shard_map/ppermute | solution.py:350
  28.9 3.2 %collective-permute-start.9 = (f32[8,8,128]{2,1,0:T(8,128)S(1)}, f32[8,8,128]{2,1,0:T(8,128)S(1)}, u32[]{:S(2)}, u32[]{:S(2)}) collective-permute-start(f32[8,8,128]{2,1,0:T(8,128)S(1)} %get-tuple-element.75), channel_id=1, source_target_pairs={{0,4},{1,5},{2,6},{3,7},{4,0},{5,1},{6,2},{7,3},{8,12},{9,13},{10,... | collective-permute-start | bytes 98312 | tf_op jit(solution)/shard_map/ppermute | solution.py:350
  32.1 2.9 %collective-permute-start.10 = (f32[8,8,128]{2,1,0:T(8,128)S(1)}, f32[8,8,128]{2,1,0:T(8,128)S(1)}, u32[]{:S(2)}, u32[]{:S(2)}) collective-permute-start(f32[8,8,128]{2,1,0:T(8,128)S(1)} %get-tuple-element.76), channel_id=1, source_target_pairs={{0,4},{1,2},{2,1},{3,7},{4,0},{5,6},{6,5},{7,3},{8,12},{9,10},{10,... | collective-permute-start | bytes 98312 | tf_op jit(solution)/shard_map/ppermute | solution.py:350
  33.3 2.8 %collective-permute-start.11 = (f32[8,8,128]{2,1,0:T(8,128)S(1)}, f32[8,8,128]{2,1,0:T(8,128)S(1)}, u32[]{:S(2)}, u32[]{:S(2)}) collective-permute-start(f32[8,8,128]{2,1,0:T(8,128)S(1)} %get-tuple-element.77), channel_id=1, source_target_pairs={{0,1},{1,0},{2,3},{3,2},{4,5},{5,4},{6,7},{7,6},{8,9},{9,8},{10,11... | collective-permute-start | bytes 98312 | tf_op jit(solution)/shard_map/ppermute | solution.py:350
  36.9 2.9 %collective-permute-start.14 = (f32[448,128]{1,0:T(8,128)S(1)}, f32[448,128]{1,0:T(8,128)S(1)}, u32[]{:S(2)}, u32[]{:S(2)}) collective-permute-start(f32[448,128]{1,0:T(8,128)S(1)} %get-tuple-element.95), channel_id=1, source_target_pairs={{0,4},{1,5},{2,6},{3,7},{4,0},{5,1},{6,2},{7,3},{8,12},{9,13},{10,... | collective-permute-start | bytes 688136 | tf_op jit(solution)/shard_map/ppermute | solution.py:359
  40.6 15.5 %all-to-all-start = ((f32[16,1,3584]{2,1,0:T(1,128)}), f32[16,1,3584]{2,1,0:T(1,128)S(1)}, u32[]{:S(2)}, u32[]{:S(2)}) async-start(f32[16,1,3584]{2,1,0:T(1,128)} %bitcast.3), calls=%async_computation | async-start | bytes 458752 | tf_op jit(solution)/shard_map/all_to_all | solution.py:379
  48.2 2.6 %collective-permute-start.12 = (f32[8,8,128]{2,1,0:T(8,128)S(1)}, f32[8,8,128]{2,1,0:T(8,128)S(1)}, u32[]{:S(2)}, u32[]{:S(2)}) collective-permute-start(f32[8,8,128]{2,1,0:T(8,128)S(1)} %get-tuple-element.92.after), channel_id=1, source_target_pairs={{0,4},{1,2},{2,1},{3,7},{4,0},{5,6},{6,5},{7,3},{8,12},{9,10},{10,... | collective-permute-start | bytes 98312 | tf_op jit(solution)/shard_map/ppermute | solution.py:350
  49.1 4.0 %collective-permute-start.13 = (f32[8,8,128]{2,1,0:T(8,128)S(1)}, f32[8,8,128]{2,1,0:T(8,128)S(1)}, u32[]{:S(2)}, u32[]{:S(2)}) collective-permute-start(f32[8,8,128]{2,1,0:T(8,128)S(1)} %get-tuple-element.93), channel_id=1, source_target_pairs={{0,1},{1,0},{2,3},{3,2},{4,5},{5,4},{6,7},{7,6},{8,9},{9,8},{10,11... | collective-permute-start | bytes 98312 | tf_op jit(solution)/shard_map/ppermute | solution.py:350
  56.7 16.0 %all-to-all-start.1 = ((f32[8,1,3584]{2,1,0:T(1,128)}), f32[8,1,3584]{2,1,0:T(1,128)S(1)}, u32[]{:S(2)}, u32[]{:S(2)}) async-start(f32[8,1,3584]{2,1,0:T(1,128)} %bitcast.5), calls=%async_computation.1 | async-start | bytes 229376 | tf_op jit(solution)/shard_map/all_to_all | solution.py:379
  64.9 3.3 %collective-permute-start.15 = (f32[8,8,128]{2,1,0:T(8,128)S(1)}, f32[8,8,128]{2,1,0:T(8,128)S(1)}, u32[]{:S(2)}, u32[]{:S(2)}) collective-permute-start(f32[8,8,128]{2,1,0:T(8,128)S(1)} %get-tuple-element.96), channel_id=1, source_target_pairs={{0,1},{1,0},{2,3},{3,2},{4,8},{5,9},{6,10},{7,11},{8,4},{9,5},{10,... | collective-permute-start | bytes 98312 | tf_op jit(solution)/shard_map/ppermute | solution.py:350
  66.2 2.2 %collective-permute-start.16 = (f32[8,8,128]{2,1,0:T(8,128)S(1)}, f32[8,8,128]{2,1,0:T(8,128)S(1)}, u32[]{:S(2)}, u32[]{:S(2)}) collective-permute-start(f32[8,8,128]{2,1,0:T(8,128)S(1)} %get-tuple-element.97), channel_id=1, source_target_pairs={{0,4},{1,5},{2,6},{3,7},{4,0},{5,1},{6,2},{7,3},{8,12},{9,13},{10,... | collective-permute-start | bytes 98312 | tf_op jit(solution)/shard_map/ppermute | solution.py:350
  83.2 9.4 %collective-permute-start.19 = (f32[448,128]{1,0:T(8,128)S(1)}, f32[448,128]{1,0:T(8,128)S(1)}, u32[]{:S(2)}, u32[]{:S(2)}) collective-permute-start(f32[448,128]{1,0:T(8,128)S(1)} %bitcast.12), channel_id=1, source_target_pairs={{0,4},{1,5},{2,6},{3,7},{4,0},{5,1},{6,2},{7,3},{8,12},{9,13},{10,... | collective-permute-start | bytes 688136 | tf_op jit(solution)/shard_map/ppermute | solution.py:359
  87.5 4.1 %collective-permute-start.17 = (f32[8,8,128]{2,1,0:T(8,128)S(1)}, f32[8,8,128]{2,1,0:T(8,128)S(1)}, u32[]{:S(2)}, u32[]{:S(2)}) collective-permute-start(f32[8,8,128]{2,1,0:T(8,128)S(1)} %get-tuple-element.99), channel_id=1, source_target_pairs={{0,4},{1,5},{2,6},{3,7},{4,0},{5,1},{6,2},{7,3},{8,12},{9,13},{10,... | collective-permute-start | bytes 98312 | tf_op jit(solution)/shard_map/ppermute | solution.py:350
  87.5 4.3 %collective-permute-start.18 = (f32[8,8,128]{2,1,0:T(8,128)S(1)}, f32[8,8,128]{2,1,0:T(8,128)S(1)}, u32[]{:S(2)}, u32[]{:S(2)}) collective-permute-start(f32[8,8,128]{2,1,0:T(8,128)S(1)} %get-tuple-element.100), channel_id=1, source_target_pairs={{0,16},{1,17},{2,18},{3,19},{4,20},{5,21},{6,22},{7,23},{8,24},{9,... | collective-permute-start | bytes 98312 | tf_op jit(solution)/shard_map/ppermute | solution.py:350
